TPU v7x, 256 devices: a whole 4x4x8 slice. The times are simulated.
256 devices in a mesh: rep: 16 (over z_lo, y, core), shard: 16 (over x, z_hi).
Axes of the slice: x: 4, y: 4, z: 8 (z_hi: 4, z_lo: 2; z = z_hi * 2 + z_lo), core: 2. Of those that a mesh axis runs over, the one named last changes fastest.
Arguments:
- hidden: bfloat16 [114688, 3584], P(('rep', 'shard')), may hold values from -144 to 144
- cotangent: bfloat16 [114688, 1024], P(('rep', 'shard')), may hold values from -6 to 6
- seq_ids: int32 [256, 448], P(('rep', 'shard')), may hold values from 0 to 3, as said below
- response_mask: int32 [256, 448], P(('rep', 'shard')), may hold values from 0 to 1, as said below
- group_ids: int32 [256, 4], P(('rep', 'shard')), may hold values from 0 to 127
- rewards: float32 [256, 4], P(('rep', 'shard')), may hold values from -6 to 6
- new_logp: float32 [256, 448], P(('rep', 'shard')), may hold values from -1.5 to -0.1
- old_logp: float32 [256, 448], P(('rep', 'shard')), may hold values from -1.5 to -0.1
- ref_logp: float32 [256, 448], P(('rep', 'shard')), may hold values from -1.5 to -0.1
- master: float32 [3, 3584, 1024], P(None, 'shard'), may hold values from -6 to 6
Outputs:
- new_master: float32 [3584, 1024], P('shard')
- rollout: bfloat16 [3, 3584, 4096], P(None, None, 'shard')
Inputs may be any that keep to these rules, and one draw needn't show every extreme that they name: `seq_ids`: each row numbers its device's 4 sequences in token order, never falling, each with one token or more. `response_mask`: within a sequence, prompt tokens come before response tokens; a sequence may have no response tokens.
All inputs are finite; a program needn't handle non-finite values.
Results may differ from a plain program's by a relative error of at most 0.0095.
Values may be sent and summed in bfloat16 or wider, within the bound.
No kernel may reach another device: no remote copies, remote signals or barrier semaphores. Data moves between devices by JAX's collectives and lax.ppermute only.
A program may use at most 128 MiB of HBM per device.

v0:
```python
import jax
import jax.numpy as jnp
from jax import lax
from jax.sharding import Mesh
from jax.sharding import PartitionSpec as P

HEAD = 128
KV_HEADS = 4
TP = 8
SEQ_DEV = 4
SHARD = ("shard_0", "shard_1")
REP = ("rep_0", "rep_1", "rep_2")
REP_SHARD = ("rep_0", "rep_1", "rep_2", "shard_0", "shard_1")


def one_axis_at_a_time(shard, axes):
    for axis in axes:
        shard = lax.psum(shard, axis)
    return shard


def sum_by_axis(terms, axes):
    so_far = terms.astype(jnp.bfloat16)
    for axis in axes:
        so_far = lax.psum_scatter(so_far, axis, scatter_dimension=0, tiled=True)
    return so_far.astype(jnp.float32)


def sent_to_all(shard, axis):
    copies = jnp.broadcast_to(shard, (lax.axis_size(axis), *shard.shape))
    return lax.all_to_all(copies, axis, split_axis=0, concat_axis=0, tiled=True)


def of_everyone(shard, axis):
    return sent_to_all(shard, axis).sum(axis=0)


def token_coef(seq_row, mask_row, adv_row, new_row, old_row, ref_row):
    onehot = (seq_row[:, None] == jnp.arange(SEQ_DEV, dtype=jnp.int32)[None, :]).astype(jnp.float32)
    maskf = mask_row.astype(jnp.float32)
    lengths = jnp.maximum(jnp.dot(maskf, onehot, precision=lax.Precision.HIGHEST), 1.0)
    tok_len = jnp.dot(onehot, lengths, precision=lax.Precision.HIGHEST)
    tok_adv = jnp.dot(onehot, adv_row, precision=lax.Precision.HIGHEST)
    surrogate = -tok_adv * jnp.exp(new_row - old_row) + 0.2 * (1.0 - jnp.exp(ref_row - new_row))
    return maskf / tok_len * surrogate


def group_advantage(group_flat, reward_flat, stats):
    groups = stats.shape[1]
    onehot = (group_flat[:, None] == jnp.arange(groups, dtype=jnp.int32)[None, :]).astype(
        jnp.float32
    )
    count = jnp.maximum(stats[0], 1.0)
    mean = stats[1] / count
    spread = jnp.sqrt(jnp.maximum(stats[2] / count - mean * mean, 0.0))
    tok_mean = jnp.dot(onehot, mean, precision=lax.Precision.HIGHEST)
    tok_std = jnp.dot(onehot, jnp.maximum(spread, 0.5), precision=lax.Precision.HIGHEST)
    return (reward_flat - tok_mean) / tok_std


def group_sums(group_flat, reward_flat, groups):
    onehot = (group_flat[:, None] == jnp.arange(groups, dtype=jnp.int32)[None, :]).astype(
        jnp.float32
    )
    values = jnp.stack([jnp.ones_like(reward_flat), reward_flat, reward_flat * reward_flat], axis=0)
    return jnp.dot(values, onehot, precision=lax.Precision.HIGHEST)


def rounded(term):
    return lax.optimization_barrier(term.astype(jnp.bfloat16)).astype(jnp.float32)


def rollout_blocks(weights):
    layer_count = weights.shape[0]
    row_count = weights.shape[1]
    paired = weights.reshape(layer_count, row_count, 2, KV_HEADS, HEAD).transpose(0, 1, 3, 2, 4)
    paired = paired.reshape(layer_count, row_count, KV_HEADS, 2 * HEAD)
    by_rank = jnp.repeat(paired, TP // KV_HEADS, axis=2)
    copies = jnp.tile(by_rank, (1, 1, lax.axis_size(SHARD) // TP, 1))
    return copies.reshape(layer_count, row_count, lax.axis_size(SHARD) * 2 * HEAD)


def per_device(
    hidden,
    cotangent,
    seq_ids,
    response_mask,
    group_ids,
    rewards,
    new_logp,
    old_logp,
    ref_logp,
    master,
):
    n_rep = lax.axis_size(REP)
    n_shard = lax.axis_size(SHARD)
    groups = n_rep * n_shard * SEQ_DEV // 8
    rest_cols = lax.all_to_all(
        rollout_blocks(master[1:].astype(jnp.bfloat16)),
        SHARD,
        split_axis=2,
        concat_axis=1,
        tiled=True,
    )
    local_sums = group_sums(group_ids[0], rewards[0], groups)
    stats = one_axis_at_a_time(local_sums, REP_SHARD)
    advantage = group_advantage(group_ids[0], rewards[0], stats)
    coef = token_coef(
        seq_ids[0], response_mask[0], advantage, new_logp[0], old_logp[0], ref_logp[0]
    )
    delta = (coef[:, None] * cotangent.astype(jnp.float32)).astype(jnp.bfloat16)
    feature_count = hidden.shape[1]
    partial_value = sum_by_axis(
        rounded(
            lax.dot_general(
                hidden, delta, (((0,), (0,)), ((), ())), preferred_element_type=jnp.float32
            )
        ),
        SHARD,
    )
    grad = lax.psum(partial_value.astype(jnp.bfloat16), REP).astype(jnp.float32)
    squares = of_everyone(jnp.sum(grad * grad), SHARD)
    rms = jnp.sqrt(squares / (feature_count * grad.shape[1]) + 1e-06)
    new_master = master[0] - 0.5 * grad / rms
    first_cols = lax.all_to_all(
        rollout_blocks(new_master[None].astype(jnp.bfloat16)),
        SHARD,
        split_axis=2,
        concat_axis=1,
        tiled=True,
    )
    rollout = jnp.concatenate([first_cols, rest_cols], axis=0)
    return (new_master, rollout)


def solution(mesh):
    split = Mesh(
        mesh.devices.reshape(2, 4, 2, 4, 4), ("rep_0", "rep_1", "rep_2", "shard_0", "shard_1")
    )
    placed = (
        P(REP_SHARD, None),
        P(REP_SHARD, None),
        P(REP_SHARD, None),
        P(REP_SHARD, None),
        P(REP_SHARD, None),
        P(REP_SHARD, None),
        P(REP_SHARD, None),
        P(REP_SHARD, None),
        P(REP_SHARD, None),
        P(None, SHARD, None),
    )
    return jax.shard_map(
        per_device,
        mesh=split,
        in_specs=placed,
        out_specs=(P(SHARD, None), P(None, None, SHARD)),
        check_vma=False,
    )
```

profile of v0, /device:TPU:33, one launch (start us, length us, event | category | flops | bytes accessed | tf_op | source)
XLA Modules:
  0.0 522.9 jit_solution(2379302001166275438)
XLA Ops:
  9.0 3.8 psum.42
  12.8 8.7 %psum.43 = f32[3,128]{1,0:T(4,128)S(1)} all-reduce(f32[3,128]{1,0:T(4,128)S(1)} %psum.42), channel_id=1, replica_groups=mesh['rep_0'=2,'rep_1'=4,'rep_2'=2,'shard_0'=4,'shard_1'=4] {'rep_1'}, use_global_device_ids=true, to_apply=%region_1.0 | all-reduce | flops 384 | bytes 3072 | tf_op jit(solution)/shard_map/psum | solution.py:18
  21.5 6.0 %psum.44 = f32[3,128]{1,0:T(4,128)S(1)} all-reduce(f32[3,128]{1,0:T(4,128)S(1)} %psum.43), channel_id=1, replica_groups=mesh['rep_0'=2,'rep_1'=4,'rep_2'=2,'shard_0'=4,'shard_1'=4] {'rep_2'}, use_global_device_ids=true, to_apply=%region_2.0 | all-reduce | flops 384 | bytes 3072 | tf_op jit(solution)/shard_map/psum | solution.py:18
  27.4 8.4 %psum.45 = f32[3,128]{1,0:T(4,128)S(1)} all-reduce(f32[3,128]{1,0:T(4,128)S(1)} %psum.44), channel_id=1, replica_groups=mesh['rep_0'=2,'rep_1'=4,'rep_2'=2,'shard_0'=4,'shard_1'=4] {'shard_0'}, use_global_device_ids=true, to_apply=%region_3.0 | all-reduce | flops 384 | bytes 3072 | tf_op jit(solution)/shard_map/psum | solution.py:18
  35.9 12.0 %psum.46 = f32[3,128]{1,0:T(4,128)S(1)} all-reduce(f32[3,128]{1,0:T(4,128)S(1)} %psum.45), channel_id=1, replica_groups=mesh['rep_0'=2,'rep_1'=4,'rep_2'=2,'shard_0'=4,'shard_1'=4] {'shard_1'}, use_global_device_ids=true, to_apply=%region_4.0 | all-reduce | flops 384 | bytes 3072 | tf_op jit(solution)/shard_map/psum | solution.py:18
  54.0 7.5 %fusion = bf16[3584,1024]{0,1:T(8,128)(2,1)} fusion(bf16[448,3584]{1,0:T(8,128)(2,1)S(1)} %copy-done, bf16[448,1024]{1,0:T(8,128)(2,1)} %param.11, f32[448]{0:T(512)S(1)} %add_multiply_fusion), kind=kOutput, calls=%fused_computation.1 | convolution fusion | flops 3293380608 | bytes 11470592 | tf_op jit(solution)/shard_map/dot_general | solution.py:115
  61.6 10.4 %copy.59 = bf16[3584,1024]{1,0:T(8,128)(2,1)} copy(bf16[3584,1024]{0,1:T(8,128)(2,1)} %fusion) | data formatting | bytes 14680064
  72.1 73.0 %reduce-scatter.7.cloned.1.call-done = bf16[896,1024]{1,0:T(8,128)(2,1)} async-done(((bf16[3584,1024]{1,0:T(8,128)(2,1)}), bf16[896,1024]{1,0:T(8,128)(2,1)}) %reduce-scatter.7.cloned.1.call-update) | async-done | bytes 1835024
  145.1 46.8 %reduce-scatter.9.cloned.1.call-done = bf16[224,1024]{1,0:T(8,128)(2,1)} async-done(((bf16[896,1024]{1,0:T(8,128)(2,1)}), bf16[224,1024]{1,0:T(8,128)(2,1)}) %reduce-scatter.9.cloned.1.call-update) | async-done | bytes 458768
  192.0 2.0 copy.62
  194.0 1.6 slice.36
  196.3 120.9 %all-reduce.2.cloned.1.call-done = bf16[224,1024]{0,1:T(8,128)(2,1)} async-done(((bf16[224,1024]{0,1:T(8,128)(2,1)}), bf16[224,1024]{0,1:T(8,128)(2,1)}) %all-reduce.2.cloned.1.call-update) | async-done | bytes 458768 | tf_op jit(solution)/shard_map/psum | solution.py:121
  317.2 1.9 fusion.8
  320.4 9.3 %all-to-all-start = ((f32[16,1,1]{2,1,0:T(1,128)}), f32[16,1,1]{2,1,0:T(1,128)S(1)}, u32[]{:S(2)}, u32[]{:S(2)}) async-start(f32[16,1,1]{2,1,0:T(1,128)} %broadcast_in_dim.16), calls=%async_computation | async-start | bytes 16384 | tf_op jit(solution)/shard_map/all_to_all | solution.py:31
  329.6 1.9 copy.68
  331.6 6.8 %all-to-all-done = f32[16,1,1]{2,1,0:T(1,128)S(1)} async-done(((f32[16,1,1]{2,1,0:T(1,128)}), f32[16,1,1]{2,1,0:T(1,128)S(1)}, u32[]{:S(2)}, u32[]{:S(2)}) %all-to-all-start) | async-done | bytes 96 | tf_op jit(solution)/shard_map/all_to_all | solution.py:31
  339.5 5.3 %tile.19.clone = bf16[2,224,2,8,1,256]{1,0,5,3,2,4:T(2,128)(2,1)} broadcast(bf16[2,224,8,256]{1,0,3,2:T(2,128)(2,1)S(1)} %bitcast.92), dimensions={0,1,3,5} | broadcast | bytes 5505024 | tf_op jit(solution)/shard_map/tile | solution.py:79
  344.7 4.8 all-to-all-start.2
  355.5 1.3 tile.16
  356.8 1.8 tile.17
  358.6 10.0 %copy.48 = bf16[1,224,4096]{1,0,2:T(2,128)(2,1)} copy(bf16[1,224,4096]{2,1,0:T(8,128)(2,1)} %tile.17) | data formatting | bytes 3670016 | tf_op jit(solution)/shard_map/tile | solution.py:79
  369.0 23.6 %reduce.1 = bf16[4096,224]{1,0:T(8,128)(2,1)S(1)} reduce(bf16[4096,1,224]{2,1,0:T(2,128)(2,1)} %bitcast.89, bf16[]{:T(256)} %broadcast.31), dimensions={1}, to_apply=%bitcast.82.reduce_sub_computation | reduce | bytes 3670018
  392.7 4.5 reshape.70
  397.2 49.6 %all-to-all-done.2 = bf16[2,224,4096]{1,0,2:T(2,128)(2,1)} async-done(((bf16[2,224,4096]{1,0,2:T(2,128)(2,1)}), bf16[2,224,4096]{1,0,2:T(2,128)(2,1)}, u32[]{:S(2)}, u32[]{:S(2)}) %all-to-all-start.2) | async-done | bytes 3670048 | tf_op jit(solution)/shard_map/all_to_all | solution.py:98
  446.8 7.8 %all-to-all-start.1 = ((bf16[16,2,28672]{2,1,0:T(2,128)(2,1)}), bf16[16,2,28672]{2,1,0:T(2,128)(2,1)S(1)}, u32[]{:S(2)}, u32[]{:S(2)}) async-start(bf16[16,2,28672]{2,1,0:T(2,128)(2,1)} %reshape.70), calls=%async_computation.1 | async-start | bytes 3670016 | tf_op jit(solution)/shard_map/all_to_all | solution.py:125
  454.6 11.0 %copy.58 = bf16[2,224,16,256]{3,1,2,0:T(8,128)(2,1)} copy(bf16[2,224,16,256]{1,0,3,2:T(2,128)(2,1)} %bitcast.27) | data formatting | bytes 7340032 | tf_op jit(solution)/shard_map/all_to_all | solution.py:98
  466.8 31.1 %all-to-all-done.1 = bf16[16,2,28672]{2,1,0:T(2,128)(2,1)S(1)} async-done(((bf16[16,2,28672]{2,1,0:T(2,128)(2,1)}), bf16[16,2,28672]{2,1,0:T(2,128)(2,1)S(1)}, u32[]{:S(2)}, u32[]{:S(2)}) %all-to-all-start.1) | async-done | bytes 1835040 | tf_op jit(solution)/shard_map/all_to_all | solution.py:125
  497.9 8.0 %reshape.71 = bf16[4096,1,224]{2,1,0:T(2,128)(2,1)} reshape(bf16[16,2,28672]{2,1,0:T(2,128)(2,1)S(1)} %all-to-all-done.1) | data formatting | bytes 3670016
  505.9 2.5 copy.63
  508.5 2.4 copy.55
  510.9 2.3 copy.50
  513.5 2.9 pad_maximum_fusion
  (39 shorter events, 18.3 us)
Async XLA Ops:
  7.2 46.9 %copy-start = (bf16[448,3584]{1,0:T(8,128)(2,1)S(1)}, bf16[448,3584]{1,0:T(8,128)(2,1)}, u32[]{:S(2)}) copy-start(bf16[448,3584]{1,0:T(8,128)(2,1)} %param.10) | copy-start | bytes 9633796
  7.2 137.9 %reduce-scatter.7.cloned.1.call-start = ((), (), s32[]{:S(2)}) async-start(), calls=%async_computation.6 | async-start | bytes 9175040
  72.0 119.9 %reduce-scatter.9.cloned.1.call-start = ((), (), s32[]{:S(2)}) async-start(), calls=%async_computation.7 | async-start | bytes 2293760
  145.1 172.1 %all-reduce.2.cloned.1.call-start = ((), (), s32[]{:S(2)}) async-start(), calls=%async_computation.5 | async-start | bytes 1048576 | tf_op jit(solution)/shard_map/psum | solution.py:121
  320.4 18.0 %all-to-all-start = ((f32[16,1,1]{2,1,0:T(1,128)}), f32[16,1,1]{2,1,0:T(1,128)S(1)}, u32[]{:S(2)}, u32[]{:S(2)}) async-start(f32[16,1,1]{2,1,0:T(1,128)} %broadcast_in_dim.16), calls=%async_computation | async-start | bytes 16384 | tf_op jit(solution)/shard_map/all_to_all | solution.py:31
  344.7 4.9 slice-start
  344.7 102.0 %all-to-all-start.2 = ((bf16[2,224,4096]{1,0,2:T(2,128)(2,1)}), bf16[2,224,4096]{1,0,2:T(2,128)(2,1)}, u32[]{:S(2)}, u32[]{:S(2)}) async-start(bf16[2,224,4096]{1,0,2:T(2,128)(2,1)} %bitcast.88), calls=%async_computation.2 | async-start | bytes 8388608 | tf_op jit(solution)/shard_map/all_to_all | solution.py:98
  446.8 51.1 %all-to-all-start.1 = ((bf16[16,2,28672]{2,1,0:T(2,128)(2,1)}), bf16[16,2,28672]{2,1,0:T(2,128)(2,1)S(1)}, u32[]{:S(2)}, u32[]{:S(2)}) async-start(bf16[16,2,28672]{2,1,0:T(2,128)(2,1)} %reshape.70), calls=%async_computation.1 | async-start | bytes 3670016 | tf_op jit(solution)/shard_map/all_to_all | solution.py:125
  510.9 2.6 copy-start.2
  513.2 3.2 copy-start.1
Sparse Core Ops, SparseCore 0:
  72.1 72.8 reduce-scatter.6
  147.6 44.3 reduce-scatter.8
  195.2 122.0 all-reduce.1
where the time goes:
time: 527 us; the launch traced here: 523 us
  waiting for transfers between devices  328 us (62%)
  local copies, waits for them, and re-layouts  73.4 us (14%)
  blocking collectives  38.9 us (7%)
  other arithmetic  32.6 us (6%)
  starting transfers between devices  22 us (4%)
  between operations  14.6 us (3%)
  matrix products  13.2 us (3%)
    psum x1, waiting for transfers between devices, per_device(): grad = lax.psum(partial_value.astype(jnp.bfloat16), REP).astype(jnp.float32)  121 us
    unnamed x5, waiting for transfers between devices  120 us
    all_to_all x1, waiting for transfers between devices, per_device(): lax.all_to_all(rollout_blocks(master[1:].astype(jnp.bfloat16)), SHARD, sp...  49.6 us
    psum x5, blocking collectives, one_axis_at_a_time(): shard = lax.psum(shard, axis)  38.9 us
    unnamed x15, local copies, waits for them, and re-layouts  31.8 us
    all_to_all x1, waiting for transfers between devices, per_device(): lax.all_to_all(rollout_blocks(new_master[None].astype(jnp.bfloat16)), SHA...  31.1 us
    unnamed x1, other arithmetic  23.6 us
    another operation x4, local copies, waits for them, and re-layouts, rollout_blocks(): copies = jnp.tile(by_rank, (1, 1, lax.axis_size(SHARD) // TP, 1))  18.3 us
  transfers between devices with their start and end apart: 6, of which 6 were waited for; matrix products, arithmetic and copies ran while one was open for 12% of the time, Pallas kernels for 0%

commit v1 on v0

v1 whole, which is shorter than its diff:
```python
import jax
import jax.numpy as jnp
from jax import lax
from jax.experimental import pallas as pl
from jax.experimental.pallas import tpu as pltpu
from jax.sharding import Mesh
from jax.sharding import PartitionSpec as P

HEAD = 128
KV_HEADS = 4
SEQ_DEV = 4
LANES = 128
REP = ("zl", "y", "c")
SHARD = ("x", "zh")
VMEM_LIMIT = 60 * 1024 * 1024
f32 = jnp.float32
bf16 = jnp.bfloat16


def swapped(value):
    return lax.ppermute(value, "c", [(0, 1), (1, 0)])


def exchanged(blocks, axis):
    return lax.all_to_all(blocks, axis, split_axis=0, concat_axis=0, tiled=True)


def sent_to_all(shard, axis):
    copies = jnp.broadcast_to(shard, (lax.axis_size(axis), *shard.shape))
    return exchanged(copies, axis)


def params(**kw):
    return pltpu.CompilerParams(vmem_limit_bytes=VMEM_LIMIT, **kw)


def cost(flops, nbytes):
    return pl.CostEstimate(flops=flops, bytes_accessed=nbytes, transcendentals=0)


def group_sums(group_flat, reward_flat, groups):
    onehot = (group_flat[:, None] == jnp.arange(groups, dtype=jnp.int32)[None, :]).astype(f32)
    values = jnp.stack([jnp.ones_like(reward_flat), reward_flat, reward_flat * reward_flat], axis=0)
    return jnp.dot(values, onehot, precision=lax.Precision.HIGHEST)


def token_rows(seq_row, mask_row, group_row, reward_row, new_row, old_row, ref_row):
    onehot = (seq_row[:, None] == jnp.arange(SEQ_DEV, dtype=jnp.int32)[None, :]).astype(f32)
    maskf = mask_row.astype(f32)
    lengths = jnp.maximum(jnp.dot(maskf, onehot, precision=lax.Precision.HIGHEST), 1.0)
    tok_len = jnp.dot(onehot, lengths, precision=lax.Precision.HIGHEST)
    tok_reward = jnp.dot(onehot, reward_row, precision=lax.Precision.HIGHEST)
    tok_group = jnp.dot(onehot, group_row.astype(f32), precision=lax.Precision.HIGHEST)
    weight = maskf / tok_len
    ratio = jnp.exp(new_row - old_row)
    penalty = 0.2 * (1.0 - jnp.exp(ref_row - new_row))
    zero = jnp.zeros_like(weight)
    return jnp.stack([weight, ratio, penalty, tok_reward, tok_group, zero, zero, zero], axis=0)


def partial_kernel(core, stats, tok_a, tok_b, cot_a, cot_b, hid_a, hid_b, out, delta_a, delta_b):
    half = cot_a.shape[1] // 2

    @pl.when(pl.program_id(0) == 0)
    def _():
        sums = jnp.sum(stats[...], axis=0)
        count = jnp.maximum(sums[0:1, :], 1.0)
        mean = sums[1:2, :] / count
        spread = jnp.maximum(jnp.sqrt(jnp.maximum(sums[2:3, :] / count - mean * mean, 0.0)), 0.5)
        cols = pl.ds(pl.multiple_of(core[0] * half, half), half)
        for tok, cot, delta in ((tok_a, cot_a, delta_a), (tok_b, cot_b, delta_b)):
            t = tok[...]
            lane = lax.broadcasted_iota(jnp.int32, (t.shape[0], LANES), 1).astype(f32)
            pick = lane == t[:, 4:5]
            tok_mean = jnp.sum(jnp.where(pick, mean, 0.0), axis=1, keepdims=True)
            tok_std = jnp.sum(jnp.where(pick, spread, 0.0), axis=1, keepdims=True)
            adv = (t[:, 3:4] - tok_mean) / tok_std
            coef = t[:, 0:1] * (-adv * t[:, 1:2] + t[:, 2:3])
            delta[...] = (coef * cot[:, cols].astype(f32)).T.astype(bf16)

    acc = jnp.dot(delta_a[...], hid_a[...], preferred_element_type=f32)
    acc = acc + jnp.dot(delta_b[...], hid_b[...], preferred_element_type=f32)
    out[...] = acc.astype(bf16).reshape(out.shape)


def partial_product(core, stats, tok_a, tok_b, cot_a, cot_b, hid_a, hid_b, nx, ny):
    toks, width = hid_a.shape
    kv = cot_a.shape[1]
    half = kv // 2
    blk = width // nx
    whole = lambda a: pl.BlockSpec(a.shape, lambda i, c: (0,) * a.ndim)
    hid = pl.BlockSpec((toks, blk), lambda i, c: (0, i))
    return pl.pallas_call(
        partial_kernel,
        out_shape=jax.ShapeDtypeStruct((nx, ny, half // ny, blk), bf16),
        grid_spec=pltpu.PrefetchScalarGridSpec(
            num_scalar_prefetch=1,
            grid=(nx,),
            in_specs=[whole(stats), whole(tok_a), whole(tok_b), whole(cot_a), whole(cot_b), hid, hid],
            out_specs=pl.BlockSpec((1, ny, half // ny, blk), lambda i, c: (i, 0, 0, 0)),
            scratch_shapes=[pltpu.VMEM((half, toks), bf16), pltpu.VMEM((half, toks), bf16)],
        ),
        compiler_params=params(),
        cost_estimate=cost(4 * toks * width * half, 4 * toks * width + 2 * width * half),
        name="partial_product",
    )(core, stats, tok_a, tok_b, cot_a, cot_b, hid_a, hid_b)


def sum_turn_kernel(src, out):
    out[...] = jnp.sum(src[...].astype(f32), axis=0).T.astype(bf16)


def sum_turn(blocks):
    n, rows, width = blocks.shape
    return pl.pallas_call(
        sum_turn_kernel,
        out_shape=jax.ShapeDtypeStruct((width, rows), bf16),
        grid=(width // LANES,),
        in_specs=[pl.BlockSpec((n, rows, LANES), lambda i: (0, 0, i))],
        out_specs=pl.BlockSpec((LANES, rows), lambda i: (i, 0)),
        compiler_params=params(),
        cost_estimate=cost(n * rows * width, 2 * n * rows * width),
        name="sum_turn",
    )(blocks)


def sum_spread_kernel(src, out):
    total = jnp.sum(src[...].astype(f32), axis=0).astype(bf16)
    for i in range(out.shape[0]):
        out[i] = total


def sum_spread(blocks, copies):
    n, rows, width = blocks.shape
    return pl.pallas_call(
        sum_spread_kernel,
        out_shape=jax.ShapeDtypeStruct((copies, rows, width), bf16),
        compiler_params=params(),
        cost_estimate=cost(n * rows * width, 4 * n * rows * width),
        name="sum_spread",
    )(blocks)


def squares_kernel(own, other, out):
    a = own[...].astype(f32)
    b = other[...].astype(f32)
    s = jnp.sum(jnp.sum(a * a + b * b, axis=0), axis=0, keepdims=True)
    s = jnp.sum(s, axis=1, keepdims=True)
    out[...] = jnp.broadcast_to(s.reshape(1, 1, 1), out.shape)


def squares_of(own, other, copies):
    return pl.pallas_call(
        squares_kernel,
        out_shape=jax.ShapeDtypeStruct((copies, 1, LANES), f32),
        compiler_params=params(),
        cost_estimate=cost(4 * own.size, 4 * own.size),
        name="squares_of",
    )(own, other)


def update_kernel(entries, core, squares, own, other, master, new, blocks):
    zl, ny, rows, width = own.shape
    total = jnp.sum(jnp.sum(squares[...], axis=0), axis=1, keepdims=True) / LANES
    rms = jnp.sqrt(total / entries + 1e-06)
    mine = core[0] == 0
    for kv in range(2):
        for y in range(ny):
            for z in range(zl):
                a, b = own[z, y], other[z, y]
                grad = (jnp.where(mine, a, b) if kv == 0 else jnp.where(mine, b, a)).astype(f32)
                r = slice(z * rows, (z + 1) * rows)
                c = slice((kv * ny + y) * width, (kv * ny + y + 1) * width)
                new[r, c] = master[0, r, c] - 0.5 * grad / rms
    sent = pl.ds(pl.multiple_of(core[0] * rows, rows), rows)
    for h in range(KV_HEADS):
        for kv in range(2):
            c = slice((kv * KV_HEADS + h) * HEAD, (kv * KV_HEADS + h + 1) * HEAD)
            value = new[sent, c].astype(bf16)
            for i in range(2):
                for j in range(2):
                    blocks[i, h, j, :, kv * HEAD : (kv + 1) * HEAD] = value


def update(core, squares, own, other, master, entries):
    _, rows, kv = master.shape
    return pl.pallas_call(
        lambda *refs: update_kernel(entries, *refs),
        out_shape=(
            jax.ShapeDtypeStruct((rows, kv), f32),
            jax.ShapeDtypeStruct((2, KV_HEADS, 2, rows // 2, 2 * HEAD), bf16),
        ),
        grid_spec=pltpu.PrefetchScalarGridSpec(
            num_scalar_prefetch=1,
            grid=(1,),
            in_specs=[
                pl.BlockSpec(squares.shape, lambda i, c: (0, 0, 0)),
                pl.BlockSpec(own.shape, lambda i, c: (0, 0, 0, 0)),
                pl.BlockSpec(other.shape, lambda i, c: (0, 0, 0, 0)),
                pl.BlockSpec((1, rows, kv), lambda i, c: (0, 0, 0)),
            ],
            out_specs=(
                pl.BlockSpec((rows, kv), lambda i, c: (0, 0)),
                pl.BlockSpec((2, KV_HEADS, 2, rows // 2, 2 * HEAD), lambda i, c: (0, 0, 0, 0, 0)),
            ),
        ),
        compiler_params=params(),
        cost_estimate=cost(4 * rows * kv, 12 * rows * kv),
        name="update",
    )(core, squares, own, other, master)


def rest_kernel(core, *refs):
    masters, out = refs[:-1], refs[-1]
    for l in range(2):
        for kv in range(2):
            value = masters[kv][1 + l].astype(bf16)
            for i in range(2):
                for j in range(2):
                    out[i, 0, j, l, :, kv * HEAD : (kv + 1) * HEAD] = value


def rest_blocks(core, master):
    layers, rows, kv = master.shape
    half = rows // 2
    spec = lambda k: pl.BlockSpec((layers, half, HEAD), lambda h, c: (0, c[0], k * KV_HEADS + h))
    return pl.pallas_call(
        rest_kernel,
        out_shape=jax.ShapeDtypeStruct((2, KV_HEADS, 2, layers - 1, half, 2 * HEAD), bf16),
        grid_spec=pltpu.PrefetchScalarGridSpec(
            num_scalar_prefetch=1,
            grid=(KV_HEADS,),
            in_specs=[spec(0), spec(1)],
            out_specs=pl.BlockSpec((2, 1, 2, layers - 1, half, 2 * HEAD), lambda h, c: (0, h, 0, 0, 0, 0)),
        ),
        compiler_params=params(),
        cost_estimate=cost(layers * rows * kv, 16 * rows * kv),
        name="rest_blocks",
    )(core, master, master)


def place_kernel(core, own, other, *refs):
    out = refs[-1]

    @pl.when(pl.program_id(2) == 0)
    def _():
        out[0, :, 0] = own[:, 0]

    @pl.when(pl.program_id(2) == 1)
    def _():
        out[0, :, 0] = other[:, 0]


def place(core, own, other, first, layers, into=None):
    n, count, half, width = own.shape
    group = n // 2
    src = pl.BlockSpec((group, 1, half, width), lambda l, s, w, c: (s, l, 0, 0))
    specs = [src, src]
    args = [core, own, other]
    alias = {}
    if into is not None:
        specs.append(pl.BlockSpec(memory_space=pl.ANY))
        args.append(into)
        alias = {3: 0}
    return pl.pallas_call(
        place_kernel,
        out_shape=jax.ShapeDtypeStruct((layers, n, 2, half, width), bf16),
        grid_spec=pltpu.PrefetchScalarGridSpec(
            num_scalar_prefetch=1,
            grid=(count, 2, 2),
            in_specs=specs,
            out_specs=pl.BlockSpec(
                (1, group, 1, half, width), lambda l, s, w, c: (first + l, s, (c[0] + w) % 2, 0, 0)
            ),
        ),
        input_output_aliases=alias,
        compiler_params=params(),
        cost_estimate=cost(own.size, 8 * own.size),
        name="place",
    )(*args)


def per_device(
    hidden,
    cotangent,
    seq_ids,
    response_mask,
    group_ids,
    rewards,
    new_logp,
    old_logp,
    ref_logp,
    master,
):
    n_x, n_y, n_z = lax.axis_size("x"), lax.axis_size("y"), lax.axis_size(("zh", "zl"))
    n_shard = lax.axis_size(SHARD)
    groups = lax.axis_size(REP) * n_shard * SEQ_DEV // 8
    layers, rows, kv = master.shape
    core = lax.axis_index("c").astype(jnp.int32).reshape(1)

    local_sums = group_sums(group_ids[0], rewards[0], groups)
    stats = sent_to_all(local_sums, REP).sum(axis=0)
    stats = sent_to_all(stats, SHARD)

    hidden_b = swapped(hidden)
    cotangent_b = swapped(cotangent)
    tok = token_rows(
        seq_ids[0], response_mask[0], group_ids[0], rewards[0], new_logp[0], old_logp[0], ref_logp[0]
    )
    tok_b = swapped(tok)

    sent = partial_product(
        core, stats, tok.T, tok_b.T, cotangent, cotangent_b, hidden, hidden_b, n_x, n_y
    )
    sent = sent.reshape(n_x * n_y, *sent.shape[2:])
    part = sum_turn(exchanged(sent, ("x", "y")))
    part = part.reshape(n_z, part.shape[0] // n_z, part.shape[1])
    zl = lax.axis_size("zl")
    own = exchanged(sum_spread(exchanged(part, ("zh", "zl")), zl * n_y), ("zl", "y"))
    other = swapped(own)
    squares = exchanged(squares_of(own, other, n_shard), SHARD)
    own = own.reshape(zl, n_y, *own.shape[1:])
    other = other.reshape(own.shape)
    new_master, first = update(core, squares, own, other, master, hidden.shape[1] * kv)

    rest = rest_blocks(core, master).reshape(n_shard, layers - 1, rows // 2, 2 * HEAD)
    rest = exchanged(rest, SHARD)
    out = place(core, rest, swapped(rest), 1, layers)
    first = exchanged(first.reshape(n_shard, 1, rows // 2, 2 * HEAD), SHARD)
    out = place(core, first, swapped(first), 0, layers, out)
    return (new_master, out.reshape(layers, n_shard * rows, 2 * HEAD))


def solution(mesh):
    split = Mesh(mesh.devices.reshape(2, 4, 2, 4, 4), REP + SHARD)
    row = P(REP + SHARD, None)
    return jax.shard_map(
        per_device,
        mesh=split,
        in_specs=(row,) * 9 + (P(None, SHARD, None),),
        out_specs=(P(SHARD, None), P(None, None, SHARD)),
        check_vma=False,
    )
```

time: 527 us -> 239 us (0.45)
  waiting for transfers between devices: 328 us -> 72.7 us
  local copies, waits for them, and re-layouts: 73.4 us -> 3.75 us
  Pallas kernels: 0 us -> 36.2 us
  blocking collectives: 38.9 us -> 69.7 us
  other arithmetic: 32.6 us -> 2.28 us
  starting transfers between devices: 22 us -> 47.2 us
  between operations: 14.6 us -> 0.75 us
  matrix products: 13.2 us -> 4.73 us
    psum x1 -> x0, waiting for transfers between devices: 121 us -> none  [per_device(): grad = lax.psum(partial_value.astype(jnp.bfloat16), REP).astype(jnp.float32)]
    unnamed x5 -> x0, waiting for transfers between devices: 120 us -> none
    all_to_all x0 -> x3, blocking collectives: none -> 69.7 us  [exchanged(): return lax.all_to_all(blocks, axis, split_axis=0, concat_axis=0, tiled=True)]
    psum x5 -> x0, blocking collectives: 38.9 us -> none  [one_axis_at_a_time(): shard = lax.psum(shard, axis)]
    pallas_call x0 -> x8, Pallas kernels: none -> 36.2 us  [the longest x2 10.5 us: place(): pl.pallas_call(place_kernel, out_shape=jax.ShapeDtypeStruct((layers, n, 2...]
    unnamed x15 -> x16, local copies, waits for them, and re-layouts: 31.8 us -> 2.33 us
    unnamed x1 -> x0, other arithmetic: 23.6 us -> none
    another operation x4, local copies, waits for them, and re-layouts: 18.3 us -> 0.16 us  [token_rows(): jnp.stack([weight, ratio, penalty, tok_reward, tok_group, zero, zero, zer...]
  transfers between devices with their start and end apart: 6 -> 11, of which waited for: 6 -> 7; matrix products, arithmetic and copies ran while one was open for 12% -> 4% of each run, Pallas kernels for 0% -> 6%
where the time goes in v1:
time: 239 us; the launch traced here: 237 us
  waiting for transfers between devices  72.7 us (30%)
  blocking collectives  69.7 us (29%)
  starting transfers between devices  47.2 us (20%)
  Pallas kernels  36.2 us (15%)
  matrix products  4.73 us (2%)
  local copies, waits for them, and re-layouts  3.75 us (2%)
    all_to_all x5, waiting for transfers between devices, exchanged(): return lax.all_to_all(blocks, axis, split_axis=0, concat_axis=0, tiled=True)  70.4 us
    all_to_all x3, blocking collectives, exchanged(): return lax.all_to_all(blocks, axis, split_axis=0, concat_axis=0, tiled=True)  69.7 us
    all_to_all x5, starting transfers between devices, exchanged(): return lax.all_to_all(blocks, axis, split_axis=0, concat_axis=0, tiled=True)  36.2 us
    ppermute x6, starting transfers between devices, swapped(): return lax.ppermute(value, 'c', [(0, 1), (1, 0)])  11 us
    pallas_call x2, Pallas kernels, place(): pl.pallas_call(place_kernel, out_shape=jax.ShapeDtypeStruct((layers, n, 2...  10.5 us
    pallas_call x1, Pallas kernels, partial_product(): pl.pallas_call(partial_kernel, out_shape=jax.ShapeDtypeStruct((nx, ny, ha...  9.94 us
    pallas_call x1, Pallas kernels, sum_turn(): pl.pallas_call(sum_turn_kernel, out_shape=jax.ShapeDtypeStruct((width, ro...  5.49 us
  transfers between devices with their start and end apart: 11, of which 7 were waited for; matrix products, arithmetic and copies ran while one was open for 4% of the time, Pallas kernels for 6%

profile of v1, /device:TPU:33, one launch (start us, length us, event | category | flops | bytes accessed | tf_op | source)
XLA Modules:
  0.0 237.3 jit_solution(1975470926820761878)
XLA Ops:
  2.1 0.9 fusion.9
  3.6 5.7 %all-to-all-start = ((f32[16,3,128]{2,1,0:T(4,128)}), f32[16,3,128]{2,1,0:T(4,128)S(1)}, u32[]{:S(2)}, u32[]{:S(2)}) async-start(f32[16,3,128]{2,1,0:T(4,128)} %broadcast_in_dim.8), calls=%async_computation | async-start | bytes 65536 | tf_op jit(solution)/shard_map/all_to_all | solution.py:25
  9.7 1.0 fusion.3
  10.6 1.0 fusion.2
  11.6 0.8 subtract_multiply_fusion
  12.4 0.9 fusion.1
  14.7 9.9 %all-to-all-start.1 = ((f32[16,3,128]{2,1,0:T(4,128)}), f32[16,3,128]{2,1,0:T(4,128)S(1)}, u32[]{:S(2)}, u32[]{:S(2)}) async-start(f32[16,3,128]{2,1,0:T(4,128)} %broadcast_in_dim.9), calls=%async_computation.1 | async-start | bytes 65536 | tf_op jit(solution)/shard_map/all_to_all | solution.py:25
  24.5 1.0 fusion.4
  27.2 1.2 collective-permute-done
  28.4 5.0 %all-to-all-done.1.stats = f32[16,3,128]{2,1,0:T(4,128)S(1)} async-done(((f32[16,3,128]{2,1,0:T(4,128)}), f32[16,3,128]{2,1,0:T(4,128)S(1)}, u32[]{:S(2)}, u32[]{:S(2)}) %all-to-all-start.1) | async-done | bytes 24608 | tf_op jit(solution)/shard_map/all_to_all | solution.py:25
  34.1 1.1 copy-done.2
  35.1 9.9 %partial_product.1 = bf16[4,4,128,896]{3,2,1,0:T(8,128)(2,1)} custom-call(s32[1]{0:T(128)} %bitcast.core.refs_0_, f32[16,3,128]{2,1,0:T(4,128)} %copy-done.6, f32[448,8]{1,0:T(8,128)} %bitcast.47, f32[448,8]{1,0:T(8,128)} %bitcast.15.tok_b, bf16[448,1024]{1,0:T(8,128)(2,1)} %cot_a.1, bf16[448,1024]{1,0:T(8,128)(2,1)} %collective-permute-done.1.cot_b, ...), custom_call_target="tpu_custom_call" | custom-call | flops 3288334336 | bytes 10092544 | tf_op jit(solution)/shard_map/partial_product/pallas_call | solution.py:93
  45.1 47.4 %all_to_all.40.src = bf16[16,128,896]{2,1,0:T(8,128)(2,1)} all-to-all(bf16[16,128,896]{2,1,0:T(8,128)(2,1)} %bitcast.42), channel_id=1, replica_groups=mesh['zl'=2,'y'=4,'c'=2,'x'=4,'zh'=4] {'x','y'}, dimensions={0} | all-to-all | bytes 7340032 | tf_op jit(solution)/shard_map/all_to_all | solution.py:25
  92.5 5.5 %sum_turn.1 = bf16[896,128]{1,0:T(8,128)(2,1)} custom-call(bf16[16,128,896]{2,1,0:T(8,128)(2,1)} %all_to_all.40.src), custom_call_target="tpu_custom_call" | custom-call | flops 1835008 | bytes 3670016 | tf_op jit(solution)/shard_map/sum_turn/pallas_call | solution.py:115
  98.0 12.7 %all_to_all.41.src = bf16[8,112,128]{2,1,0:T(8,128)(2,1)} all-to-all(bf16[8,112,128]{2,1,0:T(8,128)(2,1)} %bitcast.48), channel_id=1, replica_groups=mesh['zl'=2,'y'=4,'c'=2,'x'=4,'zh'=4] {'zh','zl'}, dimensions={0} | all-to-all | bytes 458752 | tf_op jit(solution)/shard_map/all_to_all | solution.py:25
  110.7 1.7 sum_spread.1
  112.4 9.5 %all_to_all.42.own = bf16[8,112,128]{2,1,0:T(8,128)(2,1)S(1)} all-to-all(bf16[8,112,128]{2,1,0:T(8,128)(2,1)} %sum_spread.1), channel_id=1, replica_groups=mesh['zl'=2,'y'=4,'c'=2,'x'=4,'zh'=4] {'zl','y'}, dimensions={0} | all-to-all | bytes 458752 | tf_op jit(solution)/shard_map/all_to_all | solution.py:25
  121.9 5.4 %collective-permute-start.3 = (bf16[8,112,128]{2,1,0:T(8,128)(2,1)S(1)}, bf16[8,112,128]{2,1,0:T(8,128)(2,1)S(1)}, u32[]{:S(2)}, u32[]{:S(2)}) collective-permute-start(bf16[8,112,128]{2,1,0:T(8,128)(2,1)S(1)} %all_to_all.42.own), channel_id=1, source_target_pairs={{0,16},{16,0},{1,17},{17,1},{2,18},{18,2},{3,19},{19,3},{4,20},{20... | collective-permute-start | bytes 688136 | tf_op jit(solution)/shard_map/ppermute | solution.py:21
  127.4 1.1 collective-permute-done.3.other
  129.2 1.9 squares_of.1
  131.0 3.5 %all-to-all-start.5 = ((f32[16,1,128]{2,1,0:T(1,128)}), f32[16,1,128]{2,1,0:T(1,128)S(1)}, u32[]{:S(2)}, u32[]{:S(2)}) async-start(f32[16,1,128]{2,1,0:T(1,128)} %squares_of.1), calls=%async_computation.5 | async-start | bytes 16384 | tf_op jit(solution)/shard_map/all_to_all | solution.py:25
  134.5 3.7 %rest_blocks.1 = bf16[2,4,2,2,112,256]{5,4,3,2,1,0:T(8,128)(2,1)} custom-call(s32[1]{0:T(128)} %bitcast.core.refs_0_, f32[3,224,1024]{2,1,0:T(8,128)} %refs_1_.1, f32[3,224,1024]{2,1,0:T(8,128)} %refs_1_.1), custom_call_target="tpu_custom_call" | custom-call | flops 688128 | bytes 3670016 | tf_op jit(solution)/shard_map/rest_blocks/pallas_call | solution.py:227
  138.3 5.0 %all-to-all-done.5.refs_1_ = f32[16,1,128]{2,1,0:T(1,128)S(1)} async-done(((f32[16,1,128]{2,1,0:T(1,128)}), f32[16,1,128]{2,1,0:T(1,128)S(1)}, u32[]{:S(2)}, u32[]{:S(2)}) %all-to-all-start.5) | async-done | bytes 8224 | tf_op jit(solution)/shard_map/all_to_all | solution.py:25
  143.2 4.0 %all-to-all-start.7 = ((bf16[16,2,112,256]{3,2,1,0:T(8,128)(2,1)}), bf16[16,2,112,256]{3,2,1,0:T(8,128)(2,1)S(1)}, u32[]{:S(2)}, u32[]{:S(2)}) async-start(bf16[16,2,112,256]{3,2,1,0:T(8,128)(2,1)} %bitcast.43), calls=%async_computation.7 | async-start | bytes 3670016 | tf_op jit(solution)/shard_map/all_to_all | solution.py:25
  147.3 3.0 %update.1 = (f32[224,1024]{1,0:T(8,128)}, bf16[2,4,2,112,256]{4,3,2,1,0:T(8,128)(2,1)}) custom-call(s32[1]{0:T(128)} %bitcast.core.refs_0_, f32[16,1,128]{2,1,0:T(1,128)} %copy-done.7, bf16[2,4,112,128]{3,2,1,0:T(8,128)(2,1)} %bitcast.44, bf16[2,4,112,128]{3,2,1,0:T(8,128)(2,1)} %bitcast.46, f32[3,224,1024]{2,1,0:T(8,128)} %refs_1_.1), custom_call_target="tpu_custom_call" | custom-call | flops 917504 | bytes 2752512 | tf_op jit(solution)/shard_map/update/pallas_call | solution.py:187
  150.2 35.4 %all-to-all-done.7.own = bf16[16,2,112,256]{3,2,1,0:T(8,128)(2,1)S(1)} async-done(((bf16[16,2,112,256]{3,2,1,0:T(8,128)(2,1)}), bf16[16,2,112,256]{3,2,1,0:T(8,128)(2,1)S(1)}, u32[]{:S(2)}, u32[]{:S(2)}) %all-to-all-start.7) | async-done | bytes 1835040 | tf_op jit(solution)/shard_map/all_to_all | solution.py:25
  185.7 13.2 %all-to-all-start.6 = ((bf16[16,1,112,256]{3,2,1,0:T(8,128)(2,1)}), bf16[16,1,112,256]{3,2,1,0:T(8,128)(2,1)S(1)}, u32[]{:S(2)}, u32[]{:S(2)}) async-start(bf16[16,1,112,256]{3,2,1,0:T(8,128)(2,1)} %bitcast.45), calls=%async_computation.6 | async-start | bytes 1835008 | tf_op jit(solution)/shard_map/all_to_all | solution.py:25
  198.9 1.0 collective-permute-start.5
  199.9 24.3 %all-to-all-done.6.own = bf16[16,1,112,256]{3,2,1,0:T(8,128)(2,1)S(1)} async-done(((bf16[16,1,112,256]{3,2,1,0:T(8,128)(2,1)}), bf16[16,1,112,256]{3,2,1,0:T(8,128)(2,1)S(1)}, u32[]{:S(2)}, u32[]{:S(2)}) %all-to-all-start.6) | async-done | bytes 917536 | tf_op jit(solution)/shard_map/all_to_all | solution.py:25
  224.2 2.6 %collective-permute-start.4 = (bf16[16,1,112,256]{3,2,1,0:T(8,128)(2,1)S(1)}, bf16[16,1,112,256]{3,2,1,0:T(8,128)(2,1)}, u32[]{:S(2)}, u32[]{:S(2)}) collective-permute-start(bf16[16,1,112,256]{3,2,1,0:T(8,128)(2,1)S(1)} %all-to-all-done.6.own), channel_id=1, source_target_pairs={{0,16},{16,0},{1,17},{17,1},{2,18},{18,2},{3,19},{19,3},{4,20},{20... | collective-permute-start | bytes 2752520 | tf_op jit(solution)/shard_map/ppermute | solution.py:21
  226.8 6.8 %place.2.refs_0_ = bf16[3,16,2,112,256]{4,3,2,1,0:T(8,128)(2,1)} custom-call(s32[1]{0:T(128)} %bitcast.core.refs_0_, bf16[16,2,112,256]{3,2,1,0:T(8,128)(2,1)} %copy-done, bf16[16,2,112,256]{3,2,1,0:T(8,128)(2,1)} %collective-permute-done.5.other), custom_call_target="tpu_custom_call" | custom-call | flops 917504 | bytes 7340032 | tf_op jit(solution)/shard_map/place/pallas_call | solution.py:265
  233.6 3.7 %place.3 = bf16[3,16,2,112,256]{4,3,2,1,0:T(8,128)(2,1)} custom-call(s32[1]{0:T(128)} %bitcast.core.refs_0_, bf16[16,1,112,256]{3,2,1,0:T(8,128)(2,1)} %copy-done.1, bf16[16,1,112,256]{3,2,1,0:T(8,128)(2,1)} %collective-permute-done.4.other, bf16[3,16,2,112,256]{4,3,2,1,0:T(8,128)(2,1)} %place.2.refs_0_), custom_call_target="tpu_custom_call", output_to_operand_aliasing={{}: (3, {})} | custom-call | flops 458752 | bytes 3670016 | tf_op jit(solution)/shard_map/place/pallas_call | solution.py:265
  (34 shorter events, 6.8 us)
Async XLA Ops:
  0.6 32.9 %collective-permute-start.2 = (bf16[448,3584]{1,0:T(8,128)(2,1)}, bf16[448,3584]{1,0:T(8,128)(2,1)S(1)}, u32[]{:S(2)}, u32[]{:S(2)}) collective-permute-start(bf16[448,3584]{1,0:T(8,128)(2,1)} %hid_a.1), channel_id=1, source_target_pairs={{0,16},{16,0},{1,17},{17,1},{2,18},{18,2},{3,19},{19,3},{4,20},{20... | collective-permute-start | bytes 9633800 | tf_op jit(solution)/shard_map/ppermute | solution.py:21
  3.6 10.4 %all-to-all-start = ((f32[16,3,128]{2,1,0:T(4,128)}), f32[16,3,128]{2,1,0:T(4,128)S(1)}, u32[]{:S(2)}, u32[]{:S(2)}) async-start(f32[16,3,128]{2,1,0:T(4,128)} %broadcast_in_dim.8), calls=%async_computation | async-start | bytes 65536 | tf_op jit(solution)/shard_map/all_to_all | solution.py:25
  9.3 24.2 %collective-permute-start.1 = (bf16[448,1024]{1,0:T(8,128)(2,1)}, bf16[448,1024]{1,0:T(8,128)(2,1)}, u32[]{:S(2)}, u32[]{:S(2)}) collective-permute-start(bf16[448,1024]{1,0:T(8,128)(2,1)} %cot_a.1), channel_id=1, source_target_pairs={{0,16},{16,0},{1,17},{17,1},{2,18},{18,2},{3,19},{19,3},{4,20},{20... | collective-permute-start | bytes 2752520 | tf_op jit(solution)/shard_map/ppermute | solution.py:21
  14.7 18.8 %all-to-all-start.1 = ((f32[16,3,128]{2,1,0:T(4,128)}), f32[16,3,128]{2,1,0:T(4,128)S(1)}, u32[]{:S(2)}, u32[]{:S(2)}) async-start(f32[16,3,128]{2,1,0:T(4,128)} %broadcast_in_dim.9), calls=%async_computation.1 | async-start | bytes 65536 | tf_op jit(solution)/shard_map/all_to_all | solution.py:25
  26.4 7.1 %copy-start.5 = (f32[8,448]{0,1:T(8,128)}, f32[8,448]{0,1:T(8,128)S(1)}, u32[]{:S(2)}) copy-start(f32[8,448]{0,1:T(8,128)S(1)} %copy.29) | copy-start | bytes 43012
  26.4 2.0 collective-permute-start
  33.5 0.6 copy-start.6
  33.5 1.7 copy-start.2
  121.9 6.6 %copy-start.3 = (bf16[8,112,128]{2,1,0:T(8,128)(2,1)}, bf16[8,112,128]{2,1,0:T(8,128)(2,1)S(1)}, u32[]{:S(2)}) copy-start(bf16[8,112,128]{2,1,0:T(8,128)(2,1)S(1)} %all_to_all.42.own) | copy-start | bytes 688132
  121.9 6.6 %collective-permute-start.3 = (bf16[8,112,128]{2,1,0:T(8,128)(2,1)S(1)}, bf16[8,112,128]{2,1,0:T(8,128)(2,1)S(1)}, u32[]{:S(2)}, u32[]{:S(2)}) collective-permute-start(bf16[8,112,128]{2,1,0:T(8,128)(2,1)S(1)} %all_to_all.42.own), channel_id=1, source_target_pairs={{0,16},{16,0},{1,17},{17,1},{2,18},{18,2},{3,19},{19,3},{4,20},{20... | collective-permute-start | bytes 688136 | tf_op jit(solution)/shard_map/ppermute | solution.py:21
  128.5 0.7 copy-start.4
  131.0 12.2 %all-to-all-start.5 = ((f32[16,1,128]{2,1,0:T(1,128)}), f32[16,1,128]{2,1,0:T(1,128)S(1)}, u32[]{:S(2)}, u32[]{:S(2)}) async-start(f32[16,1,128]{2,1,0:T(1,128)} %squares_of.1), calls=%async_computation.5 | async-start | bytes 16384 | tf_op jit(solution)/shard_map/all_to_all | solution.py:25
  143.2 4.0 %copy-start.7 = (f32[16,1,128]{2,1,0:T(1,128)}, f32[16,1,128]{2,1,0:T(1,128)S(1)}, u32[]{:S(2)}) copy-start(f32[16,1,128]{2,1,0:T(1,128)S(1)} %all-to-all-done.5.refs_1_) | copy-start | bytes 24580
  143.2 42.5 %all-to-all-start.7 = ((bf16[16,2,112,256]{3,2,1,0:T(8,128)(2,1)}), bf16[16,2,112,256]{3,2,1,0:T(8,128)(2,1)S(1)}, u32[]{:S(2)}, u32[]{:S(2)}) async-start(bf16[16,2,112,256]{3,2,1,0:T(8,128)(2,1)} %bitcast.43), calls=%async_computation.7 | async-start | bytes 3670016 | tf_op jit(solution)/shard_map/all_to_all | solution.py:25
  185.7 41.1 %copy-start = (bf16[16,2,112,256]{3,2,1,0:T(8,128)(2,1)}, bf16[16,2,112,256]{3,2,1,0:T(8,128)(2,1)S(1)}, u32[]{:S(2)}) copy-start(bf16[16,2,112,256]{3,2,1,0:T(8,128)(2,1)S(1)} %all-to-all-done.7.own) | copy-start | bytes 5505028
  185.7 38.5 %all-to-all-start.6 = ((bf16[16,1,112,256]{3,2,1,0:T(8,128)(2,1)}), bf16[16,1,112,256]{3,2,1,0:T(8,128)(2,1)S(1)}, u32[]{:S(2)}, u32[]{:S(2)}) async-start(bf16[16,1,112,256]{3,2,1,0:T(8,128)(2,1)} %bitcast.45), calls=%async_computation.6 | async-start | bytes 1835008 | tf_op jit(solution)/shard_map/all_to_all | solution.py:25
  198.9 27.9 %collective-permute-start.5 = (bf16[16,2,112,256]{3,2,1,0:T(8,128)(2,1)S(1)}, bf16[16,2,112,256]{3,2,1,0:T(8,128)(2,1)}, u32[]{:S(2)}, u32[]{:S(2)}) collective-permute-start(bf16[16,2,112,256]{3,2,1,0:T(8,128)(2,1)S(1)} %all-to-all-done.7.own), channel_id=1, source_target_pairs={{0,16},{16,0},{1,17},{17,1},{2,18},{18,2},{3,19},{19,3},{4,20},{20... | collective-permute-start | bytes 5505032 | tf_op jit(solution)/shard_map/ppermute | solution.py:21
  224.2 9.4 %copy-start.1 = (bf16[16,1,112,256]{3,2,1,0:T(8,128)(2,1)}, bf16[16,1,112,256]{3,2,1,0:T(8,128)(2,1)S(1)}, u32[]{:S(2)}) copy-start(bf16[16,1,112,256]{3,2,1,0:T(8,128)(2,1)S(1)} %all-to-all-done.6.own) | copy-start | bytes 2752516
  224.2 9.4 %collective-permute-start.4 = (bf16[16,1,112,256]{3,2,1,0:T(8,128)(2,1)S(1)}, bf16[16,1,112,256]{3,2,1,0:T(8,128)(2,1)}, u32[]{:S(2)}, u32[]{:S(2)}) collective-permute-start(bf16[16,1,112,256]{3,2,1,0:T(8,128)(2,1)S(1)} %all-to-all-done.6.own), channel_id=1, source_target_pairs={{0,16},{16,0},{1,17},{17,1},{2,18},{18,2},{3,19},{19,3},{4,20},{20... | collective-permute-start | bytes 2752520 | tf_op jit(solution)/shard_map/ppermute | solution.py:21

commit v2 on v1

v2 whole, which is shorter than its diff:
```python
import jax
import jax.numpy as jnp
from jax import lax
from jax.experimental import pallas as pl
from jax.experimental.pallas import tpu as pltpu
from jax.sharding import Mesh
from jax.sharding import PartitionSpec as P

HEAD = 128
KV_HEADS = 4
SEQ_DEV = 4
LANES = 128
REP = ("zl", "y", "c")
SHARD = ("x", "zh")
VMEM_LIMIT = 24 * 1024 * 1024
f32 = jnp.float32
bf16 = jnp.bfloat16


def swapped(value):
    return lax.ppermute(value, "c", [(0, 1), (1, 0)])


def shifted(value, axis, by):
    n = lax.axis_size(axis)
    return lax.ppermute(value, axis, [(i, (i + by) % n) for i in range(n)])


def exchanged(blocks, axis):
    return lax.all_to_all(blocks, axis, split_axis=0, concat_axis=0, tiled=True)


def sent_to_all(shard, axis):
    copies = jnp.broadcast_to(shard, (lax.axis_size(axis), *shard.shape))
    return exchanged(copies, axis)


def params(**kw):
    return pltpu.CompilerParams(vmem_limit_bytes=VMEM_LIMIT, **kw)


def cost(flops, nbytes):
    return pl.CostEstimate(flops=flops, bytes_accessed=nbytes, transcendentals=0)


def group_sums(group_flat, reward_flat, groups):
    onehot = (group_flat[:, None] == jnp.arange(groups, dtype=jnp.int32)[None, :]).astype(f32)
    values = jnp.stack([jnp.ones_like(reward_flat), reward_flat, reward_flat * reward_flat], axis=0)
    return jnp.dot(values, onehot, precision=lax.Precision.HIGHEST)


def token_rows(seq_row, mask_row, group_row, reward_row, new_row, old_row, ref_row):
    onehot = (seq_row[:, None] == jnp.arange(SEQ_DEV, dtype=jnp.int32)[None, :]).astype(f32)
    maskf = mask_row.astype(f32)
    lengths = jnp.maximum(jnp.dot(maskf, onehot, precision=lax.Precision.HIGHEST), 1.0)
    tok_len = jnp.dot(onehot, lengths, precision=lax.Precision.HIGHEST)
    tok_reward = jnp.dot(onehot, reward_row, precision=lax.Precision.HIGHEST)
    tok_group = jnp.dot(onehot, group_row.astype(f32), precision=lax.Precision.HIGHEST)
    weight = maskf / tok_len
    ratio = jnp.exp(new_row - old_row)
    penalty = 0.2 * (1.0 - jnp.exp(ref_row - new_row))
    zero = jnp.zeros_like(weight)
    return jnp.stack([weight, ratio, penalty, tok_reward, tok_group, zero, zero, zero], axis=0)


def partial_kernel(core, stats, tok_a, tok_b, cot_a, cot_b, hid_a, hid_b, after, out, delta_a, delta_b):
    half = cot_a.shape[1] // 2

    @pl.when(pl.program_id(0) == 0)
    def _():
        sums = jnp.sum(stats[...], axis=0)
        count = jnp.maximum(sums[0:1, :], 1.0)
        mean = sums[1:2, :] / count
        spread = jnp.maximum(jnp.sqrt(jnp.maximum(sums[2:3, :] / count - mean * mean, 0.0)), 0.5)
        cols = pl.ds(pl.multiple_of(core[0] * half, half), half)
        for tok, cot, delta in ((tok_a, cot_a, delta_a), (tok_b, cot_b, delta_b)):
            t = tok[...]
            lane = lax.broadcasted_iota(jnp.int32, (t.shape[0], LANES), 1).astype(f32)
            pick = lane == t[:, 4:5]
            tok_mean = jnp.sum(jnp.where(pick, mean, 0.0), axis=1, keepdims=True)
            tok_std = jnp.sum(jnp.where(pick, spread, 0.0), axis=1, keepdims=True)
            adv = (t[:, 3:4] - tok_mean) / tok_std
            coef = t[:, 0:1] * (-adv * t[:, 1:2] + t[:, 2:3])
            delta[...] = (coef * cot[:, cols].astype(f32)).T.astype(bf16)

    acc = jnp.dot(delta_a[...], hid_a[...], preferred_element_type=f32)
    acc = acc + jnp.dot(delta_b[...], hid_b[...], preferred_element_type=f32)
    out[...] = acc.astype(bf16).reshape(out.shape)


def partial_product(core, stats, tok_a, tok_b, cot_a, cot_b, hid_a, hid_b, after, nx, ny):
    toks, width = hid_a.shape
    kv = cot_a.shape[1]
    half = kv // 2
    blk = width // nx
    whole = lambda a: pl.BlockSpec(a.shape, lambda i, c: (0,) * a.ndim)
    hid = pl.BlockSpec((toks, blk), lambda i, c: (0, i))
    return pl.pallas_call(
        partial_kernel,
        out_shape=jax.ShapeDtypeStruct((nx, ny, half // ny, blk), bf16),
        grid_spec=pltpu.PrefetchScalarGridSpec(
            num_scalar_prefetch=1,
            grid=(nx,),
            in_specs=[whole(stats), whole(tok_a), whole(tok_b), whole(cot_a), whole(cot_b), hid, hid, pl.BlockSpec(memory_space=pl.ANY)],
            out_specs=pl.BlockSpec((1, ny, half // ny, blk), lambda i, c: (i, 0, 0, 0)),
            scratch_shapes=[pltpu.VMEM((half, toks), bf16), pltpu.VMEM((half, toks), bf16)],
        ),
        compiler_params=params(),
        cost_estimate=cost(4 * toks * width * half, 4 * toks * width + 2 * width * half),
        name="partial_product",
    )(core, stats, tok_a, tok_b, cot_a, cot_b, hid_a, hid_b, after)


def sum_turn_kernel(src, out, acc):
    step = pl.program_id(0)
    total = jnp.sum(src[...].astype(f32), axis=0)

    @pl.when(step == 0)
    def _():
        acc[...] = total

    @pl.when(step > 0)
    def _():
        acc[...] += total

    @pl.when(step == pl.num_programs(0) - 1)
    def _():
        out[...] = acc[...].T.astype(bf16)


def sum_turn(blocks):
    n, rows, width = blocks.shape
    return pl.pallas_call(
        sum_turn_kernel,
        out_shape=jax.ShapeDtypeStruct((width, rows), bf16),
        grid=(4,),
        in_specs=[pl.BlockSpec((n // 4, rows, width), lambda i: (i, 0, 0))],
        out_specs=pl.BlockSpec((width, rows), lambda i: (0, 0)),
        scratch_shapes=[pltpu.VMEM((rows, width), f32)],
        compiler_params=params(),
        cost_estimate=cost(n * rows * width, 2 * n * rows * width),
        name="sum_turn",
    )(blocks)


def sum_spread_kernel(src, out):
    total = jnp.sum(src[...].astype(f32), axis=0).astype(bf16)
    for i in range(out.shape[0]):
        out[i] = total


def sum_spread(blocks, copies):
    n, rows, width = blocks.shape
    return pl.pallas_call(
        sum_spread_kernel,
        out_shape=jax.ShapeDtypeStruct((copies, rows, width), bf16),
        compiler_params=params(),
        cost_estimate=cost(n * rows * width, 4 * n * rows * width),
        name="sum_spread",
    )(blocks)


def squares_kernel(grad, out):
    g = grad[...].astype(f32)
    s = jnp.sum(jnp.sum(g * g, axis=0), axis=0, keepdims=True)
    s = jnp.sum(s, axis=1, keepdims=True)
    out[...] = jnp.broadcast_to(s.reshape(1, 1, 1), out.shape)


def squares_of(grad, copies):
    return pl.pallas_call(
        squares_kernel,
        out_shape=jax.ShapeDtypeStruct((copies, 1, LANES), f32),
        compiler_params=params(),
        cost_estimate=cost(2 * grad.size, 2 * grad.size),
        name="squares_of",
    )(grad)


def update_kernel(entries, core, squares, grad, master, new, blocks):
    zl, ny, _, rows, width = grad.shape
    total = jnp.sum(jnp.sum(squares[...], axis=0), axis=1, keepdims=True) / LANES
    rms = jnp.sqrt(total / entries + 1e-06)
    for kv in range(2):
        for y in range(ny):
            for z in range(zl):
                r = slice(z * rows, (z + 1) * rows)
                c = slice((kv * ny + y) * width, (kv * ny + y + 1) * width)
                new[r, c] = master[0, r, c] - 0.5 * grad[z, y, kv].astype(f32) / rms
    sent = pl.ds(pl.multiple_of(core[0] * rows, rows), rows)
    for h in range(KV_HEADS):
        for kv in range(2):
            c = slice((kv * KV_HEADS + h) * HEAD, (kv * KV_HEADS + h + 1) * HEAD)
            value = new[sent, c].astype(bf16)
            for i in range(2):
                for j in range(2):
                    blocks[i, h, j, :, kv * HEAD : (kv + 1) * HEAD] = value


def update(core, squares, grad, master, entries):
    _, rows, kv = master.shape
    return pl.pallas_call(
        lambda *refs: update_kernel(entries, *refs),
        out_shape=(
            jax.ShapeDtypeStruct((rows, kv), f32),
            jax.ShapeDtypeStruct((2, KV_HEADS, 2, rows // 2, 2 * HEAD), bf16),
        ),
        grid_spec=pltpu.PrefetchScalarGridSpec(
            num_scalar_prefetch=1,
            grid=(1,),
            in_specs=[
                pl.BlockSpec(squares.shape, lambda i, c: (0, 0, 0)),
                pl.BlockSpec(grad.shape, lambda i, c: (0, 0, 0, 0, 0)),
                pl.BlockSpec((1, rows, kv), lambda i, c: (0, 0, 0)),
            ],
            out_specs=(
                pl.BlockSpec((rows, kv), lambda i, c: (0, 0)),
                pl.BlockSpec((2, KV_HEADS, 2, rows // 2, 2 * HEAD), lambda i, c: (0, 0, 0, 0, 0)),
            ),
        ),
        compiler_params=params(),
        cost_estimate=cost(4 * rows * kv, 12 * rows * kv),
        name="update",
    )(core, squares, grad, master)


def rest_kernel(pos, after, *refs):
    masters, outs = refs[:8], refs[8:]
    for d in range(4):
        for l in range(2):
            for kv in range(2):
                outs[d][0, l, :, kv * HEAD : (kv + 1) * HEAD] = masters[2 * d + kv][1 + l].astype(bf16)


def rest_blocks(pos, master, after):
    layers, rows, kv = master.shape
    half = rows // 2

    def spec(d, k):
        return pl.BlockSpec(
            (layers, half, HEAD),
            lambda xl, p: (0, p[0], k * KV_HEADS + xl * 2 + ((p[2] + d) % 4) // 2),
        )

    shape = (2, layers - 1, half, 2 * HEAD)
    return pl.pallas_call(
        rest_kernel,
        out_shape=[jax.ShapeDtypeStruct(shape, bf16)] * 4,
        grid_spec=pltpu.PrefetchScalarGridSpec(
            num_scalar_prefetch=1,
            grid=(2,),
            in_specs=[pl.BlockSpec(memory_space=pl.ANY)] + [spec(d, k) for d in range(4) for k in range(2)],
            out_specs=[pl.BlockSpec((1, *shape[1:]), lambda xl, p: (xl, 0, 0, 0))] * 4,
        ),
        compiler_params=params(),
        cost_estimate=cost(layers * rows * kv, 12 * rows * kv),
        name="rest_blocks",
    )(pos, after, *([master] * 8))


def regroup_kernel(pos, after, *refs):
    parts, (same, cross) = refs[:4], refs[4:]
    xl = pos[1] % 2
    for d in range(4):
        same[d] = parts[d][xl]
        cross[d] = parts[d][1 - xl]


def regroup(pos, parts, after):
    shape = (4, *parts[0].shape[1:])
    whole = lambda s: pl.BlockSpec(s, lambda i, p: (0,) * len(s))
    return pl.pallas_call(
        regroup_kernel,
        out_shape=[jax.ShapeDtypeStruct(shape, bf16)] * 2,
        grid_spec=pltpu.PrefetchScalarGridSpec(
            num_scalar_prefetch=1,
            grid=(1,),
            in_specs=[pl.BlockSpec(memory_space=pl.ANY)] + [whole(parts[0].shape)] * 4,
            out_specs=[whole(shape)] * 2,
        ),
        compiler_params=params(),
        cost_estimate=cost(parts[0].size, 16 * parts[0].size),
        name="regroup",
    )(pos, after, *parts)


def place_rest_kernel(pos, *refs):
    srcs, out = refs[:8], refs[8]
    zh = pos[2]
    for w in range(2):
        for dx in range(4):

            @pl.when((pl.program_id(1) == dx) & (pl.program_id(2) == w))
            def _():
                for dz in range(4):
                    out[0, 0, (zh - dz + 4) % 4, 0] = srcs[4 * w + dx][dz, 0]


def place_rest(pos, own, other, layers):
    _, count, half, width = own[0].shape
    src = pl.BlockSpec((4, 1, half, width), lambda l, d, w, p: (0, l, 0, 0))
    return pl.pallas_call(
        place_rest_kernel,
        out_shape=jax.ShapeDtypeStruct((layers, 4, 4, 2, half, width), bf16),
        grid_spec=pltpu.PrefetchScalarGridSpec(
            num_scalar_prefetch=1,
            grid=(count, 4, 2),
            in_specs=[src] * 8,
            out_specs=pl.BlockSpec(
                (1, 1, 4, 1, half, width),
                lambda l, d, w, p: (1 + l, (p[1] - d + 4) % 4, 0, (p[0] + w) % 2, 0, 0),
            ),
        ),
        compiler_params=params(),
        cost_estimate=cost(own[0].size, 32 * own[0].size),
        name="place_rest",
    )(pos, *own, *other)


def place_first_kernel(pos, own, other, into, out):
    @pl.when(pl.program_id(1) == 0)
    def _():
        out[0, :, 0] = own[...]

    @pl.when(pl.program_id(1) == 1)
    def _():
        out[0, :, 0] = other[...]


def place_first(pos, own, other, into):
    n, half, width = own.shape
    group = n // 2
    src = pl.BlockSpec((group, half, width), lambda s, w, p: (s, 0, 0))
    return pl.pallas_call(
        place_first_kernel,
        out_shape=jax.ShapeDtypeStruct(into.shape, bf16),
        grid_spec=pltpu.PrefetchScalarGridSpec(
            num_scalar_prefetch=1,
            grid=(2, 2),
            in_specs=[src, src, pl.BlockSpec(memory_space=pl.ANY)],
            out_specs=pl.BlockSpec((1, group, 1, half, width), lambda s, w, p: (0, s, (p[0] + w) % 2, 0, 0)),
        ),
        input_output_aliases={3: 0},
        compiler_params=params(),
        cost_estimate=cost(own.size, 8 * own.size),
        name="place_first",
    )(pos, own, other, into)


def per_device(
    hidden,
    cotangent,
    seq_ids,
    response_mask,
    group_ids,
    rewards,
    new_logp,
    old_logp,
    ref_logp,
    master,
):
    n_x, n_y, n_z = lax.axis_size("x"), lax.axis_size("y"), lax.axis_size(("zh", "zl"))
    n_shard = lax.axis_size(SHARD)
    groups = lax.axis_size(REP) * n_shard * SEQ_DEV // 8
    layers, rows, kv = master.shape
    pos = jnp.stack([lax.axis_index(a).astype(jnp.int32) for a in ("c", "x", "zh")])

    local_sums = group_sums(group_ids[0], rewards[0], groups)
    stats = sent_to_all(local_sums, REP).sum(axis=0)
    parts = rest_blocks(pos, master, stats)
    stats = sent_to_all(stats, SHARD)
    parts = [parts[0]] + [shifted(parts[d], "zh", d) for d in range(1, 4)]

    hidden_b = swapped(hidden)
    cotangent_b = swapped(cotangent)
    tok = token_rows(
        seq_ids[0], response_mask[0], group_ids[0], rewards[0], new_logp[0], old_logp[0], ref_logp[0]
    )
    tok_b = swapped(tok)

    sent = partial_product(
        pos, stats, tok.T, tok_b.T, cotangent, cotangent_b, hidden, hidden_b, parts[0], n_x, n_y
    )
    sent = sent.reshape(n_x * n_y, *sent.shape[2:])
    part = sum_turn(exchanged(sent, ("x", "y")))
    same, cross = regroup(pos, parts, part)
    rest = [same] + [shifted(same if d % 2 == 0 else cross, "x", d) for d in range(1, 4)]
    part = part.reshape(n_z, part.shape[0] // n_z, part.shape[1])
    zl = lax.axis_size("zl")
    part = exchanged(part, ("zh", "zl"))
    grad = exchanged(sum_spread(part, zl * n_y * 2), REP)
    squares = exchanged(squares_of(grad, n_shard), SHARD)
    grad = grad.reshape(zl, n_y, 2, *grad.shape[1:])
    new_master, first = update(pos, squares, grad, master, hidden.shape[1] * kv)

    other = [swapped(r) for r in rest]
    out = place_rest(pos, rest, other, layers)
    out = out.reshape(layers, n_shard, 2, rows // 2, 2 * HEAD)
    first = exchanged(first.reshape(n_shard, rows // 2, 2 * HEAD), SHARD)
    out = place_first(pos, first, swapped(first), out)
    return (new_master, out.reshape(layers, n_shard * rows, 2 * HEAD))


def solution(mesh):
    split = Mesh(mesh.devices.reshape(2, 4, 2, 4, 4), REP + SHARD)
    row = P(REP + SHARD, None)
    return jax.shard_map(
        per_device,
        mesh=split,
        in_specs=(row,) * 9 + (P(None, SHARD, None),),
        out_specs=(P(SHARD, None), P(None, None, SHARD)),
        check_vma=False,
    )
```

time: 239 us -> 226 us (0.946)
  waiting for transfers between devices: 72.7 us -> 46.7 us
  blocking collectives: 69.7 us -> 89.8 us
  Pallas kernels: 36.2 us -> 23.4 us
  local copies, waits for them, and re-layouts: 3.75 us -> 8.1 us
    all_to_all x5 -> x3, waiting for transfers between devices: 70.4 us -> 2.63 us  [exchanged(): return lax.all_to_all(blocks, axis, split_axis=0, concat_axis=0, tiled=True)]
    ppermute x0 -> x6, waiting for transfers between devices: none -> 42 us  [shifted(): return lax.ppermute(value, axis, [(i, (i + by) % n) for i in range(n)])]
    all_to_all x3 -> x4, blocking collectives: 69.7 us -> 89.8 us  [exchanged(): return lax.all_to_all(blocks, axis, split_axis=0, concat_axis=0, tiled=True)]
    all_to_all x5 -> x3, starting transfers between devices: 36.2 us -> 19.2 us  [exchanged(): return lax.all_to_all(blocks, axis, split_axis=0, concat_axis=0, tiled=True)]
    ppermute x0 -> x6, starting transfers between devices: none -> 13.2 us  [shifted(): return lax.ppermute(value, axis, [(i, (i + by) % n) for i in range(n)])]
    ppermute x6 -> x8, starting transfers between devices: 11 us -> 16.6 us  [swapped(): return lax.ppermute(value, 'c', [(0, 1), (1, 0)])]
    pallas_call x1, Pallas kernels: 5.49 us -> 0.96 us  [sum_turn(): pl.pallas_call(sum_turn_kernel, out_shape=jax.ShapeDtypeStruct((width, ro...]
    unnamed x16 -> x26, local copies, waits for them, and re-layouts: 2.33 us -> 6.68 us
  transfers between devices with their start and end apart: 11 -> 17, of which waited for: 7 -> 5; matrix products, arithmetic and copies ran while one was open for 4% -> 4% of each run, Pallas kernels for 6% -> 4%
where the time goes in v2:
time: 226 us; the launch traced here: 225 us
  blocking collectives  89.8 us (40%)
  starting transfers between devices  49 us (22%)
  waiting for transfers between devices  46.7 us (21%)
  Pallas kernels  23.4 us (10%)
  local copies, waits for them, and re-layouts  8.1 us (4%)
  matrix products  4.75 us (2%)
  other arithmetic  2.36 us (1%)
    all_to_all x4, blocking collectives, exchanged(): return lax.all_to_all(blocks, axis, split_axis=0, concat_axis=0, tiled=True)  89.8 us
    ppermute x6, waiting for transfers between devices, shifted(): return lax.ppermute(value, axis, [(i, (i + by) % n) for i in range(n)])  42 us
    all_to_all x3, starting transfers between devices, exchanged(): return lax.all_to_all(blocks, axis, split_axis=0, concat_axis=0, tiled=True)  19.2 us
    ppermute x8, starting transfers between devices, swapped(): return lax.ppermute(value, 'c', [(0, 1), (1, 0)])  16.6 us
    ppermute x6, starting transfers between devices, shifted(): return lax.ppermute(value, axis, [(i, (i + by) % n) for i in range(n)])  13.2 us
    pallas_call x1, Pallas kernels, partial_product(): pl.pallas_call(partial_kernel, out_shape=jax.ShapeDtypeStruct((nx, ny, ha...  8.61 us
    pallas_call x1, Pallas kernels, place_rest(): pl.pallas_call(place_rest_kernel, out_shape=jax.ShapeDtypeStruct((layers,...  7.12 us
    unnamed x26, local copies, waits for them, and re-layouts  6.68 us
  transfers between devices with their start and end apart: 17, of which 5 were waited for; matrix products, arithmetic and copies ran while one was open for 4% of the time, Pallas kernels for 4%

profile of v2, /device:TPU:33, one launch (start us, length us, event | category | flops | bytes accessed | tf_op | source)
XLA Modules:
  0.0 224.9 jit_solution(8444491372407043461)
XLA Ops:
  3.6 5.7 %all-to-all-start = ((f32[16,3,128]{2,1,0:T(4,128)}), f32[16,3,128]{2,1,0:T(4,128)S(1)}, u32[]{:S(2)}, u32[]{:S(2)}) async-start(f32[16,3,128]{2,1,0:T(4,128)} %broadcast_in_dim.8), calls=%async_computation | async-start | bytes 65536 | tf_op jit(solution)/shard_map/all_to_all | solution.py:30
  9.7 1.0 fusion.2
  10.6 1.0 fusion.1
  11.6 1.0 fusion.3
  13.4 1.0 fusion.4
  16.1 9.9 %all-to-all-start.1 = ((f32[16,3,128]{2,1,0:T(4,128)}), f32[16,3,128]{2,1,0:T(4,128)S(1)}, u32[]{:S(2)}, u32[]{:S(2)}) async-start(f32[16,3,128]{2,1,0:T(4,128)} %broadcast_in_dim.9), calls=%async_computation.1 | async-start | bytes 65536 | tf_op jit(solution)/shard_map/all_to_all | solution.py:30
  26.1 1.8 copy-done
  27.9 1.6 rest_blocks.1
  32.2 2.6 %all-to-all-done.1.stats = f32[16,3,128]{2,1,0:T(4,128)S(1)} async-done(((f32[16,3,128]{2,1,0:T(4,128)}), f32[16,3,128]{2,1,0:T(4,128)S(1)}, u32[]{:S(2)}, u32[]{:S(2)}) %all-to-all-start.1) | async-done | bytes 24608 | tf_op jit(solution)/shard_map/all_to_all | solution.py:30
  34.9 1.2 copy-done.3
  36.0 0.9 copy-done.5
  37.0 8.6 %partial_product.1 = bf16[4,4,128,896]{3,2,1,0:T(8,128)(2,1)S(1)} custom-call(s32[3]{0:T(128)S(1)} %pad_add_fusion.pos.core.refs_0_, f32[16,3,128]{2,1,0:T(4,128)S(1)} %all-to-all-done.1.stats, f32[448,8]{1,0:T(8,128)S(1)} %bitcast.45, f32[448,8]{1,0:T(8,128)} %bitcast.17.tok_b, bf16[448,1024]{1,0:T(8,128)(2,1)S(1)} %copy-done.3, ...), custom_call_target="tpu_custom_call" | custom-call | flops 3288334336 | bytes 10092544 | tf_op jit(solution)/shard_map/partial_product/pallas_call | solution.py:98
  45.6 47.6 %all_to_all.35.src = bf16[16,128,896]{2,1,0:T(8,128)(2,1)S(1)} all-to-all(bf16[16,128,896]{2,1,0:T(8,128)(2,1)S(1)} %bitcast.42), channel_id=1, replica_groups=mesh['zl'=2,'y'=4,'c'=2,'x'=4,'zh'=4] {'x','y'}, dimensions={0} | all-to-all | bytes 7340032 | tf_op jit(solution)/shard_map/all_to_all | solution.py:30
  93.2 1.0 sum_turn.1.after
  94.2 14.1 %all_to_all.36.src = bf16[8,112,128]{2,1,0:T(8,128)(2,1)S(1)} all-to-all(bf16[8,112,128]{2,1,0:T(8,128)(2,1)S(1)} %bitcast.44), channel_id=1, replica_groups=mesh['zl'=2,'y'=4,'c'=2,'x'=4,'zh'=4] {'zh','zl'}, dimensions={0} | all-to-all | bytes 458752 | tf_op jit(solution)/shard_map/all_to_all | solution.py:30
  108.4 16.4 %all_to_all.37.grad = bf16[16,112,128]{2,1,0:T(8,128)(2,1)S(1)} all-to-all(bf16[16,112,128]{2,1,0:T(8,128)(2,1)S(1)} %sum_spread.1), channel_id=1, replica_groups=mesh['zl'=2,'y'=4,'c'=2,'x'=4,'zh'=4] {'zl','y','c'}, dimensions={0} | all-to-all | bytes 917504 | tf_op jit(solution)/shard_map/all_to_all | solution.py:30
  124.9 11.7 %all_to_all.38.refs_1_ = f32[16,1,128]{2,1,0:T(1,128)S(1)} all-to-all(f32[16,1,128]{2,1,0:T(1,128)S(1)} %squares_of.1), channel_id=1, replica_groups=mesh['zl'=2,'y'=4,'c'=2,'x'=4,'zh'=4] {'x','zh'}, dimensions={0} | all-to-all | bytes 16384 | tf_op jit(solution)/shard_map/all_to_all | solution.py:30
  136.5 2.0 update.1
  138.6 3.6 %all-to-all-start.6 = ((bf16[16,112,256]{2,1,0:T(8,128)(2,1)}), bf16[16,112,256]{2,1,0:T(8,128)(2,1)S(1)}, u32[]{:S(2)}, u32[]{:S(2)}) async-start(bf16[16,112,256]{2,1,0:T(8,128)(2,1)} %bitcast.21), calls=%async_computation.6 | async-start | bytes 1835008 | tf_op jit(solution)/shard_map/all_to_all | solution.py:30
  142.2 2.2 collective-permute-start.4
  144.4 3.3 %collective-permute-start.5 = (bf16[2,2,112,256]{3,2,1,0:T(8,128)(2,1)S(1)}, bf16[2,2,112,256]{3,2,1,0:T(8,128)(2,1)S(1)}, u32[]{:S(2)}, u32[]{:S(2)}) collective-permute-start(bf16[2,2,112,256]{3,2,1,0:T(8,128)(2,1)S(1)} %copy-done.10), channel_id=1, source_target_pairs={{0,2},{1,3},{2,0},{3,1},{4,6},{5,7},{6,4},{7,5},{8,10},{9,11},{10,... | collective-permute-start | bytes 688136 | tf_op jit(solution)/shard_map/ppermute | solution.py:26
  147.8 3.3 %collective-permute-start.6 = (bf16[2,2,112,256]{3,2,1,0:T(8,128)(2,1)S(1)}, bf16[2,2,112,256]{3,2,1,0:T(8,128)(2,1)S(1)}, u32[]{:S(2)}, u32[]{:S(2)}) collective-permute-start(bf16[2,2,112,256]{3,2,1,0:T(8,128)(2,1)S(1)} %copy-done.8), channel_id=1, source_target_pairs={{0,3},{1,0},{2,1},{3,2},{4,7},{5,4},{6,5},{7,6},{8,11},{9,8},{10,9... | collective-permute-start | bytes 688136 | tf_op jit(solution)/shard_map/ppermute | solution.py:26
  151.0 34.9 %collective-permute-done.4.refs_1_ = bf16[2,2,112,256]{3,2,1,0:T(8,128)(2,1)S(1)} collective-permute-done((bf16[2,2,112,256]{3,2,1,0:T(8,128)(2,1)S(1)}, bf16[2,2,112,256]{3,2,1,0:T(8,128)(2,1)S(1)}, u32[]{:S(2)}, u32[]{:S(2)}) %collective-permute-start.4) | collective-permute-done | bytes 229408 | tf_op jit(solution)/shard_map/ppermute | solution.py:26
  186.6 2.7 %collective-permute-start.9 = (bf16[4,2,112,256]{3,2,1,0:T(8,128)(2,1)S(1)}, bf16[4,2,112,256]{3,2,1,0:T(8,128)(2,1)S(1)}, u32[]{:S(2)}, u32[]{:S(2)}) collective-permute-start(bf16[4,2,112,256]{3,2,1,0:T(8,128)(2,1)S(1)} %get-tuple-element.17), channel_id=1, source_target_pairs={{0,12},{4,0},{8,4},{12,8},{1,13},{5,1},{9,5},{13,9},{2,14},{6,2},{... | collective-permute-start | bytes 1376264 | tf_op jit(solution)/shard_map/ppermute | solution.py:26
  189.3 1.7 collective-permute-start.8
  191.1 1.5 collective-permute-start.3
  192.5 7.0 %collective-permute-done.9.refs_3_ = bf16[4,2,112,256]{3,2,1,0:T(8,128)(2,1)S(1)} collective-permute-done((bf16[4,2,112,256]{3,2,1,0:T(8,128)(2,1)S(1)}, bf16[4,2,112,256]{3,2,1,0:T(8,128)(2,1)S(1)}, u32[]{:S(2)}, u32[]{:S(2)}) %collective-permute-start.9) | collective-permute-done | bytes 458784 | tf_op jit(solution)/shard_map/ppermute | solution.py:26
  199.5 10.4 %collective-permute-start.13 = (bf16[4,2,112,256]{3,2,1,0:T(8,128)(2,1)S(1)}, bf16[4,2,112,256]{3,2,1,0:T(8,128)(2,1)S(1)}, u32[]{:S(2)}, u32[]{:S(2)}) collective-permute-start(bf16[4,2,112,256]{3,2,1,0:T(8,128)(2,1)S(1)} %collective-permute-done.9.refs_3_), channel_id=1, source_target_pairs={{0,16},{16,0},{1,17},{17,1},{2,18},{18,2},{3,19},{19,3},{4,20},{20... | collective-permute-start | bytes 1376264 | tf_op jit(solution)/shard_map/ppermute | solution.py:21
  209.9 3.4 %collective-permute-start.11 = (bf16[4,2,112,256]{3,2,1,0:T(8,128)(2,1)S(1)}, bf16[4,2,112,256]{3,2,1,0:T(8,128)(2,1)S(1)}, u32[]{:S(2)}, u32[]{:S(2)}) collective-permute-start(bf16[4,2,112,256]{3,2,1,0:T(8,128)(2,1)S(1)} %collective-permute-done.7.refs_1_), channel_id=1, source_target_pairs={{0,16},{16,0},{1,17},{17,1},{2,18},{18,2},{3,19},{19,3},{4,20},{20... | collective-permute-start | bytes 1376264 | tf_op jit(solution)/shard_map/ppermute | solution.py:21
  213.3 1.4 collective-permute-done.11.refs_5_
  215.4 7.1 %place_rest.1 = bf16[3,4,4,2,112,256]{5,4,3,2,1,0:T(8,128)(2,1)} custom-call(s32[3]{0:T(128)S(1)} %pad_add_fusion.pos.core.refs_0_, bf16[4,2,112,256]{3,2,1,0:T(8,128)(2,1)S(1)} %get-tuple-element.16.refs_0_, bf16[4,2,112,256]{3,2,1,0:T(8,128)(2,1)S(1)} %collective-permute-done.7.refs_1_, bf16[4,2,112,256]{3,2,1,0:T(8,128)(2,1)S(1)} %collective-permute-done.8.refs_2_, ...), custom_call_target="tpu_custom_call" | custom-call | flops 229376 | bytes 7340032 | tf_op jit(solution)/shard_map/place_rest/pallas_call | solution.py:302
  222.5 2.4 %place_first.1 = bf16[3,16,2,112,256]{4,3,2,1,0:T(8,128)(2,1)} custom-call(s32[3]{0:T(128)S(1)} %pad_add_fusion.pos.core.refs_0_, bf16[16,112,256]{2,1,0:T(8,128)(2,1)S(1)} %all-to-all-done.6.own, bf16[16,112,256]{2,1,0:T(8,128)(2,1)S(1)} %collective-permute-done.3.other, bf16[3,16,2,112,256]{4,3,2,1,0:T(8,128)(2,1)} %bitcast.46), custom_call_target="tpu_custom_call", output_to_operand_aliasing={{}: (3, {})} | custom-call | flops 458752 | bytes 3670016 | tf_op jit(solution)/shard_map/place_first/pallas_call | solution.py:334
  (59 shorter events, 10.3 us)
Async XLA Ops:
  0.6 34.2 %collective-permute-start.2 = (bf16[448,3584]{1,0:T(8,128)(2,1)}, bf16[448,3584]{1,0:T(8,128)(2,1)}, u32[]{:S(2)}, u32[]{:S(2)}) collective-permute-start(bf16[448,3584]{1,0:T(8,128)(2,1)} %hid_a.1), channel_id=1, source_target_pairs={{0,16},{16,0},{1,17},{17,1},{2,18},{18,2},{3,19},{19,3},{4,20},{20... | collective-permute-start | bytes 9633800 | tf_op jit(solution)/shard_map/ppermute | solution.py:21
  3.6 11.9 %all-to-all-start = ((f32[16,3,128]{2,1,0:T(4,128)}), f32[16,3,128]{2,1,0:T(4,128)S(1)}, u32[]{:S(2)}, u32[]{:S(2)}) async-start(f32[16,3,128]{2,1,0:T(4,128)} %broadcast_in_dim.8), calls=%async_computation | async-start | bytes 65536 | tf_op jit(solution)/shard_map/all_to_all | solution.py:30
  9.3 25.6 %collective-permute-start.1 = (bf16[448,1024]{1,0:T(8,128)(2,1)}, bf16[448,1024]{1,0:T(8,128)(2,1)}, u32[]{:S(2)}, u32[]{:S(2)}) collective-permute-start(bf16[448,1024]{1,0:T(8,128)(2,1)} %cot_a.1), channel_id=1, source_target_pairs={{0,16},{16,0},{1,17},{17,1},{2,18},{18,2},{3,19},{19,3},{4,20},{20... | collective-permute-start | bytes 2752520 | tf_op jit(solution)/shard_map/ppermute | solution.py:21
  15.3 16.9 %collective-permute-start = (f32[8,448]{0,1:T(8,128)S(1)}, f32[8,448]{0,1:T(8,128)}, u32[]{:S(2)}, u32[]{:S(2)}) collective-permute-start(f32[8,448]{0,1:T(8,128)S(1)} %copy.29), channel_id=1, source_target_pairs={{0,16},{16,0},{1,17},{17,1},{2,18},{18,2},{3,19},{19,3},{4,20},{20... | collective-permute-start | bytes 43016 | tf_op jit(solution)/shard_map/ppermute | solution.py:21
  16.1 18.7 %all-to-all-start.1 = ((f32[16,3,128]{2,1,0:T(4,128)}), f32[16,3,128]{2,1,0:T(4,128)S(1)}, u32[]{:S(2)}, u32[]{:S(2)}) async-start(f32[16,3,128]{2,1,0:T(4,128)} %broadcast_in_dim.9), calls=%async_computation.1 | async-start | bytes 65536 | tf_op jit(solution)/shard_map/all_to_all | solution.py:30
  26.1 1.8 copy-start
  27.9 7.0 %copy-start.2 = (bf16[448,3584]{1,0:T(8,128)(2,1)S(1)}, bf16[448,3584]{1,0:T(8,128)(2,1)}, u32[]{:S(2)}) copy-start(bf16[448,3584]{1,0:T(8,128)(2,1)} %hid_a.1) | copy-start | bytes 9633796
  29.4 0.7 copy-start.4
  30.1 0.7 copy-start.7
  30.8 0.7 copy-start.9
  31.5 0.7 copy-start.11
  34.9 1.2 copy-start.3
  36.0 0.9 copy-start.5
  93.2 43.3 %copy-start.1 = (f32[3,224,1024]{2,1,0:T(8,128)S(1)}, f32[3,224,1024]{2,1,0:T(8,128)}, u32[]{:S(2)}) copy-start(f32[3,224,1024]{2,1,0:T(8,128)} %refs_3_.3) | copy-start | bytes 8257540
  108.3 33.9 %copy-start.12 = (bf16[2,2,112,256]{3,2,1,0:T(8,128)(2,1)S(1)}, bf16[2,2,112,256]{3,2,1,0:T(8,128)(2,1)}, u32[]{:S(2)}) copy-start(bf16[2,2,112,256]{3,2,1,0:T(8,128)(2,1)} %copy-done.11) | copy-start | bytes 688132
  108.3 36.1 %copy-start.10 = (bf16[2,2,112,256]{3,2,1,0:T(8,128)(2,1)S(1)}, bf16[2,2,112,256]{3,2,1,0:T(8,128)(2,1)}, u32[]{:S(2)}) copy-start(bf16[2,2,112,256]{3,2,1,0:T(8,128)(2,1)} %copy-done.9) | copy-start | bytes 688132
  108.3 39.4 %copy-start.8 = (bf16[2,2,112,256]{3,2,1,0:T(8,128)(2,1)S(1)}, bf16[2,2,112,256]{3,2,1,0:T(8,128)(2,1)}, u32[]{:S(2)}) copy-start(bf16[2,2,112,256]{3,2,1,0:T(8,128)(2,1)} %copy-done.7) | copy-start | bytes 688132
  108.3 77.7 %copy-start.6 = (bf16[2,2,112,256]{3,2,1,0:T(8,128)(2,1)S(1)}, bf16[2,2,112,256]{3,2,1,0:T(8,128)(2,1)}, u32[]{:S(2)}) copy-start(bf16[2,2,112,256]{3,2,1,0:T(8,128)(2,1)} %copy-done.4) | copy-start | bytes 688132
  138.6 52.5 %all-to-all-start.6 = ((bf16[16,112,256]{2,1,0:T(8,128)(2,1)}), bf16[16,112,256]{2,1,0:T(8,128)(2,1)S(1)}, u32[]{:S(2)}, u32[]{:S(2)}) async-start(bf16[16,112,256]{2,1,0:T(8,128)(2,1)} %bitcast.21), calls=%async_computation.6 | async-start | bytes 1835008 | tf_op jit(solution)/shard_map/all_to_all | solution.py:30
  142.2 43.8 %collective-permute-start.4 = (bf16[2,2,112,256]{3,2,1,0:T(8,128)(2,1)S(1)}, bf16[2,2,112,256]{3,2,1,0:T(8,128)(2,1)S(1)}, u32[]{:S(2)}, u32[]{:S(2)}) collective-permute-start(bf16[2,2,112,256]{3,2,1,0:T(8,128)(2,1)S(1)} %copy-done.12), channel_id=1, source_target_pairs={{0,1},{1,2},{2,3},{3,0},{4,5},{5,6},{6,7},{7,4},{8,9},{9,10},{10,1... | collective-permute-start | bytes 688136 | tf_op jit(solution)/shard_map/ppermute | solution.py:26
  144.4 41.5 %collective-permute-start.5 = (bf16[2,2,112,256]{3,2,1,0:T(8,128)(2,1)S(1)}, bf16[2,2,112,256]{3,2,1,0:T(8,128)(2,1)S(1)}, u32[]{:S(2)}, u32[]{:S(2)}) collective-permute-start(bf16[2,2,112,256]{3,2,1,0:T(8,128)(2,1)S(1)} %copy-done.10), channel_id=1, source_target_pairs={{0,2},{1,3},{2,0},{3,1},{4,6},{5,7},{6,4},{7,5},{8,10},{9,11},{10,... | collective-permute-start | bytes 688136 | tf_op jit(solution)/shard_map/ppermute | solution.py:26
  147.8 38.2 %collective-permute-start.6 = (bf16[2,2,112,256]{3,2,1,0:T(8,128)(2,1)S(1)}, bf16[2,2,112,256]{3,2,1,0:T(8,128)(2,1)S(1)}, u32[]{:S(2)}, u32[]{:S(2)}) collective-permute-start(bf16[2,2,112,256]{3,2,1,0:T(8,128)(2,1)S(1)} %copy-done.8), channel_id=1, source_target_pairs={{0,3},{1,0},{2,1},{3,2},{4,7},{5,4},{6,5},{7,6},{8,11},{9,8},{10,9... | collective-permute-start | bytes 688136 | tf_op jit(solution)/shard_map/ppermute | solution.py:26
  186.6 12.9 %collective-permute-start.9 = (bf16[4,2,112,256]{3,2,1,0:T(8,128)(2,1)S(1)}, bf16[4,2,112,256]{3,2,1,0:T(8,128)(2,1)S(1)}, u32[]{:S(2)}, u32[]{:S(2)}) collective-permute-start(bf16[4,2,112,256]{3,2,1,0:T(8,128)(2,1)S(1)} %get-tuple-element.17), channel_id=1, source_target_pairs={{0,12},{4,0},{8,4},{12,8},{1,13},{5,1},{9,5},{13,9},{2,14},{6,2},{... | collective-permute-start | bytes 1376264 | tf_op jit(solution)/shard_map/ppermute | solution.py:26
  189.3 20.6 %collective-permute-start.7 = (bf16[4,2,112,256]{3,2,1,0:T(8,128)(2,1)S(1)}, bf16[4,2,112,256]{3,2,1,0:T(8,128)(2,1)S(1)}, u32[]{:S(2)}, u32[]{:S(2)}) collective-permute-start(bf16[4,2,112,256]{3,2,1,0:T(8,128)(2,1)S(1)} %get-tuple-element.17), channel_id=1, source_target_pairs={{0,4},{4,8},{8,12},{12,0},{1,5},{5,9},{9,13},{13,1},{2,6},{6,10},{... | collective-permute-start | bytes 1376264 | tf_op jit(solution)/shard_map/ppermute | solution.py:26
  189.3 24.0 %collective-permute-start.8 = (bf16[4,2,112,256]{3,2,1,0:T(8,128)(2,1)S(1)}, bf16[4,2,112,256]{3,2,1,0:T(8,128)(2,1)S(1)}, u32[]{:S(2)}, u32[]{:S(2)}) collective-permute-start(bf16[4,2,112,256]{3,2,1,0:T(8,128)(2,1)S(1)} %get-tuple-element.16.refs_0_), channel_id=1, source_target_pairs={{0,8},{4,12},{8,0},{12,4},{1,9},{5,13},{9,1},{13,5},{2,10},{6,14},... | collective-permute-start | bytes 1376264 | tf_op jit(solution)/shard_map/ppermute | solution.py:26
  191.1 31.5 %collective-permute-start.3 = (bf16[16,112,256]{2,1,0:T(8,128)(2,1)S(1)}, bf16[16,112,256]{2,1,0:T(8,128)(2,1)S(1)}, u32[]{:S(2)}, u32[]{:S(2)}) collective-permute-start(bf16[16,112,256]{2,1,0:T(8,128)(2,1)S(1)} %all-to-all-done.6.own), channel_id=1, source_target_pairs={{0,16},{16,0},{1,17},{17,1},{2,18},{18,2},{3,19},{19,3},{4,20},{20... | collective-permute-start | bytes 2752520 | tf_op jit(solution)/shard_map/ppermute | solution.py:21
  192.5 20.8 %collective-permute-start.10 = (bf16[4,2,112,256]{3,2,1,0:T(8,128)(2,1)S(1)}, bf16[4,2,112,256]{3,2,1,0:T(8,128)(2,1)S(1)}, u32[]{:S(2)}, u32[]{:S(2)}) collective-permute-start(bf16[4,2,112,256]{3,2,1,0:T(8,128)(2,1)S(1)} %get-tuple-element.16.refs_0_), channel_id=1, source_target_pairs={{0,16},{16,0},{1,17},{17,1},{2,18},{18,2},{3,19},{19,3},{4,20},{20... | collective-permute-start | bytes 1376264 | tf_op jit(solution)/shard_map/ppermute | solution.py:21
  199.5 13.8 %collective-permute-start.13 = (bf16[4,2,112,256]{3,2,1,0:T(8,128)(2,1)S(1)}, bf16[4,2,112,256]{3,2,1,0:T(8,128)(2,1)S(1)}, u32[]{:S(2)}, u32[]{:S(2)}) collective-permute-start(bf16[4,2,112,256]{3,2,1,0:T(8,128)(2,1)S(1)} %collective-permute-done.9.refs_3_), channel_id=1, source_target_pairs={{0,16},{16,0},{1,17},{17,1},{2,18},{18,2},{3,19},{19,3},{4,20},{20... | collective-permute-start | bytes 1376264 | tf_op jit(solution)/shard_map/ppermute | solution.py:21
  209.9 4.9 %collective-permute-start.11 = (bf16[4,2,112,256]{3,2,1,0:T(8,128)(2,1)S(1)}, bf16[4,2,112,256]{3,2,1,0:T(8,128)(2,1)S(1)}, u32[]{:S(2)}, u32[]{:S(2)}) collective-permute-start(bf16[4,2,112,256]{3,2,1,0:T(8,128)(2,1)S(1)} %collective-permute-done.7.refs_1_), channel_id=1, source_target_pairs={{0,16},{16,0},{1,17},{17,1},{2,18},{18,2},{3,19},{19,3},{4,20},{20... | collective-permute-start | bytes 1376264 | tf_op jit(solution)/shard_map/ppermute | solution.py:21
  213.3 2.1 collective-permute-start.12

commit v3 on v2

--- a/solution.py
+++ b/solution.py
@@ -24,6 +24,10 @@
 def shifted(value, axis, by):
     n = lax.axis_size(axis)
     return lax.ppermute(value, axis, [(i, (i + by) % n) for i in range(n)])
+
+
+def spread_out(blocks, axis):
+    return [blocks[0]] + [shifted(blocks[d], axis, d) for d in range(1, 4)]
 
 
 def exchanged(blocks, axis):
@@ -63,16 +67,19 @@
     return jnp.stack([weight, ratio, penalty, tok_reward, tok_group, zero, zero, zero], axis=0)
 
 
-def partial_kernel(core, stats, tok_a, tok_b, cot_a, cot_b, hid_a, hid_b, after, out, delta_a, delta_b):
+def partial_kernel(pos, stats, tok_a, tok_b, cot_a, cot_b, hid_a, hid_b, *refs):
+    outs, (delta_a, delta_b) = refs[:8], refs[8:]
     half = cot_a.shape[1] // 2
-
-    @pl.when(pl.program_id(0) == 0)
+    rows = outs[0].shape[1]
+    step = pl.program_id(0)
+
+    @pl.when(step == 0)
     def _():
         sums = jnp.sum(stats[...], axis=0)
         count = jnp.maximum(sums[0:1, :], 1.0)
         mean = sums[1:2, :] / count
         spread = jnp.maximum(jnp.sqrt(jnp.maximum(sums[2:3, :] / count - mean * mean, 0.0)), 0.5)
-        cols = pl.ds(pl.multiple_of(core[0] * half, half), half)
+        cols = pl.ds(pl.multiple_of(pos[0] * half, half), half)
         for tok, cot, delta in ((tok_a, cot_a, delta_a), (tok_b, cot_b, delta_b)):
             t = tok[...]
             lane = lax.broadcasted_iota(jnp.int32, (t.shape[0], LANES), 1).astype(f32)
@@ -81,66 +88,91 @@
             tok_std = jnp.sum(jnp.where(pick, spread, 0.0), axis=1, keepdims=True)
             adv = (t[:, 3:4] - tok_mean) / tok_std
             coef = t[:, 0:1] * (-adv * t[:, 1:2] + t[:, 2:3])
-            delta[...] = (coef * cot[:, cols].astype(f32)).T.astype(bf16)
+            turned = (coef * cot[:, cols].astype(f32)).T.astype(bf16)
+            for y in range(4):
+                delta[y * rows : (y + 1) * rows, :] = turned[2 * y * rows : (2 * y + 1) * rows]
+                to = pl.multiple_of((4 + (y - pos[3] + 4) % 4) * rows, rows)
+                delta[pl.ds(to, rows), :] = turned[(2 * y + 1) * rows : (2 * y + 2) * rows]
 
     acc = jnp.dot(delta_a[...], hid_a[...], preferred_element_type=f32)
     acc = acc + jnp.dot(delta_b[...], hid_b[...], preferred_element_type=f32)
-    out[...] = acc.astype(bf16).reshape(out.shape)
-
-
-def partial_product(core, stats, tok_a, tok_b, cot_a, cot_b, hid_a, hid_b, after, nx, ny):
+    acc = acc.astype(bf16).reshape(8, rows, acc.shape[1])
+    for d in range(4):
+
+        @pl.when(step == d)
+        def _():
+            outs[d][...] = acc[:4]
+
+        outs[4 + d][(pos[1] + step) % 4] = acc[4 + d]
+
+
+def partial_product(pos, stats, tok_a, tok_b, cot_a, cot_b, hid_a, hid_b):
     toks, width = hid_a.shape
-    kv = cot_a.shape[1]
-    half = kv // 2
-    blk = width // nx
-    whole = lambda a: pl.BlockSpec(a.shape, lambda i, c: (0,) * a.ndim)
-    hid = pl.BlockSpec((toks, blk), lambda i, c: (0, i))
+    half = cot_a.shape[1] // 2
+    blk = width // 4
+    shape = (4, half // 8, blk)
+    whole = lambda a: pl.BlockSpec(a.shape, lambda i, p: (0,) * a.ndim)
+    hid = pl.BlockSpec((toks, blk), lambda i, p: (0, (p[1] + i) % 4))
     return pl.pallas_call(
         partial_kernel,
-        out_shape=jax.ShapeDtypeStruct((nx, ny, half // ny, blk), bf16),
-        grid_spec=pltpu.PrefetchScalarGridSpec(
-            num_scalar_prefetch=1,
-            grid=(nx,),
-            in_specs=[whole(stats), whole(tok_a), whole(tok_b), whole(cot_a), whole(cot_b), hid, hid, pl.BlockSpec(memory_space=pl.ANY)],
-            out_specs=pl.BlockSpec((1, ny, half // ny, blk), lambda i, c: (i, 0, 0, 0)),
+        out_shape=[jax.ShapeDtypeStruct(shape, bf16)] * 8,
+        grid_spec=pltpu.PrefetchScalarGridSpec(
+            num_scalar_prefetch=1,
+            grid=(4,),
+            in_specs=[whole(stats), whole(tok_a), whole(tok_b), whole(cot_a), whole(cot_b), hid, hid],
+            out_specs=[pl.BlockSpec(shape, lambda i, p: (0, 0, 0))] * 8,
             scratch_shapes=[pltpu.VMEM((half, toks), bf16), pltpu.VMEM((half, toks), bf16)],
         ),
         compiler_params=params(),
         cost_estimate=cost(4 * toks * width * half, 4 * toks * width + 2 * width * half),
         name="partial_product",
-    )(core, stats, tok_a, tok_b, cot_a, cot_b, hid_a, hid_b, after)
-
-
-def sum_turn_kernel(src, out, acc):
-    step = pl.program_id(0)
-    total = jnp.sum(src[...].astype(f32), axis=0)
-
-    @pl.when(step == 0)
-    def _():
-        acc[...] = total
-
-    @pl.when(step > 0)
-    def _():
-        acc[...] += total
-
-    @pl.when(step == pl.num_programs(0) - 1)
-    def _():
-        out[...] = acc[...].T.astype(bf16)
-
-
-def sum_turn(blocks):
-    n, rows, width = blocks.shape
+    )(pos, stats, tok_a, tok_b, cot_a, cot_b, hid_a, hid_b)
+
+
+def sum_mid_kernel(pos, *refs):
+    for half in range(2):
+        srcs, outs = refs[4 * half : 4 * half + 4], refs[8 + 4 * half : 12 + 4 * half]
+        at = pos[3] if half == 0 else pos[1]
+        for d in range(4):
+            k = (at + d) % 4
+            outs[d][...] = sum(src[k].astype(f32) for src in srcs).astype(bf16)
+
+
+def sum_mid(pos, first, second):
+    _, rows, width = first[0].shape
+    whole = lambda *shape: pl.BlockSpec(shape, lambda i, p: (0,) * len(shape))
+    out = pl.pallas_call(
+        sum_mid_kernel,
+        out_shape=[jax.ShapeDtypeStruct((rows, width), bf16)] * 8,
+        grid_spec=pltpu.PrefetchScalarGridSpec(
+            num_scalar_prefetch=1,
+            grid=(1,),
+            in_specs=[whole(4, rows, width)] * 8,
+            out_specs=[whole(rows, width)] * 8,
+        ),
+        compiler_params=params(),
+        cost_estimate=cost(32 * rows * width, 80 * rows * width),
+        name="sum_mid",
+    )(pos, *first, *second)
+    return out[:4], out[4:]
+
+
+def sum_turn_kernel(*refs):
+    srcs, out = refs[:8], refs[8]
+    first = sum(src[...].astype(f32) for src in srcs[:4])
+    second = sum(src[...].astype(f32) for src in srcs[4:])
+    out[...] = jnp.concatenate([first, second], axis=0).T.astype(bf16)
+
+
+def sum_turn(first, second):
+    rows, width = first[0].shape
     return pl.pallas_call(
         sum_turn_kernel,
-        out_shape=jax.ShapeDtypeStruct((width, rows), bf16),
-        grid=(4,),
-        in_specs=[pl.BlockSpec((n // 4, rows, width), lambda i: (i, 0, 0))],
-        out_specs=pl.BlockSpec((width, rows), lambda i: (0, 0)),
-        scratch_shapes=[pltpu.VMEM((rows, width), f32)],
-        compiler_params=params(),
-        cost_estimate=cost(n * rows * width, 2 * n * rows * width),
+        out_shape=jax.ShapeDtypeStruct((width, 2 * rows), bf16),
+        compiler_params=params(),
+        cost_estimate=cost(8 * rows * width, 20 * rows * width),
         name="sum_turn",
-    )(blocks)
+    )(*first, *second)
 
 
 def sum_spread_kernel(src, out):
@@ -224,7 +256,7 @@
     )(core, squares, grad, master)
 
 
-def rest_kernel(pos, after, *refs):
+def rest_kernel(pos, *refs):
     masters, outs = refs[:8], refs[8:]
     for d in range(4):
         for l in range(2):
@@ -232,7 +264,7 @@
                 outs[d][0, l, :, kv * HEAD : (kv + 1) * HEAD] = masters[2 * d + kv][1 + l].astype(bf16)
 
 
-def rest_blocks(pos, master, after):
+def rest_blocks(pos, master):
     layers, rows, kv = master.shape
     half = rows // 2
 
@@ -249,16 +281,16 @@
         grid_spec=pltpu.PrefetchScalarGridSpec(
             num_scalar_prefetch=1,
             grid=(2,),
-            in_specs=[pl.BlockSpec(memory_space=pl.ANY)] + [spec(d, k) for d in range(4) for k in range(2)],
+            in_specs=[spec(d, k) for d in range(4) for k in range(2)],
             out_specs=[pl.BlockSpec((1, *shape[1:]), lambda xl, p: (xl, 0, 0, 0))] * 4,
         ),
         compiler_params=params(),
         cost_estimate=cost(layers * rows * kv, 12 * rows * kv),
         name="rest_blocks",
-    )(pos, after, *([master] * 8))
-
-
-def regroup_kernel(pos, after, *refs):
+    )(pos, *([master] * 8))
+
+
+def regroup_kernel(pos, *refs):
     parts, (same, cross) = refs[:4], refs[4:]
     xl = pos[1] % 2
     for d in range(4):
@@ -266,7 +298,7 @@
         cross[d] = parts[d][1 - xl]
 
 
-def regroup(pos, parts, after):
+def regroup(pos, parts):
     shape = (4, *parts[0].shape[1:])
     whole = lambda s: pl.BlockSpec(s, lambda i, p: (0,) * len(s))
     return pl.pallas_call(
@@ -275,13 +307,13 @@
         grid_spec=pltpu.PrefetchScalarGridSpec(
             num_scalar_prefetch=1,
             grid=(1,),
-            in_specs=[pl.BlockSpec(memory_space=pl.ANY)] + [whole(parts[0].shape)] * 4,
+            in_specs=[whole(parts[0].shape)] * 4,
             out_specs=[whole(shape)] * 2,
         ),
         compiler_params=params(),
         cost_estimate=cost(parts[0].size, 16 * parts[0].size),
         name="regroup",
-    )(pos, after, *parts)
+    )(pos, *parts)
 
 
 def place_rest_kernel(pos, *refs):
@@ -359,17 +391,15 @@
     ref_logp,
     master,
 ):
-    n_x, n_y, n_z = lax.axis_size("x"), lax.axis_size("y"), lax.axis_size(("zh", "zl"))
+    n_y, n_z = lax.axis_size("y"), lax.axis_size(("zh", "zl"))
     n_shard = lax.axis_size(SHARD)
     groups = lax.axis_size(REP) * n_shard * SEQ_DEV // 8
     layers, rows, kv = master.shape
-    pos = jnp.stack([lax.axis_index(a).astype(jnp.int32) for a in ("c", "x", "zh")])
+    pos = jnp.stack([lax.axis_index(a).astype(jnp.int32) for a in ("c", "x", "zh", "y")])
 
     local_sums = group_sums(group_ids[0], rewards[0], groups)
     stats = sent_to_all(local_sums, REP).sum(axis=0)
-    parts = rest_blocks(pos, master, stats)
     stats = sent_to_all(stats, SHARD)
-    parts = [parts[0]] + [shifted(parts[d], "zh", d) for d in range(1, 4)]
 
     hidden_b = swapped(hidden)
     cotangent_b = swapped(cotangent)
@@ -378,13 +408,18 @@
     )
     tok_b = swapped(tok)
 
-    sent = partial_product(
-        pos, stats, tok.T, tok_b.T, cotangent, cotangent_b, hidden, hidden_b, parts[0], n_x, n_y
-    )
-    sent = sent.reshape(n_x * n_y, *sent.shape[2:])
-    part = sum_turn(exchanged(sent, ("x", "y")))
-    same, cross = regroup(pos, parts, part)
-    rest = [same] + [shifted(same if d % 2 == 0 else cross, "x", d) for d in range(1, 4)]
+    partial = partial_product(pos, stats, tok.T, tok_b.T, cotangent, cotangent_b, hidden, hidden_b)
+    to_x = spread_out(partial[:4], "x")
+    to_y = spread_out(partial[4:], "y")
+    to_y, to_x = sum_mid(pos, to_x, to_y)
+    to_y = spread_out(to_y, "y")
+    to_x = spread_out(to_x, "x")
+    part = sum_turn(to_y, to_x)
+
+    parts = rest_blocks(pos, master)
+    parts = spread_out(parts, "zh")
+    same, cross = regroup(pos, parts)
+    rest = spread_out([same, cross, same, cross], "x")
     part = part.reshape(n_z, part.shape[0] // n_z, part.shape[1])
     zl = lax.axis_size("zl")
     part = exchanged(part, ("zh", "zl"))

time: 226 us -> 224 us (level)
  blocking collectives: 89.8 us -> 48.7 us
  waiting for transfers between devices: 46.7 us -> 77 us
  starting transfers between devices: 49 us -> 59.4 us
  local copies, waits for them, and re-layouts: 8.1 us -> 5.43 us
    all_to_all x4 -> x3, blocking collectives: 89.8 us -> 48.7 us  [exchanged(): return lax.all_to_all(blocks, axis, split_axis=0, concat_axis=0, tiled=True)]
    ppermute x6 -> x18, waiting for transfers between devices: 42 us -> 66.1 us  [shifted(): return lax.ppermute(value, axis, [(i, (i + by) % n) for i in range(n)])]
    ppermute x6 -> x18, starting transfers between devices: 13.2 us -> 33.8 us  [shifted(): return lax.ppermute(value, axis, [(i, (i + by) % n) for i in range(n)])]
    ppermute x8, starting transfers between devices: 16.6 us -> 5.79 us  [swapped(): return lax.ppermute(value, 'c', [(0, 1), (1, 0)])]
    all_to_all x3, waiting for transfers between devices: 2.63 us -> 8.77 us  [exchanged(): return lax.all_to_all(blocks, axis, split_axis=0, concat_axis=0, tiled=True)]
    unnamed x26 -> x8, local copies, waits for them, and re-layouts: 6.68 us -> 4.01 us
    pallas_call x2 -> x3, Pallas kernels: 9.57 us -> 10 us  [the longest x1 8.84 us: partial_product(): pl.pallas_call(partial_kernel, out_shape=[jax.ShapeDtypeStruct(shape, bf1...]
  transfers between devices with their start and end apart: 17 -> 29, of which waited for: 5 -> 12; matrix products, arithmetic and copies ran while one was open for 4% -> 4% of each run, Pallas kernels for 4% -> 4%
where the time goes in v3:
time: 224 us
  waiting for transfers between devices  77 us (34%)
  starting transfers between devices  59.4 us (27%)
  blocking collectives  48.7 us (22%)
  Pallas kernels  25.1 us (11%)
  local copies, waits for them, and re-layouts  5.43 us (2%)
  matrix products  4.75 us (2%)
  other arithmetic  2.36 us (1%)
    ppermute x18, waiting for transfers between devices, shifted(): return lax.ppermute(value, axis, [(i, (i + by) % n) for i in range(n)])  66.1 us
    all_to_all x3, blocking collectives, exchanged(): return lax.all_to_all(blocks, axis, split_axis=0, concat_axis=0, tiled=True)  48.7 us
    ppermute x18, starting transfers between devices, shifted(): return lax.ppermute(value, axis, [(i, (i + by) % n) for i in range(n)])  33.8 us
    all_to_all x3, starting transfers between devices, exchanged(): return lax.all_to_all(blocks, axis, split_axis=0, concat_axis=0, tiled=True)  19.8 us
    pallas_call x1, Pallas kernels, partial_product(): pl.pallas_call(partial_kernel, out_shape=[jax.ShapeDtypeStruct(shape, bf1...  8.84 us
    all_to_all x3, waiting for transfers between devices, exchanged(): return lax.all_to_all(blocks, axis, split_axis=0, concat_axis=0, tiled=True)  8.77 us
    pallas_call x1, Pallas kernels, place_rest(): pl.pallas_call(place_rest_kernel, out_shape=jax.ShapeDtypeStruct((layers,...  7.12 us
    ppermute x8, starting transfers between devices, swapped(): return lax.ppermute(value, 'c', [(0, 1), (1, 0)])  5.79 us
  transfers between devices with their start and end apart: 29, of which 12 were waited for; matrix products, arithmetic and copies ran while one was open for 4% of the time, Pallas kernels for 4%

profile of v3, /device:TPU:33, one launch (start us, length us, event | category | flops | bytes accessed | tf_op | source)
XLA Modules:
  0.0 223.6 jit_solution(11753296093056182781)
XLA Ops:
  3.6 5.7 %all-to-all-start = ((f32[16,3,128]{2,1,0:T(4,128)}), f32[16,3,128]{2,1,0:T(4,128)S(1)}, u32[]{:S(2)}, u32[]{:S(2)}) async-start(f32[16,3,128]{2,1,0:T(4,128)} %broadcast_in_dim.8), calls=%async_computation | async-start | bytes 65536 | tf_op jit(solution)/shard_map/all_to_all | solution.py:34
  16.1 9.9 %all-to-all-start.1 = ((f32[16,3,128]{2,1,0:T(4,128)}), f32[16,3,128]{2,1,0:T(4,128)S(1)}, u32[]{:S(2)}, u32[]{:S(2)}) async-start(f32[16,3,128]{2,1,0:T(4,128)} %broadcast_in_dim.9), calls=%async_computation.1 | async-start | bytes 65536 | tf_op jit(solution)/shard_map/all_to_all | solution.py:34
  26.1 8.8 %all-to-all-done.1.stats = f32[16,3,128]{2,1,0:T(4,128)S(1)} async-done(((f32[16,3,128]{2,1,0:T(4,128)}), f32[16,3,128]{2,1,0:T(4,128)S(1)}, u32[]{:S(2)}, u32[]{:S(2)}) %all-to-all-start.1) | async-done | bytes 24608 | tf_op jit(solution)/shard_map/all_to_all | solution.py:34
  34.9 1.9 copy-done.2
  37.9 8.8 %partial_product.1 = (bf16[4,64,896]{2,1,0:T(8,128)(2,1)S(1)}, bf16[4,64,896]{2,1,0:T(8,128)(2,1)S(1)}, bf16[4,64,896]{2,1,0:T(8,128)(2,1)S(1)}, bf16[4,64,896]{...) custom-call(s32[4]{0:T(128)S(1)} %pad_add_fusion.pos.refs_0_, ...), custom_call_target="tpu_custom_call" | custom-call | flops 3288334336 | bytes 10092544 | tf_op jit(solution)/shard_map/partial_product/pallas_call | solution.py:116
  47.2 1.8 collective-permute-start.4
  51.0 2.4 %collective-permute-start.7 = (bf16[4,64,896]{2,1,0:T(8,128)(2,1)S(1)}, bf16[4,64,896]{2,1,0:T(8,128)(2,1)S(1)}, u32[]{:S(2)}, u32[]{:S(2)}) collective-permute-start(bf16[4,64,896]{2,1,0:T(8,128)(2,1)S(1)} %get-tuple-element.32), channel_id=1, source_target_pairs={{0,64},{32,96},{64,0},{96,32},{1,65},{33,97},{65,1},{97,33},{2,66}... | collective-permute-start | bytes 1376264 | tf_op jit(solution)/shard_map/ppermute | solution.py:26
  53.4 5.5 %collective-permute-done.3.refs_1_ = bf16[4,64,896]{2,1,0:T(8,128)(2,1)S(1)} collective-permute-done((bf16[4,64,896]{2,1,0:T(8,128)(2,1)S(1)}, bf16[4,64,896]{2,1,0:T(8,128)(2,1)S(1)}, u32[]{:S(2)}, u32[]{:S(2)}) %collective-permute-start.3) | collective-permute-done | bytes 458784 | tf_op jit(solution)/shard_map/ppermute | solution.py:26
  58.9 2.5 %collective-permute-start.8 = (bf16[4,64,896]{2,1,0:T(8,128)(2,1)S(1)}, bf16[4,64,896]{2,1,0:T(8,128)(2,1)S(1)}, u32[]{:S(2)}, u32[]{:S(2)}) collective-permute-start(bf16[4,64,896]{2,1,0:T(8,128)(2,1)S(1)} %get-tuple-element.33), channel_id=1, source_target_pairs={{0,96},{32,0},{64,32},{96,64},{1,97},{33,1},{65,33},{97,65},{2,98}... | collective-permute-start | bytes 1376264 | tf_op jit(solution)/shard_map/ppermute | solution.py:26
  61.4 6.2 %collective-permute-done.4.refs_2_ = bf16[4,64,896]{2,1,0:T(8,128)(2,1)S(1)} collective-permute-done((bf16[4,64,896]{2,1,0:T(8,128)(2,1)S(1)}, bf16[4,64,896]{2,1,0:T(8,128)(2,1)S(1)}, u32[]{:S(2)}, u32[]{:S(2)}) %collective-permute-start.4) | collective-permute-done | bytes 458784 | tf_op jit(solution)/shard_map/ppermute | solution.py:26
  67.6 2.3 %collective-permute-done.5.refs_3_ = bf16[4,64,896]{2,1,0:T(8,128)(2,1)S(1)} collective-permute-done((bf16[4,64,896]{2,1,0:T(8,128)(2,1)S(1)}, bf16[4,64,896]{2,1,0:T(8,128)(2,1)S(1)}, u32[]{:S(2)}, u32[]{:S(2)}) %collective-permute-start.5) | collective-permute-done | bytes 458784 | tf_op jit(solution)/shard_map/ppermute | solution.py:26
  72.3 2.3 %collective-permute-start.10 = (bf16[64,896]{1,0:T(8,128)(2,1)S(1)}, bf16[64,896]{1,0:T(8,128)(2,1)S(1)}, u32[]{:S(2)}, u32[]{:S(2)}) collective-permute-start(bf16[64,896]{1,0:T(8,128)(2,1)S(1)} %get-tuple-element.36), channel_id=1, source_target_pairs={{0,64},{32,96},{64,0},{96,32},{1,65},{33,97},{65,1},{97,33},{2,66}... | collective-permute-start | bytes 344072 | tf_op jit(solution)/shard_map/ppermute | solution.py:26
  75.8 2.8 %collective-permute-start.12 = (bf16[64,896]{1,0:T(8,128)(2,1)S(1)}, bf16[64,896]{1,0:T(8,128)(2,1)S(1)}, u32[]{:S(2)}, u32[]{:S(2)}) collective-permute-start(bf16[64,896]{1,0:T(8,128)(2,1)S(1)} %get-tuple-element.39), channel_id=1, source_target_pairs={{0,4},{4,8},{8,12},{12,0},{1,5},{5,9},{9,13},{13,1},{2,6},{6,10},{... | collective-permute-start | bytes 344072 | tf_op jit(solution)/shard_map/ppermute | solution.py:26
  78.6 2.4 %collective-permute-start.13 = (bf16[64,896]{1,0:T(8,128)(2,1)S(1)}, bf16[64,896]{1,0:T(8,128)(2,1)S(1)}, u32[]{:S(2)}, u32[]{:S(2)}) collective-permute-start(bf16[64,896]{1,0:T(8,128)(2,1)S(1)} %get-tuple-element.40), channel_id=1, source_target_pairs={{0,8},{4,12},{8,0},{12,4},{1,9},{5,13},{9,1},{13,5},{2,10},{6,14},... | collective-permute-start | bytes 344072 | tf_op jit(solution)/shard_map/ppermute | solution.py:26
  81.0 2.1 collective-permute-start.14
  85.0 10.2 %all_to_all.30.src = bf16[8,112,128]{2,1,0:T(8,128)(2,1)S(1)} all-to-all(bf16[8,112,128]{2,1,0:T(8,128)(2,1)S(1)} %bitcast.44), channel_id=1, replica_groups=mesh['zl'=2,'y'=4,'c'=2,'x'=4,'zh'=4] {'zh','zl'}, dimensions={0} | all-to-all | bytes 458752 | tf_op jit(solution)/shard_map/all_to_all | solution.py:34
  95.3 26.1 %all_to_all.31.grad = bf16[16,112,128]{2,1,0:T(8,128)(2,1)S(1)} all-to-all(bf16[16,112,128]{2,1,0:T(8,128)(2,1)S(1)} %sum_spread.1), channel_id=1, replica_groups=mesh['zl'=2,'y'=4,'c'=2,'x'=4,'zh'=4] {'zl','y','c'}, dimensions={0} | all-to-all | bytes 917504 | tf_op jit(solution)/shard_map/all_to_all | solution.py:34
  121.6 12.3 %all_to_all.32.refs_1_ = f32[16,1,128]{2,1,0:T(1,128)S(1)} all-to-all(f32[16,1,128]{2,1,0:T(1,128)S(1)} %squares_of.1), channel_id=1, replica_groups=mesh['zl'=2,'y'=4,'c'=2,'x'=4,'zh'=4] {'x','zh'}, dimensions={0} | all-to-all | bytes 16384 | tf_op jit(solution)/shard_map/all_to_all | solution.py:34
  133.9 1.7 update.1
  136.5 4.3 %all-to-all-start.5 = ((bf16[16,112,256]{2,1,0:T(8,128)(2,1)}), bf16[16,112,256]{2,1,0:T(8,128)(2,1)}, u32[]{:S(2)}, u32[]{:S(2)}) async-start(bf16[16,112,256]{2,1,0:T(8,128)(2,1)} %bitcast.43), calls=%async_computation.5 | async-start | bytes 1835008 | tf_op jit(solution)/shard_map/all_to_all | solution.py:34
  140.9 1.6 rest_blocks.1
  142.5 2.2 collective-permute-start.16
  144.6 3.3 %collective-permute-start.17 = (bf16[2,2,112,256]{3,2,1,0:T(8,128)(2,1)S(1)}, bf16[2,2,112,256]{3,2,1,0:T(8,128)(2,1)S(1)}, u32[]{:S(2)}, u32[]{:S(2)}) collective-permute-start(bf16[2,2,112,256]{3,2,1,0:T(8,128)(2,1)S(1)} %get-tuple-element.46), channel_id=1, source_target_pairs={{0,2},{1,3},{2,0},{3,1},{4,6},{5,7},{6,4},{7,5},{8,10},{9,11},{10,... | collective-permute-start | bytes 688136 | tf_op jit(solution)/shard_map/ppermute | solution.py:26
  147.9 3.3 %collective-permute-start.18 = (bf16[2,2,112,256]{3,2,1,0:T(8,128)(2,1)S(1)}, bf16[2,2,112,256]{3,2,1,0:T(8,128)(2,1)S(1)}, u32[]{:S(2)}, u32[]{:S(2)}) collective-permute-start(bf16[2,2,112,256]{3,2,1,0:T(8,128)(2,1)S(1)} %get-tuple-element.47), channel_id=1, source_target_pairs={{0,3},{1,0},{2,1},{3,2},{4,7},{5,4},{6,5},{7,6},{8,11},{9,8},{10,9... | collective-permute-start | bytes 688136 | tf_op jit(solution)/shard_map/ppermute | solution.py:26
  151.2 33.3 %collective-permute-done.16.refs_1_ = bf16[2,2,112,256]{3,2,1,0:T(8,128)(2,1)S(1)} collective-permute-done((bf16[2,2,112,256]{3,2,1,0:T(8,128)(2,1)S(1)}, bf16[2,2,112,256]{3,2,1,0:T(8,128)(2,1)S(1)}, u32[]{:S(2)}, u32[]{:S(2)}) %collective-permute-start.16) | collective-permute-done | bytes 229408 | tf_op jit(solution)/shard_map/ppermute | solution.py:26
  185.1 1.5 collective-permute-start.19
  186.6 2.4 %collective-permute-start.20 = (bf16[4,2,112,256]{3,2,1,0:T(8,128)(2,1)S(1)}, bf16[4,2,112,256]{3,2,1,0:T(8,128)(2,1)S(1)}, u32[]{:S(2)}, u32[]{:S(2)}) collective-permute-start(bf16[4,2,112,256]{3,2,1,0:T(8,128)(2,1)S(1)} %get-tuple-element.48.refs_0_), channel_id=1, source_target_pairs={{0,8},{4,12},{8,0},{12,4},{1,9},{5,13},{9,1},{13,5},{2,10},{6,14},... | collective-permute-start | bytes 1376264 | tf_op jit(solution)/shard_map/ppermute | solution.py:26
  191.7 6.2 %collective-permute-done.19.refs_1_ = bf16[4,2,112,256]{3,2,1,0:T(8,128)(2,1)S(1)} collective-permute-done((bf16[4,2,112,256]{3,2,1,0:T(8,128)(2,1)S(1)}, bf16[4,2,112,256]{3,2,1,0:T(8,128)(2,1)S(1)}, u32[]{:S(2)}, u32[]{:S(2)}) %collective-permute-start.19) | collective-permute-done | bytes 458784 | tf_op jit(solution)/shard_map/ppermute | solution.py:26
  197.9 1.5 collective-permute-start.23
  199.4 9.5 %collective-permute-done.20.refs_2_ = bf16[4,2,112,256]{3,2,1,0:T(8,128)(2,1)S(1)} collective-permute-done((bf16[4,2,112,256]{3,2,1,0:T(8,128)(2,1)S(1)}, bf16[4,2,112,256]{3,2,1,0:T(8,128)(2,1)S(1)}, u32[]{:S(2)}, u32[]{:S(2)}) %collective-permute-start.20) | collective-permute-done | bytes 458784 | tf_op jit(solution)/shard_map/ppermute | solution.py:26
  212.5 7.1 %place_rest.1 = bf16[3,4,4,2,112,256]{5,4,3,2,1,0:T(8,128)(2,1)} custom-call(s32[4]{0:T(128)S(1)} %pad_add_fusion.pos.refs_0_, bf16[4,2,112,256]{3,2,1,0:T(8,128)(2,1)S(1)} %get-tuple-element.48.refs_0_, bf16[4,2,112,256]{3,2,1,0:T(8,128)(2,1)S(1)} %collective-permute-done.19.refs_1_, bf16[4,2,112,256]{3,2,1,0:T(8,128)(2,1)S(1)} %collective-permute-done.20.refs_2_, ...), custom_call_target="tpu_custom_call" | custom-call | flops 229376 | bytes 7340032 | tf_op jit(solution)/shard_map/place_rest/pallas_call | solution.py:334
  219.6 3.9 %place_first.1 = bf16[3,16,2,112,256]{4,3,2,1,0:T(8,128)(2,1)} custom-call(s32[4]{0:T(128)S(1)} %pad_add_fusion.pos.refs_0_, bf16[16,112,256]{2,1,0:T(8,128)(2,1)} %all-to-all-done.5.own, bf16[16,112,256]{2,1,0:T(8,128)(2,1)S(1)} %collective-permute-done.15.other, bf16[3,16,2,112,256]{4,3,2,1,0:T(8,128)(2,1)} %bitcast.47), custom_call_target="tpu_custom_call", output_to_operand_aliasing={{}: (3, {})} | custom-call | flops 458752 | bytes 3670016 | tf_op jit(solution)/shard_map/place_first/pallas_call | solution.py:366
  (65 shorter events, 27.0 us)
Async XLA Ops:
  0.6 34.2 %collective-permute-start.2 = (bf16[448,3584]{1,0:T(8,128)(2,1)}, bf16[448,3584]{1,0:T(8,128)(2,1)}, u32[]{:S(2)}, u32[]{:S(2)}) collective-permute-start(bf16[448,3584]{1,0:T(8,128)(2,1)} %hid_a.1), channel_id=1, source_target_pairs={{0,16},{16,0},{1,17},{17,1},{2,18},{18,2},{3,19},{19,3},{4,20},{20... | collective-permute-start | bytes 9633800 | tf_op jit(solution)/shard_map/ppermute | solution.py:21
  3.6 11.9 %all-to-all-start = ((f32[16,3,128]{2,1,0:T(4,128)}), f32[16,3,128]{2,1,0:T(4,128)S(1)}, u32[]{:S(2)}, u32[]{:S(2)}) async-start(f32[16,3,128]{2,1,0:T(4,128)} %broadcast_in_dim.8), calls=%async_computation | async-start | bytes 65536 | tf_op jit(solution)/shard_map/all_to_all | solution.py:34
  9.3 25.6 %collective-permute-start.1 = (bf16[448,1024]{1,0:T(8,128)(2,1)}, bf16[448,1024]{1,0:T(8,128)(2,1)S(1)}, u32[]{:S(2)}, u32[]{:S(2)}) collective-permute-start(bf16[448,1024]{1,0:T(8,128)(2,1)} %cot_a.1), channel_id=1, source_target_pairs={{0,16},{16,0},{1,17},{17,1},{2,18},{18,2},{3,19},{19,3},{4,20},{20... | collective-permute-start | bytes 2752520 | tf_op jit(solution)/shard_map/ppermute | solution.py:21
  15.3 10.8 %collective-permute-start = (f32[8,448]{0,1:T(8,128)S(1)}, f32[8,448]{0,1:T(8,128)S(1)}, u32[]{:S(2)}, u32[]{:S(2)}) collective-permute-start(f32[8,448]{0,1:T(8,128)S(1)} %copy.29), channel_id=1, source_target_pairs={{0,16},{16,0},{1,17},{17,1},{2,18},{18,2},{3,19},{19,3},{4,20},{20... | collective-permute-start | bytes 43016 | tf_op jit(solution)/shard_map/ppermute | solution.py:21
  16.1 18.7 %all-to-all-start.1 = ((f32[16,3,128]{2,1,0:T(4,128)}), f32[16,3,128]{2,1,0:T(4,128)S(1)}, u32[]{:S(2)}, u32[]{:S(2)}) async-start(f32[16,3,128]{2,1,0:T(4,128)} %broadcast_in_dim.9), calls=%async_computation.1 | async-start | bytes 65536 | tf_op jit(solution)/shard_map/all_to_all | solution.py:34
  34.9 1.9 copy-start.2
  36.8 1.2 copy-start.3
  46.8 12.1 %collective-permute-start.3 = (bf16[4,64,896]{2,1,0:T(8,128)(2,1)S(1)}, bf16[4,64,896]{2,1,0:T(8,128)(2,1)S(1)}, u32[]{:S(2)}, u32[]{:S(2)}) collective-permute-start(bf16[4,64,896]{2,1,0:T(8,128)(2,1)S(1)} %get-tuple-element.27), channel_id=1, source_target_pairs={{0,4},{4,8},{8,12},{12,0},{1,5},{5,9},{9,13},{13,1},{2,6},{6,10},{... | collective-permute-start | bytes 1376264 | tf_op jit(solution)/shard_map/ppermute | solution.py:26
  47.2 20.5 %collective-permute-start.4 = (bf16[4,64,896]{2,1,0:T(8,128)(2,1)S(1)}, bf16[4,64,896]{2,1,0:T(8,128)(2,1)S(1)}, u32[]{:S(2)}, u32[]{:S(2)}) collective-permute-start(bf16[4,64,896]{2,1,0:T(8,128)(2,1)S(1)} %get-tuple-element.28), channel_id=1, source_target_pairs={{0,8},{4,12},{8,0},{12,4},{1,9},{5,13},{9,1},{13,5},{2,10},{6,14},... | collective-permute-start | bytes 1376264 | tf_op jit(solution)/shard_map/ppermute | solution.py:26
  48.9 21.0 %collective-permute-start.5 = (bf16[4,64,896]{2,1,0:T(8,128)(2,1)S(1)}, bf16[4,64,896]{2,1,0:T(8,128)(2,1)S(1)}, u32[]{:S(2)}, u32[]{:S(2)}) collective-permute-start(bf16[4,64,896]{2,1,0:T(8,128)(2,1)S(1)} %get-tuple-element.29), channel_id=1, source_target_pairs={{0,12},{4,0},{8,4},{12,8},{1,13},{5,1},{9,5},{13,9},{2,14},{6,2},{... | collective-permute-start | bytes 1376264 | tf_op jit(solution)/shard_map/ppermute | solution.py:26
  49.9 20.1 %collective-permute-start.6 = (bf16[4,64,896]{2,1,0:T(8,128)(2,1)S(1)}, bf16[4,64,896]{2,1,0:T(8,128)(2,1)S(1)}, u32[]{:S(2)}, u32[]{:S(2)}) collective-permute-start(bf16[4,64,896]{2,1,0:T(8,128)(2,1)S(1)} %get-tuple-element.31), channel_id=1, source_target_pairs={{0,32},{32,64},{64,96},{96,0},{1,33},{33,65},{65,97},{97,1},{2,34}... | collective-permute-start | bytes 1376264 | tf_op jit(solution)/shard_map/ppermute | solution.py:26
  51.0 20.2 %collective-permute-start.7 = (bf16[4,64,896]{2,1,0:T(8,128)(2,1)S(1)}, bf16[4,64,896]{2,1,0:T(8,128)(2,1)S(1)}, u32[]{:S(2)}, u32[]{:S(2)}) collective-permute-start(bf16[4,64,896]{2,1,0:T(8,128)(2,1)S(1)} %get-tuple-element.32), channel_id=1, source_target_pairs={{0,64},{32,96},{64,0},{96,32},{1,65},{33,97},{65,1},{97,33},{2,66}... | collective-permute-start | bytes 1376264 | tf_op jit(solution)/shard_map/ppermute | solution.py:26
  58.9 12.3 %collective-permute-start.8 = (bf16[4,64,896]{2,1,0:T(8,128)(2,1)S(1)}, bf16[4,64,896]{2,1,0:T(8,128)(2,1)S(1)}, u32[]{:S(2)}, u32[]{:S(2)}) collective-permute-start(bf16[4,64,896]{2,1,0:T(8,128)(2,1)S(1)} %get-tuple-element.33), channel_id=1, source_target_pairs={{0,96},{32,0},{64,32},{96,64},{1,97},{33,1},{65,33},{97,65},{2,98}... | collective-permute-start | bytes 1376264 | tf_op jit(solution)/shard_map/ppermute | solution.py:26
  71.2 62.7 %copy-start = (f32[3,224,1024]{2,1,0:T(8,128)S(1)}, f32[3,224,1024]{2,1,0:T(8,128)}, u32[]{:S(2)}) copy-start(f32[3,224,1024]{2,1,0:T(8,128)} %refs_7_.1) | copy-start | bytes 8257540
  72.2 8.8 %collective-permute-start.9 = (bf16[64,896]{1,0:T(8,128)(2,1)S(1)}, bf16[64,896]{1,0:T(8,128)(2,1)S(1)}, u32[]{:S(2)}, u32[]{:S(2)}) collective-permute-start(bf16[64,896]{1,0:T(8,128)(2,1)S(1)} %get-tuple-element.35), channel_id=1, source_target_pairs={{0,32},{32,64},{64,96},{96,0},{1,33},{33,65},{65,97},{97,1},{2,34}... | collective-permute-start | bytes 344072 | tf_op jit(solution)/shard_map/ppermute | solution.py:26
  72.3 10.8 %collective-permute-start.10 = (bf16[64,896]{1,0:T(8,128)(2,1)S(1)}, bf16[64,896]{1,0:T(8,128)(2,1)S(1)}, u32[]{:S(2)}, u32[]{:S(2)}) collective-permute-start(bf16[64,896]{1,0:T(8,128)(2,1)S(1)} %get-tuple-element.36), channel_id=1, source_target_pairs={{0,64},{32,96},{64,0},{96,32},{1,65},{33,97},{65,1},{97,33},{2,66}... | collective-permute-start | bytes 344072 | tf_op jit(solution)/shard_map/ppermute | solution.py:26
  74.6 8.5 %collective-permute-start.11 = (bf16[64,896]{1,0:T(8,128)(2,1)S(1)}, bf16[64,896]{1,0:T(8,128)(2,1)S(1)}, u32[]{:S(2)}, u32[]{:S(2)}) collective-permute-start(bf16[64,896]{1,0:T(8,128)(2,1)S(1)} %get-tuple-element.37), channel_id=1, source_target_pairs={{0,96},{32,0},{64,32},{96,64},{1,97},{33,1},{65,33},{97,65},{2,98}... | collective-permute-start | bytes 344072 | tf_op jit(solution)/shard_map/ppermute | solution.py:26
  75.8 7.3 %collective-permute-start.12 = (bf16[64,896]{1,0:T(8,128)(2,1)S(1)}, bf16[64,896]{1,0:T(8,128)(2,1)S(1)}, u32[]{:S(2)}, u32[]{:S(2)}) collective-permute-start(bf16[64,896]{1,0:T(8,128)(2,1)S(1)} %get-tuple-element.39), channel_id=1, source_target_pairs={{0,4},{4,8},{8,12},{12,0},{1,5},{5,9},{9,13},{13,1},{2,6},{6,10},{... | collective-permute-start | bytes 344072 | tf_op jit(solution)/shard_map/ppermute | solution.py:26
  78.6 5.8 %collective-permute-start.13 = (bf16[64,896]{1,0:T(8,128)(2,1)S(1)}, bf16[64,896]{1,0:T(8,128)(2,1)S(1)}, u32[]{:S(2)}, u32[]{:S(2)}) collective-permute-start(bf16[64,896]{1,0:T(8,128)(2,1)S(1)} %get-tuple-element.40), channel_id=1, source_target_pairs={{0,8},{4,12},{8,0},{12,4},{1,9},{5,13},{9,1},{13,5},{2,10},{6,14},... | collective-permute-start | bytes 344072 | tf_op jit(solution)/shard_map/ppermute | solution.py:26
  81.0 3.9 %collective-permute-start.14 = (bf16[64,896]{1,0:T(8,128)(2,1)S(1)}, bf16[64,896]{1,0:T(8,128)(2,1)S(1)}, u32[]{:S(2)}, u32[]{:S(2)}) collective-permute-start(bf16[64,896]{1,0:T(8,128)(2,1)S(1)} %get-tuple-element.41), channel_id=1, source_target_pairs={{0,12},{4,0},{8,4},{12,8},{1,13},{5,1},{9,5},{13,9},{2,14},{6,2},{... | collective-permute-start | bytes 344072 | tf_op jit(solution)/shard_map/ppermute | solution.py:26
  136.5 53.7 %all-to-all-start.5 = ((bf16[16,112,256]{2,1,0:T(8,128)(2,1)}), bf16[16,112,256]{2,1,0:T(8,128)(2,1)}, u32[]{:S(2)}, u32[]{:S(2)}) async-start(bf16[16,112,256]{2,1,0:T(8,128)(2,1)} %bitcast.43), calls=%async_computation.5 | async-start | bytes 1835008 | tf_op jit(solution)/shard_map/all_to_all | solution.py:34
  142.5 42.0 %collective-permute-start.16 = (bf16[2,2,112,256]{3,2,1,0:T(8,128)(2,1)S(1)}, bf16[2,2,112,256]{3,2,1,0:T(8,128)(2,1)S(1)}, u32[]{:S(2)}, u32[]{:S(2)}) collective-permute-start(bf16[2,2,112,256]{3,2,1,0:T(8,128)(2,1)S(1)} %get-tuple-element.45), channel_id=1, source_target_pairs={{0,1},{1,2},{2,3},{3,0},{4,5},{5,6},{6,7},{7,4},{8,9},{9,10},{10,1... | collective-permute-start | bytes 688136 | tf_op jit(solution)/shard_map/ppermute | solution.py:26
  144.6 39.9 %collective-permute-start.17 = (bf16[2,2,112,256]{3,2,1,0:T(8,128)(2,1)S(1)}, bf16[2,2,112,256]{3,2,1,0:T(8,128)(2,1)S(1)}, u32[]{:S(2)}, u32[]{:S(2)}) collective-permute-start(bf16[2,2,112,256]{3,2,1,0:T(8,128)(2,1)S(1)} %get-tuple-element.46), channel_id=1, source_target_pairs={{0,2},{1,3},{2,0},{3,1},{4,6},{5,7},{6,4},{7,5},{8,10},{9,11},{10,... | collective-permute-start | bytes 688136 | tf_op jit(solution)/shard_map/ppermute | solution.py:26
  147.9 36.6 %collective-permute-start.18 = (bf16[2,2,112,256]{3,2,1,0:T(8,128)(2,1)S(1)}, bf16[2,2,112,256]{3,2,1,0:T(8,128)(2,1)S(1)}, u32[]{:S(2)}, u32[]{:S(2)}) collective-permute-start(bf16[2,2,112,256]{3,2,1,0:T(8,128)(2,1)S(1)} %get-tuple-element.47), channel_id=1, source_target_pairs={{0,3},{1,0},{2,1},{3,2},{4,7},{5,4},{6,5},{7,6},{8,11},{9,8},{10,9... | collective-permute-start | bytes 688136 | tf_op jit(solution)/shard_map/ppermute | solution.py:26
  185.1 12.8 %collective-permute-start.19 = (bf16[4,2,112,256]{3,2,1,0:T(8,128)(2,1)S(1)}, bf16[4,2,112,256]{3,2,1,0:T(8,128)(2,1)S(1)}, u32[]{:S(2)}, u32[]{:S(2)}) collective-permute-start(bf16[4,2,112,256]{3,2,1,0:T(8,128)(2,1)S(1)} %get-tuple-element.49), channel_id=1, source_target_pairs={{0,4},{4,8},{8,12},{12,0},{1,5},{5,9},{9,13},{13,1},{2,6},{6,10},{... | collective-permute-start | bytes 1376264 | tf_op jit(solution)/shard_map/ppermute | solution.py:26
  186.6 22.3 %collective-permute-start.20 = (bf16[4,2,112,256]{3,2,1,0:T(8,128)(2,1)S(1)}, bf16[4,2,112,256]{3,2,1,0:T(8,128)(2,1)S(1)}, u32[]{:S(2)}, u32[]{:S(2)}) collective-permute-start(bf16[4,2,112,256]{3,2,1,0:T(8,128)(2,1)S(1)} %get-tuple-element.48.refs_0_), channel_id=1, source_target_pairs={{0,8},{4,12},{8,0},{12,4},{1,9},{5,13},{9,1},{13,5},{2,10},{6,14},... | collective-permute-start | bytes 1376264 | tf_op jit(solution)/shard_map/ppermute | solution.py:26
  189.1 21.3 %collective-permute-start.21 = (bf16[4,2,112,256]{3,2,1,0:T(8,128)(2,1)S(1)}, bf16[4,2,112,256]{3,2,1,0:T(8,128)(2,1)S(1)}, u32[]{:S(2)}, u32[]{:S(2)}) collective-permute-start(bf16[4,2,112,256]{3,2,1,0:T(8,128)(2,1)S(1)} %get-tuple-element.49), channel_id=1, source_target_pairs={{0,12},{4,0},{8,4},{12,8},{1,13},{5,1},{9,5},{13,9},{2,14},{6,2},{... | collective-permute-start | bytes 1376264 | tf_op jit(solution)/shard_map/ppermute | solution.py:26
  190.2 29.4 %collective-permute-start.15 = (bf16[16,112,256]{2,1,0:T(8,128)(2,1)}, bf16[16,112,256]{2,1,0:T(8,128)(2,1)S(1)}, u32[]{:S(2)}, u32[]{:S(2)}) collective-permute-start(bf16[16,112,256]{2,1,0:T(8,128)(2,1)} %all-to-all-done.5.own), channel_id=1, source_target_pairs={{0,16},{16,0},{1,17},{17,1},{2,18},{18,2},{3,19},{19,3},{4,20},{20... | collective-permute-start | bytes 2752520 | tf_op jit(solution)/shard_map/ppermute | solution.py:21
  191.7 18.7 %collective-permute-start.22 = (bf16[4,2,112,256]{3,2,1,0:T(8,128)(2,1)S(1)}, bf16[4,2,112,256]{3,2,1,0:T(8,128)(2,1)S(1)}, u32[]{:S(2)}, u32[]{:S(2)}) collective-permute-start(bf16[4,2,112,256]{3,2,1,0:T(8,128)(2,1)S(1)} %get-tuple-element.48.refs_0_), channel_id=1, source_target_pairs={{0,16},{16,0},{1,17},{17,1},{2,18},{18,2},{3,19},{19,3},{4,20},{20... | collective-permute-start | bytes 1376264 | tf_op jit(solution)/shard_map/ppermute | solution.py:21
  197.9 12.5 %collective-permute-start.23 = (bf16[4,2,112,256]{3,2,1,0:T(8,128)(2,1)S(1)}, bf16[4,2,112,256]{3,2,1,0:T(8,128)(2,1)S(1)}, u32[]{:S(2)}, u32[]{:S(2)}) collective-permute-start(bf16[4,2,112,256]{3,2,1,0:T(8,128)(2,1)S(1)} %collective-permute-done.19.refs_1_), channel_id=1, source_target_pairs={{0,16},{16,0},{1,17},{17,1},{2,18},{18,2},{3,19},{19,3},{4,20},{20... | collective-permute-start | bytes 1376264 | tf_op jit(solution)/shard_map/ppermute | solution.py:21
  208.9 2.9 %collective-permute-start.24 = (bf16[4,2,112,256]{3,2,1,0:T(8,128)(2,1)S(1)}, bf16[4,2,112,256]{3,2,1,0:T(8,128)(2,1)S(1)}, u32[]{:S(2)}, u32[]{:S(2)}) collective-permute-start(bf16[4,2,112,256]{3,2,1,0:T(8,128)(2,1)S(1)} %collective-permute-done.20.refs_2_), channel_id=1, source_target_pairs={{0,16},{16,0},{1,17},{17,1},{2,18},{18,2},{3,19},{19,3},{4,20},{20... | collective-permute-start | bytes 1376264 | tf_op jit(solution)/shard_map/ppermute | solution.py:21
  210.4 2.1 collective-permute-start.25
  (1 other events, 0.9 us)

commit v4 on v3

--- a/solution.py
+++ b/solution.py
@@ -192,76 +192,80 @@
     )(blocks)
 
 
-def squares_kernel(grad, out):
+def send_kernel(pos, grad, blocks):
     g = grad[...].astype(f32)
-    s = jnp.sum(jnp.sum(g * g, axis=0), axis=0, keepdims=True)
-    s = jnp.sum(s, axis=1, keepdims=True)
-    out[...] = jnp.broadcast_to(s.reshape(1, 1, 1), out.shape)
-
-
-def squares_of(grad, copies):
-    return pl.pallas_call(
-        squares_kernel,
-        out_shape=jax.ShapeDtypeStruct((copies, 1, LANES), f32),
-        compiler_params=params(),
-        cost_estimate=cost(2 * grad.size, 2 * grad.size),
-        name="squares_of",
-    )(grad)
-
-
-def update_kernel(entries, core, squares, grad, master, new, blocks):
+    s = jnp.sum(g * g, axis=(0, 1, 2))
+    s = jnp.sum(jnp.sum(s, axis=0, keepdims=True), axis=1, keepdims=True)
+    high = s.astype(bf16).astype(f32)
+    mid = (s - high).astype(bf16).astype(f32)
+    low = s - high - mid
+    rows = grad.shape[3]
+    row = lax.broadcasted_iota(jnp.int32, (8, 2 * HEAD), 0)
+    tail = jnp.where(row == 0, high, jnp.where(row == 1, mid, jnp.where(row == 2, low, 0.0))).astype(bf16)
+    for h in range(KV_HEADS):
+        for i in range(2):
+            for j in range(2):
+                for kv in range(2):
+                    blocks[i, h, j, :rows, kv * HEAD : (kv + 1) * HEAD] = grad[pos[0], h, kv]
+                blocks[i, h, j, rows:, :] = tail
+
+
+def send_blocks(pos, grad):
+    rows = grad.shape[3]
+    whole = lambda s: pl.BlockSpec(s, lambda i, p: (0,) * len(s))
+    shape = (2, KV_HEADS, 2, rows + 8, 2 * HEAD)
+    return pl.pallas_call(
+        send_kernel,
+        out_shape=jax.ShapeDtypeStruct(shape, bf16),
+        grid_spec=pltpu.PrefetchScalarGridSpec(
+            num_scalar_prefetch=1, grid=(1,), in_specs=[whole(grad.shape)], out_specs=whole(shape)
+        ),
+        compiler_params=params(),
+        cost_estimate=cost(4 * grad.size, 8 * grad.size),
+        name="send_blocks",
+    )(pos, grad)
+
+
+def step_size(squares, entries):
+    s = jnp.sum(squares[...].astype(f32), axis=0)[:, 0:1]
+    total = s[0:1] + s[1:2] + s[2:3]
+    return 0.5 / jnp.sqrt(total / entries + 1e-06)
+
+
+def update_kernel(entries, squares, grad, master, new):
     zl, ny, _, rows, width = grad.shape
-    total = jnp.sum(jnp.sum(squares[...], axis=0), axis=1, keepdims=True) / LANES
-    rms = jnp.sqrt(total / entries + 1e-06)
+    step = step_size(squares, entries)
     for kv in range(2):
         for y in range(ny):
             for z in range(zl):
                 r = slice(z * rows, (z + 1) * rows)
                 c = slice((kv * ny + y) * width, (kv * ny + y + 1) * width)
-                new[r, c] = master[0, r, c] - 0.5 * grad[z, y, kv].astype(f32) / rms
-    sent = pl.ds(pl.multiple_of(core[0] * rows, rows), rows)
-    for h in range(KV_HEADS):
-        for kv in range(2):
-            c = slice((kv * KV_HEADS + h) * HEAD, (kv * KV_HEADS + h + 1) * HEAD)
-            value = new[sent, c].astype(bf16)
-            for i in range(2):
-                for j in range(2):
-                    blocks[i, h, j, :, kv * HEAD : (kv + 1) * HEAD] = value
-
-
-def update(core, squares, grad, master, entries):
+                new[r, c] = master[0, r, c] - grad[z, y, kv].astype(f32) * step
+
+
+def update(received, grad, master, entries):
     _, rows, kv = master.shape
     return pl.pallas_call(
         lambda *refs: update_kernel(entries, *refs),
-        out_shape=(
-            jax.ShapeDtypeStruct((rows, kv), f32),
-            jax.ShapeDtypeStruct((2, KV_HEADS, 2, rows // 2, 2 * HEAD), bf16),
-        ),
-        grid_spec=pltpu.PrefetchScalarGridSpec(
-            num_scalar_prefetch=1,
-            grid=(1,),
-            in_specs=[
-                pl.BlockSpec(squares.shape, lambda i, c: (0, 0, 0)),
-                pl.BlockSpec(grad.shape, lambda i, c: (0, 0, 0, 0, 0)),
-                pl.BlockSpec((1, rows, kv), lambda i, c: (0, 0, 0)),
-            ],
-            out_specs=(
-                pl.BlockSpec((rows, kv), lambda i, c: (0, 0)),
-                pl.BlockSpec((2, KV_HEADS, 2, rows // 2, 2 * HEAD), lambda i, c: (0, 0, 0, 0, 0)),
-            ),
-        ),
-        compiler_params=params(),
-        cost_estimate=cost(4 * rows * kv, 12 * rows * kv),
+        out_shape=jax.ShapeDtypeStruct((rows, kv), f32),
+        grid=(1,),
+        in_specs=[
+            pl.BlockSpec((received.shape[0], 8, LANES), lambda i: (0, rows // 16, 0)),
+            pl.BlockSpec(grad.shape, lambda i: (0, 0, 0, 0, 0)),
+            pl.BlockSpec((1, rows, kv), lambda i: (0, 0, 0)),
+        ],
+        out_specs=pl.BlockSpec((rows, kv), lambda i: (0, 0)),
+        compiler_params=params(),
+        cost_estimate=cost(4 * rows * kv, 10 * rows * kv),
         name="update",
-    )(core, squares, grad, master)
+    )(received, grad, master)
 
 
 def rest_kernel(pos, *refs):
     masters, outs = refs[:8], refs[8:]
     for d in range(4):
-        for l in range(2):
-            for kv in range(2):
-                outs[d][0, l, :, kv * HEAD : (kv + 1) * HEAD] = masters[2 * d + kv][1 + l].astype(bf16)
+        for kv in range(2):
+            outs[d][0, :, :, kv * HEAD : (kv + 1) * HEAD] = masters[2 * d + kv][...].astype(bf16)
 
 
 def rest_blocks(pos, master):
@@ -274,7 +278,7 @@
             lambda xl, p: (0, p[0], k * KV_HEADS + xl * 2 + ((p[2] + d) % 4) // 2),
         )
 
-    shape = (2, layers - 1, half, 2 * HEAD)
+    shape = (2, layers, half, 2 * HEAD)
     return pl.pallas_call(
         rest_kernel,
         out_shape=[jax.ShapeDtypeStruct(shape, bf16)] * 4,
@@ -291,11 +295,16 @@
 
 
 def regroup_kernel(pos, *refs):
-    parts, (same, cross) = refs[:4], refs[4:]
+    parts, (same, cross), sems = refs[:4], refs[4:6], refs[6]
     xl = pos[1] % 2
+    copies = []
     for d in range(4):
-        same[d] = parts[d][xl]
-        cross[d] = parts[d][1 - xl]
+        copies.append(pltpu.make_async_copy(parts[d].at[xl], same.at[d], sems.at[2 * d]))
+        copies.append(pltpu.make_async_copy(parts[d].at[1 - xl], cross.at[d], sems.at[2 * d + 1]))
+    for copy in copies:
+        copy.start()
+    for copy in copies:
+        copy.wait()
 
 
 def regroup(pos, parts):
@@ -307,8 +316,9 @@
         grid_spec=pltpu.PrefetchScalarGridSpec(
             num_scalar_prefetch=1,
             grid=(1,),
-            in_specs=[whole(parts[0].shape)] * 4,
+            in_specs=[pl.BlockSpec(memory_space=pltpu.HBM)] * 4,
             out_specs=[whole(shape)] * 2,
+            scratch_shapes=[pltpu.SemaphoreType.DMA((8,))],
         ),
         compiler_params=params(),
         cost_estimate=cost(parts[0].size, 16 * parts[0].size),
@@ -330,13 +340,13 @@
 
 def place_rest(pos, own, other, layers):
     _, count, half, width = own[0].shape
-    src = pl.BlockSpec((4, 1, half, width), lambda l, d, w, p: (0, l, 0, 0))
+    src = pl.BlockSpec((4, 1, half, width), lambda l, d, w, p: (0, 1 + l, 0, 0))
     return pl.pallas_call(
         place_rest_kernel,
         out_shape=jax.ShapeDtypeStruct((layers, 4, 4, 2, half, width), bf16),
         grid_spec=pltpu.PrefetchScalarGridSpec(
             num_scalar_prefetch=1,
-            grid=(count, 4, 2),
+            grid=(count - 1, 4, 2),
             in_specs=[src] * 8,
             out_specs=pl.BlockSpec(
                 (1, 1, 4, 1, half, width),
@@ -349,34 +359,46 @@
     )(pos, *own, *other)
 
 
-def place_first_kernel(pos, own, other, into, out):
-    @pl.when(pl.program_id(1) == 0)
-    def _():
-        out[0, :, 0] = own[...]
-
-    @pl.when(pl.program_id(1) == 1)
-    def _():
-        out[0, :, 0] = other[...]
-
-
-def place_first(pos, own, other, into):
-    n, half, width = own.shape
-    group = n // 2
-    src = pl.BlockSpec((group, half, width), lambda s, w, p: (s, 0, 0))
-    return pl.pallas_call(
-        place_first_kernel,
+def finish_kernel(entries, pos, squares, grad_a, grad_b, *refs):
+    masters, out = refs[:8], refs[9]
+    zh = pos[2]
+    step = step_size(squares, entries)
+    half = out.shape[4]
+    for w in range(2):
+        grad = (grad_a, grad_b)[w]
+        for dx in range(4):
+
+            @pl.when((pl.program_id(0) == dx) & (pl.program_id(1) == w))
+            def _():
+                for dz in range(4):
+                    k = (zh - dz + 4) % 4
+                    value = masters[4 * w + dx][dz, 0].astype(f32) - grad[k, :half].astype(f32) * step
+                    out[0, 0, k, 0] = value.astype(bf16)
+
+
+def finish(pos, grad_a, grad_b, own, other, into, entries):
+    n, padded, width = grad_a.shape
+    half = padded - 8
+    grad = pl.BlockSpec((4, padded, width), lambda d, w, p: ((p[1] - d + 4) % 4, 0, 0))
+    src = pl.BlockSpec((4, 1, half, width), lambda d, w, p: (0, 0, 0, 0))
+    return pl.pallas_call(
+        lambda *refs: finish_kernel(entries, *refs),
         out_shape=jax.ShapeDtypeStruct(into.shape, bf16),
         grid_spec=pltpu.PrefetchScalarGridSpec(
             num_scalar_prefetch=1,
-            grid=(2, 2),
-            in_specs=[src, src, pl.BlockSpec(memory_space=pl.ANY)],
-            out_specs=pl.BlockSpec((1, group, 1, half, width), lambda s, w, p: (0, s, (p[0] + w) % 2, 0, 0)),
-        ),
-        input_output_aliases={3: 0},
-        compiler_params=params(),
-        cost_estimate=cost(own.size, 8 * own.size),
-        name="place_first",
-    )(pos, own, other, into)
+            grid=(4, 2),
+            in_specs=[pl.BlockSpec((n, 8, LANES), lambda d, w, p: (0, half // 8, 0)), grad, grad]
+            + [src] * 8
+            + [pl.BlockSpec(memory_space=pl.ANY)],
+            out_specs=pl.BlockSpec(
+                (1, 1, 4, 1, half, width), lambda d, w, p: (0, (p[1] - d + 4) % 4, 0, (p[0] + w) % 2, 0, 0)
+            ),
+        ),
+        input_output_aliases={12: 0},
+        compiler_params=params(),
+        cost_estimate=cost(8 * grad_a.size, 24 * grad_a.size),
+        name="finish",
+    )(pos, grad_a, grad_a, grad_b, *own, *other, into)
 
 
 def per_device(
@@ -424,15 +446,16 @@
     zl = lax.axis_size("zl")
     part = exchanged(part, ("zh", "zl"))
     grad = exchanged(sum_spread(part, zl * n_y * 2), REP)
-    squares = exchanged(squares_of(grad, n_shard), SHARD)
     grad = grad.reshape(zl, n_y, 2, *grad.shape[1:])
-    new_master, first = update(pos, squares, grad, master, hidden.shape[1] * kv)
+    first = send_blocks(pos, grad)
+    first = exchanged(first.reshape(n_shard, *first.shape[3:]), SHARD)
 
     other = [swapped(r) for r in rest]
     out = place_rest(pos, rest, other, layers)
-    out = out.reshape(layers, n_shard, 2, rows // 2, 2 * HEAD)
-    first = exchanged(first.reshape(n_shard, rows // 2, 2 * HEAD), SHARD)
-    out = place_first(pos, first, swapped(first), out)
+    entries = hidden.shape[1] * kv
+    first_b = swapped(first)
+    new_master = update(first, grad, master, entries)
+    out = finish(pos, first, first_b, rest, other, out, entries)
     return (new_master, out.reshape(layers, n_shard * rows, 2 * HEAD))
 
 

time: 224 us -> 243 us (1.085)
  waiting for transfers between devices: 77 us -> 102 us
  blocking collectives: 48.7 us -> 32.1 us
  Pallas kernels: 25.1 us -> 33.5 us
    ppermute x18, waiting for transfers between devices: 66.1 us -> 91 us  [shifted(): return lax.ppermute(value, axis, [(i, (i + by) % n) for i in range(n)])]
    all_to_all x3 -> x2, blocking collectives: 48.7 us -> 32.1 us  [exchanged(): return lax.all_to_all(blocks, axis, split_axis=0, concat_axis=0, tiled=True)]
    pallas_call x3, Pallas kernels: 5.77 us -> 9.43 us  [the longest x1 6.83 us: finish(): pl.pallas_call(lambda *refs: finish_kernel(entries, *refs), out_shape=jax...]
    pallas_call x1, Pallas kernels: 0.61 us -> 3.48 us  [regroup(): pl.pallas_call(regroup_kernel, out_shape=[jax.ShapeDtypeStruct(shape, bf1...]
  transfers between devices with their start and end apart: 29 -> 29, of which waited for: 12 -> 13; matrix products, arithmetic and copies ran while one was open for 4% -> 4% of each run, Pallas kernels for 4% -> 7%
where the time goes in v4:
time: 243 us; the launch traced here: 241 us
  waiting for transfers between devices  102 us (42%)
  starting transfers between devices  59.9 us (25%)
  Pallas kernels  33.5 us (14%)
  blocking collectives  32.1 us (13%)
  local copies, waits for them, and re-layouts  5.45 us (2%)
  matrix products  4.75 us (2%)
    ppermute x18, waiting for transfers between devices, shifted(): return lax.ppermute(value, axis, [(i, (i + by) % n) for i in range(n)])  91 us
    ppermute x18, starting transfers between devices, shifted(): return lax.ppermute(value, axis, [(i, (i + by) % n) for i in range(n)])  33.7 us
    all_to_all x2, blocking collectives, exchanged(): return lax.all_to_all(blocks, axis, split_axis=0, concat_axis=0, tiled=True)  32.1 us
    all_to_all x3, starting transfers between devices, exchanged(): return lax.all_to_all(blocks, axis, split_axis=0, concat_axis=0, tiled=True)  20.1 us
    pallas_call x1, Pallas kernels, place_rest(): pl.pallas_call(place_rest_kernel, out_shape=jax.ShapeDtypeStruct((layers,...  8.89 us
    pallas_call x1, Pallas kernels, partial_product(): pl.pallas_call(partial_kernel, out_shape=[jax.ShapeDtypeStruct(shape, bf1...  8.85 us
    all_to_all x3, waiting for transfers between devices, exchanged(): return lax.all_to_all(blocks, axis, split_axis=0, concat_axis=0, tiled=True)  8.77 us
    pallas_call x1, Pallas kernels, finish(): pl.pallas_call(lambda *refs: finish_kernel(entries, *refs), out_shape=jax...  6.83 us
  transfers between devices with their start and end apart: 29, of which 13 were waited for; matrix products, arithmetic and copies ran while one was open for 4% of the time, Pallas kernels for 7%

profile of v4, /device:TPU:33, one launch (start us, length us, event | category | flops | bytes accessed | tf_op | source)
XLA Modules:
  0.0 241.1 jit_solution(15226322550055378648)
XLA Ops:
  3.7 6.0 %all-to-all-start = ((f32[16,3,128]{2,1,0:T(4,128)}), f32[16,3,128]{2,1,0:T(4,128)S(1)}, u32[]{:S(2)}, u32[]{:S(2)}) async-start(f32[16,3,128]{2,1,0:T(4,128)} %broadcast_in_dim.8), calls=%async_computation | async-start | bytes 65536 | tf_op jit(solution)/shard_map/all_to_all | solution.py:34
  16.4 9.9 %all-to-all-start.1 = ((f32[16,3,128]{2,1,0:T(4,128)}), f32[16,3,128]{2,1,0:T(4,128)S(1)}, u32[]{:S(2)}, u32[]{:S(2)}) async-start(f32[16,3,128]{2,1,0:T(4,128)} %broadcast_in_dim.9), calls=%async_computation.1 | async-start | bytes 65536 | tf_op jit(solution)/shard_map/all_to_all | solution.py:34
  26.4 8.8 %all-to-all-done.1.stats = f32[16,3,128]{2,1,0:T(4,128)S(1)} async-done(((f32[16,3,128]{2,1,0:T(4,128)}), f32[16,3,128]{2,1,0:T(4,128)S(1)}, u32[]{:S(2)}, u32[]{:S(2)}) %all-to-all-start.1) | async-done | bytes 24608 | tf_op jit(solution)/shard_map/all_to_all | solution.py:34
  35.1 1.9 copy-done.2
  38.2 8.8 %partial_product.1 = (bf16[4,64,896]{2,1,0:T(8,128)(2,1)S(1)}, bf16[4,64,896]{2,1,0:T(8,128)(2,1)S(1)}, bf16[4,64,896]{2,1,0:T(8,128)(2,1)S(1)}, bf16[4,64,896]{...) custom-call(s32[4]{0:T(128)S(1)} %pad_add_fusion.pos.refs_0_, ...), custom_call_target="tpu_custom_call" | custom-call | flops 3288334336 | bytes 10092544 | tf_op jit(solution)/shard_map/partial_product/pallas_call | solution.py:116
  47.4 1.8 collective-permute-start.4
  51.6 2.4 collective-permute-start.7
  54.0 5.5 %collective-permute-done.3.refs_1_ = bf16[4,64,896]{2,1,0:T(8,128)(2,1)S(1)} collective-permute-done((bf16[4,64,896]{2,1,0:T(8,128)(2,1)S(1)}, bf16[4,64,896]{2,1,0:T(8,128)(2,1)S(1)}, u32[]{:S(2)}, u32[]{:S(2)}) %collective-permute-start.3) | collective-permute-done | bytes 458784 | tf_op jit(solution)/shard_map/ppermute | solution.py:26
  59.5 2.4 %collective-permute-start.8 = (bf16[4,64,896]{2,1,0:T(8,128)(2,1)S(1)}, bf16[4,64,896]{2,1,0:T(8,128)(2,1)S(1)}, u32[]{:S(2)}, u32[]{:S(2)}) collective-permute-start(bf16[4,64,896]{2,1,0:T(8,128)(2,1)S(1)} %get-tuple-element.31), channel_id=1, source_target_pairs={{0,96},{32,0},{64,32},{96,64},{1,97},{33,1},{65,33},{97,65},{2,98}... | collective-permute-start | bytes 1376264 | tf_op jit(solution)/shard_map/ppermute | solution.py:26
  61.9 6.3 %collective-permute-done.4.refs_2_ = bf16[4,64,896]{2,1,0:T(8,128)(2,1)S(1)} collective-permute-done((bf16[4,64,896]{2,1,0:T(8,128)(2,1)S(1)}, bf16[4,64,896]{2,1,0:T(8,128)(2,1)S(1)}, u32[]{:S(2)}, u32[]{:S(2)}) %collective-permute-start.4) | collective-permute-done | bytes 458784 | tf_op jit(solution)/shard_map/ppermute | solution.py:26
  68.2 2.0 collective-permute-done.5.refs_3_
  70.2 2.2 collective-permute-done.7.refs_6_
  75.3 3.9 %collective-permute-start.12 = (bf16[64,896]{1,0:T(8,128)(2,1)S(1)}, bf16[64,896]{1,0:T(8,128)(2,1)S(1)}, u32[]{:S(2)}, u32[]{:S(2)}) collective-permute-start(bf16[64,896]{1,0:T(8,128)(2,1)S(1)} %get-tuple-element.37), channel_id=1, source_target_pairs={{0,4},{4,8},{8,12},{12,0},{1,5},{5,9},{9,13},{13,1},{2,6},{6,10},{... | collective-permute-start | bytes 344072 | tf_op jit(solution)/shard_map/ppermute | solution.py:26
  79.1 2.1 collective-permute-start.13
  81.2 2.1 collective-permute-start.14
  85.1 4.3 %collective-permute-done.9.refs_1_ = bf16[64,896]{1,0:T(8,128)(2,1)S(1)} collective-permute-done((bf16[64,896]{1,0:T(8,128)(2,1)S(1)}, bf16[64,896]{1,0:T(8,128)(2,1)S(1)}, u32[]{:S(2)}, u32[]{:S(2)}) %collective-permute-start.9) | collective-permute-done | bytes 114720 | tf_op jit(solution)/shard_map/ppermute | solution.py:26
  89.6 11.0 %all_to_all.25.src = bf16[8,112,128]{2,1,0:T(8,128)(2,1)S(1)} all-to-all(bf16[8,112,128]{2,1,0:T(8,128)(2,1)S(1)} %bitcast.44), channel_id=1, replica_groups=mesh['zl'=2,'y'=4,'c'=2,'x'=4,'zh'=4] {'zh','zl'}, dimensions={0} | all-to-all | bytes 458752 | tf_op jit(solution)/shard_map/all_to_all | solution.py:34
  100.6 21.1 %all_to_all.26 = bf16[16,112,128]{2,1,0:T(8,128)(2,1)S(1)} all-to-all(bf16[16,112,128]{2,1,0:T(8,128)(2,1)S(1)} %sum_spread.1), channel_id=1, replica_groups=mesh['zl'=2,'y'=4,'c'=2,'x'=4,'zh'=4] {'zl','y','c'}, dimensions={0} | all-to-all | bytes 917504 | tf_op jit(solution)/shard_map/all_to_all | solution.py:34
  123.3 4.3 %all-to-all-start.4 = ((bf16[16,120,256]{2,1,0:T(8,128)(2,1)}), bf16[16,120,256]{2,1,0:T(8,128)(2,1)}, u32[]{:S(2)}, u32[]{:S(2)}) async-start(bf16[16,120,256]{2,1,0:T(8,128)(2,1)} %bitcast.43), calls=%async_computation.4 | async-start | bytes 1966080 | tf_op jit(solution)/shard_map/all_to_all | solution.py:34
  129.3 2.2 collective-permute-start.16
  131.5 3.3 %collective-permute-start.17 = (bf16[2,3,112,256]{3,2,1,0:T(8,128)(2,1)S(1)}, bf16[2,3,112,256]{3,2,1,0:T(8,128)(2,1)S(1)}, u32[]{:S(2)}, u32[]{:S(2)}) collective-permute-start(bf16[2,3,112,256]{3,2,1,0:T(8,128)(2,1)S(1)} %get-tuple-element.42), channel_id=1, source_target_pairs={{0,2},{1,3},{2,0},{3,1},{4,6},{5,7},{6,4},{7,5},{8,10},{9,11},{10,... | collective-permute-start | bytes 1032200 | tf_op jit(solution)/shard_map/ppermute | solution.py:26
  134.8 3.3 %collective-permute-start.18 = (bf16[2,3,112,256]{3,2,1,0:T(8,128)(2,1)S(1)}, bf16[2,3,112,256]{3,2,1,0:T(8,128)(2,1)S(1)}, u32[]{:S(2)}, u32[]{:S(2)}) collective-permute-start(bf16[2,3,112,256]{3,2,1,0:T(8,128)(2,1)S(1)} %get-tuple-element.43), channel_id=1, source_target_pairs={{0,3},{1,0},{2,1},{3,2},{4,7},{5,4},{6,5},{7,6},{8,11},{9,8},{10,9... | collective-permute-start | bytes 1032200 | tf_op jit(solution)/shard_map/ppermute | solution.py:26
  138.1 44.4 %collective-permute-done.16.refs_1_ = bf16[2,3,112,256]{3,2,1,0:T(8,128)(2,1)S(1)} collective-permute-done((bf16[2,3,112,256]{3,2,1,0:T(8,128)(2,1)S(1)}, bf16[2,3,112,256]{3,2,1,0:T(8,128)(2,1)S(1)}, u32[]{:S(2)}, u32[]{:S(2)}) %collective-permute-start.16) | collective-permute-done | bytes 344096 | tf_op jit(solution)/shard_map/ppermute | solution.py:26
  182.5 3.5 %regroup.1 = (bf16[4,3,112,256]{3,2,1,0:T(8,128)(2,1)}, bf16[4,3,112,256]{3,2,1,0:T(8,128)(2,1)}) custom-call(s32[4]{0:T(128)S(1)} %pad_add_fusion.pos.refs_0_, bf16[2,3,112,256]{3,2,1,0:T(8,128)(2,1)S(1)} %get-tuple-element.40.refs_0_, bf16[2,3,112,256]{3,2,1,0:T(8,128)(2,1)S(1)} %collective-permute-done.16.refs_1_, ...), custom_call_target="tpu_custom_call" | custom-call | flops 172032 | bytes 2752512 | tf_op jit(solution)/shard_map/regroup/pallas_call | solution.py:313
  186.0 3.0 %collective-permute-start.20 = (bf16[4,3,112,256]{3,2,1,0:T(8,128)(2,1)}, bf16[4,3,112,256]{3,2,1,0:T(8,128)(2,1)}, u32[]{:S(2)}, u32[]{:S(2)}) collective-permute-start(bf16[4,3,112,256]{3,2,1,0:T(8,128)(2,1)} %get-tuple-element.44.refs_0_.refs_4_), channel_id=1, source_target_pairs={{0,8},{4,12},{8,0},{12,4},{1,9},{5,13},{9,1},{13,5},{2,10},{6,14},... | collective-permute-start | bytes 2064392 | tf_op jit(solution)/shard_map/ppermute | solution.py:26
  189.5 2.2 collective-permute-start.21
  193.1 11.3 %collective-permute-done.20.refs_2_.refs_6_ = bf16[4,3,112,256]{3,2,1,0:T(8,128)(2,1)} collective-permute-done((bf16[4,3,112,256]{3,2,1,0:T(8,128)(2,1)}, bf16[4,3,112,256]{3,2,1,0:T(8,128)(2,1)}, u32[]{:S(2)}, u32[]{:S(2)}) %collective-permute-start.20) | collective-permute-done | bytes 688160 | tf_op jit(solution)/shard_map/ppermute | solution.py:26
  204.4 2.4 collective-permute-start.24
  206.8 13.2 %collective-permute-done.19.refs_1_.refs_5_ = bf16[4,3,112,256]{3,2,1,0:T(8,128)(2,1)} collective-permute-done((bf16[4,3,112,256]{3,2,1,0:T(8,128)(2,1)}, bf16[4,3,112,256]{3,2,1,0:T(8,128)(2,1)}, u32[]{:S(2)}, u32[]{:S(2)}) %collective-permute-start.19) | collective-permute-done | bytes 688160 | tf_op jit(solution)/shard_map/ppermute | solution.py:26
  223.5 8.9 %place_rest.1.refs_12_ = bf16[3,4,4,2,112,256]{5,4,3,2,1,0:T(8,128)(2,1)} custom-call(s32[4]{0:T(128)S(1)} %pad_add_fusion.pos.refs_0_, bf16[4,3,112,256]{3,2,1,0:T(8,128)(2,1)} %get-tuple-element.44.refs_0_.refs_4_, bf16[4,3,112,256]{3,2,1,0:T(8,128)(2,1)} %collective-permute-done.19.refs_1_.refs_5_, ...), custom_call_target="tpu_custom_call" | custom-call | flops 344064 | bytes 11010048 | tf_op jit(solution)/shard_map/place_rest/pallas_call | solution.py:344
  232.4 1.9 update.1
  234.2 6.8 %finish.1 = bf16[3,4,4,2,112,256]{5,4,3,2,1,0:T(8,128)(2,1)} custom-call(s32[4]{0:T(128)S(1)} %pad_add_fusion.pos.refs_0_, bf16[16,120,256]{2,1,0:T(8,128)(2,1)} %all-to-all-done.4.refs_0_.refs_1_.refs_2_, bf16[16,120,256]{2,1,0:T(8,128)(2,1)} %all-to-all-done.4.refs_0_.refs_1_.refs_2_, ...), custom_call_target="tpu_custom_call", output_to_operand_aliasing={{}: (12, {})} | custom-call | flops 3932160 | bytes 11796480 | tf_op jit(solution)/shard_map/finish/pallas_call | solution.py:384
  (64 shorter events, 27.3 us)
Async XLA Ops:
  0.6 34.5 %collective-permute-start.2 = (bf16[448,3584]{1,0:T(8,128)(2,1)}, bf16[448,3584]{1,0:T(8,128)(2,1)}, u32[]{:S(2)}, u32[]{:S(2)}) collective-permute-start(bf16[448,3584]{1,0:T(8,128)(2,1)} %hid_a.1), channel_id=1, source_target_pairs={{0,16},{16,0},{1,17},{17,1},{2,18},{18,2},{3,19},{19,3},{4,20},{20... | collective-permute-start | bytes 9633800 | tf_op jit(solution)/shard_map/ppermute | solution.py:21
  1.4 33.7 %collective-permute-start.1 = (bf16[448,1024]{1,0:T(8,128)(2,1)}, bf16[448,1024]{1,0:T(8,128)(2,1)S(1)}, u32[]{:S(2)}, u32[]{:S(2)}) collective-permute-start(bf16[448,1024]{1,0:T(8,128)(2,1)} %cot_a.1), channel_id=1, source_target_pairs={{0,16},{16,0},{1,17},{17,1},{2,18},{18,2},{3,19},{19,3},{4,20},{20... | collective-permute-start | bytes 2752520 | tf_op jit(solution)/shard_map/ppermute | solution.py:21
  3.7 12.0 %all-to-all-start = ((f32[16,3,128]{2,1,0:T(4,128)}), f32[16,3,128]{2,1,0:T(4,128)S(1)}, u32[]{:S(2)}, u32[]{:S(2)}) async-start(f32[16,3,128]{2,1,0:T(4,128)} %broadcast_in_dim.8), calls=%async_computation | async-start | bytes 65536 | tf_op jit(solution)/shard_map/all_to_all | solution.py:34
  15.3 11.1 %collective-permute-start = (f32[8,448]{0,1:T(8,128)S(1)}, f32[8,448]{0,1:T(8,128)S(1)}, u32[]{:S(2)}, u32[]{:S(2)}) collective-permute-start(f32[8,448]{0,1:T(8,128)S(1)} %copy.29), channel_id=1, source_target_pairs={{0,16},{16,0},{1,17},{17,1},{2,18},{18,2},{3,19},{19,3},{4,20},{20... | collective-permute-start | bytes 43016 | tf_op jit(solution)/shard_map/ppermute | solution.py:21
  16.4 18.7 %all-to-all-start.1 = ((f32[16,3,128]{2,1,0:T(4,128)}), f32[16,3,128]{2,1,0:T(4,128)S(1)}, u32[]{:S(2)}, u32[]{:S(2)}) async-start(f32[16,3,128]{2,1,0:T(4,128)} %broadcast_in_dim.9), calls=%async_computation.1 | async-start | bytes 65536 | tf_op jit(solution)/shard_map/all_to_all | solution.py:34
  35.1 1.9 copy-start.2
  37.0 1.2 copy-start.3
  47.1 12.4 %collective-permute-start.3 = (bf16[4,64,896]{2,1,0:T(8,128)(2,1)S(1)}, bf16[4,64,896]{2,1,0:T(8,128)(2,1)S(1)}, u32[]{:S(2)}, u32[]{:S(2)}) collective-permute-start(bf16[4,64,896]{2,1,0:T(8,128)(2,1)S(1)} %get-tuple-element.25), channel_id=1, source_target_pairs={{0,4},{4,8},{8,12},{12,0},{1,5},{5,9},{9,13},{13,1},{2,6},{6,10},{... | collective-permute-start | bytes 1376264 | tf_op jit(solution)/shard_map/ppermute | solution.py:26
  47.4 20.8 %collective-permute-start.4 = (bf16[4,64,896]{2,1,0:T(8,128)(2,1)S(1)}, bf16[4,64,896]{2,1,0:T(8,128)(2,1)S(1)}, u32[]{:S(2)}, u32[]{:S(2)}) collective-permute-start(bf16[4,64,896]{2,1,0:T(8,128)(2,1)S(1)} %get-tuple-element.26), channel_id=1, source_target_pairs={{0,8},{4,12},{8,0},{12,4},{1,9},{5,13},{9,1},{13,5},{2,10},{6,14},... | collective-permute-start | bytes 1376264 | tf_op jit(solution)/shard_map/ppermute | solution.py:26
  49.2 21.0 %collective-permute-start.5 = (bf16[4,64,896]{2,1,0:T(8,128)(2,1)S(1)}, bf16[4,64,896]{2,1,0:T(8,128)(2,1)S(1)}, u32[]{:S(2)}, u32[]{:S(2)}) collective-permute-start(bf16[4,64,896]{2,1,0:T(8,128)(2,1)S(1)} %get-tuple-element.27), channel_id=1, source_target_pairs={{0,12},{4,0},{8,4},{12,8},{1,13},{5,1},{9,5},{13,9},{2,14},{6,2},{... | collective-permute-start | bytes 1376264 | tf_op jit(solution)/shard_map/ppermute | solution.py:26
  50.4 19.8 %collective-permute-start.6 = (bf16[4,64,896]{2,1,0:T(8,128)(2,1)S(1)}, bf16[4,64,896]{2,1,0:T(8,128)(2,1)S(1)}, u32[]{:S(2)}, u32[]{:S(2)}) collective-permute-start(bf16[4,64,896]{2,1,0:T(8,128)(2,1)S(1)} %get-tuple-element.29), channel_id=1, source_target_pairs={{0,32},{32,64},{64,96},{96,0},{1,33},{33,65},{65,97},{97,1},{2,34}... | collective-permute-start | bytes 1376264 | tf_op jit(solution)/shard_map/ppermute | solution.py:26
  51.6 20.8 %collective-permute-start.7 = (bf16[4,64,896]{2,1,0:T(8,128)(2,1)S(1)}, bf16[4,64,896]{2,1,0:T(8,128)(2,1)S(1)}, u32[]{:S(2)}, u32[]{:S(2)}) collective-permute-start(bf16[4,64,896]{2,1,0:T(8,128)(2,1)S(1)} %get-tuple-element.30), channel_id=1, source_target_pairs={{0,64},{32,96},{64,0},{96,32},{1,65},{33,97},{65,1},{97,33},{2,66}... | collective-permute-start | bytes 1376264 | tf_op jit(solution)/shard_map/ppermute | solution.py:26
  59.5 12.9 %collective-permute-start.8 = (bf16[4,64,896]{2,1,0:T(8,128)(2,1)S(1)}, bf16[4,64,896]{2,1,0:T(8,128)(2,1)S(1)}, u32[]{:S(2)}, u32[]{:S(2)}) collective-permute-start(bf16[4,64,896]{2,1,0:T(8,128)(2,1)S(1)} %get-tuple-element.31), channel_id=1, source_target_pairs={{0,96},{32,0},{64,32},{96,64},{1,97},{33,1},{65,33},{97,65},{2,98}... | collective-permute-start | bytes 1376264 | tf_op jit(solution)/shard_map/ppermute | solution.py:26
  73.4 9.9 %collective-permute-start.10 = (bf16[64,896]{1,0:T(8,128)(2,1)S(1)}, bf16[64,896]{1,0:T(8,128)(2,1)S(1)}, u32[]{:S(2)}, u32[]{:S(2)}) collective-permute-start(bf16[64,896]{1,0:T(8,128)(2,1)S(1)} %get-tuple-element.34), channel_id=1, source_target_pairs={{0,64},{32,96},{64,0},{96,32},{1,65},{33,97},{65,1},{97,33},{2,66}... | collective-permute-start | bytes 344072 | tf_op jit(solution)/shard_map/ppermute | solution.py:26
  74.1 9.2 %collective-permute-start.11 = (bf16[64,896]{1,0:T(8,128)(2,1)S(1)}, bf16[64,896]{1,0:T(8,128)(2,1)S(1)}, u32[]{:S(2)}, u32[]{:S(2)}) collective-permute-start(bf16[64,896]{1,0:T(8,128)(2,1)S(1)} %get-tuple-element.35), channel_id=1, source_target_pairs={{0,96},{32,0},{64,32},{96,64},{1,97},{33,1},{65,33},{97,65},{2,98}... | collective-permute-start | bytes 344072 | tf_op jit(solution)/shard_map/ppermute | solution.py:26
  75.3 8.1 %collective-permute-start.12 = (bf16[64,896]{1,0:T(8,128)(2,1)S(1)}, bf16[64,896]{1,0:T(8,128)(2,1)S(1)}, u32[]{:S(2)}, u32[]{:S(2)}) collective-permute-start(bf16[64,896]{1,0:T(8,128)(2,1)S(1)} %get-tuple-element.37), channel_id=1, source_target_pairs={{0,4},{4,8},{8,12},{12,0},{1,5},{5,9},{9,13},{13,1},{2,6},{6,10},{... | collective-permute-start | bytes 344072 | tf_op jit(solution)/shard_map/ppermute | solution.py:26
  79.1 5.5 %collective-permute-start.13 = (bf16[64,896]{1,0:T(8,128)(2,1)S(1)}, bf16[64,896]{1,0:T(8,128)(2,1)S(1)}, u32[]{:S(2)}, u32[]{:S(2)}) collective-permute-start(bf16[64,896]{1,0:T(8,128)(2,1)S(1)} %get-tuple-element.38), channel_id=1, source_target_pairs={{0,8},{4,12},{8,0},{12,4},{1,9},{5,13},{9,1},{13,5},{2,10},{6,14},... | collective-permute-start | bytes 344072 | tf_op jit(solution)/shard_map/ppermute | solution.py:26
  81.2 3.9 %collective-permute-start.14 = (bf16[64,896]{1,0:T(8,128)(2,1)S(1)}, bf16[64,896]{1,0:T(8,128)(2,1)S(1)}, u32[]{:S(2)}, u32[]{:S(2)}) collective-permute-start(bf16[64,896]{1,0:T(8,128)(2,1)S(1)} %get-tuple-element.39), channel_id=1, source_target_pairs={{0,12},{4,0},{8,4},{12,8},{1,13},{5,1},{9,5},{13,9},{2,14},{6,2},{... | collective-permute-start | bytes 344072 | tf_op jit(solution)/shard_map/ppermute | solution.py:26
  83.3 6.1 %collective-permute-start.9 = (bf16[64,896]{1,0:T(8,128)(2,1)S(1)}, bf16[64,896]{1,0:T(8,128)(2,1)S(1)}, u32[]{:S(2)}, u32[]{:S(2)}) collective-permute-start(bf16[64,896]{1,0:T(8,128)(2,1)S(1)} %get-tuple-element.33), channel_id=1, source_target_pairs={{0,32},{32,64},{64,96},{96,0},{1,33},{33,65},{65,97},{97,1},{2,34}... | collective-permute-start | bytes 344072 | tf_op jit(solution)/shard_map/ppermute | solution.py:26
  89.4 38.3 %copy-start = (f32[3,224,1024]{2,1,0:T(8,128)S(1)}, f32[3,224,1024]{2,1,0:T(8,128)}, u32[]{:S(2)}) copy-start(f32[3,224,1024]{2,1,0:T(8,128)} %refs_7_.1) | copy-start | bytes 8257540
  123.3 68.4 %all-to-all-start.4 = ((bf16[16,120,256]{2,1,0:T(8,128)(2,1)}), bf16[16,120,256]{2,1,0:T(8,128)(2,1)}, u32[]{:S(2)}, u32[]{:S(2)}) async-start(bf16[16,120,256]{2,1,0:T(8,128)(2,1)} %bitcast.43), calls=%async_computation.4 | async-start | bytes 1966080 | tf_op jit(solution)/shard_map/all_to_all | solution.py:34
  129.3 53.2 %collective-permute-start.16 = (bf16[2,3,112,256]{3,2,1,0:T(8,128)(2,1)S(1)}, bf16[2,3,112,256]{3,2,1,0:T(8,128)(2,1)S(1)}, u32[]{:S(2)}, u32[]{:S(2)}) collective-permute-start(bf16[2,3,112,256]{3,2,1,0:T(8,128)(2,1)S(1)} %get-tuple-element.41), channel_id=1, source_target_pairs={{0,1},{1,2},{2,3},{3,0},{4,5},{5,6},{6,7},{7,4},{8,9},{9,10},{10,1... | collective-permute-start | bytes 1032200 | tf_op jit(solution)/shard_map/ppermute | solution.py:26
  131.5 51.0 %collective-permute-start.17 = (bf16[2,3,112,256]{3,2,1,0:T(8,128)(2,1)S(1)}, bf16[2,3,112,256]{3,2,1,0:T(8,128)(2,1)S(1)}, u32[]{:S(2)}, u32[]{:S(2)}) collective-permute-start(bf16[2,3,112,256]{3,2,1,0:T(8,128)(2,1)S(1)} %get-tuple-element.42), channel_id=1, source_target_pairs={{0,2},{1,3},{2,0},{3,1},{4,6},{5,7},{6,4},{7,5},{8,10},{9,11},{10,... | collective-permute-start | bytes 1032200 | tf_op jit(solution)/shard_map/ppermute | solution.py:26
  134.8 47.7 %collective-permute-start.18 = (bf16[2,3,112,256]{3,2,1,0:T(8,128)(2,1)S(1)}, bf16[2,3,112,256]{3,2,1,0:T(8,128)(2,1)S(1)}, u32[]{:S(2)}, u32[]{:S(2)}) collective-permute-start(bf16[2,3,112,256]{3,2,1,0:T(8,128)(2,1)S(1)} %get-tuple-element.43), channel_id=1, source_target_pairs={{0,3},{1,0},{2,1},{3,2},{4,7},{5,4},{6,5},{7,6},{8,11},{9,8},{10,9... | collective-permute-start | bytes 1032200 | tf_op jit(solution)/shard_map/ppermute | solution.py:26
  186.0 18.4 %collective-permute-start.20 = (bf16[4,3,112,256]{3,2,1,0:T(8,128)(2,1)}, bf16[4,3,112,256]{3,2,1,0:T(8,128)(2,1)}, u32[]{:S(2)}, u32[]{:S(2)}) collective-permute-start(bf16[4,3,112,256]{3,2,1,0:T(8,128)(2,1)} %get-tuple-element.44.refs_0_.refs_4_), channel_id=1, source_target_pairs={{0,8},{4,12},{8,0},{12,4},{1,9},{5,13},{9,1},{13,5},{2,10},{6,14},... | collective-permute-start | bytes 2064392 | tf_op jit(solution)/shard_map/ppermute | solution.py:26
  189.0 31.0 %collective-permute-start.19 = (bf16[4,3,112,256]{3,2,1,0:T(8,128)(2,1)}, bf16[4,3,112,256]{3,2,1,0:T(8,128)(2,1)}, u32[]{:S(2)}, u32[]{:S(2)}) collective-permute-start(bf16[4,3,112,256]{3,2,1,0:T(8,128)(2,1)} %get-tuple-element.45), channel_id=1, source_target_pairs={{0,4},{4,8},{8,12},{12,0},{1,5},{5,9},{9,13},{13,1},{2,6},{6,10},{... | collective-permute-start | bytes 2064392 | tf_op jit(solution)/shard_map/ppermute | solution.py:26
  189.5 31.0 %collective-permute-start.21 = (bf16[4,3,112,256]{3,2,1,0:T(8,128)(2,1)}, bf16[4,3,112,256]{3,2,1,0:T(8,128)(2,1)}, u32[]{:S(2)}, u32[]{:S(2)}) collective-permute-start(bf16[4,3,112,256]{3,2,1,0:T(8,128)(2,1)} %get-tuple-element.45), channel_id=1, source_target_pairs={{0,12},{4,0},{8,4},{12,8},{1,13},{5,1},{9,5},{13,9},{2,14},{6,2},{... | collective-permute-start | bytes 2064392 | tf_op jit(solution)/shard_map/ppermute | solution.py:26
  191.7 42.5 %collective-permute-start.15 = (bf16[16,120,256]{2,1,0:T(8,128)(2,1)}, bf16[16,120,256]{2,1,0:T(8,128)(2,1)S(1)}, u32[]{:S(2)}, u32[]{:S(2)}) collective-permute-start(bf16[16,120,256]{2,1,0:T(8,128)(2,1)} %all-to-all-done.4.refs_0_.refs_1_.refs_2_), channel_id=1, source_target_pairs={{0,16},{16,0},{1,17},{17,1},{2,18},{18,2},{3,19},{19,3},{4,20},{20... | collective-permute-start | bytes 2949128 | tf_op jit(solution)/shard_map/ppermute | solution.py:21
  193.1 27.9 %collective-permute-start.22 = (bf16[4,3,112,256]{3,2,1,0:T(8,128)(2,1)}, bf16[4,3,112,256]{3,2,1,0:T(8,128)(2,1)S(1)}, u32[]{:S(2)}, u32[]{:S(2)}) collective-permute-start(bf16[4,3,112,256]{3,2,1,0:T(8,128)(2,1)} %get-tuple-element.44.refs_0_.refs_4_), channel_id=1, source_target_pairs={{0,16},{16,0},{1,17},{17,1},{2,18},{18,2},{3,19},{19,3},{4,20},{20... | collective-permute-start | bytes 2064392 | tf_op jit(solution)/shard_map/ppermute | solution.py:21
  204.4 16.6 %collective-permute-start.24 = (bf16[4,3,112,256]{3,2,1,0:T(8,128)(2,1)}, bf16[4,3,112,256]{3,2,1,0:T(8,128)(2,1)S(1)}, u32[]{:S(2)}, u32[]{:S(2)}) collective-permute-start(bf16[4,3,112,256]{3,2,1,0:T(8,128)(2,1)} %collective-permute-done.20.refs_2_.refs_6_), channel_id=1, source_target_pairs={{0,16},{16,0},{1,17},{17,1},{2,18},{18,2},{3,19},{19,3},{4,20},{20... | collective-permute-start | bytes 2064392 | tf_op jit(solution)/shard_map/ppermute | solution.py:21
  220.0 2.5 %collective-permute-start.23 = (bf16[4,3,112,256]{3,2,1,0:T(8,128)(2,1)}, bf16[4,3,112,256]{3,2,1,0:T(8,128)(2,1)S(1)}, u32[]{:S(2)}, u32[]{:S(2)}) collective-permute-start(bf16[4,3,112,256]{3,2,1,0:T(8,128)(2,1)} %collective-permute-done.19.refs_1_.refs_5_), channel_id=1, source_target_pairs={{0,16},{16,0},{1,17},{17,1},{2,18},{18,2},{3,19},{19,3},{4,20},{20... | collective-permute-start | bytes 2064392 | tf_op jit(solution)/shard_map/ppermute | solution.py:21
  220.5 3.0 %collective-permute-start.25 = (bf16[4,3,112,256]{3,2,1,0:T(8,128)(2,1)}, bf16[4,3,112,256]{3,2,1,0:T(8,128)(2,1)S(1)}, u32[]{:S(2)}, u32[]{:S(2)}) collective-permute-start(bf16[4,3,112,256]{3,2,1,0:T(8,128)(2,1)} %collective-permute-done.21.refs_3_.refs_7_), channel_id=1, source_target_pairs={{0,16},{16,0},{1,17},{17,1},{2,18},{18,2},{3,19},{19,3},{4,20},{20... | collective-permute-start | bytes 2064392 | tf_op jit(solution)/shard_map/ppermute | solution.py:21
  (1 other events, 0.9 us)

commit v5 on v4

--- a/solution.py
+++ b/solution.py
@@ -67,61 +67,89 @@
     return jnp.stack([weight, ratio, penalty, tok_reward, tok_group, zero, zero, zero], axis=0)
 
 
+def turn_kernel(pos, cot_a, cot_b, out_a, out_b):
+    half, _ = out_a.shape
+    rows = half // 8
+    cols = pl.ds(pl.multiple_of(pos[0] * half, half), half)
+    for cot, out in ((cot_a, out_a), (cot_b, out_b)):
+        turned = cot[:, cols].astype(f32).T.astype(bf16)
+        for y in range(4):
+            out[y * rows : (y + 1) * rows, :] = turned[2 * y * rows : (2 * y + 1) * rows]
+            to = pl.multiple_of((4 + (y - pos[3] + 4) % 4) * rows, rows)
+            out[pl.ds(to, rows), :] = turned[(2 * y + 1) * rows : (2 * y + 2) * rows]
+
+
+def turn(pos, cot_a, cot_b):
+    toks, kv = cot_a.shape
+    whole = lambda *shape: pl.BlockSpec(shape, lambda i, p: (0,) * len(shape))
+    return pl.pallas_call(
+        turn_kernel,
+        out_shape=[jax.ShapeDtypeStruct((kv // 2, toks), bf16)] * 2,
+        grid_spec=pltpu.PrefetchScalarGridSpec(
+            num_scalar_prefetch=1,
+            grid=(1,),
+            in_specs=[whole(toks, kv)] * 2,
+            out_specs=[whole(kv // 2, toks)] * 2,
+        ),
+        compiler_params=params(),
+        cost_estimate=cost(4 * cot_a.size, 6 * cot_a.size),
+        name="turn",
+    )(pos, cot_a, cot_b)
+
+
 def partial_kernel(pos, stats, tok_a, tok_b, cot_a, cot_b, hid_a, hid_b, *refs):
-    outs, (delta_a, delta_b) = refs[:8], refs[8:]
-    half = cot_a.shape[1] // 2
-    rows = outs[0].shape[1]
-    step = pl.program_id(0)
-
-    @pl.when(step == 0)
-    def _():
-        sums = jnp.sum(stats[...], axis=0)
-        count = jnp.maximum(sums[0:1, :], 1.0)
-        mean = sums[1:2, :] / count
-        spread = jnp.maximum(jnp.sqrt(jnp.maximum(sums[2:3, :] / count - mean * mean, 0.0)), 0.5)
-        cols = pl.ds(pl.multiple_of(pos[0] * half, half), half)
-        for tok, cot, delta in ((tok_a, cot_a, delta_a), (tok_b, cot_b, delta_b)):
-            t = tok[...]
-            lane = lax.broadcasted_iota(jnp.int32, (t.shape[0], LANES), 1).astype(f32)
-            pick = lane == t[:, 4:5]
-            tok_mean = jnp.sum(jnp.where(pick, mean, 0.0), axis=1, keepdims=True)
-            tok_std = jnp.sum(jnp.where(pick, spread, 0.0), axis=1, keepdims=True)
-            adv = (t[:, 3:4] - tok_mean) / tok_std
-            coef = t[:, 0:1] * (-adv * t[:, 1:2] + t[:, 2:3])
-            turned = (coef * cot[:, cols].astype(f32)).T.astype(bf16)
-            for y in range(4):
-                delta[y * rows : (y + 1) * rows, :] = turned[2 * y * rows : (2 * y + 1) * rows]
-                to = pl.multiple_of((4 + (y - pos[3] + 4) % 4) * rows, rows)
-                delta[pl.ds(to, rows), :] = turned[(2 * y + 1) * rows : (2 * y + 2) * rows]
-
-    acc = jnp.dot(delta_a[...], hid_a[...], preferred_element_type=f32)
-    acc = acc + jnp.dot(delta_b[...], hid_b[...], preferred_element_type=f32)
-    acc = acc.astype(bf16).reshape(8, rows, acc.shape[1])
+    outs, (hid, sems) = refs[:8], refs[8:]
+    rows, blk = outs[0].shape[1:]
+    copies = []
     for d in range(4):
-
-        @pl.when(step == d)
-        def _():
-            outs[d][...] = acc[:4]
-
-        outs[4 + d][(pos[1] + step) % 4] = acc[4 + d]
+        cols = pl.ds(pl.multiple_of((pos[1] + d) % 4 * blk, LANES), blk)
+        for k, src in enumerate((hid_a, hid_b)):
+            copies.append(pltpu.make_async_copy(src.at[:, cols], hid.at[d, k], sems.at[d, k]))
+    for copy in copies:
+        copy.start()
+    sums = jnp.sum(stats[...], axis=0)
+    count = jnp.maximum(sums[0:1, :], 1.0)
+    mean = sums[1:2, :] / count
+    spread = jnp.maximum(jnp.sqrt(jnp.maximum(sums[2:3, :] / count - mean * mean, 0.0)), 0.5)
+    table = jnp.concatenate([jnp.broadcast_to(mean, (8, LANES)), jnp.broadcast_to(spread, (8, LANES))], axis=0).T
+    mean, spread = table[:, 0:1], table[:, 8:9]
+    delta = []
+    for tok, cot in ((tok_a, cot_a), (tok_b, cot_b)):
+        t = tok[...]
+        group = lax.broadcasted_iota(jnp.int32, (LANES, t.shape[1]), 0).astype(f32)
+        pick = group == t[4:5]
+        tok_mean = jnp.sum(jnp.where(pick, mean, 0.0), axis=0, keepdims=True)
+        tok_std = jnp.sum(jnp.where(pick, spread, 0.0), axis=0, keepdims=True)
+        adv = (t[3:4] - tok_mean) / tok_std
+        coef = t[0:1] * (-adv * t[1:2] + t[2:3])
+        delta.append((cot[...].astype(f32) * coef).astype(bf16))
+    for d in range(4):
+        copies[2 * d].wait()
+        acc = jnp.dot(delta[0], hid[d, 0], preferred_element_type=f32)
+        copies[2 * d + 1].wait()
+        acc = acc + jnp.dot(delta[1], hid[d, 1], preferred_element_type=f32)
+        acc = acc.astype(bf16).reshape(8, rows, blk)
+        outs[d][...] = acc[:4]
+        for e in range(4):
+            outs[4 + e][(pos[1] + d) % 4] = acc[4 + e]
 
 
 def partial_product(pos, stats, tok_a, tok_b, cot_a, cot_b, hid_a, hid_b):
     toks, width = hid_a.shape
-    half = cot_a.shape[1] // 2
+    half = cot_a.shape[0]
     blk = width // 4
     shape = (4, half // 8, blk)
-    whole = lambda a: pl.BlockSpec(a.shape, lambda i, p: (0,) * a.ndim)
-    hid = pl.BlockSpec((toks, blk), lambda i, p: (0, (p[1] + i) % 4))
+    whole = lambda s: pl.BlockSpec(s, lambda i, p: (0,) * len(s))
+    far = pl.BlockSpec(memory_space=pltpu.HBM)
     return pl.pallas_call(
         partial_kernel,
         out_shape=[jax.ShapeDtypeStruct(shape, bf16)] * 8,
         grid_spec=pltpu.PrefetchScalarGridSpec(
             num_scalar_prefetch=1,
-            grid=(4,),
-            in_specs=[whole(stats), whole(tok_a), whole(tok_b), whole(cot_a), whole(cot_b), hid, hid],
-            out_specs=[pl.BlockSpec(shape, lambda i, p: (0, 0, 0))] * 8,
-            scratch_shapes=[pltpu.VMEM((half, toks), bf16), pltpu.VMEM((half, toks), bf16)],
+            grid=(1,),
+            in_specs=[whole(a.shape) for a in (stats, tok_a, tok_b, cot_a, cot_b)] + [far, far],
+            out_specs=[whole(shape)] * 8,
+            scratch_shapes=[pltpu.VMEM((4, 2, toks, blk), bf16), pltpu.SemaphoreType.DMA((4, 2))],
         ),
         compiler_params=params(),
         cost_estimate=cost(4 * toks * width * half, 4 * toks * width + 2 * width * half),
@@ -129,32 +157,28 @@
     )(pos, stats, tok_a, tok_b, cot_a, cot_b, hid_a, hid_b)
 
 
-def sum_mid_kernel(pos, *refs):
-    for half in range(2):
-        srcs, outs = refs[4 * half : 4 * half + 4], refs[8 + 4 * half : 12 + 4 * half]
-        at = pos[3] if half == 0 else pos[1]
-        for d in range(4):
-            k = (at + d) % 4
-            outs[d][...] = sum(src[k].astype(f32) for src in srcs).astype(bf16)
-
-
-def sum_mid(pos, first, second):
-    _, rows, width = first[0].shape
+def sum_mid_kernel(axis, pos, *refs):
+    srcs, outs = refs[:4], refs[4:]
+    for d in range(4):
+        k = (pos[axis] + d) % 4
+        outs[d][...] = sum(src[k].astype(f32) for src in srcs).astype(bf16)
+
+
+def sum_mid(pos, parts, axis):
+    _, rows, width = parts[0].shape
     whole = lambda *shape: pl.BlockSpec(shape, lambda i, p: (0,) * len(shape))
-    out = pl.pallas_call(
-        sum_mid_kernel,
-        out_shape=[jax.ShapeDtypeStruct((rows, width), bf16)] * 8,
+    return pl.pallas_call(
+        lambda *refs: sum_mid_kernel(axis, *refs),
+        out_shape=[jax.ShapeDtypeStruct((rows, width), bf16)] * 4,
         grid_spec=pltpu.PrefetchScalarGridSpec(
             num_scalar_prefetch=1,
             grid=(1,),
-            in_specs=[whole(4, rows, width)] * 8,
-            out_specs=[whole(rows, width)] * 8,
-        ),
-        compiler_params=params(),
-        cost_estimate=cost(32 * rows * width, 80 * rows * width),
-        name="sum_mid",
-    )(pos, *first, *second)
-    return out[:4], out[4:]
+            in_specs=[whole(4, rows, width)] * 4,
+            out_specs=[whole(rows, width)] * 4,
+        ),
+        compiler_params=params(),
+        cost_estimate=cost(16 * rows * width, 40 * rows * width),
+    )(pos, *parts)
 
 
 def sum_turn_kernel(*refs):
@@ -328,29 +352,28 @@
 
 def place_rest_kernel(pos, *refs):
     srcs, out = refs[:8], refs[8]
-    zh = pos[2]
-    for w in range(2):
-        for dx in range(4):
-
-            @pl.when((pl.program_id(1) == dx) & (pl.program_id(2) == w))
-            def _():
+    zh, core = pos[2], pos[0]
+    for dx in range(4):
+
+        @pl.when(pl.program_id(1) == dx)
+        def _():
+            for w in range(2):
                 for dz in range(4):
-                    out[0, 0, (zh - dz + 4) % 4, 0] = srcs[4 * w + dx][dz, 0]
+                    out[0, 0, (zh - dz + 4) % 4, (core + w) % 2] = srcs[4 * w + dx][dz, 0]
 
 
 def place_rest(pos, own, other, layers):
     _, count, half, width = own[0].shape
-    src = pl.BlockSpec((4, 1, half, width), lambda l, d, w, p: (0, 1 + l, 0, 0))
+    src = pl.BlockSpec((4, 1, half, width), lambda l, d, p: (0, 1 + l, 0, 0))
     return pl.pallas_call(
         place_rest_kernel,
         out_shape=jax.ShapeDtypeStruct((layers, 4, 4, 2, half, width), bf16),
         grid_spec=pltpu.PrefetchScalarGridSpec(
             num_scalar_prefetch=1,
-            grid=(count - 1, 4, 2),
+            grid=(count - 1, 4),
             in_specs=[src] * 8,
             out_specs=pl.BlockSpec(
-                (1, 1, 4, 1, half, width),
-                lambda l, d, w, p: (1 + l, (p[1] - d + 4) % 4, 0, (p[0] + w) % 2, 0, 0),
+                (1, 1, 4, 2, half, width), lambda l, d, p: (1 + l, (p[1] - d + 4) % 4, 0, 0, 0, 0)
             ),
         ),
         compiler_params=params(),
@@ -361,37 +384,37 @@
 
 def finish_kernel(entries, pos, squares, grad_a, grad_b, *refs):
     masters, out = refs[:8], refs[9]
-    zh = pos[2]
+    zh, core = pos[2], pos[0]
     step = step_size(squares, entries)
     half = out.shape[4]
-    for w in range(2):
-        grad = (grad_a, grad_b)[w]
-        for dx in range(4):
-
-            @pl.when((pl.program_id(0) == dx) & (pl.program_id(1) == w))
-            def _():
+    for dx in range(4):
+
+        @pl.when(pl.program_id(0) == dx)
+        def _():
+            for w in range(2):
+                grad = (grad_a, grad_b)[w]
                 for dz in range(4):
                     k = (zh - dz + 4) % 4
                     value = masters[4 * w + dx][dz, 0].astype(f32) - grad[k, :half].astype(f32) * step
-                    out[0, 0, k, 0] = value.astype(bf16)
+                    out[0, 0, k, (core + w) % 2] = value.astype(bf16)
 
 
 def finish(pos, grad_a, grad_b, own, other, into, entries):
     n, padded, width = grad_a.shape
     half = padded - 8
-    grad = pl.BlockSpec((4, padded, width), lambda d, w, p: ((p[1] - d + 4) % 4, 0, 0))
-    src = pl.BlockSpec((4, 1, half, width), lambda d, w, p: (0, 0, 0, 0))
+    grad = pl.BlockSpec((4, padded, width), lambda d, p: ((p[1] - d + 4) % 4, 0, 0))
+    src = pl.BlockSpec((4, 1, half, width), lambda d, p: (0, 0, 0, 0))
     return pl.pallas_call(
         lambda *refs: finish_kernel(entries, *refs),
         out_shape=jax.ShapeDtypeStruct(into.shape, bf16),
         grid_spec=pltpu.PrefetchScalarGridSpec(
             num_scalar_prefetch=1,
-            grid=(4, 2),
-            in_specs=[pl.BlockSpec((n, 8, LANES), lambda d, w, p: (0, half // 8, 0)), grad, grad]
+            grid=(4,),
+            in_specs=[pl.BlockSpec((n, 8, LANES), lambda d, p: (0, half // 8, 0)), grad, grad]
             + [src] * 8
             + [pl.BlockSpec(memory_space=pl.ANY)],
             out_specs=pl.BlockSpec(
-                (1, 1, 4, 1, half, width), lambda d, w, p: (0, (p[1] - d + 4) % 4, 0, (p[0] + w) % 2, 0, 0)
+                (1, 1, 4, 2, half, width), lambda d, p: (0, (p[1] - d + 4) % 4, 0, 0, 0, 0)
             ),
         ),
         input_output_aliases={12: 0},
@@ -430,13 +453,15 @@
     )
     tok_b = swapped(tok)
 
-    partial = partial_product(pos, stats, tok.T, tok_b.T, cotangent, cotangent_b, hidden, hidden_b)
+    turned = turn(pos, cotangent, cotangent_b)
+    partial = partial_product(pos, stats, tok, tok_b, *turned, hidden, hidden_b)
     to_x = spread_out(partial[:4], "x")
     to_y = spread_out(partial[4:], "y")
-    to_y, to_x = sum_mid(pos, to_x, to_y)
-    to_y = spread_out(to_y, "y")
-    to_x = spread_out(to_x, "x")
-    part = sum_turn(to_y, to_x)
+    to_x = sum_mid(pos, to_x, 3)
+    to_x = spread_out(to_x, "y")
+    to_y = sum_mid(pos, to_y, 1)
+    to_y = spread_out(to_y, "x")
+    part = sum_turn(to_x, to_y)
 
     parts = rest_blocks(pos, master)
     parts = spread_out(parts, "zh")

time: 243 us -> 231 us (0.951)
  waiting for transfers between devices: 102 us -> 94.5 us
  local copies, waits for them, and re-layouts: 5.45 us -> 11.1 us
  Pallas kernels: 33.5 us -> 28.7 us
  starting transfers between devices: 59.9 us -> 56.3 us
    all_to_all x3, waiting for transfers between devices: 8.77 us -> 2.96 us  [exchanged(): return lax.all_to_all(blocks, axis, split_axis=0, concat_axis=0, tiled=True)]
    unnamed x8 -> x20, local copies, waits for them, and re-layouts: 4.03 us -> 9.8 us
    ppermute x18, starting transfers between devices: 33.7 us -> 30.2 us  [shifted(): return lax.ppermute(value, axis, [(i, (i + by) % n) for i in range(n)])]
    pallas_call x1, Pallas kernels: 8.89 us -> 6.24 us  [place_rest(): pl.pallas_call(place_rest_kernel, out_shape=jax.ShapeDtypeStruct((layers,...]
  transfers between devices with their start and end apart: 29 -> 29, of which waited for: 13 -> 12; matrix products, arithmetic and copies ran while one was open for 4% -> 4% of each run, Pallas kernels for 7% -> 7%
where the time goes in v5:
time: 231 us; the launch traced here: 229 us
  waiting for transfers between devices  94.5 us (41%)
  starting transfers between devices  56.3 us (24%)
  blocking collectives  30.2 us (13%)
  Pallas kernels  28.7 us (12%)
  local copies, waits for them, and re-layouts  11.1 us (5%)
  matrix products  4.75 us (2%)
  other arithmetic  2.36 us (1%)
    ppermute x18, waiting for transfers between devices, shifted(): return lax.ppermute(value, axis, [(i, (i + by) % n) for i in range(n)])  89 us
    all_to_all x2, blocking collectives, exchanged(): return lax.all_to_all(blocks, axis, split_axis=0, concat_axis=0, tiled=True)  30.2 us
    ppermute x18, starting transfers between devices, shifted(): return lax.ppermute(value, axis, [(i, (i + by) % n) for i in range(n)])  30.2 us
    all_to_all x3, starting transfers between devices, exchanged(): return lax.all_to_all(blocks, axis, split_axis=0, concat_axis=0, tiled=True)  20.1 us
    unnamed x20, local copies, waits for them, and re-layouts  9.8 us
    pallas_call x1, Pallas kernels, partial_product(): pl.pallas_call(partial_kernel, out_shape=[jax.ShapeDtypeStruct(shape, bf1...  7.08 us
    pallas_call x1, Pallas kernels, place_rest(): pl.pallas_call(place_rest_kernel, out_shape=jax.ShapeDtypeStruct((layers,...  6.24 us
    ppermute x8, starting transfers between devices, swapped(): return lax.ppermute(value, 'c', [(0, 1), (1, 0)])  6 us
  transfers between devices with their start and end apart: 29, of which 12 were waited for; matrix products, arithmetic and copies ran while one was open for 4% of the time, Pallas kernels for 7%

profile of v5, /device:TPU:33, one launch (start us, length us, event | category | flops | bytes accessed | tf_op | source)
XLA Modules:
  0.0 228.7 jit_solution(5902006973314419329)
XLA Ops:
  3.7 6.0 %all-to-all-start = ((f32[16,3,128]{2,1,0:T(4,128)}), f32[16,3,128]{2,1,0:T(4,128)S(1)}, u32[]{:S(2)}, u32[]{:S(2)}) async-start(f32[16,3,128]{2,1,0:T(4,128)} %broadcast_in_dim.8), calls=%async_computation | async-start | bytes 65536 | tf_op jit(solution)/shard_map/all_to_all | solution.py:34
  16.3 9.9 %all-to-all-start.1 = ((f32[16,3,128]{2,1,0:T(4,128)}), f32[16,3,128]{2,1,0:T(4,128)S(1)}, u32[]{:S(2)}, u32[]{:S(2)}) async-start(f32[16,3,128]{2,1,0:T(4,128)} %broadcast_in_dim.9), calls=%async_computation.1 | async-start | bytes 65536 | tf_op jit(solution)/shard_map/all_to_all | solution.py:34
  32.0 3.0 %all-to-all-done.1.stats = f32[16,3,128]{2,1,0:T(4,128)S(1)} async-done(((f32[16,3,128]{2,1,0:T(4,128)}), f32[16,3,128]{2,1,0:T(4,128)S(1)}, u32[]{:S(2)}, u32[]{:S(2)}) %all-to-all-start.1) | async-done | bytes 24608 | tf_op jit(solution)/shard_map/all_to_all | solution.py:34
  35.0 1.9 copy-done.5
  39.0 7.1 %partial_product.1 = (bf16[4,64,896]{2,1,0:T(8,128)(2,1)S(1)}, bf16[4,64,896]{2,1,0:T(8,128)(2,1)S(1)}, bf16[4,64,896]{2,1,0:T(8,128)(2,1)S(1)}, bf16[4,64,896]{...) custom-call(s32[4]{0:T(128)S(1)} %pad_add_fusion.pos.refs_0_, ...), custom_call_target="tpu_custom_call" | custom-call | flops 3288334336 | bytes 10092544 | tf_op jit(solution)/shard_map/partial_product/pallas_call | solution.py:144
  46.1 2.8 %collective-permute-start.10 = (bf16[4,64,896]{2,1,0:T(8,128)(2,1)S(1)}, bf16[4,64,896]{2,1,0:T(8,128)(2,1)S(1)}, u32[]{:S(2)}, u32[]{:S(2)}) collective-permute-start(bf16[4,64,896]{2,1,0:T(8,128)(2,1)S(1)} %get-tuple-element.38), channel_id=1, source_target_pairs={{0,64},{32,96},{64,0},{96,32},{1,65},{33,97},{65,1},{97,33},{2,66}... | collective-permute-start | bytes 1376264 | tf_op jit(solution)/shard_map/ppermute | solution.py:26
  50.7 1.8 collective-permute-start.4
  52.5 5.8 %collective-permute-done.10.refs_3_ = bf16[4,64,896]{2,1,0:T(8,128)(2,1)S(1)} collective-permute-done((bf16[4,64,896]{2,1,0:T(8,128)(2,1)S(1)}, bf16[4,64,896]{2,1,0:T(8,128)(2,1)S(1)}, u32[]{:S(2)}, u32[]{:S(2)}) %collective-permute-start.10) | collective-permute-done | bytes 458784 | tf_op jit(solution)/shard_map/ppermute | solution.py:26
  59.2 9.8 %collective-permute-done.11.refs_4_ = bf16[4,64,896]{2,1,0:T(8,128)(2,1)S(1)} collective-permute-done((bf16[4,64,896]{2,1,0:T(8,128)(2,1)S(1)}, bf16[4,64,896]{2,1,0:T(8,128)(2,1)S(1)}, u32[]{:S(2)}, u32[]{:S(2)}) %collective-permute-start.11) | collective-permute-done | bytes 458784 | tf_op jit(solution)/shard_map/ppermute | solution.py:26
  71.3 1.8 collective-permute-start.13
  75.1 1.3 collective-permute-start.6
  76.3 2.4 %collective-permute-start.7 = (bf16[64,896]{1,0:T(8,128)(2,1)S(1)}, bf16[64,896]{1,0:T(8,128)(2,1)S(1)}, u32[]{:S(2)}, u32[]{:S(2)}) collective-permute-start(bf16[64,896]{1,0:T(8,128)(2,1)S(1)} %get-tuple-element.34), channel_id=1, source_target_pairs={{0,64},{32,96},{64,0},{96,32},{1,65},{33,97},{65,1},{97,33},{2,66}... | collective-permute-start | bytes 344072 | tf_op jit(solution)/shard_map/ppermute | solution.py:26
  80.0 2.8 %collective-permute-done.7.refs_2_ = bf16[64,896]{1,0:T(8,128)(2,1)S(1)} collective-permute-done((bf16[64,896]{1,0:T(8,128)(2,1)S(1)}, bf16[64,896]{1,0:T(8,128)(2,1)S(1)}, u32[]{:S(2)}, u32[]{:S(2)}) %collective-permute-start.7) | collective-permute-done | bytes 114720 | tf_op jit(solution)/shard_map/ppermute | solution.py:26
  83.6 12.8 %all_to_all.25.src = bf16[8,112,128]{2,1,0:T(8,128)(2,1)S(1)} all-to-all(bf16[8,112,128]{2,1,0:T(8,128)(2,1)S(1)} %bitcast.42), channel_id=1, replica_groups=mesh['zl'=2,'y'=4,'c'=2,'x'=4,'zh'=4] {'zh','zl'}, dimensions={0} | all-to-all | bytes 458752 | tf_op jit(solution)/shard_map/all_to_all | solution.py:34
  96.5 17.4 %all_to_all.26 = bf16[16,112,128]{2,1,0:T(8,128)(2,1)S(1)} all-to-all(bf16[16,112,128]{2,1,0:T(8,128)(2,1)S(1)} %sum_spread.1), channel_id=1, replica_groups=mesh['zl'=2,'y'=4,'c'=2,'x'=4,'zh'=4] {'zl','y','c'}, dimensions={0} | all-to-all | bytes 917504 | tf_op jit(solution)/shard_map/all_to_all | solution.py:34
  115.5 4.3 %all-to-all-start.4 = ((bf16[16,120,256]{2,1,0:T(8,128)(2,1)}), bf16[16,120,256]{2,1,0:T(8,128)(2,1)}, u32[]{:S(2)}, u32[]{:S(2)}) async-start(bf16[16,120,256]{2,1,0:T(8,128)(2,1)} %bitcast.41), calls=%async_computation.4 | async-start | bytes 1966080 | tf_op jit(solution)/shard_map/all_to_all | solution.py:34
  119.9 1.6 rest_blocks.1
  121.5 2.2 collective-permute-start.16
  123.7 3.3 %collective-permute-start.17 = (bf16[2,3,112,256]{3,2,1,0:T(8,128)(2,1)S(1)}, bf16[2,3,112,256]{3,2,1,0:T(8,128)(2,1)S(1)}, u32[]{:S(2)}, u32[]{:S(2)}) collective-permute-start(bf16[2,3,112,256]{3,2,1,0:T(8,128)(2,1)S(1)} %get-tuple-element.46), channel_id=1, source_target_pairs={{0,2},{1,3},{2,0},{3,1},{4,6},{5,7},{6,4},{7,5},{8,10},{9,11},{10,... | collective-permute-start | bytes 1032200 | tf_op jit(solution)/shard_map/ppermute | solution.py:26
  127.0 3.3 %collective-permute-start.18 = (bf16[2,3,112,256]{3,2,1,0:T(8,128)(2,1)S(1)}, bf16[2,3,112,256]{3,2,1,0:T(8,128)(2,1)S(1)}, u32[]{:S(2)}, u32[]{:S(2)}) collective-permute-start(bf16[2,3,112,256]{3,2,1,0:T(8,128)(2,1)S(1)} %get-tuple-element.47), channel_id=1, source_target_pairs={{0,3},{1,0},{2,1},{3,2},{4,7},{5,4},{6,5},{7,6},{8,11},{9,8},{10,9... | collective-permute-start | bytes 1032200 | tf_op jit(solution)/shard_map/ppermute | solution.py:26
  130.3 44.4 %collective-permute-done.16.refs_1_ = bf16[2,3,112,256]{3,2,1,0:T(8,128)(2,1)S(1)} collective-permute-done((bf16[2,3,112,256]{3,2,1,0:T(8,128)(2,1)S(1)}, bf16[2,3,112,256]{3,2,1,0:T(8,128)(2,1)S(1)}, u32[]{:S(2)}, u32[]{:S(2)}) %collective-permute-start.16) | collective-permute-done | bytes 344096 | tf_op jit(solution)/shard_map/ppermute | solution.py:26
  174.7 3.5 %regroup.1 = (bf16[4,3,112,256]{3,2,1,0:T(8,128)(2,1)}, bf16[4,3,112,256]{3,2,1,0:T(8,128)(2,1)}) custom-call(s32[4]{0:T(128)S(1)} %pad_add_fusion.pos.refs_0_, bf16[2,3,112,256]{3,2,1,0:T(8,128)(2,1)S(1)} %get-tuple-element.44.refs_0_, bf16[2,3,112,256]{3,2,1,0:T(8,128)(2,1)S(1)} %collective-permute-done.16.refs_1_, ...), custom_call_target="tpu_custom_call" | custom-call | flops 172032 | bytes 2752512 | tf_op jit(solution)/shard_map/regroup/pallas_call | solution.py:337
  178.2 3.1 %collective-permute-start.20 = (bf16[4,3,112,256]{3,2,1,0:T(8,128)(2,1)}, bf16[4,3,112,256]{3,2,1,0:T(8,128)(2,1)}, u32[]{:S(2)}, u32[]{:S(2)}) collective-permute-start(bf16[4,3,112,256]{3,2,1,0:T(8,128)(2,1)} %get-tuple-element.48.refs_0_.refs_4_), channel_id=1, source_target_pairs={{0,8},{4,12},{8,0},{12,4},{1,9},{5,13},{9,1},{13,5},{2,10},{6,14},... | collective-permute-start | bytes 2064392 | tf_op jit(solution)/shard_map/ppermute | solution.py:26
  181.7 2.3 collective-permute-start.21
  183.9 1.4 collective-permute-start.15
  185.3 11.3 %collective-permute-done.20.refs_2_.refs_6_ = bf16[4,3,112,256]{3,2,1,0:T(8,128)(2,1)} collective-permute-done((bf16[4,3,112,256]{3,2,1,0:T(8,128)(2,1)}, bf16[4,3,112,256]{3,2,1,0:T(8,128)(2,1)}, u32[]{:S(2)}, u32[]{:S(2)}) %collective-permute-start.20) | collective-permute-done | bytes 688160 | tf_op jit(solution)/shard_map/ppermute | solution.py:26
  196.6 2.3 %collective-permute-start.24 = (bf16[4,3,112,256]{3,2,1,0:T(8,128)(2,1)}, bf16[4,3,112,256]{3,2,1,0:T(8,128)(2,1)S(1)}, u32[]{:S(2)}, u32[]{:S(2)}) collective-permute-start(bf16[4,3,112,256]{3,2,1,0:T(8,128)(2,1)} %collective-permute-done.20.refs_2_.refs_6_), channel_id=1, source_target_pairs={{0,16},{16,0},{1,17},{17,1},{2,18},{18,2},{3,19},{19,3},{4,20},{20... | collective-permute-start | bytes 2064392 | tf_op jit(solution)/shard_map/ppermute | solution.py:21
  199.0 13.2 %collective-permute-done.19.refs_1_.refs_5_ = bf16[4,3,112,256]{3,2,1,0:T(8,128)(2,1)} collective-permute-done((bf16[4,3,112,256]{3,2,1,0:T(8,128)(2,1)}, bf16[4,3,112,256]{3,2,1,0:T(8,128)(2,1)}, u32[]{:S(2)}, u32[]{:S(2)}) %collective-permute-start.19) | collective-permute-done | bytes 688160 | tf_op jit(solution)/shard_map/ppermute | solution.py:26
  213.2 1.5 collective-permute-done.23.refs_5_.refs_9_
  215.7 6.2 %place_rest.1.refs_12_ = bf16[3,4,4,2,112,256]{5,4,3,2,1,0:T(8,128)(2,1)} custom-call(s32[4]{0:T(128)S(1)} %pad_add_fusion.pos.refs_0_, bf16[4,3,112,256]{3,2,1,0:T(8,128)(2,1)} %get-tuple-element.48.refs_0_.refs_4_, bf16[4,3,112,256]{3,2,1,0:T(8,128)(2,1)} %collective-permute-done.19.refs_1_.refs_5_, ...), custom_call_target="tpu_custom_call" | custom-call | flops 344064 | bytes 11010048 | tf_op jit(solution)/shard_map/place_rest/pallas_call | solution.py:368
  221.9 1.9 update.1
  223.8 4.9 %finish.1 = bf16[3,4,4,2,112,256]{5,4,3,2,1,0:T(8,128)(2,1)} custom-call(s32[4]{0:T(128)S(1)} %pad_add_fusion.pos.refs_0_, bf16[16,120,256]{2,1,0:T(8,128)(2,1)} %all-to-all-done.4.refs_0_.refs_1_.refs_2_, bf16[16,120,256]{2,1,0:T(8,128)(2,1)} %all-to-all-done.4.refs_0_.refs_1_.refs_2_, ...), custom_call_target="tpu_custom_call", output_to_operand_aliasing={{}: (12, {})} | custom-call | flops 3932160 | bytes 11796480 | tf_op jit(solution)/shard_map/finish/pallas_call | solution.py:407
  (77 shorter events, 30.6 us)
Async XLA Ops:
  0.6 34.4 %collective-permute-start.2 = (bf16[448,3584]{1,0:T(8,128)(2,1)}, bf16[448,3584]{1,0:T(8,128)(2,1)}, u32[]{:S(2)}, u32[]{:S(2)}) collective-permute-start(bf16[448,3584]{1,0:T(8,128)(2,1)} %hid_a.1), channel_id=1, source_target_pairs={{0,16},{16,0},{1,17},{17,1},{2,18},{18,2},{3,19},{19,3},{4,20},{20... | collective-permute-start | bytes 9633800 | tf_op jit(solution)/shard_map/ppermute | solution.py:21
  1.4 24.8 %collective-permute-start.1 = (bf16[448,1024]{1,0:T(8,128)(2,1)}, bf16[448,1024]{1,0:T(8,128)(2,1)S(1)}, u32[]{:S(2)}, u32[]{:S(2)}) collective-permute-start(bf16[448,1024]{1,0:T(8,128)(2,1)} %cot_a.1), channel_id=1, source_target_pairs={{0,16},{16,0},{1,17},{17,1},{2,18},{18,2},{3,19},{19,3},{4,20},{20... | collective-permute-start | bytes 2752520 | tf_op jit(solution)/shard_map/ppermute | solution.py:21
  3.7 11.9 %all-to-all-start = ((f32[16,3,128]{2,1,0:T(4,128)}), f32[16,3,128]{2,1,0:T(4,128)S(1)}, u32[]{:S(2)}, u32[]{:S(2)}) async-start(f32[16,3,128]{2,1,0:T(4,128)} %broadcast_in_dim.8), calls=%async_computation | async-start | bytes 65536 | tf_op jit(solution)/shard_map/all_to_all | solution.py:34
  15.2 16.9 %collective-permute-start = (f32[8,448]{1,0:T(8,128)S(1)}, f32[8,448]{1,0:T(8,128)S(1)}, u32[]{:S(2)}, u32[]{:S(2)}) collective-permute-start(f32[8,448]{1,0:T(8,128)S(1)} %stack.46.tok_a), channel_id=1, source_target_pairs={{0,16},{16,0},{1,17},{17,1},{2,18},{18,2},{3,19},{19,3},{4,20},{20... | collective-permute-start | bytes 43016 | tf_op jit(solution)/shard_map/ppermute | solution.py:21
  16.3 18.7 %all-to-all-start.1 = ((f32[16,3,128]{2,1,0:T(4,128)}), f32[16,3,128]{2,1,0:T(4,128)S(1)}, u32[]{:S(2)}, u32[]{:S(2)}) async-start(f32[16,3,128]{2,1,0:T(4,128)} %broadcast_in_dim.9), calls=%async_computation.1 | async-start | bytes 65536 | tf_op jit(solution)/shard_map/all_to_all | solution.py:34
  27.2 1.2 copy-start.2
  35.0 1.9 copy-start.5
  46.1 12.2 %collective-permute-start.10 = (bf16[4,64,896]{2,1,0:T(8,128)(2,1)S(1)}, bf16[4,64,896]{2,1,0:T(8,128)(2,1)S(1)}, u32[]{:S(2)}, u32[]{:S(2)}) collective-permute-start(bf16[4,64,896]{2,1,0:T(8,128)(2,1)S(1)} %get-tuple-element.38), channel_id=1, source_target_pairs={{0,64},{32,96},{64,0},{96,32},{1,65},{33,97},{65,1},{97,33},{2,66}... | collective-permute-start | bytes 1376264 | tf_op jit(solution)/shard_map/ppermute | solution.py:26
  48.9 20.1 %collective-permute-start.11 = (bf16[4,64,896]{2,1,0:T(8,128)(2,1)S(1)}, bf16[4,64,896]{2,1,0:T(8,128)(2,1)S(1)}, u32[]{:S(2)}, u32[]{:S(2)}) collective-permute-start(bf16[4,64,896]{2,1,0:T(8,128)(2,1)S(1)} %get-tuple-element.39), channel_id=1, source_target_pairs={{0,96},{32,0},{64,32},{96,64},{1,97},{33,1},{65,33},{97,65},{2,98}... | collective-permute-start | bytes 1376264 | tf_op jit(solution)/shard_map/ppermute | solution.py:26
  49.8 20.2 %collective-permute-start.9 = (bf16[4,64,896]{2,1,0:T(8,128)(2,1)S(1)}, bf16[4,64,896]{2,1,0:T(8,128)(2,1)S(1)}, u32[]{:S(2)}, u32[]{:S(2)}) collective-permute-start(bf16[4,64,896]{2,1,0:T(8,128)(2,1)S(1)} %get-tuple-element.37), channel_id=1, source_target_pairs={{0,32},{32,64},{64,96},{96,0},{1,33},{33,65},{65,97},{97,1},{2,34}... | collective-permute-start | bytes 1376264 | tf_op jit(solution)/shard_map/ppermute | solution.py:26
  50.4 22.7 %collective-permute-start.3 = (bf16[4,64,896]{2,1,0:T(8,128)(2,1)S(1)}, bf16[4,64,896]{2,1,0:T(8,128)(2,1)S(1)}, u32[]{:S(2)}, u32[]{:S(2)}) collective-permute-start(bf16[4,64,896]{2,1,0:T(8,128)(2,1)S(1)} %get-tuple-element.29), channel_id=1, source_target_pairs={{0,4},{4,8},{8,12},{12,0},{1,5},{5,9},{9,13},{13,1},{2,6},{6,10},{... | collective-permute-start | bytes 1376264 | tf_op jit(solution)/shard_map/ppermute | solution.py:26
  50.7 23.6 %collective-permute-start.4 = (bf16[4,64,896]{2,1,0:T(8,128)(2,1)S(1)}, bf16[4,64,896]{2,1,0:T(8,128)(2,1)S(1)}, u32[]{:S(2)}, u32[]{:S(2)}) collective-permute-start(bf16[4,64,896]{2,1,0:T(8,128)(2,1)S(1)} %get-tuple-element.30), channel_id=1, source_target_pairs={{0,8},{4,12},{8,0},{12,4},{1,9},{5,13},{9,1},{13,5},{2,10},{6,14},... | collective-permute-start | bytes 1376264 | tf_op jit(solution)/shard_map/ppermute | solution.py:26
  58.2 16.1 %collective-permute-start.5 = (bf16[4,64,896]{2,1,0:T(8,128)(2,1)S(1)}, bf16[4,64,896]{2,1,0:T(8,128)(2,1)S(1)}, u32[]{:S(2)}, u32[]{:S(2)}) collective-permute-start(bf16[4,64,896]{2,1,0:T(8,128)(2,1)S(1)} %get-tuple-element.31), channel_id=1, source_target_pairs={{0,12},{4,0},{8,4},{12,8},{1,13},{5,1},{9,5},{13,9},{2,14},{6,2},{... | collective-permute-start | bytes 1376264 | tf_op jit(solution)/shard_map/ppermute | solution.py:26
  70.7 8.0 %collective-permute-start.12 = (bf16[64,896]{1,0:T(8,128)(2,1)S(1)}, bf16[64,896]{1,0:T(8,128)(2,1)S(1)}, u32[]{:S(2)}, u32[]{:S(2)}) collective-permute-start(bf16[64,896]{1,0:T(8,128)(2,1)S(1)} %get-tuple-element.41), channel_id=1, source_target_pairs={{0,4},{4,8},{8,12},{12,0},{1,5},{5,9},{9,13},{13,1},{2,6},{6,10},{... | collective-permute-start | bytes 344072 | tf_op jit(solution)/shard_map/ppermute | solution.py:26
  71.3 8.6 %collective-permute-start.13 = (bf16[64,896]{1,0:T(8,128)(2,1)S(1)}, bf16[64,896]{1,0:T(8,128)(2,1)S(1)}, u32[]{:S(2)}, u32[]{:S(2)}) collective-permute-start(bf16[64,896]{1,0:T(8,128)(2,1)S(1)} %get-tuple-element.42), channel_id=1, source_target_pairs={{0,8},{4,12},{8,0},{12,4},{1,9},{5,13},{9,1},{13,5},{2,10},{6,14},... | collective-permute-start | bytes 344072 | tf_op jit(solution)/shard_map/ppermute | solution.py:26
  73.1 6.9 %collective-permute-start.14 = (bf16[64,896]{1,0:T(8,128)(2,1)S(1)}, bf16[64,896]{1,0:T(8,128)(2,1)S(1)}, u32[]{:S(2)}, u32[]{:S(2)}) collective-permute-start(bf16[64,896]{1,0:T(8,128)(2,1)S(1)} %get-tuple-element.43), channel_id=1, source_target_pairs={{0,12},{4,0},{8,4},{12,8},{1,13},{5,1},{9,5},{13,9},{2,14},{6,2},{... | collective-permute-start | bytes 344072 | tf_op jit(solution)/shard_map/ppermute | solution.py:26
  75.1 4.9 %collective-permute-start.6 = (bf16[64,896]{1,0:T(8,128)(2,1)S(1)}, bf16[64,896]{1,0:T(8,128)(2,1)S(1)}, u32[]{:S(2)}, u32[]{:S(2)}) collective-permute-start(bf16[64,896]{1,0:T(8,128)(2,1)S(1)} %get-tuple-element.33), channel_id=1, source_target_pairs={{0,32},{32,64},{64,96},{96,0},{1,33},{33,65},{65,97},{97,1},{2,34}... | collective-permute-start | bytes 344072 | tf_op jit(solution)/shard_map/ppermute | solution.py:26
  76.3 6.5 %collective-permute-start.7 = (bf16[64,896]{1,0:T(8,128)(2,1)S(1)}, bf16[64,896]{1,0:T(8,128)(2,1)S(1)}, u32[]{:S(2)}, u32[]{:S(2)}) collective-permute-start(bf16[64,896]{1,0:T(8,128)(2,1)S(1)} %get-tuple-element.34), channel_id=1, source_target_pairs={{0,64},{32,96},{64,0},{96,32},{1,65},{33,97},{65,1},{97,33},{2,66}... | collective-permute-start | bytes 344072 | tf_op jit(solution)/shard_map/ppermute | solution.py:26
  78.8 4.6 %collective-permute-start.8 = (bf16[64,896]{1,0:T(8,128)(2,1)S(1)}, bf16[64,896]{1,0:T(8,128)(2,1)S(1)}, u32[]{:S(2)}, u32[]{:S(2)}) collective-permute-start(bf16[64,896]{1,0:T(8,128)(2,1)S(1)} %get-tuple-element.35), channel_id=1, source_target_pairs={{0,96},{32,0},{64,32},{96,64},{1,97},{33,1},{65,33},{97,65},{2,98}... | collective-permute-start | bytes 344072 | tf_op jit(solution)/shard_map/ppermute | solution.py:26
  83.4 36.5 %copy-start = (f32[3,224,1024]{2,1,0:T(8,128)S(1)}, f32[3,224,1024]{2,1,0:T(8,128)}, u32[]{:S(2)}) copy-start(f32[3,224,1024]{2,1,0:T(8,128)} %refs_7_.1) | copy-start | bytes 8257540
  115.5 68.4 %all-to-all-start.4 = ((bf16[16,120,256]{2,1,0:T(8,128)(2,1)}), bf16[16,120,256]{2,1,0:T(8,128)(2,1)}, u32[]{:S(2)}, u32[]{:S(2)}) async-start(bf16[16,120,256]{2,1,0:T(8,128)(2,1)} %bitcast.41), calls=%async_computation.4 | async-start | bytes 1966080 | tf_op jit(solution)/shard_map/all_to_all | solution.py:34
  121.5 53.2 %collective-permute-start.16 = (bf16[2,3,112,256]{3,2,1,0:T(8,128)(2,1)S(1)}, bf16[2,3,112,256]{3,2,1,0:T(8,128)(2,1)S(1)}, u32[]{:S(2)}, u32[]{:S(2)}) collective-permute-start(bf16[2,3,112,256]{3,2,1,0:T(8,128)(2,1)S(1)} %get-tuple-element.45), channel_id=1, source_target_pairs={{0,1},{1,2},{2,3},{3,0},{4,5},{5,6},{6,7},{7,4},{8,9},{9,10},{10,1... | collective-permute-start | bytes 1032200 | tf_op jit(solution)/shard_map/ppermute | solution.py:26
  123.7 51.0 %collective-permute-start.17 = (bf16[2,3,112,256]{3,2,1,0:T(8,128)(2,1)S(1)}, bf16[2,3,112,256]{3,2,1,0:T(8,128)(2,1)S(1)}, u32[]{:S(2)}, u32[]{:S(2)}) collective-permute-start(bf16[2,3,112,256]{3,2,1,0:T(8,128)(2,1)S(1)} %get-tuple-element.46), channel_id=1, source_target_pairs={{0,2},{1,3},{2,0},{3,1},{4,6},{5,7},{6,4},{7,5},{8,10},{9,11},{10,... | collective-permute-start | bytes 1032200 | tf_op jit(solution)/shard_map/ppermute | solution.py:26
  127.0 47.7 %collective-permute-start.18 = (bf16[2,3,112,256]{3,2,1,0:T(8,128)(2,1)S(1)}, bf16[2,3,112,256]{3,2,1,0:T(8,128)(2,1)S(1)}, u32[]{:S(2)}, u32[]{:S(2)}) collective-permute-start(bf16[2,3,112,256]{3,2,1,0:T(8,128)(2,1)S(1)} %get-tuple-element.47), channel_id=1, source_target_pairs={{0,3},{1,0},{2,1},{3,2},{4,7},{5,4},{6,5},{7,6},{8,11},{9,8},{10,9... | collective-permute-start | bytes 1032200 | tf_op jit(solution)/shard_map/ppermute | solution.py:26
  178.2 18.5 %collective-permute-start.20 = (bf16[4,3,112,256]{3,2,1,0:T(8,128)(2,1)}, bf16[4,3,112,256]{3,2,1,0:T(8,128)(2,1)}, u32[]{:S(2)}, u32[]{:S(2)}) collective-permute-start(bf16[4,3,112,256]{3,2,1,0:T(8,128)(2,1)} %get-tuple-element.48.refs_0_.refs_4_), channel_id=1, source_target_pairs={{0,8},{4,12},{8,0},{12,4},{1,9},{5,13},{9,1},{13,5},{2,10},{6,14},... | collective-permute-start | bytes 2064392 | tf_op jit(solution)/shard_map/ppermute | solution.py:26
  181.2 31.0 %collective-permute-start.19 = (bf16[4,3,112,256]{3,2,1,0:T(8,128)(2,1)}, bf16[4,3,112,256]{3,2,1,0:T(8,128)(2,1)}, u32[]{:S(2)}, u32[]{:S(2)}) collective-permute-start(bf16[4,3,112,256]{3,2,1,0:T(8,128)(2,1)} %get-tuple-element.49), channel_id=1, source_target_pairs={{0,4},{4,8},{8,12},{12,0},{1,5},{5,9},{9,13},{13,1},{2,6},{6,10},{... | collective-permute-start | bytes 2064392 | tf_op jit(solution)/shard_map/ppermute | solution.py:26
  181.7 31.0 %collective-permute-start.21 = (bf16[4,3,112,256]{3,2,1,0:T(8,128)(2,1)}, bf16[4,3,112,256]{3,2,1,0:T(8,128)(2,1)}, u32[]{:S(2)}, u32[]{:S(2)}) collective-permute-start(bf16[4,3,112,256]{3,2,1,0:T(8,128)(2,1)} %get-tuple-element.49), channel_id=1, source_target_pairs={{0,12},{4,0},{8,4},{12,8},{1,13},{5,1},{9,5},{13,9},{2,14},{6,2},{... | collective-permute-start | bytes 2064392 | tf_op jit(solution)/shard_map/ppermute | solution.py:26
  183.9 39.9 %collective-permute-start.15 = (bf16[16,120,256]{2,1,0:T(8,128)(2,1)}, bf16[16,120,256]{2,1,0:T(8,128)(2,1)S(1)}, u32[]{:S(2)}, u32[]{:S(2)}) collective-permute-start(bf16[16,120,256]{2,1,0:T(8,128)(2,1)} %all-to-all-done.4.refs_0_.refs_1_.refs_2_), channel_id=1, source_target_pairs={{0,16},{16,0},{1,17},{17,1},{2,18},{18,2},{3,19},{19,3},{4,20},{20... | collective-permute-start | bytes 2949128 | tf_op jit(solution)/shard_map/ppermute | solution.py:21
  185.3 27.9 %collective-permute-start.22 = (bf16[4,3,112,256]{3,2,1,0:T(8,128)(2,1)}, bf16[4,3,112,256]{3,2,1,0:T(8,128)(2,1)S(1)}, u32[]{:S(2)}, u32[]{:S(2)}) collective-permute-start(bf16[4,3,112,256]{3,2,1,0:T(8,128)(2,1)} %get-tuple-element.48.refs_0_.refs_4_), channel_id=1, source_target_pairs={{0,16},{16,0},{1,17},{17,1},{2,18},{18,2},{3,19},{19,3},{4,20},{20... | collective-permute-start | bytes 2064392 | tf_op jit(solution)/shard_map/ppermute | solution.py:21
  196.6 16.5 %collective-permute-start.24 = (bf16[4,3,112,256]{3,2,1,0:T(8,128)(2,1)}, bf16[4,3,112,256]{3,2,1,0:T(8,128)(2,1)S(1)}, u32[]{:S(2)}, u32[]{:S(2)}) collective-permute-start(bf16[4,3,112,256]{3,2,1,0:T(8,128)(2,1)} %collective-permute-done.20.refs_2_.refs_6_), channel_id=1, source_target_pairs={{0,16},{16,0},{1,17},{17,1},{2,18},{18,2},{3,19},{19,3},{4,20},{20... | collective-permute-start | bytes 2064392 | tf_op jit(solution)/shard_map/ppermute | solution.py:21
  212.2 2.5 %collective-permute-start.23 = (bf16[4,3,112,256]{3,2,1,0:T(8,128)(2,1)}, bf16[4,3,112,256]{3,2,1,0:T(8,128)(2,1)S(1)}, u32[]{:S(2)}, u32[]{:S(2)}) collective-permute-start(bf16[4,3,112,256]{3,2,1,0:T(8,128)(2,1)} %collective-permute-done.19.refs_1_.refs_5_), channel_id=1, source_target_pairs={{0,16},{16,0},{1,17},{17,1},{2,18},{18,2},{3,19},{19,3},{4,20},{20... | collective-permute-start | bytes 2064392 | tf_op jit(solution)/shard_map/ppermute | solution.py:21
  212.7 3.0 %collective-permute-start.25 = (bf16[4,3,112,256]{3,2,1,0:T(8,128)(2,1)}, bf16[4,3,112,256]{3,2,1,0:T(8,128)(2,1)S(1)}, u32[]{:S(2)}, u32[]{:S(2)}) collective-permute-start(bf16[4,3,112,256]{3,2,1,0:T(8,128)(2,1)} %collective-permute-done.21.refs_3_.refs_7_), channel_id=1, source_target_pairs={{0,16},{16,0},{1,17},{17,1},{2,18},{18,2},{3,19},{19,3},{4,20},{20... | collective-permute-start | bytes 2064392 | tf_op jit(solution)/shard_map/ppermute | solution.py:21
  (7 other events, 6.7 us)

commit v6 on v5

--- a/solution.py
+++ b/solution.py
@@ -39,8 +39,8 @@
     return exchanged(copies, axis)
 
 
-def params(**kw):
-    return pltpu.CompilerParams(vmem_limit_bytes=VMEM_LIMIT, **kw)
+def params(limit=VMEM_LIMIT):
+    return pltpu.CompilerParams(vmem_limit_bytes=limit)
 
 
 def cost(flops, nbytes):
@@ -151,7 +151,7 @@
             out_specs=[whole(shape)] * 8,
             scratch_shapes=[pltpu.VMEM((4, 2, toks, blk), bf16), pltpu.SemaphoreType.DMA((4, 2))],
         ),
-        compiler_params=params(),
+        compiler_params=params(50 * 1024 * 1024),
         cost_estimate=cost(4 * toks * width * half, 4 * toks * width + 2 * width * half),
         name="partial_product",
     )(pos, stats, tok_a, tok_b, cot_a, cot_b, hid_a, hid_b)
@@ -443,8 +443,8 @@
     pos = jnp.stack([lax.axis_index(a).astype(jnp.int32) for a in ("c", "x", "zh", "y")])
 
     local_sums = group_sums(group_ids[0], rewards[0], groups)
-    stats = sent_to_all(local_sums, REP).sum(axis=0)
-    stats = sent_to_all(stats, SHARD)
+    stats = sent_to_all(local_sums, ("x", "y")).sum(axis=0)
+    stats = sent_to_all(stats, ("zh", "zl", "c"))
 
     hidden_b = swapped(hidden)
     cotangent_b = swapped(cotangent)

time: 231 us -> 228 us (0.987)
  local copies, waits for them, and re-layouts: 11.1 us -> 7.08 us
    unnamed x20 -> x14, local copies, waits for them, and re-layouts: 9.8 us -> 5.8 us
    all_to_all x3, waiting for transfers between devices: 2.96 us -> 0.62 us  [exchanged(): return lax.all_to_all(blocks, axis, split_axis=0, concat_axis=0, tiled=True)]
  transfers between devices with their start and end apart: 29 -> 29, of which waited for: 12 -> 13; matrix products, arithmetic and copies ran while one was open for 4% -> 4% of each run, Pallas kernels for 7% -> 7%
where the time goes in v6:
time: 228 us; the launch traced here: 226 us
  waiting for transfers between devices  92.2 us (40%)
  starting transfers between devices  57.3 us (25%)
  blocking collectives  31.2 us (14%)
  Pallas kernels  30.4 us (13%)
  local copies, waits for them, and re-layouts  7.08 us (3%)
  matrix products  4.75 us (2%)
  other arithmetic  2.35 us (1%)
    ppermute x18, waiting for transfers between devices, shifted(): return lax.ppermute(value, axis, [(i, (i + by) % n) for i in range(n)])  89.1 us
    all_to_all x2, blocking collectives, exchanged(): return lax.all_to_all(blocks, axis, split_axis=0, concat_axis=0, tiled=True)  31.2 us
    ppermute x18, starting transfers between devices, shifted(): return lax.ppermute(value, axis, [(i, (i + by) % n) for i in range(n)])  30 us
    all_to_all x3, starting transfers between devices, exchanged(): return lax.all_to_all(blocks, axis, split_axis=0, concat_axis=0, tiled=True)  21.1 us
    pallas_call x1, Pallas kernels, partial_product(): pl.pallas_call(partial_kernel, out_shape=[jax.ShapeDtypeStruct(shape, bf1...  8.77 us
    ppermute x8, starting transfers between devices, swapped(): return lax.ppermute(value, 'c', [(0, 1), (1, 0)])  6.29 us
    pallas_call x1, Pallas kernels, place_rest(): pl.pallas_call(place_rest_kernel, out_shape=jax.ShapeDtypeStruct((layers,...  6.24 us
    unnamed x14, local copies, waits for them, and re-layouts  5.8 us
  transfers between devices with their start and end apart: 29, of which 13 were waited for; matrix products, arithmetic and copies ran while one was open for 4% of the time, Pallas kernels for 7%

profile of v6, /device:TPU:33, one launch (start us, length us, event | category | flops | bytes accessed | tf_op | source)
XLA Modules:
  0.0 226.1 jit_solution(3103436893336645778)
XLA Ops:
  3.7 6.8 %all-to-all-start = ((f32[16,3,128]{2,1,0:T(4,128)}), f32[16,3,128]{2,1,0:T(4,128)S(1)}, u32[]{:S(2)}, u32[]{:S(2)}) async-start(f32[16,3,128]{2,1,0:T(4,128)} %broadcast_in_dim.8), calls=%async_computation | async-start | bytes 65536 | tf_op jit(solution)/shard_map/all_to_all | solution.py:34
  17.6 10.0 %all-to-all-start.1 = ((f32[16,3,128]{2,1,0:T(4,128)}), f32[16,3,128]{2,1,0:T(4,128)S(1)}, u32[]{:S(2)}, u32[]{:S(2)}) async-start(f32[16,3,128]{2,1,0:T(4,128)} %broadcast_in_dim.9), calls=%async_computation.1 | async-start | bytes 65536 | tf_op jit(solution)/shard_map/all_to_all | solution.py:34
  33.9 8.8 %partial_product.1 = (bf16[4,64,896]{2,1,0:T(8,128)(2,1)S(1)}, bf16[4,64,896]{2,1,0:T(8,128)(2,1)S(1)}, bf16[4,64,896]{2,1,0:T(8,128)(2,1)S(1)}, bf16[4,64,896]{...) custom-call(s32[4]{0:T(128)S(1)} %pad_add_fusion.pos.refs_0_, ...), custom_call_target="tpu_custom_call" | custom-call | flops 3288334336 | bytes 10092544 | tf_op jit(solution)/shard_map/partial_product/pallas_call | solution.py:144
  42.7 1.3 collective-permute-start.10
  44.0 1.5 collective-permute-start.11
  46.6 2.4 %collective-permute-start.4 = (bf16[4,64,896]{2,1,0:T(8,128)(2,1)S(1)}, bf16[4,64,896]{2,1,0:T(8,128)(2,1)S(1)}, u32[]{:S(2)}, u32[]{:S(2)}) collective-permute-start(bf16[4,64,896]{2,1,0:T(8,128)(2,1)S(1)} %get-tuple-element.30), channel_id=1, source_target_pairs={{0,8},{4,12},{8,0},{12,4},{1,9},{5,13},{9,1},{13,5},{2,10},{6,14},... | collective-permute-start | bytes 1376264 | tf_op jit(solution)/shard_map/ppermute | solution.py:26
  49.0 7.0 %collective-permute-done.10.refs_3_ = bf16[4,64,896]{2,1,0:T(8,128)(2,1)S(1)} collective-permute-done((bf16[4,64,896]{2,1,0:T(8,128)(2,1)S(1)}, bf16[4,64,896]{2,1,0:T(8,128)(2,1)S(1)}, u32[]{:S(2)}, u32[]{:S(2)}) %collective-permute-start.10) | collective-permute-done | bytes 458784 | tf_op jit(solution)/shard_map/ppermute | solution.py:26
  56.9 7.5 %collective-permute-done.11.refs_4_ = bf16[4,64,896]{2,1,0:T(8,128)(2,1)S(1)} collective-permute-done((bf16[4,64,896]{2,1,0:T(8,128)(2,1)S(1)}, bf16[4,64,896]{2,1,0:T(8,128)(2,1)S(1)}, u32[]{:S(2)}, u32[]{:S(2)}) %collective-permute-start.11) | collective-permute-done | bytes 458784 | tf_op jit(solution)/shard_map/ppermute | solution.py:26
  64.4 2.2 collective-permute-done.9.refs_2_
  67.7 1.8 collective-permute-start.13
  71.5 1.3 collective-permute-start.6
  72.8 2.4 %collective-permute-start.7 = (bf16[64,896]{1,0:T(8,128)(2,1)S(1)}, bf16[64,896]{1,0:T(8,128)(2,1)S(1)}, u32[]{:S(2)}, u32[]{:S(2)}) collective-permute-start(bf16[64,896]{1,0:T(8,128)(2,1)S(1)} %get-tuple-element.34), channel_id=1, source_target_pairs={{0,64},{32,96},{64,0},{96,32},{1,65},{33,97},{65,1},{97,33},{2,66}... | collective-permute-start | bytes 344072 | tf_op jit(solution)/shard_map/ppermute | solution.py:26
  76.4 2.8 %collective-permute-done.7.refs_2_ = bf16[64,896]{1,0:T(8,128)(2,1)S(1)} collective-permute-done((bf16[64,896]{1,0:T(8,128)(2,1)S(1)}, bf16[64,896]{1,0:T(8,128)(2,1)S(1)}, u32[]{:S(2)}, u32[]{:S(2)}) %collective-permute-start.7) | collective-permute-done | bytes 114720 | tf_op jit(solution)/shard_map/ppermute | solution.py:26
  80.0 13.8 %all_to_all.25.src = bf16[8,112,128]{2,1,0:T(8,128)(2,1)S(1)} all-to-all(bf16[8,112,128]{2,1,0:T(8,128)(2,1)S(1)} %bitcast.42), channel_id=1, replica_groups=mesh['zl'=2,'y'=4,'c'=2,'x'=4,'zh'=4] {'zh','zl'}, dimensions={0} | all-to-all | bytes 458752 | tf_op jit(solution)/shard_map/all_to_all | solution.py:34
  93.8 17.4 %all_to_all.26 = bf16[16,112,128]{2,1,0:T(8,128)(2,1)S(1)} all-to-all(bf16[16,112,128]{2,1,0:T(8,128)(2,1)S(1)} %sum_spread.1), channel_id=1, replica_groups=mesh['zl'=2,'y'=4,'c'=2,'x'=4,'zh'=4] {'zl','y','c'}, dimensions={0} | all-to-all | bytes 917504 | tf_op jit(solution)/shard_map/all_to_all | solution.py:34
  112.9 4.3 %all-to-all-start.4 = ((bf16[16,120,256]{2,1,0:T(8,128)(2,1)}), bf16[16,120,256]{2,1,0:T(8,128)(2,1)}, u32[]{:S(2)}, u32[]{:S(2)}) async-start(bf16[16,120,256]{2,1,0:T(8,128)(2,1)} %bitcast.41), calls=%async_computation.4 | async-start | bytes 1966080 | tf_op jit(solution)/shard_map/all_to_all | solution.py:34
  117.2 1.6 rest_blocks.1
  118.9 2.2 collective-permute-start.16
  121.0 3.3 %collective-permute-start.17 = (bf16[2,3,112,256]{3,2,1,0:T(8,128)(2,1)S(1)}, bf16[2,3,112,256]{3,2,1,0:T(8,128)(2,1)S(1)}, u32[]{:S(2)}, u32[]{:S(2)}) collective-permute-start(bf16[2,3,112,256]{3,2,1,0:T(8,128)(2,1)S(1)} %get-tuple-element.46), channel_id=1, source_target_pairs={{0,2},{1,3},{2,0},{3,1},{4,6},{5,7},{6,4},{7,5},{8,10},{9,11},{10,... | collective-permute-start | bytes 1032200 | tf_op jit(solution)/shard_map/ppermute | solution.py:26
  124.3 3.3 %collective-permute-start.18 = (bf16[2,3,112,256]{3,2,1,0:T(8,128)(2,1)S(1)}, bf16[2,3,112,256]{3,2,1,0:T(8,128)(2,1)S(1)}, u32[]{:S(2)}, u32[]{:S(2)}) collective-permute-start(bf16[2,3,112,256]{3,2,1,0:T(8,128)(2,1)S(1)} %get-tuple-element.47), channel_id=1, source_target_pairs={{0,3},{1,0},{2,1},{3,2},{4,7},{5,4},{6,5},{7,6},{8,11},{9,8},{10,9... | collective-permute-start | bytes 1032200 | tf_op jit(solution)/shard_map/ppermute | solution.py:26
  127.6 44.4 %collective-permute-done.16.refs_1_ = bf16[2,3,112,256]{3,2,1,0:T(8,128)(2,1)S(1)} collective-permute-done((bf16[2,3,112,256]{3,2,1,0:T(8,128)(2,1)S(1)}, bf16[2,3,112,256]{3,2,1,0:T(8,128)(2,1)S(1)}, u32[]{:S(2)}, u32[]{:S(2)}) %collective-permute-start.16) | collective-permute-done | bytes 344096 | tf_op jit(solution)/shard_map/ppermute | solution.py:26
  172.0 3.5 %regroup.1 = (bf16[4,3,112,256]{3,2,1,0:T(8,128)(2,1)}, bf16[4,3,112,256]{3,2,1,0:T(8,128)(2,1)}) custom-call(s32[4]{0:T(128)S(1)} %pad_add_fusion.pos.refs_0_, bf16[2,3,112,256]{3,2,1,0:T(8,128)(2,1)S(1)} %get-tuple-element.44.refs_0_, bf16[2,3,112,256]{3,2,1,0:T(8,128)(2,1)S(1)} %collective-permute-done.16.refs_1_, ...), custom_call_target="tpu_custom_call" | custom-call | flops 172032 | bytes 2752512 | tf_op jit(solution)/shard_map/regroup/pallas_call | solution.py:337
  175.5 3.1 %collective-permute-start.20 = (bf16[4,3,112,256]{3,2,1,0:T(8,128)(2,1)}, bf16[4,3,112,256]{3,2,1,0:T(8,128)(2,1)}, u32[]{:S(2)}, u32[]{:S(2)}) collective-permute-start(bf16[4,3,112,256]{3,2,1,0:T(8,128)(2,1)} %get-tuple-element.48.refs_0_.refs_4_), channel_id=1, source_target_pairs={{0,8},{4,12},{8,0},{12,4},{1,9},{5,13},{9,1},{13,5},{2,10},{6,14},... | collective-permute-start | bytes 2064392 | tf_op jit(solution)/shard_map/ppermute | solution.py:26
  179.0 2.3 collective-permute-start.21
  181.3 1.4 collective-permute-start.15
  182.6 11.3 %collective-permute-done.20.refs_2_.refs_6_ = bf16[4,3,112,256]{3,2,1,0:T(8,128)(2,1)} collective-permute-done((bf16[4,3,112,256]{3,2,1,0:T(8,128)(2,1)}, bf16[4,3,112,256]{3,2,1,0:T(8,128)(2,1)}, u32[]{:S(2)}, u32[]{:S(2)}) %collective-permute-start.20) | collective-permute-done | bytes 688160 | tf_op jit(solution)/shard_map/ppermute | solution.py:26
  194.0 2.3 %collective-permute-start.24 = (bf16[4,3,112,256]{3,2,1,0:T(8,128)(2,1)}, bf16[4,3,112,256]{3,2,1,0:T(8,128)(2,1)S(1)}, u32[]{:S(2)}, u32[]{:S(2)}) collective-permute-start(bf16[4,3,112,256]{3,2,1,0:T(8,128)(2,1)} %collective-permute-done.20.refs_2_.refs_6_), channel_id=1, source_target_pairs={{0,16},{16,0},{1,17},{17,1},{2,18},{18,2},{3,19},{19,3},{4,20},{20... | collective-permute-start | bytes 2064392 | tf_op jit(solution)/shard_map/ppermute | solution.py:21
  196.3 13.2 %collective-permute-done.19.refs_1_.refs_5_ = bf16[4,3,112,256]{3,2,1,0:T(8,128)(2,1)} collective-permute-done((bf16[4,3,112,256]{3,2,1,0:T(8,128)(2,1)}, bf16[4,3,112,256]{3,2,1,0:T(8,128)(2,1)}, u32[]{:S(2)}, u32[]{:S(2)}) %collective-permute-start.19) | collective-permute-done | bytes 688160 | tf_op jit(solution)/shard_map/ppermute | solution.py:26
  210.5 1.5 collective-permute-done.23.refs_5_.refs_9_
  213.0 6.2 %place_rest.1.refs_12_ = bf16[3,4,4,2,112,256]{5,4,3,2,1,0:T(8,128)(2,1)} custom-call(s32[4]{0:T(128)S(1)} %pad_add_fusion.pos.refs_0_, bf16[4,3,112,256]{3,2,1,0:T(8,128)(2,1)} %get-tuple-element.48.refs_0_.refs_4_, bf16[4,3,112,256]{3,2,1,0:T(8,128)(2,1)} %collective-permute-done.19.refs_1_.refs_5_, ...), custom_call_target="tpu_custom_call" | custom-call | flops 344064 | bytes 11010048 | tf_op jit(solution)/shard_map/place_rest/pallas_call | solution.py:368
  219.2 1.9 update.1
  221.2 4.9 %finish.1 = bf16[3,4,4,2,112,256]{5,4,3,2,1,0:T(8,128)(2,1)} custom-call(s32[4]{0:T(128)S(1)} %pad_add_fusion.pos.refs_0_, bf16[16,120,256]{2,1,0:T(8,128)(2,1)} %all-to-all-done.4.refs_0_.refs_1_.refs_2_, bf16[16,120,256]{2,1,0:T(8,128)(2,1)} %all-to-all-done.4.refs_0_.refs_1_.refs_2_, ...), custom_call_target="tpu_custom_call", output_to_operand_aliasing={{}: (12, {})} | custom-call | flops 3932160 | bytes 11796480 | tf_op jit(solution)/shard_map/finish/pallas_call | solution.py:407
  (71 shorter events, 27.7 us)
Async XLA Ops:
  0.6 33.3 %collective-permute-start.2 = (bf16[448,3584]{1,0:T(8,128)(2,1)}, bf16[448,3584]{1,0:T(8,128)(2,1)}, u32[]{:S(2)}, u32[]{:S(2)}) collective-permute-start(bf16[448,3584]{1,0:T(8,128)(2,1)} %hid_a.1), channel_id=1, source_target_pairs={{0,16},{16,0},{1,17},{17,1},{2,18},{18,2},{3,19},{19,3},{4,20},{20... | collective-permute-start | bytes 9633800 | tf_op jit(solution)/shard_map/ppermute | solution.py:21
  1.4 26.3 %collective-permute-start.1 = (bf16[448,1024]{1,0:T(8,128)(2,1)}, bf16[448,1024]{1,0:T(8,128)(2,1)S(1)}, u32[]{:S(2)}, u32[]{:S(2)}) collective-permute-start(bf16[448,1024]{1,0:T(8,128)(2,1)} %cot_a.1), channel_id=1, source_target_pairs={{0,16},{16,0},{1,17},{17,1},{2,18},{18,2},{3,19},{19,3},{4,20},{20... | collective-permute-start | bytes 2752520 | tf_op jit(solution)/shard_map/ppermute | solution.py:21
  3.7 13.2 %all-to-all-start = ((f32[16,3,128]{2,1,0:T(4,128)}), f32[16,3,128]{2,1,0:T(4,128)S(1)}, u32[]{:S(2)}, u32[]{:S(2)}) async-start(f32[16,3,128]{2,1,0:T(4,128)} %broadcast_in_dim.8), calls=%async_computation | async-start | bytes 65536 | tf_op jit(solution)/shard_map/all_to_all | solution.py:34
  16.0 17.6 %collective-permute-start = (f32[8,448]{1,0:T(8,128)S(1)}, f32[8,448]{1,0:T(8,128)S(1)}, u32[]{:S(2)}, u32[]{:S(2)}) collective-permute-start(f32[8,448]{1,0:T(8,128)S(1)} %stack.46.tok_a), channel_id=1, source_target_pairs={{0,16},{16,0},{1,17},{17,1},{2,18},{18,2},{3,19},{19,3},{4,20},{20... | collective-permute-start | bytes 43016 | tf_op jit(solution)/shard_map/ppermute | solution.py:21
  17.6 16.3 %all-to-all-start.1 = ((f32[16,3,128]{2,1,0:T(4,128)}), f32[16,3,128]{2,1,0:T(4,128)S(1)}, u32[]{:S(2)}, u32[]{:S(2)}) async-start(f32[16,3,128]{2,1,0:T(4,128)} %broadcast_in_dim.9), calls=%async_computation.1 | async-start | bytes 65536 | tf_op jit(solution)/shard_map/all_to_all | solution.py:34
  28.6 1.2 copy-start.2
  29.8 1.2 copy-start.4
  42.7 13.3 %collective-permute-start.10 = (bf16[4,64,896]{2,1,0:T(8,128)(2,1)S(1)}, bf16[4,64,896]{2,1,0:T(8,128)(2,1)S(1)}, u32[]{:S(2)}, u32[]{:S(2)}) collective-permute-start(bf16[4,64,896]{2,1,0:T(8,128)(2,1)S(1)} %get-tuple-element.38), channel_id=1, source_target_pairs={{0,64},{32,96},{64,0},{96,32},{1,65},{33,97},{65,1},{97,33},{2,66}... | collective-permute-start | bytes 1376264 | tf_op jit(solution)/shard_map/ppermute | solution.py:26
  44.0 20.4 %collective-permute-start.11 = (bf16[4,64,896]{2,1,0:T(8,128)(2,1)S(1)}, bf16[4,64,896]{2,1,0:T(8,128)(2,1)S(1)}, u32[]{:S(2)}, u32[]{:S(2)}) collective-permute-start(bf16[4,64,896]{2,1,0:T(8,128)(2,1)S(1)} %get-tuple-element.39), channel_id=1, source_target_pairs={{0,96},{32,0},{64,32},{96,64},{1,97},{33,1},{65,33},{97,65},{2,98}... | collective-permute-start | bytes 1376264 | tf_op jit(solution)/shard_map/ppermute | solution.py:26
  45.5 21.1 %collective-permute-start.9 = (bf16[4,64,896]{2,1,0:T(8,128)(2,1)S(1)}, bf16[4,64,896]{2,1,0:T(8,128)(2,1)S(1)}, u32[]{:S(2)}, u32[]{:S(2)}) collective-permute-start(bf16[4,64,896]{2,1,0:T(8,128)(2,1)S(1)} %get-tuple-element.37), channel_id=1, source_target_pairs={{0,32},{32,64},{64,96},{96,0},{1,33},{33,65},{65,97},{97,1},{2,34}... | collective-permute-start | bytes 1376264 | tf_op jit(solution)/shard_map/ppermute | solution.py:26
  45.5 24.1 %collective-permute-start.3 = (bf16[4,64,896]{2,1,0:T(8,128)(2,1)S(1)}, bf16[4,64,896]{2,1,0:T(8,128)(2,1)S(1)}, u32[]{:S(2)}, u32[]{:S(2)}) collective-permute-start(bf16[4,64,896]{2,1,0:T(8,128)(2,1)S(1)} %get-tuple-element.29), channel_id=1, source_target_pairs={{0,4},{4,8},{8,12},{12,0},{1,5},{5,9},{9,13},{13,1},{2,6},{6,10},{... | collective-permute-start | bytes 1376264 | tf_op jit(solution)/shard_map/ppermute | solution.py:26
  46.6 24.1 %collective-permute-start.4 = (bf16[4,64,896]{2,1,0:T(8,128)(2,1)S(1)}, bf16[4,64,896]{2,1,0:T(8,128)(2,1)S(1)}, u32[]{:S(2)}, u32[]{:S(2)}) collective-permute-start(bf16[4,64,896]{2,1,0:T(8,128)(2,1)S(1)} %get-tuple-element.30), channel_id=1, source_target_pairs={{0,8},{4,12},{8,0},{12,4},{1,9},{5,13},{9,1},{13,5},{2,10},{6,14},... | collective-permute-start | bytes 1376264 | tf_op jit(solution)/shard_map/ppermute | solution.py:26
  56.0 14.7 %collective-permute-start.5 = (bf16[4,64,896]{2,1,0:T(8,128)(2,1)S(1)}, bf16[4,64,896]{2,1,0:T(8,128)(2,1)S(1)}, u32[]{:S(2)}, u32[]{:S(2)}) collective-permute-start(bf16[4,64,896]{2,1,0:T(8,128)(2,1)S(1)} %get-tuple-element.31), channel_id=1, source_target_pairs={{0,12},{4,0},{8,4},{12,8},{1,13},{5,1},{9,5},{13,9},{2,14},{6,2},{... | collective-permute-start | bytes 1376264 | tf_op jit(solution)/shard_map/ppermute | solution.py:26
  67.3 7.8 %collective-permute-start.12 = (bf16[64,896]{1,0:T(8,128)(2,1)S(1)}, bf16[64,896]{1,0:T(8,128)(2,1)S(1)}, u32[]{:S(2)}, u32[]{:S(2)}) collective-permute-start(bf16[64,896]{1,0:T(8,128)(2,1)S(1)} %get-tuple-element.41), channel_id=1, source_target_pairs={{0,4},{4,8},{8,12},{12,0},{1,5},{5,9},{9,13},{13,1},{2,6},{6,10},{... | collective-permute-start | bytes 344072 | tf_op jit(solution)/shard_map/ppermute | solution.py:26
  67.7 8.6 %collective-permute-start.13 = (bf16[64,896]{1,0:T(8,128)(2,1)S(1)}, bf16[64,896]{1,0:T(8,128)(2,1)S(1)}, u32[]{:S(2)}, u32[]{:S(2)}) collective-permute-start(bf16[64,896]{1,0:T(8,128)(2,1)S(1)} %get-tuple-element.42), channel_id=1, source_target_pairs={{0,8},{4,12},{8,0},{12,4},{1,9},{5,13},{9,1},{13,5},{2,10},{6,14},... | collective-permute-start | bytes 344072 | tf_op jit(solution)/shard_map/ppermute | solution.py:26
  69.5 6.8 %collective-permute-start.14 = (bf16[64,896]{1,0:T(8,128)(2,1)S(1)}, bf16[64,896]{1,0:T(8,128)(2,1)S(1)}, u32[]{:S(2)}, u32[]{:S(2)}) collective-permute-start(bf16[64,896]{1,0:T(8,128)(2,1)S(1)} %get-tuple-element.43), channel_id=1, source_target_pairs={{0,12},{4,0},{8,4},{12,8},{1,13},{5,1},{9,5},{13,9},{2,14},{6,2},{... | collective-permute-start | bytes 344072 | tf_op jit(solution)/shard_map/ppermute | solution.py:26
  71.5 4.9 %collective-permute-start.6 = (bf16[64,896]{1,0:T(8,128)(2,1)S(1)}, bf16[64,896]{1,0:T(8,128)(2,1)S(1)}, u32[]{:S(2)}, u32[]{:S(2)}) collective-permute-start(bf16[64,896]{1,0:T(8,128)(2,1)S(1)} %get-tuple-element.33), channel_id=1, source_target_pairs={{0,32},{32,64},{64,96},{96,0},{1,33},{33,65},{65,97},{97,1},{2,34}... | collective-permute-start | bytes 344072 | tf_op jit(solution)/shard_map/ppermute | solution.py:26
  72.8 6.5 %collective-permute-start.7 = (bf16[64,896]{1,0:T(8,128)(2,1)S(1)}, bf16[64,896]{1,0:T(8,128)(2,1)S(1)}, u32[]{:S(2)}, u32[]{:S(2)}) collective-permute-start(bf16[64,896]{1,0:T(8,128)(2,1)S(1)} %get-tuple-element.34), channel_id=1, source_target_pairs={{0,64},{32,96},{64,0},{96,32},{1,65},{33,97},{65,1},{97,33},{2,66}... | collective-permute-start | bytes 344072 | tf_op jit(solution)/shard_map/ppermute | solution.py:26
  75.2 4.6 %collective-permute-start.8 = (bf16[64,896]{1,0:T(8,128)(2,1)S(1)}, bf16[64,896]{1,0:T(8,128)(2,1)S(1)}, u32[]{:S(2)}, u32[]{:S(2)}) collective-permute-start(bf16[64,896]{1,0:T(8,128)(2,1)S(1)} %get-tuple-element.35), channel_id=1, source_target_pairs={{0,96},{32,0},{64,32},{96,64},{1,97},{33,1},{65,33},{97,65},{2,98}... | collective-permute-start | bytes 344072 | tf_op jit(solution)/shard_map/ppermute | solution.py:26
  79.8 37.4 %copy-start = (f32[3,224,1024]{2,1,0:T(8,128)S(1)}, f32[3,224,1024]{2,1,0:T(8,128)}, u32[]{:S(2)}) copy-start(f32[3,224,1024]{2,1,0:T(8,128)} %refs_7_.1) | copy-start | bytes 8257540
  112.9 68.4 %all-to-all-start.4 = ((bf16[16,120,256]{2,1,0:T(8,128)(2,1)}), bf16[16,120,256]{2,1,0:T(8,128)(2,1)}, u32[]{:S(2)}, u32[]{:S(2)}) async-start(bf16[16,120,256]{2,1,0:T(8,128)(2,1)} %bitcast.41), calls=%async_computation.4 | async-start | bytes 1966080 | tf_op jit(solution)/shard_map/all_to_all | solution.py:34
  118.9 53.2 %collective-permute-start.16 = (bf16[2,3,112,256]{3,2,1,0:T(8,128)(2,1)S(1)}, bf16[2,3,112,256]{3,2,1,0:T(8,128)(2,1)S(1)}, u32[]{:S(2)}, u32[]{:S(2)}) collective-permute-start(bf16[2,3,112,256]{3,2,1,0:T(8,128)(2,1)S(1)} %get-tuple-element.45), channel_id=1, source_target_pairs={{0,1},{1,2},{2,3},{3,0},{4,5},{5,6},{6,7},{7,4},{8,9},{9,10},{10,1... | collective-permute-start | bytes 1032200 | tf_op jit(solution)/shard_map/ppermute | solution.py:26
  121.0 51.0 %collective-permute-start.17 = (bf16[2,3,112,256]{3,2,1,0:T(8,128)(2,1)S(1)}, bf16[2,3,112,256]{3,2,1,0:T(8,128)(2,1)S(1)}, u32[]{:S(2)}, u32[]{:S(2)}) collective-permute-start(bf16[2,3,112,256]{3,2,1,0:T(8,128)(2,1)S(1)} %get-tuple-element.46), channel_id=1, source_target_pairs={{0,2},{1,3},{2,0},{3,1},{4,6},{5,7},{6,4},{7,5},{8,10},{9,11},{10,... | collective-permute-start | bytes 1032200 | tf_op jit(solution)/shard_map/ppermute | solution.py:26
  124.3 47.7 %collective-permute-start.18 = (bf16[2,3,112,256]{3,2,1,0:T(8,128)(2,1)S(1)}, bf16[2,3,112,256]{3,2,1,0:T(8,128)(2,1)S(1)}, u32[]{:S(2)}, u32[]{:S(2)}) collective-permute-start(bf16[2,3,112,256]{3,2,1,0:T(8,128)(2,1)S(1)} %get-tuple-element.47), channel_id=1, source_target_pairs={{0,3},{1,0},{2,1},{3,2},{4,7},{5,4},{6,5},{7,6},{8,11},{9,8},{10,9... | collective-permute-start | bytes 1032200 | tf_op jit(solution)/shard_map/ppermute | solution.py:26
  175.5 18.5 %collective-permute-start.20 = (bf16[4,3,112,256]{3,2,1,0:T(8,128)(2,1)}, bf16[4,3,112,256]{3,2,1,0:T(8,128)(2,1)}, u32[]{:S(2)}, u32[]{:S(2)}) collective-permute-start(bf16[4,3,112,256]{3,2,1,0:T(8,128)(2,1)} %get-tuple-element.48.refs_0_.refs_4_), channel_id=1, source_target_pairs={{0,8},{4,12},{8,0},{12,4},{1,9},{5,13},{9,1},{13,5},{2,10},{6,14},... | collective-permute-start | bytes 2064392 | tf_op jit(solution)/shard_map/ppermute | solution.py:26
  178.6 31.0 %collective-permute-start.19 = (bf16[4,3,112,256]{3,2,1,0:T(8,128)(2,1)}, bf16[4,3,112,256]{3,2,1,0:T(8,128)(2,1)}, u32[]{:S(2)}, u32[]{:S(2)}) collective-permute-start(bf16[4,3,112,256]{3,2,1,0:T(8,128)(2,1)} %get-tuple-element.49), channel_id=1, source_target_pairs={{0,4},{4,8},{8,12},{12,0},{1,5},{5,9},{9,13},{13,1},{2,6},{6,10},{... | collective-permute-start | bytes 2064392 | tf_op jit(solution)/shard_map/ppermute | solution.py:26
  179.0 31.0 %collective-permute-start.21 = (bf16[4,3,112,256]{3,2,1,0:T(8,128)(2,1)}, bf16[4,3,112,256]{3,2,1,0:T(8,128)(2,1)}, u32[]{:S(2)}, u32[]{:S(2)}) collective-permute-start(bf16[4,3,112,256]{3,2,1,0:T(8,128)(2,1)} %get-tuple-element.49), channel_id=1, source_target_pairs={{0,12},{4,0},{8,4},{12,8},{1,13},{5,1},{9,5},{13,9},{2,14},{6,2},{... | collective-permute-start | bytes 2064392 | tf_op jit(solution)/shard_map/ppermute | solution.py:26
  181.3 39.9 %collective-permute-start.15 = (bf16[16,120,256]{2,1,0:T(8,128)(2,1)}, bf16[16,120,256]{2,1,0:T(8,128)(2,1)S(1)}, u32[]{:S(2)}, u32[]{:S(2)}) collective-permute-start(bf16[16,120,256]{2,1,0:T(8,128)(2,1)} %all-to-all-done.4.refs_0_.refs_1_.refs_2_), channel_id=1, source_target_pairs={{0,16},{16,0},{1,17},{17,1},{2,18},{18,2},{3,19},{19,3},{4,20},{20... | collective-permute-start | bytes 2949128 | tf_op jit(solution)/shard_map/ppermute | solution.py:21
  182.6 27.9 %collective-permute-start.22 = (bf16[4,3,112,256]{3,2,1,0:T(8,128)(2,1)}, bf16[4,3,112,256]{3,2,1,0:T(8,128)(2,1)S(1)}, u32[]{:S(2)}, u32[]{:S(2)}) collective-permute-start(bf16[4,3,112,256]{3,2,1,0:T(8,128)(2,1)} %get-tuple-element.48.refs_0_.refs_4_), channel_id=1, source_target_pairs={{0,16},{16,0},{1,17},{17,1},{2,18},{18,2},{3,19},{19,3},{4,20},{20... | collective-permute-start | bytes 2064392 | tf_op jit(solution)/shard_map/ppermute | solution.py:21
  194.0 16.5 %collective-permute-start.24 = (bf16[4,3,112,256]{3,2,1,0:T(8,128)(2,1)}, bf16[4,3,112,256]{3,2,1,0:T(8,128)(2,1)S(1)}, u32[]{:S(2)}, u32[]{:S(2)}) collective-permute-start(bf16[4,3,112,256]{3,2,1,0:T(8,128)(2,1)} %collective-permute-done.20.refs_2_.refs_6_), channel_id=1, source_target_pairs={{0,16},{16,0},{1,17},{17,1},{2,18},{18,2},{3,19},{19,3},{4,20},{20... | collective-permute-start | bytes 2064392 | tf_op jit(solution)/shard_map/ppermute | solution.py:21
  209.5 2.5 %collective-permute-start.23 = (bf16[4,3,112,256]{3,2,1,0:T(8,128)(2,1)}, bf16[4,3,112,256]{3,2,1,0:T(8,128)(2,1)S(1)}, u32[]{:S(2)}, u32[]{:S(2)}) collective-permute-start(bf16[4,3,112,256]{3,2,1,0:T(8,128)(2,1)} %collective-permute-done.19.refs_1_.refs_5_), channel_id=1, source_target_pairs={{0,16},{16,0},{1,17},{17,1},{2,18},{18,2},{3,19},{19,3},{4,20},{20... | collective-permute-start | bytes 2064392 | tf_op jit(solution)/shard_map/ppermute | solution.py:21
  210.0 3.0 %collective-permute-start.25 = (bf16[4,3,112,256]{3,2,1,0:T(8,128)(2,1)}, bf16[4,3,112,256]{3,2,1,0:T(8,128)(2,1)S(1)}, u32[]{:S(2)}, u32[]{:S(2)}) collective-permute-start(bf16[4,3,112,256]{3,2,1,0:T(8,128)(2,1)} %collective-permute-done.21.refs_3_.refs_7_), channel_id=1, source_target_pairs={{0,16},{16,0},{1,17},{17,1},{2,18},{18,2},{3,19},{19,3},{4,20},{20... | collective-permute-start | bytes 2064392 | tf_op jit(solution)/shard_map/ppermute | solution.py:21
  (4 other events, 3.5 us)

commit v7 on v6

--- a/solution.py
+++ b/solution.py
@@ -34,11 +34,6 @@
     return lax.all_to_all(blocks, axis, split_axis=0, concat_axis=0, tiled=True)
 
 
-def sent_to_all(shard, axis):
-    copies = jnp.broadcast_to(shard, (lax.axis_size(axis), *shard.shape))
-    return exchanged(copies, axis)
-
-
 def params(limit=VMEM_LIMIT):
     return pltpu.CompilerParams(vmem_limit_bytes=limit)
 
@@ -47,10 +42,44 @@
     return pl.CostEstimate(flops=flops, bytes_accessed=nbytes, transcendentals=0)
 
 
-def group_sums(group_flat, reward_flat, groups):
-    onehot = (group_flat[:, None] == jnp.arange(groups, dtype=jnp.int32)[None, :]).astype(f32)
-    values = jnp.stack([jnp.ones_like(reward_flat), reward_flat, reward_flat * reward_flat], axis=0)
-    return jnp.dot(values, onehot, precision=lax.Precision.HIGHEST)
+def sums_kernel(group, reward, out):
+    lane = lax.broadcasted_iota(jnp.int32, (1, LANES), 1)
+    count = total = squares = jnp.zeros((1, LANES), f32)
+    for k in range(SEQ_DEV):
+        value = reward[:, k : k + 1]
+        mine = lane == group[:, k : k + 1]
+        count = count + jnp.where(mine, 1.0, 0.0)
+        total = total + jnp.where(mine, value, 0.0)
+        squares = squares + jnp.where(mine, value * value, 0.0)
+    for i in range(out.shape[0]):
+        for k, row in enumerate((count, total, squares)):
+            out[i, k : k + 1] = row
+
+
+def group_sums(group, reward, copies):
+    return pl.pallas_call(
+        sums_kernel,
+        out_shape=jax.ShapeDtypeStruct((copies, 3, LANES), f32),
+        compiler_params=params(),
+        cost_estimate=cost(copies * 3 * LANES, copies * 12 * LANES),
+        name="group_sums",
+    )(group, reward)
+
+
+def stats_kernel(src, out):
+    total = jnp.sum(src[...], axis=0)
+    for i in range(out.shape[0]):
+        out[i] = total
+
+
+def stats_spread(blocks, copies):
+    return pl.pallas_call(
+        stats_kernel,
+        out_shape=jax.ShapeDtypeStruct((copies, *blocks.shape[1:]), f32),
+        compiler_params=params(),
+        cost_estimate=cost(blocks.size, 8 * blocks.size),
+        name="stats_spread",
+    )(blocks)
 
 
 def token_rows(seq_row, mask_row, group_row, reward_row, new_row, old_row, ref_row):
@@ -244,7 +273,7 @@
         grid_spec=pltpu.PrefetchScalarGridSpec(
             num_scalar_prefetch=1, grid=(1,), in_specs=[whole(grad.shape)], out_specs=whole(shape)
         ),
-        compiler_params=params(),
+        compiler_params=params(60 * 1024 * 1024),
         cost_estimate=cost(4 * grad.size, 8 * grad.size),
         name="send_blocks",
     )(pos, grad)
@@ -376,7 +405,7 @@
                 (1, 1, 4, 2, half, width), lambda l, d, p: (1 + l, (p[1] - d + 4) % 4, 0, 0, 0, 0)
             ),
         ),
-        compiler_params=params(),
+        compiler_params=params(58 * 1024 * 1024),
         cost_estimate=cost(own[0].size, 32 * own[0].size),
         name="place_rest",
     )(pos, *own, *other)
@@ -438,13 +467,13 @@
 ):
     n_y, n_z = lax.axis_size("y"), lax.axis_size(("zh", "zl"))
     n_shard = lax.axis_size(SHARD)
-    groups = lax.axis_size(REP) * n_shard * SEQ_DEV // 8
     layers, rows, kv = master.shape
     pos = jnp.stack([lax.axis_index(a).astype(jnp.int32) for a in ("c", "x", "zh", "y")])
 
-    local_sums = group_sums(group_ids[0], rewards[0], groups)
-    stats = sent_to_all(local_sums, ("x", "y")).sum(axis=0)
-    stats = sent_to_all(stats, ("zh", "zl", "c"))
+    first, second = ("x", "y"), ("zh", "zl", "c")
+    stats = exchanged(group_sums(group_ids, rewards, lax.axis_size(first)), first)
+    stats = stats_spread(stats, lax.axis_size(second))
+    stats = exchanged(stats, second)
 
     hidden_b = swapped(hidden)
     cotangent_b = swapped(cotangent)

time: 228 us -> 229 us (level)
  Pallas kernels: 30.4 us -> 34.9 us
  local copies, waits for them, and re-layouts: 7.08 us -> 4.15 us
    unnamed x14 -> x32, local copies, waits for them, and re-layouts: 5.8 us -> 4.11 us
  transfers between devices with their start and end apart: 29 -> 29, of which waited for: 13 -> 13; matrix products, arithmetic and copies ran while one was open for 4% -> 2% of each run, Pallas kernels for 7% -> 8%
where the time goes in v7:
time: 229 us; the launch traced here: 226 us
  waiting for transfers between devices  94.3 us (41%)
  starting transfers between devices  57.4 us (25%)
  Pallas kernels  34.9 us (15%)
  blocking collectives  29.2 us (13%)
  local copies, waits for them, and re-layouts  4.15 us (2%)
  matrix products  3.9 us (2%)
    ppermute x18, waiting for transfers between devices, shifted(): return lax.ppermute(value, axis, [(i, (i + by) % n) for i in range(n)])  89 us
    ppermute x18, starting transfers between devices, shifted(): return lax.ppermute(value, axis, [(i, (i + by) % n) for i in range(n)])  30 us
    all_to_all x2, blocking collectives, exchanged(): return lax.all_to_all(blocks, axis, split_axis=0, concat_axis=0, tiled=True)  29.2 us
    all_to_all x3, starting transfers between devices, exchanged(): return lax.all_to_all(blocks, axis, split_axis=0, concat_axis=0, tiled=True)  21.1 us
    pallas_call x1, Pallas kernels, partial_product(): pl.pallas_call(partial_kernel, out_shape=[jax.ShapeDtypeStruct(shape, bf1...  8.77 us
    pallas_call x1, Pallas kernels, place_rest(): pl.pallas_call(place_rest_kernel, out_shape=jax.ShapeDtypeStruct((layers,...  6.95 us
    ppermute x8, starting transfers between devices, swapped(): return lax.ppermute(value, 'c', [(0, 1), (1, 0)])  6.29 us
    pallas_call x1, Pallas kernels, finish(): pl.pallas_call(lambda *refs: finish_kernel(entries, *refs), out_shape=jax...  5.21 us
  transfers between devices with their start and end apart: 29, of which 13 were waited for; matrix products, arithmetic and copies ran while one was open for 2% of the time, Pallas kernels for 8%

profile of v7, /device:TPU:33, one launch (start us, length us, event | category | flops | bytes accessed | tf_op | source)
XLA Modules:
  0.0 226.3 jit_solution(8858628985740584244)
XLA Ops:
  3.5 6.8 %all-to-all-start = ((f32[16,3,128]{2,1,0:T(4,128)}), f32[16,3,128]{2,1,0:T(4,128)S(1)}, u32[]{:S(2)}, u32[]{:S(2)}) async-start(f32[16,3,128]{2,1,0:T(4,128)} %group_sums.1), calls=%async_computation | async-start | bytes 65536 | tf_op jit(solution)/shard_map/all_to_all | solution.py:34
  17.4 10.0 %all-to-all-start.1 = ((f32[16,3,128]{2,1,0:T(4,128)}), f32[16,3,128]{2,1,0:T(4,128)S(1)}, u32[]{:S(2)}, u32[]{:S(2)}) async-start(f32[16,3,128]{2,1,0:T(4,128)} %stats_spread.1), calls=%async_computation.1 | async-start | bytes 65536 | tf_op jit(solution)/shard_map/all_to_all | solution.py:34
  31.2 2.5 %all-to-all-done.1.stats = f32[16,3,128]{2,1,0:T(4,128)S(1)} async-done(((f32[16,3,128]{2,1,0:T(4,128)}), f32[16,3,128]{2,1,0:T(4,128)S(1)}, u32[]{:S(2)}, u32[]{:S(2)}) %all-to-all-start.1) | async-done | bytes 24608 | tf_op jit(solution)/shard_map/all_to_all | solution.py:34
  33.7 8.8 %partial_product.1 = (bf16[4,64,896]{2,1,0:T(8,128)(2,1)S(1)}, bf16[4,64,896]{2,1,0:T(8,128)(2,1)S(1)}, bf16[4,64,896]{2,1,0:T(8,128)(2,1)S(1)}, bf16[4,64,896]{...) custom-call(s32[4]{0:T(128)S(1)} %pad_add_fusion.pos.refs_0_, ...), custom_call_target="tpu_custom_call" | custom-call | flops 3288334336 | bytes 10092544 | tf_op jit(solution)/shard_map/partial_product/pallas_call | solution.py:173
  43.8 1.5 collective-permute-start.11
  46.4 2.4 %collective-permute-start.4 = (bf16[4,64,896]{2,1,0:T(8,128)(2,1)S(1)}, bf16[4,64,896]{2,1,0:T(8,128)(2,1)S(1)}, u32[]{:S(2)}, u32[]{:S(2)}) collective-permute-start(bf16[4,64,896]{2,1,0:T(8,128)(2,1)S(1)} %get-tuple-element.30), channel_id=1, source_target_pairs={{0,8},{4,12},{8,0},{12,4},{1,9},{5,13},{9,1},{13,5},{2,10},{6,14},... | collective-permute-start | bytes 1376264 | tf_op jit(solution)/shard_map/ppermute | solution.py:26
  48.8 6.9 %collective-permute-done.10.refs_3_ = bf16[4,64,896]{2,1,0:T(8,128)(2,1)S(1)} collective-permute-done((bf16[4,64,896]{2,1,0:T(8,128)(2,1)S(1)}, bf16[4,64,896]{2,1,0:T(8,128)(2,1)S(1)}, u32[]{:S(2)}, u32[]{:S(2)}) %collective-permute-start.10) | collective-permute-done | bytes 458784 | tf_op jit(solution)/shard_map/ppermute | solution.py:26
  56.7 7.4 %collective-permute-done.11.refs_4_ = bf16[4,64,896]{2,1,0:T(8,128)(2,1)S(1)} collective-permute-done((bf16[4,64,896]{2,1,0:T(8,128)(2,1)S(1)}, bf16[4,64,896]{2,1,0:T(8,128)(2,1)S(1)}, u32[]{:S(2)}, u32[]{:S(2)}) %collective-permute-start.11) | collective-permute-done | bytes 458784 | tf_op jit(solution)/shard_map/ppermute | solution.py:26
  64.2 2.2 collective-permute-done.9.refs_2_
  67.5 1.8 collective-permute-start.13
  72.6 2.4 %collective-permute-start.7 = (bf16[64,896]{1,0:T(8,128)(2,1)S(1)}, bf16[64,896]{1,0:T(8,128)(2,1)S(1)}, u32[]{:S(2)}, u32[]{:S(2)}) collective-permute-start(bf16[64,896]{1,0:T(8,128)(2,1)S(1)} %get-tuple-element.34), channel_id=1, source_target_pairs={{0,64},{32,96},{64,0},{96,32},{1,65},{33,97},{65,1},{97,33},{2,66}... | collective-permute-start | bytes 344072 | tf_op jit(solution)/shard_map/ppermute | solution.py:26
  76.2 2.8 %collective-permute-done.7.refs_2_ = bf16[64,896]{1,0:T(8,128)(2,1)S(1)} collective-permute-done((bf16[64,896]{1,0:T(8,128)(2,1)S(1)}, bf16[64,896]{1,0:T(8,128)(2,1)S(1)}, u32[]{:S(2)}, u32[]{:S(2)}) %collective-permute-start.7) | collective-permute-done | bytes 114720 | tf_op jit(solution)/shard_map/ppermute | solution.py:26
  79.8 11.7 %all_to_all.25.src = bf16[8,112,128]{2,1,0:T(8,128)(2,1)S(1)} all-to-all(bf16[8,112,128]{2,1,0:T(8,128)(2,1)S(1)} %bitcast.36), channel_id=1, replica_groups=mesh['zl'=2,'y'=4,'c'=2,'x'=4,'zh'=4] {'zh','zl'}, dimensions={0} | all-to-all | bytes 458752 | tf_op jit(solution)/shard_map/all_to_all | solution.py:34
  91.5 17.5 %all_to_all.26 = bf16[16,112,128]{2,1,0:T(8,128)(2,1)} all-to-all(bf16[16,112,128]{2,1,0:T(8,128)(2,1)S(1)} %sum_spread.1), channel_id=1, replica_groups=mesh['zl'=2,'y'=4,'c'=2,'x'=4,'zh'=4] {'zl','y','c'}, dimensions={0} | all-to-all | bytes 917504 | tf_op jit(solution)/shard_map/all_to_all | solution.py:34
  109.0 2.8 %send_blocks.1 = bf16[2,4,2,120,256]{4,3,2,1,0:T(8,128)(2,1)} custom-call(s32[4]{0:T(128)} %copy-done.9, bf16[2,4,2,112,128]{4,3,2,1,0:T(8,128)(2,1)} %bitcast.34), custom_call_target="tpu_custom_call" | custom-call | flops 917504 | bytes 1835008 | tf_op jit(solution)/shard_map/send_blocks/pallas_call | solution.py:270
  111.8 4.3 %all-to-all-start.4 = ((bf16[16,120,256]{2,1,0:T(8,128)(2,1)}), bf16[16,120,256]{2,1,0:T(8,128)(2,1)}, u32[]{:S(2)}, u32[]{:S(2)}) async-start(bf16[16,120,256]{2,1,0:T(8,128)(2,1)} %bitcast.38), calls=%async_computation.4 | async-start | bytes 1966080 | tf_op jit(solution)/shard_map/all_to_all | solution.py:34
  116.2 1.6 rest_blocks.1
  117.8 2.2 collective-permute-start.16
  120.0 3.3 %collective-permute-start.17 = (bf16[2,3,112,256]{3,2,1,0:T(8,128)(2,1)S(1)}, bf16[2,3,112,256]{3,2,1,0:T(8,128)(2,1)S(1)}, u32[]{:S(2)}, u32[]{:S(2)}) collective-permute-start(bf16[2,3,112,256]{3,2,1,0:T(8,128)(2,1)S(1)} %get-tuple-element.46), channel_id=1, source_target_pairs={{0,2},{1,3},{2,0},{3,1},{4,6},{5,7},{6,4},{7,5},{8,10},{9,11},{10,... | collective-permute-start | bytes 1032200 | tf_op jit(solution)/shard_map/ppermute | solution.py:26
  123.3 3.3 %collective-permute-start.18 = (bf16[2,3,112,256]{3,2,1,0:T(8,128)(2,1)S(1)}, bf16[2,3,112,256]{3,2,1,0:T(8,128)(2,1)S(1)}, u32[]{:S(2)}, u32[]{:S(2)}) collective-permute-start(bf16[2,3,112,256]{3,2,1,0:T(8,128)(2,1)S(1)} %get-tuple-element.47), channel_id=1, source_target_pairs={{0,3},{1,0},{2,1},{3,2},{4,7},{5,4},{6,5},{7,6},{8,11},{9,8},{10,9... | collective-permute-start | bytes 1032200 | tf_op jit(solution)/shard_map/ppermute | solution.py:26
  126.6 44.4 %collective-permute-done.16.refs_1_ = bf16[2,3,112,256]{3,2,1,0:T(8,128)(2,1)S(1)} collective-permute-done((bf16[2,3,112,256]{3,2,1,0:T(8,128)(2,1)S(1)}, bf16[2,3,112,256]{3,2,1,0:T(8,128)(2,1)S(1)}, u32[]{:S(2)}, u32[]{:S(2)}) %collective-permute-start.16) | collective-permute-done | bytes 344096 | tf_op jit(solution)/shard_map/ppermute | solution.py:26
  171.0 3.5 %regroup.1 = (bf16[4,3,112,256]{3,2,1,0:T(8,128)(2,1)}, bf16[4,3,112,256]{3,2,1,0:T(8,128)(2,1)}) custom-call(s32[4]{0:T(128)S(1)} %copy-done.10, bf16[2,3,112,256]{3,2,1,0:T(8,128)(2,1)S(1)} %get-tuple-element.44.refs_0_, bf16[2,3,112,256]{3,2,1,0:T(8,128)(2,1)S(1)} %collective-permute-done.16.refs_1_, ...), custom_call_target="tpu_custom_call" | custom-call | flops 172032 | bytes 2752512 | tf_op jit(solution)/shard_map/regroup/pallas_call | solution.py:366
  174.5 3.1 %collective-permute-start.20 = (bf16[4,3,112,256]{3,2,1,0:T(8,128)(2,1)}, bf16[4,3,112,256]{3,2,1,0:T(8,128)(2,1)}, u32[]{:S(2)}, u32[]{:S(2)}) collective-permute-start(bf16[4,3,112,256]{3,2,1,0:T(8,128)(2,1)} %get-tuple-element.48.refs_0_.refs_4_), channel_id=1, source_target_pairs={{0,8},{4,12},{8,0},{12,4},{1,9},{5,13},{9,1},{13,5},{2,10},{6,14},... | collective-permute-start | bytes 2064392 | tf_op jit(solution)/shard_map/ppermute | solution.py:26
  178.0 2.3 collective-permute-start.21
  180.2 1.4 collective-permute-start.15
  181.6 11.3 %collective-permute-done.20.refs_2_.refs_6_ = bf16[4,3,112,256]{3,2,1,0:T(8,128)(2,1)} collective-permute-done((bf16[4,3,112,256]{3,2,1,0:T(8,128)(2,1)}, bf16[4,3,112,256]{3,2,1,0:T(8,128)(2,1)}, u32[]{:S(2)}, u32[]{:S(2)}) %collective-permute-start.20) | collective-permute-done | bytes 688160 | tf_op jit(solution)/shard_map/ppermute | solution.py:26
  192.9 2.3 %collective-permute-start.24 = (bf16[4,3,112,256]{3,2,1,0:T(8,128)(2,1)}, bf16[4,3,112,256]{3,2,1,0:T(8,128)(2,1)S(1)}, u32[]{:S(2)}, u32[]{:S(2)}) collective-permute-start(bf16[4,3,112,256]{3,2,1,0:T(8,128)(2,1)} %collective-permute-done.20.refs_2_.refs_6_), channel_id=1, source_target_pairs={{0,16},{16,0},{1,17},{17,1},{2,18},{18,2},{3,19},{19,3},{4,20},{20... | collective-permute-start | bytes 2064392 | tf_op jit(solution)/shard_map/ppermute | solution.py:21
  195.2 13.2 %collective-permute-done.19.refs_1_.refs_5_ = bf16[4,3,112,256]{3,2,1,0:T(8,128)(2,1)} collective-permute-done((bf16[4,3,112,256]{3,2,1,0:T(8,128)(2,1)}, bf16[4,3,112,256]{3,2,1,0:T(8,128)(2,1)}, u32[]{:S(2)}, u32[]{:S(2)}) %collective-permute-start.19) | collective-permute-done | bytes 688160 | tf_op jit(solution)/shard_map/ppermute | solution.py:26
  209.5 1.5 collective-permute-done.23.refs_5_.refs_9_
  212.1 6.9 %place_rest.1.refs_12_ = bf16[3,4,4,2,112,256]{5,4,3,2,1,0:T(8,128)(2,1)} custom-call(s32[4]{0:T(128)} %copy-done.9, bf16[4,3,112,256]{3,2,1,0:T(8,128)(2,1)} %get-tuple-element.48.refs_0_.refs_4_, bf16[4,3,112,256]{3,2,1,0:T(8,128)(2,1)} %collective-permute-done.19.refs_1_.refs_5_, bf16[4,3,112,256]{3,2,1,0:T(8,128)(2,1)} %collective-permute-done.20.refs_2_.refs_6_, ...), custom_call_target="tpu_custom_call" | custom-call | flops 344064 | bytes 11010048 | tf_op jit(solution)/shard_map/place_rest/pallas_call | solution.py:397
  219.1 2.0 update.1
  221.1 5.2 %finish.1 = bf16[3,4,4,2,112,256]{5,4,3,2,1,0:T(8,128)(2,1)} custom-call(s32[4]{0:T(128)S(1)} %copy-done.11, bf16[16,120,256]{2,1,0:T(8,128)(2,1)} %all-to-all-done.4.refs_0_.refs_1_.refs_2_, bf16[16,120,256]{2,1,0:T(8,128)(2,1)} %all-to-all-done.4.refs_0_.refs_1_.refs_2_, ...), custom_call_target="tpu_custom_call", output_to_operand_aliasing={{}: (12, {})} | custom-call | flops 3932160 | bytes 11796480 | tf_op jit(solution)/shard_map/finish/pallas_call | solution.py:436
  (85 shorter events, 26.1 us)
Async XLA Ops:
  0.6 33.1 %collective-permute-start.2 = (bf16[448,3584]{1,0:T(8,128)(2,1)}, bf16[448,3584]{1,0:T(8,128)(2,1)}, u32[]{:S(2)}, u32[]{:S(2)}) collective-permute-start(bf16[448,3584]{1,0:T(8,128)(2,1)} %hid_a.1), channel_id=1, source_target_pairs={{0,16},{16,0},{1,17},{17,1},{2,18},{18,2},{3,19},{19,3},{4,20},{20... | collective-permute-start | bytes 9633800 | tf_op jit(solution)/shard_map/ppermute | solution.py:21
  1.4 26.1 %collective-permute-start.1 = (bf16[448,1024]{1,0:T(8,128)(2,1)}, bf16[448,1024]{1,0:T(8,128)(2,1)S(1)}, u32[]{:S(2)}, u32[]{:S(2)}) collective-permute-start(bf16[448,1024]{1,0:T(8,128)(2,1)} %cot_a.1), channel_id=1, source_target_pairs={{0,16},{16,0},{1,17},{17,1},{2,18},{18,2},{3,19},{19,3},{4,20},{20... | collective-permute-start | bytes 2752520 | tf_op jit(solution)/shard_map/ppermute | solution.py:21
  3.5 13.2 %all-to-all-start = ((f32[16,3,128]{2,1,0:T(4,128)}), f32[16,3,128]{2,1,0:T(4,128)S(1)}, u32[]{:S(2)}, u32[]{:S(2)}) async-start(f32[16,3,128]{2,1,0:T(4,128)} %group_sums.1), calls=%async_computation | async-start | bytes 65536 | tf_op jit(solution)/shard_map/all_to_all | solution.py:34
  15.8 15.4 %collective-permute-start = (f32[8,448]{1,0:T(8,128)S(1)}, f32[8,448]{1,0:T(8,128)S(1)}, u32[]{:S(2)}, u32[]{:S(2)}) collective-permute-start(f32[8,448]{1,0:T(8,128)S(1)} %stack.41.tok_a), channel_id=1, source_target_pairs={{0,16},{16,0},{1,17},{17,1},{2,18},{18,2},{3,19},{19,3},{4,20},{20... | collective-permute-start | bytes 43016 | tf_op jit(solution)/shard_map/ppermute | solution.py:21
  17.4 16.3 %all-to-all-start.1 = ((f32[16,3,128]{2,1,0:T(4,128)}), f32[16,3,128]{2,1,0:T(4,128)S(1)}, u32[]{:S(2)}, u32[]{:S(2)}) async-start(f32[16,3,128]{2,1,0:T(4,128)} %stats_spread.1), calls=%async_computation.1 | async-start | bytes 65536 | tf_op jit(solution)/shard_map/all_to_all | solution.py:34
  27.5 43.0 %copy-start.9 = (s32[4]{0:T(128)}, s32[4]{0:T(128)S(1)}, u32[]{:S(2)}) copy-start(s32[4]{0:T(128)S(1)} %pad_add_fusion.pos.refs_0_) | copy-start | bytes 52
  42.5 13.3 %collective-permute-start.10 = (bf16[4,64,896]{2,1,0:T(8,128)(2,1)S(1)}, bf16[4,64,896]{2,1,0:T(8,128)(2,1)S(1)}, u32[]{:S(2)}, u32[]{:S(2)}) collective-permute-start(bf16[4,64,896]{2,1,0:T(8,128)(2,1)S(1)} %get-tuple-element.38), channel_id=1, source_target_pairs={{0,64},{32,96},{64,0},{96,32},{1,65},{33,97},{65,1},{97,33},{2,66}... | collective-permute-start | bytes 1376264 | tf_op jit(solution)/shard_map/ppermute | solution.py:26
  43.8 20.4 %collective-permute-start.11 = (bf16[4,64,896]{2,1,0:T(8,128)(2,1)S(1)}, bf16[4,64,896]{2,1,0:T(8,128)(2,1)S(1)}, u32[]{:S(2)}, u32[]{:S(2)}) collective-permute-start(bf16[4,64,896]{2,1,0:T(8,128)(2,1)S(1)} %get-tuple-element.39), channel_id=1, source_target_pairs={{0,96},{32,0},{64,32},{96,64},{1,97},{33,1},{65,33},{97,65},{2,98}... | collective-permute-start | bytes 1376264 | tf_op jit(solution)/shard_map/ppermute | solution.py:26
  45.2 21.1 %collective-permute-start.9 = (bf16[4,64,896]{2,1,0:T(8,128)(2,1)S(1)}, bf16[4,64,896]{2,1,0:T(8,128)(2,1)S(1)}, u32[]{:S(2)}, u32[]{:S(2)}) collective-permute-start(bf16[4,64,896]{2,1,0:T(8,128)(2,1)S(1)} %get-tuple-element.37), channel_id=1, source_target_pairs={{0,32},{32,64},{64,96},{96,0},{1,33},{33,65},{65,97},{97,1},{2,34}... | collective-permute-start | bytes 1376264 | tf_op jit(solution)/shard_map/ppermute | solution.py:26
  45.3 24.1 %collective-permute-start.3 = (bf16[4,64,896]{2,1,0:T(8,128)(2,1)S(1)}, bf16[4,64,896]{2,1,0:T(8,128)(2,1)S(1)}, u32[]{:S(2)}, u32[]{:S(2)}) collective-permute-start(bf16[4,64,896]{2,1,0:T(8,128)(2,1)S(1)} %get-tuple-element.29), channel_id=1, source_target_pairs={{0,4},{4,8},{8,12},{12,0},{1,5},{5,9},{9,13},{13,1},{2,6},{6,10},{... | collective-permute-start | bytes 1376264 | tf_op jit(solution)/shard_map/ppermute | solution.py:26
  46.4 24.1 %collective-permute-start.4 = (bf16[4,64,896]{2,1,0:T(8,128)(2,1)S(1)}, bf16[4,64,896]{2,1,0:T(8,128)(2,1)S(1)}, u32[]{:S(2)}, u32[]{:S(2)}) collective-permute-start(bf16[4,64,896]{2,1,0:T(8,128)(2,1)S(1)} %get-tuple-element.30), channel_id=1, source_target_pairs={{0,8},{4,12},{8,0},{12,4},{1,9},{5,13},{9,1},{13,5},{2,10},{6,14},... | collective-permute-start | bytes 1376264 | tf_op jit(solution)/shard_map/ppermute | solution.py:26
  55.8 14.7 %collective-permute-start.5 = (bf16[4,64,896]{2,1,0:T(8,128)(2,1)S(1)}, bf16[4,64,896]{2,1,0:T(8,128)(2,1)S(1)}, u32[]{:S(2)}, u32[]{:S(2)}) collective-permute-start(bf16[4,64,896]{2,1,0:T(8,128)(2,1)S(1)} %get-tuple-element.31), channel_id=1, source_target_pairs={{0,12},{4,0},{8,4},{12,8},{1,13},{5,1},{9,5},{13,9},{2,14},{6,2},{... | collective-permute-start | bytes 1376264 | tf_op jit(solution)/shard_map/ppermute | solution.py:26
  67.1 7.8 %collective-permute-start.12 = (bf16[64,896]{1,0:T(8,128)(2,1)S(1)}, bf16[64,896]{1,0:T(8,128)(2,1)S(1)}, u32[]{:S(2)}, u32[]{:S(2)}) collective-permute-start(bf16[64,896]{1,0:T(8,128)(2,1)S(1)} %get-tuple-element.41), channel_id=1, source_target_pairs={{0,4},{4,8},{8,12},{12,0},{1,5},{5,9},{9,13},{13,1},{2,6},{6,10},{... | collective-permute-start | bytes 344072 | tf_op jit(solution)/shard_map/ppermute | solution.py:26
  67.5 8.7 %collective-permute-start.13 = (bf16[64,896]{1,0:T(8,128)(2,1)S(1)}, bf16[64,896]{1,0:T(8,128)(2,1)S(1)}, u32[]{:S(2)}, u32[]{:S(2)}) collective-permute-start(bf16[64,896]{1,0:T(8,128)(2,1)S(1)} %get-tuple-element.42), channel_id=1, source_target_pairs={{0,8},{4,12},{8,0},{12,4},{1,9},{5,13},{9,1},{13,5},{2,10},{6,14},... | collective-permute-start | bytes 344072 | tf_op jit(solution)/shard_map/ppermute | solution.py:26
  69.3 6.8 %collective-permute-start.14 = (bf16[64,896]{1,0:T(8,128)(2,1)S(1)}, bf16[64,896]{1,0:T(8,128)(2,1)S(1)}, u32[]{:S(2)}, u32[]{:S(2)}) collective-permute-start(bf16[64,896]{1,0:T(8,128)(2,1)S(1)} %get-tuple-element.43), channel_id=1, source_target_pairs={{0,12},{4,0},{8,4},{12,8},{1,13},{5,1},{9,5},{13,9},{2,14},{6,2},{... | collective-permute-start | bytes 344072 | tf_op jit(solution)/shard_map/ppermute | solution.py:26
  71.3 4.9 %collective-permute-start.6 = (bf16[64,896]{1,0:T(8,128)(2,1)S(1)}, bf16[64,896]{1,0:T(8,128)(2,1)S(1)}, u32[]{:S(2)}, u32[]{:S(2)}) collective-permute-start(bf16[64,896]{1,0:T(8,128)(2,1)S(1)} %get-tuple-element.33), channel_id=1, source_target_pairs={{0,32},{32,64},{64,96},{96,0},{1,33},{33,65},{65,97},{97,1},{2,34}... | collective-permute-start | bytes 344072 | tf_op jit(solution)/shard_map/ppermute | solution.py:26
  72.6 6.5 %collective-permute-start.7 = (bf16[64,896]{1,0:T(8,128)(2,1)S(1)}, bf16[64,896]{1,0:T(8,128)(2,1)S(1)}, u32[]{:S(2)}, u32[]{:S(2)}) collective-permute-start(bf16[64,896]{1,0:T(8,128)(2,1)S(1)} %get-tuple-element.34), channel_id=1, source_target_pairs={{0,64},{32,96},{64,0},{96,32},{1,65},{33,97},{65,1},{97,33},{2,66}... | collective-permute-start | bytes 344072 | tf_op jit(solution)/shard_map/ppermute | solution.py:26
  75.0 4.6 %collective-permute-start.8 = (bf16[64,896]{1,0:T(8,128)(2,1)S(1)}, bf16[64,896]{1,0:T(8,128)(2,1)S(1)}, u32[]{:S(2)}, u32[]{:S(2)}) collective-permute-start(bf16[64,896]{1,0:T(8,128)(2,1)S(1)} %get-tuple-element.35), channel_id=1, source_target_pairs={{0,96},{32,0},{64,32},{96,64},{1,97},{33,1},{65,33},{97,65},{2,98}... | collective-permute-start | bytes 344072 | tf_op jit(solution)/shard_map/ppermute | solution.py:26
  79.6 36.6 %copy-start.10 = (s32[4]{0:T(128)S(1)}, s32[4]{0:T(128)}, u32[]{:S(2)}) copy-start(s32[4]{0:T(128)} %copy-done.9) | copy-start | bytes 52
  111.8 68.4 %all-to-all-start.4 = ((bf16[16,120,256]{2,1,0:T(8,128)(2,1)}), bf16[16,120,256]{2,1,0:T(8,128)(2,1)}, u32[]{:S(2)}, u32[]{:S(2)}) async-start(bf16[16,120,256]{2,1,0:T(8,128)(2,1)} %bitcast.38), calls=%async_computation.4 | async-start | bytes 1966080 | tf_op jit(solution)/shard_map/all_to_all | solution.py:34
  117.8 53.2 %collective-permute-start.16 = (bf16[2,3,112,256]{3,2,1,0:T(8,128)(2,1)S(1)}, bf16[2,3,112,256]{3,2,1,0:T(8,128)(2,1)S(1)}, u32[]{:S(2)}, u32[]{:S(2)}) collective-permute-start(bf16[2,3,112,256]{3,2,1,0:T(8,128)(2,1)S(1)} %get-tuple-element.45), channel_id=1, source_target_pairs={{0,1},{1,2},{2,3},{3,0},{4,5},{5,6},{6,7},{7,4},{8,9},{9,10},{10,1... | collective-permute-start | bytes 1032200 | tf_op jit(solution)/shard_map/ppermute | solution.py:26
  120.0 51.0 %collective-permute-start.17 = (bf16[2,3,112,256]{3,2,1,0:T(8,128)(2,1)S(1)}, bf16[2,3,112,256]{3,2,1,0:T(8,128)(2,1)S(1)}, u32[]{:S(2)}, u32[]{:S(2)}) collective-permute-start(bf16[2,3,112,256]{3,2,1,0:T(8,128)(2,1)S(1)} %get-tuple-element.46), channel_id=1, source_target_pairs={{0,2},{1,3},{2,0},{3,1},{4,6},{5,7},{6,4},{7,5},{8,10},{9,11},{10,... | collective-permute-start | bytes 1032200 | tf_op jit(solution)/shard_map/ppermute | solution.py:26
  123.3 47.7 %collective-permute-start.18 = (bf16[2,3,112,256]{3,2,1,0:T(8,128)(2,1)S(1)}, bf16[2,3,112,256]{3,2,1,0:T(8,128)(2,1)S(1)}, u32[]{:S(2)}, u32[]{:S(2)}) collective-permute-start(bf16[2,3,112,256]{3,2,1,0:T(8,128)(2,1)S(1)} %get-tuple-element.47), channel_id=1, source_target_pairs={{0,3},{1,0},{2,1},{3,2},{4,7},{5,4},{6,5},{7,6},{8,11},{9,8},{10,9... | collective-permute-start | bytes 1032200 | tf_op jit(solution)/shard_map/ppermute | solution.py:26
  174.5 18.5 %collective-permute-start.20 = (bf16[4,3,112,256]{3,2,1,0:T(8,128)(2,1)}, bf16[4,3,112,256]{3,2,1,0:T(8,128)(2,1)}, u32[]{:S(2)}, u32[]{:S(2)}) collective-permute-start(bf16[4,3,112,256]{3,2,1,0:T(8,128)(2,1)} %get-tuple-element.48.refs_0_.refs_4_), channel_id=1, source_target_pairs={{0,8},{4,12},{8,0},{12,4},{1,9},{5,13},{9,1},{13,5},{2,10},{6,14},... | collective-permute-start | bytes 2064392 | tf_op jit(solution)/shard_map/ppermute | solution.py:26
  177.5 41.5 %copy-start.1 = (bf16[16,112,128]{2,1,0:T(8,128)(2,1)S(1)}, bf16[16,112,128]{2,1,0:T(8,128)(2,1)}, u32[]{:S(2)}) copy-start(bf16[16,112,128]{2,1,0:T(8,128)(2,1)} %all_to_all.26) | copy-start | bytes 1376260
  177.5 31.0 %collective-permute-start.19 = (bf16[4,3,112,256]{3,2,1,0:T(8,128)(2,1)}, bf16[4,3,112,256]{3,2,1,0:T(8,128)(2,1)}, u32[]{:S(2)}, u32[]{:S(2)}) collective-permute-start(bf16[4,3,112,256]{3,2,1,0:T(8,128)(2,1)} %get-tuple-element.49), channel_id=1, source_target_pairs={{0,4},{4,8},{8,12},{12,0},{1,5},{5,9},{9,13},{13,1},{2,6},{6,10},{... | collective-permute-start | bytes 2064392 | tf_op jit(solution)/shard_map/ppermute | solution.py:26
  178.0 31.0 %collective-permute-start.21 = (bf16[4,3,112,256]{3,2,1,0:T(8,128)(2,1)}, bf16[4,3,112,256]{3,2,1,0:T(8,128)(2,1)}, u32[]{:S(2)}, u32[]{:S(2)}) collective-permute-start(bf16[4,3,112,256]{3,2,1,0:T(8,128)(2,1)} %get-tuple-element.49), channel_id=1, source_target_pairs={{0,12},{4,0},{8,4},{12,8},{1,13},{5,1},{9,5},{13,9},{2,14},{6,2},{... | collective-permute-start | bytes 2064392 | tf_op jit(solution)/shard_map/ppermute | solution.py:26
  180.2 40.9 %collective-permute-start.15 = (bf16[16,120,256]{2,1,0:T(8,128)(2,1)}, bf16[16,120,256]{2,1,0:T(8,128)(2,1)}, u32[]{:S(2)}, u32[]{:S(2)}) collective-permute-start(bf16[16,120,256]{2,1,0:T(8,128)(2,1)} %all-to-all-done.4.refs_0_.refs_1_.refs_2_), channel_id=1, source_target_pairs={{0,16},{16,0},{1,17},{17,1},{2,18},{18,2},{3,19},{19,3},{4,20},{20... | collective-permute-start | bytes 2949128 | tf_op jit(solution)/shard_map/ppermute | solution.py:21
  181.6 27.9 %collective-permute-start.22 = (bf16[4,3,112,256]{3,2,1,0:T(8,128)(2,1)}, bf16[4,3,112,256]{3,2,1,0:T(8,128)(2,1)S(1)}, u32[]{:S(2)}, u32[]{:S(2)}) collective-permute-start(bf16[4,3,112,256]{3,2,1,0:T(8,128)(2,1)} %get-tuple-element.48.refs_0_.refs_4_), channel_id=1, source_target_pairs={{0,16},{16,0},{1,17},{17,1},{2,18},{18,2},{3,19},{19,3},{4,20},{20... | collective-permute-start | bytes 2064392 | tf_op jit(solution)/shard_map/ppermute | solution.py:21
  192.9 16.5 %collective-permute-start.24 = (bf16[4,3,112,256]{3,2,1,0:T(8,128)(2,1)}, bf16[4,3,112,256]{3,2,1,0:T(8,128)(2,1)S(1)}, u32[]{:S(2)}, u32[]{:S(2)}) collective-permute-start(bf16[4,3,112,256]{3,2,1,0:T(8,128)(2,1)} %collective-permute-done.20.refs_2_.refs_6_), channel_id=1, source_target_pairs={{0,16},{16,0},{1,17},{17,1},{2,18},{18,2},{3,19},{19,3},{4,20},{20... | collective-permute-start | bytes 2064392 | tf_op jit(solution)/shard_map/ppermute | solution.py:21
  208.5 2.5 %collective-permute-start.23 = (bf16[4,3,112,256]{3,2,1,0:T(8,128)(2,1)}, bf16[4,3,112,256]{3,2,1,0:T(8,128)(2,1)S(1)}, u32[]{:S(2)}, u32[]{:S(2)}) collective-permute-start(bf16[4,3,112,256]{3,2,1,0:T(8,128)(2,1)} %collective-permute-done.19.refs_1_.refs_5_), channel_id=1, source_target_pairs={{0,16},{16,0},{1,17},{17,1},{2,18},{18,2},{3,19},{19,3},{4,20},{20... | collective-permute-start | bytes 2064392 | tf_op jit(solution)/shard_map/ppermute | solution.py:21
  209.0 3.1 %collective-permute-start.25 = (bf16[4,3,112,256]{3,2,1,0:T(8,128)(2,1)}, bf16[4,3,112,256]{3,2,1,0:T(8,128)(2,1)}, u32[]{:S(2)}, u32[]{:S(2)}) collective-permute-start(bf16[4,3,112,256]{3,2,1,0:T(8,128)(2,1)} %collective-permute-done.21.refs_3_.refs_7_), channel_id=1, source_target_pairs={{0,16},{16,0},{1,17},{17,1},{2,18},{18,2},{3,19},{19,3},{4,20},{20... | collective-permute-start | bytes 2064392 | tf_op jit(solution)/shard_map/ppermute | solution.py:21
  (13 other events, 55.2 us)

commit v8 on v7

--- a/solution.py
+++ b/solution.py
@@ -379,36 +379,33 @@
     )(pos, *parts)
 
 
-def place_rest_kernel(pos, *refs):
-    srcs, out = refs[:8], refs[8]
+def place_rest_kernel(pos, own, other, *refs):
+    out = refs[-1]
     zh, core = pos[2], pos[0]
-    for dx in range(4):
-
-        @pl.when(pl.program_id(1) == dx)
-        def _():
-            for w in range(2):
-                for dz in range(4):
-                    out[0, 0, (zh - dz + 4) % 4, (core + w) % 2] = srcs[4 * w + dx][dz, 0]
-
-
-def place_rest(pos, own, other, layers):
-    _, count, half, width = own[0].shape
-    src = pl.BlockSpec((4, 1, half, width), lambda l, d, p: (0, 1 + l, 0, 0))
+    for w, src in enumerate((own, other)):
+        for dz in range(4):
+            out[0, 0, (zh - dz + 4) % 4, (core + w) % 2] = src[dz, 0]
+
+
+def place_rest(pos, own, other, dx, into=None):
+    _, layers, half, width = own.shape
+    src = pl.BlockSpec((4, 1, half, width), lambda l, p: (0, 1 + l, 0, 0))
+    keep = [] if into is None else [into]
     return pl.pallas_call(
         place_rest_kernel,
         out_shape=jax.ShapeDtypeStruct((layers, 4, 4, 2, half, width), bf16),
         grid_spec=pltpu.PrefetchScalarGridSpec(
             num_scalar_prefetch=1,
-            grid=(count - 1, 4),
-            in_specs=[src] * 8,
+            grid=(layers - 1,),
+            in_specs=[src, src] + [pl.BlockSpec(memory_space=pl.ANY)] * len(keep),
             out_specs=pl.BlockSpec(
-                (1, 1, 4, 2, half, width), lambda l, d, p: (1 + l, (p[1] - d + 4) % 4, 0, 0, 0, 0)
+                (1, 1, 4, 2, half, width), lambda l, p: (1 + l, (p[1] - dx + 4) % 4, 0, 0, 0, 0)
             ),
         ),
+        input_output_aliases={3: 0} if keep else {},
         compiler_params=params(58 * 1024 * 1024),
-        cost_estimate=cost(own[0].size, 32 * own[0].size),
-        name="place_rest",
-    )(pos, *own, *other)
+        cost_estimate=cost(own.size, 8 * own.size),
+    )(pos, own, other, *keep)
 
 
 def finish_kernel(entries, pos, squares, grad_a, grad_b, *refs):
@@ -495,7 +492,9 @@
     parts = rest_blocks(pos, master)
     parts = spread_out(parts, "zh")
     same, cross = regroup(pos, parts)
-    rest = spread_out([same, cross, same, cross], "x")
+    rest = [same]
+    for d in range(1, 4):
+        rest.append(shifted(cross if d % 2 else same, "x", d))
     part = part.reshape(n_z, part.shape[0] // n_z, part.shape[1])
     zl = lax.axis_size("zl")
     part = exchanged(part, ("zh", "zl"))
@@ -505,7 +504,9 @@
     first = exchanged(first.reshape(n_shard, *first.shape[3:]), SHARD)
 
     other = [swapped(r) for r in rest]
-    out = place_rest(pos, rest, other, layers)
+    out = None
+    for d in (0, 2, 1, 3):
+        out = place_rest(pos, rest[d], other[d], d, out)
     entries = hidden.shape[1] * kv
     first_b = swapped(first)
     new_master = update(first, grad, master, entries)

time: 229 us -> 232 us (1.013)
  Pallas kernels: 34.9 us -> 38.9 us
  waiting for transfers between devices: 94.3 us -> 91.5 us
  local copies, waits for them, and re-layouts: 4.15 us -> 6.72 us
    pallas_call x1 -> x4, Pallas kernels: 6.95 us -> 11.3 us  [place_rest(): pl.pallas_call(place_rest_kernel, out_shape=jax.ShapeDtypeStruct((layers,...]
    ppermute x8, waiting for transfers between devices: 2.63 us -> 0.02 us  [swapped(): return lax.ppermute(value, 'c', [(0, 1), (1, 0)])]
    unnamed x32 -> x36, local copies, waits for them, and re-layouts: 4.11 us -> 6.68 us
  transfers between devices with their start and end apart: 29 -> 29, of which waited for: 13 -> 11; matrix products, arithmetic and copies ran while one was open for 2% -> 2% of each run, Pallas kernels for 8% -> 10%
where the time goes in v8:
time: 232 us; the launch traced here: 230 us
  waiting for transfers between devices  91.5 us (39%)
  starting transfers between devices  57.4 us (25%)
  Pallas kernels  38.9 us (17%)
  blocking collectives  29 us (12%)
  local copies, waits for them, and re-layouts  6.72 us (3%)
  matrix products  3.9 us (2%)
    ppermute x18, waiting for transfers between devices, shifted(): return lax.ppermute(value, axis, [(i, (i + by) % n) for i in range(n)])  88.8 us
    ppermute x18, starting transfers between devices, shifted(): return lax.ppermute(value, axis, [(i, (i + by) % n) for i in range(n)])  30 us
    all_to_all x2, blocking collectives, exchanged(): return lax.all_to_all(blocks, axis, split_axis=0, concat_axis=0, tiled=True)  29 us
    all_to_all x3, starting transfers between devices, exchanged(): return lax.all_to_all(blocks, axis, split_axis=0, concat_axis=0, tiled=True)  21.1 us
    pallas_call x4, Pallas kernels, place_rest(): pl.pallas_call(place_rest_kernel, out_shape=jax.ShapeDtypeStruct((layers,...  11.3 us
    pallas_call x1, Pallas kernels, partial_product(): pl.pallas_call(partial_kernel, out_shape=[jax.ShapeDtypeStruct(shape, bf1...  8.77 us
    unnamed x36, local copies, waits for them, and re-layouts  6.68 us
    ppermute x8, starting transfers between devices, swapped(): return lax.ppermute(value, 'c', [(0, 1), (1, 0)])  6.29 us
  transfers between devices with their start and end apart: 29, of which 11 were waited for; matrix products, arithmetic and copies ran while one was open for 2% of the time, Pallas kernels for 10%

profile of v8, /device:TPU:33, one launch (start us, length us, event | category | flops | bytes accessed | tf_op | source)
XLA Modules:
  0.0 230.0 jit_solution(8703961577664183988)
XLA Ops:
  3.5 6.8 %all-to-all-start = ((f32[16,3,128]{2,1,0:T(4,128)}), f32[16,3,128]{2,1,0:T(4,128)S(1)}, u32[]{:S(2)}, u32[]{:S(2)}) async-start(f32[16,3,128]{2,1,0:T(4,128)} %group_sums.1), calls=%async_computation | async-start | bytes 65536 | tf_op jit(solution)/shard_map/all_to_all | solution.py:34
  17.4 10.0 %all-to-all-start.1 = ((f32[16,3,128]{2,1,0:T(4,128)}), f32[16,3,128]{2,1,0:T(4,128)S(1)}, u32[]{:S(2)}, u32[]{:S(2)}) async-start(f32[16,3,128]{2,1,0:T(4,128)} %stats_spread.1), calls=%async_computation.1 | async-start | bytes 65536 | tf_op jit(solution)/shard_map/all_to_all | solution.py:34
  31.2 2.5 %all-to-all-done.1.stats = f32[16,3,128]{2,1,0:T(4,128)S(1)} async-done(((f32[16,3,128]{2,1,0:T(4,128)}), f32[16,3,128]{2,1,0:T(4,128)S(1)}, u32[]{:S(2)}, u32[]{:S(2)}) %all-to-all-start.1) | async-done | bytes 24608 | tf_op jit(solution)/shard_map/all_to_all | solution.py:34
  33.7 8.8 %partial_product.1 = (bf16[4,64,896]{2,1,0:T(8,128)(2,1)S(1)}, bf16[4,64,896]{2,1,0:T(8,128)(2,1)S(1)}, bf16[4,64,896]{2,1,0:T(8,128)(2,1)S(1)}, bf16[4,64,896]{...) custom-call(s32[4]{0:T(128)S(1)} %pad_add_fusion.pos.refs_0_, ...), custom_call_target="tpu_custom_call" | custom-call | flops 3288334336 | bytes 10092544 | tf_op jit(solution)/shard_map/partial_product/pallas_call | solution.py:173
  46.4 2.4 %collective-permute-start.4 = (bf16[4,64,896]{2,1,0:T(8,128)(2,1)S(1)}, bf16[4,64,896]{2,1,0:T(8,128)(2,1)S(1)}, u32[]{:S(2)}, u32[]{:S(2)}) collective-permute-start(bf16[4,64,896]{2,1,0:T(8,128)(2,1)S(1)} %get-tuple-element.30), channel_id=1, source_target_pairs={{0,8},{4,12},{8,0},{12,4},{1,9},{5,13},{9,1},{13,5},{2,10},{6,14},... | collective-permute-start | bytes 1376264 | tf_op jit(solution)/shard_map/ppermute | solution.py:26
  48.8 7.0 %collective-permute-done.10.refs_3_ = bf16[4,64,896]{2,1,0:T(8,128)(2,1)S(1)} collective-permute-done((bf16[4,64,896]{2,1,0:T(8,128)(2,1)S(1)}, bf16[4,64,896]{2,1,0:T(8,128)(2,1)S(1)}, u32[]{:S(2)}, u32[]{:S(2)}) %collective-permute-start.10) | collective-permute-done | bytes 458784 | tf_op jit(solution)/shard_map/ppermute | solution.py:26
  56.7 7.4 %collective-permute-done.11.refs_4_ = bf16[4,64,896]{2,1,0:T(8,128)(2,1)S(1)} collective-permute-done((bf16[4,64,896]{2,1,0:T(8,128)(2,1)S(1)}, bf16[4,64,896]{2,1,0:T(8,128)(2,1)S(1)}, u32[]{:S(2)}, u32[]{:S(2)}) %collective-permute-start.11) | collective-permute-done | bytes 458784 | tf_op jit(solution)/shard_map/ppermute | solution.py:26
  64.2 2.2 collective-permute-done.9.refs_2_
  67.5 1.8 collective-permute-start.13
  72.6 2.4 %collective-permute-start.7 = (bf16[64,896]{1,0:T(8,128)(2,1)S(1)}, bf16[64,896]{1,0:T(8,128)(2,1)S(1)}, u32[]{:S(2)}, u32[]{:S(2)}) collective-permute-start(bf16[64,896]{1,0:T(8,128)(2,1)S(1)} %get-tuple-element.34), channel_id=1, source_target_pairs={{0,64},{32,96},{64,0},{96,32},{1,65},{33,97},{65,1},{97,33},{2,66}... | collective-permute-start | bytes 344072 | tf_op jit(solution)/shard_map/ppermute | solution.py:26
  76.2 2.8 %collective-permute-done.7.refs_2_ = bf16[64,896]{1,0:T(8,128)(2,1)S(1)} collective-permute-done((bf16[64,896]{1,0:T(8,128)(2,1)S(1)}, bf16[64,896]{1,0:T(8,128)(2,1)S(1)}, u32[]{:S(2)}, u32[]{:S(2)}) %collective-permute-start.7) | collective-permute-done | bytes 114720 | tf_op jit(solution)/shard_map/ppermute | solution.py:26
  79.8 11.5 %all_to_all.25.src = bf16[8,112,128]{2,1,0:T(8,128)(2,1)S(1)} all-to-all(bf16[8,112,128]{2,1,0:T(8,128)(2,1)S(1)} %bitcast.36), channel_id=1, replica_groups=mesh['zl'=2,'y'=4,'c'=2,'x'=4,'zh'=4] {'zh','zl'}, dimensions={0} | all-to-all | bytes 458752 | tf_op jit(solution)/shard_map/all_to_all | solution.py:34
  91.4 17.5 %all_to_all.26 = bf16[16,112,128]{2,1,0:T(8,128)(2,1)} all-to-all(bf16[16,112,128]{2,1,0:T(8,128)(2,1)S(1)} %sum_spread.1), channel_id=1, replica_groups=mesh['zl'=2,'y'=4,'c'=2,'x'=4,'zh'=4] {'zl','y','c'}, dimensions={0} | all-to-all | bytes 917504 | tf_op jit(solution)/shard_map/all_to_all | solution.py:34
  108.9 2.8 %send_blocks.1 = bf16[2,4,2,120,256]{4,3,2,1,0:T(8,128)(2,1)} custom-call(s32[4]{0:T(128)} %copy-done.11, bf16[2,4,2,112,128]{4,3,2,1,0:T(8,128)(2,1)} %bitcast.34), custom_call_target="tpu_custom_call" | custom-call | flops 917504 | bytes 1835008 | tf_op jit(solution)/shard_map/send_blocks/pallas_call | solution.py:270
  111.7 4.3 %all-to-all-start.4 = ((bf16[16,120,256]{2,1,0:T(8,128)(2,1)}), bf16[16,120,256]{2,1,0:T(8,128)(2,1)}, u32[]{:S(2)}, u32[]{:S(2)}) async-start(bf16[16,120,256]{2,1,0:T(8,128)(2,1)} %bitcast.38), calls=%async_computation.4 | async-start | bytes 1966080 | tf_op jit(solution)/shard_map/all_to_all | solution.py:34
  116.0 1.6 rest_blocks.1
  117.7 2.2 collective-permute-start.16
  119.9 3.3 %collective-permute-start.17 = (bf16[2,3,112,256]{3,2,1,0:T(8,128)(2,1)S(1)}, bf16[2,3,112,256]{3,2,1,0:T(8,128)(2,1)S(1)}, u32[]{:S(2)}, u32[]{:S(2)}) collective-permute-start(bf16[2,3,112,256]{3,2,1,0:T(8,128)(2,1)S(1)} %get-tuple-element.46), channel_id=1, source_target_pairs={{0,2},{1,3},{2,0},{3,1},{4,6},{5,7},{6,4},{7,5},{8,10},{9,11},{10,... | collective-permute-start | bytes 1032200 | tf_op jit(solution)/shard_map/ppermute | solution.py:26
  123.2 3.3 %collective-permute-start.18 = (bf16[2,3,112,256]{3,2,1,0:T(8,128)(2,1)S(1)}, bf16[2,3,112,256]{3,2,1,0:T(8,128)(2,1)S(1)}, u32[]{:S(2)}, u32[]{:S(2)}) collective-permute-start(bf16[2,3,112,256]{3,2,1,0:T(8,128)(2,1)S(1)} %get-tuple-element.47), channel_id=1, source_target_pairs={{0,3},{1,0},{2,1},{3,2},{4,7},{5,4},{6,5},{7,6},{8,11},{9,8},{10,9... | collective-permute-start | bytes 1032200 | tf_op jit(solution)/shard_map/ppermute | solution.py:26
  126.5 44.4 %collective-permute-done.16.refs_1_ = bf16[2,3,112,256]{3,2,1,0:T(8,128)(2,1)S(1)} collective-permute-done((bf16[2,3,112,256]{3,2,1,0:T(8,128)(2,1)S(1)}, bf16[2,3,112,256]{3,2,1,0:T(8,128)(2,1)S(1)}, u32[]{:S(2)}, u32[]{:S(2)}) %collective-permute-start.16) | collective-permute-done | bytes 344096 | tf_op jit(solution)/shard_map/ppermute | solution.py:26
  170.9 3.3 %regroup.1 = (bf16[4,3,112,256]{3,2,1,0:T(8,128)(2,1)S(1)}, bf16[4,3,112,256]{3,2,1,0:T(8,128)(2,1)}) custom-call(s32[4]{0:T(128)S(1)} %copy-done.12, bf16[2,3,112,256]{3,2,1,0:T(8,128)(2,1)S(1)} %get-tuple-element.44.refs_0_, bf16[2,3,112,256]{3,2,1,0:T(8,128)(2,1)S(1)} %collective-permute-done.16.refs_1_, ...), custom_call_target="tpu_custom_call" | custom-call | flops 172032 | bytes 2752512 | tf_op jit(solution)/shard_map/regroup/pallas_call | solution.py:366
  174.1 3.1 %collective-permute-start.20 = (bf16[4,3,112,256]{3,2,1,0:T(8,128)(2,1)S(1)}, bf16[4,3,112,256]{3,2,1,0:T(8,128)(2,1)}, u32[]{:S(2)}, u32[]{:S(2)}) collective-permute-start(bf16[4,3,112,256]{3,2,1,0:T(8,128)(2,1)S(1)} %get-tuple-element.48.own.refs_4_), channel_id=1, source_target_pairs={{0,8},{4,12},{8,0},{12,4},{1,9},{5,13},{9,1},{13,5},{2,10},{6,14},... | collective-permute-start | bytes 2064392 | tf_op jit(solution)/shard_map/ppermute | solution.py:26
  177.6 2.3 collective-permute-start.21
  181.3 11.1 %collective-permute-done.20.own.refs_6_ = bf16[4,3,112,256]{3,2,1,0:T(8,128)(2,1)} collective-permute-done((bf16[4,3,112,256]{3,2,1,0:T(8,128)(2,1)S(1)}, bf16[4,3,112,256]{3,2,1,0:T(8,128)(2,1)}, u32[]{:S(2)}, u32[]{:S(2)}) %collective-permute-start.20) | collective-permute-done | bytes 688160 | tf_op jit(solution)/shard_map/ppermute | solution.py:26
  192.4 2.3 %collective-permute-start.24 = (bf16[4,3,112,256]{3,2,1,0:T(8,128)(2,1)}, bf16[4,3,112,256]{3,2,1,0:T(8,128)(2,1)S(1)}, u32[]{:S(2)}, u32[]{:S(2)}) collective-permute-start(bf16[4,3,112,256]{3,2,1,0:T(8,128)(2,1)} %collective-permute-done.20.own.refs_6_), channel_id=1, source_target_pairs={{0,16},{16,0},{1,17},{17,1},{2,18},{18,2},{3,19},{19,3},{4,20},{20... | collective-permute-start | bytes 2064392 | tf_op jit(solution)/shard_map/ppermute | solution.py:21
  194.7 13.2 %collective-permute-done.19.own.refs_5_ = bf16[4,3,112,256]{3,2,1,0:T(8,128)(2,1)} collective-permute-done((bf16[4,3,112,256]{3,2,1,0:T(8,128)(2,1)}, bf16[4,3,112,256]{3,2,1,0:T(8,128)(2,1)}, u32[]{:S(2)}, u32[]{:S(2)}) %collective-permute-start.19) | collective-permute-done | bytes 688160 | tf_op jit(solution)/shard_map/ppermute | solution.py:26
  209.8 2.8 %shard_map.115.refs_0_ = bf16[3,4,4,2,112,256]{5,4,3,2,1,0:T(8,128)(2,1)} custom-call(s32[4]{0:T(128)} %copy-done.11, bf16[4,3,112,256]{3,2,1,0:T(8,128)(2,1)} %copy-done.2, bf16[4,3,112,256]{3,2,1,0:T(8,128)(2,1)} %copy-done.4), custom_call_target="tpu_custom_call" | custom-call | flops 344064 | bytes 2752512 | tf_op jit(solution)/shard_map/pallas_call | solution.py:394
  213.4 2.8 %shard_map.116.refs_0_ = bf16[3,4,4,2,112,256]{5,4,3,2,1,0:T(8,128)(2,1)} custom-call(s32[4]{0:T(128)} %copy-done.11, bf16[4,3,112,256]{3,2,1,0:T(8,128)(2,1)} %collective-permute-done.20.own.refs_6_, bf16[4,3,112,256]{3,2,1,0:T(8,128)(2,1)} %copy-done.6, bf16[3,4,4,2,112,256]{5,4,3,2,1,0:T(8,128)(2,1)} %shard_map.115.refs_0_), custom_call_target="tpu_custom_call", output_to_operand_aliasing={{}: (3, {})} | custom-call | flops 344064 | bytes 2752512 | tf_op jit(solution)/shard_map/pallas_call | solution.py:394
  217.1 2.8 %shard_map.117.refs_0_ = bf16[3,4,4,2,112,256]{5,4,3,2,1,0:T(8,128)(2,1)} custom-call(s32[4]{0:T(128)} %copy-done.11, bf16[4,3,112,256]{3,2,1,0:T(8,128)(2,1)} %collective-permute-done.19.own.refs_5_, bf16[4,3,112,256]{3,2,1,0:T(8,128)(2,1)} %copy-done.8, bf16[3,4,4,2,112,256]{5,4,3,2,1,0:T(8,128)(2,1)} %shard_map.116.refs_0_), custom_call_target="tpu_custom_call", output_to_operand_aliasing={{}: (3, {})} | custom-call | flops 344064 | bytes 2752512 | tf_op jit(solution)/shard_map/pallas_call | solution.py:394
  219.8 2.9 %shard_map.118.refs_12_ = bf16[3,4,4,2,112,256]{5,4,3,2,1,0:T(8,128)(2,1)} custom-call(s32[4]{0:T(128)} %copy-done.11, bf16[4,3,112,256]{3,2,1,0:T(8,128)(2,1)} %collective-permute-done.21.own.refs_7_, bf16[4,3,112,256]{3,2,1,0:T(8,128)(2,1)} %collective-permute-done.25.other.refs_11_, ...), custom_call_target="tpu_custom_call", output_to_operand_aliasing={{}: (3, {})} | custom-call | flops 344064 | bytes 2752512 | tf_op jit(solution)/shard_map/pallas_call | solution.py:394
  222.8 2.0 update.1
  224.9 5.1 %finish.1 = bf16[3,4,4,2,112,256]{5,4,3,2,1,0:T(8,128)(2,1)} custom-call(s32[4]{0:T(128)S(1)} %copy-done.13, bf16[16,120,256]{2,1,0:T(8,128)(2,1)} %all-to-all-done.4.refs_0_.refs_1_.refs_2_, bf16[16,120,256]{2,1,0:T(8,128)(2,1)} %all-to-all-done.4.refs_0_.refs_1_.refs_2_, ...), custom_call_target="tpu_custom_call", output_to_operand_aliasing={{}: (12, {})} | custom-call | flops 3932160 | bytes 11796480 | tf_op jit(solution)/shard_map/finish/pallas_call | solution.py:433
  (92 shorter events, 30.4 us)
Async XLA Ops:
  0.6 33.1 %collective-permute-start.2 = (bf16[448,3584]{1,0:T(8,128)(2,1)}, bf16[448,3584]{1,0:T(8,128)(2,1)}, u32[]{:S(2)}, u32[]{:S(2)}) collective-permute-start(bf16[448,3584]{1,0:T(8,128)(2,1)} %hid_a.1), channel_id=1, source_target_pairs={{0,16},{16,0},{1,17},{17,1},{2,18},{18,2},{3,19},{19,3},{4,20},{20... | collective-permute-start | bytes 9633800 | tf_op jit(solution)/shard_map/ppermute | solution.py:21
  1.4 26.1 %collective-permute-start.1 = (bf16[448,1024]{1,0:T(8,128)(2,1)}, bf16[448,1024]{1,0:T(8,128)(2,1)S(1)}, u32[]{:S(2)}, u32[]{:S(2)}) collective-permute-start(bf16[448,1024]{1,0:T(8,128)(2,1)} %cot_a.1), channel_id=1, source_target_pairs={{0,16},{16,0},{1,17},{17,1},{2,18},{18,2},{3,19},{19,3},{4,20},{20... | collective-permute-start | bytes 2752520 | tf_op jit(solution)/shard_map/ppermute | solution.py:21
  3.5 13.2 %all-to-all-start = ((f32[16,3,128]{2,1,0:T(4,128)}), f32[16,3,128]{2,1,0:T(4,128)S(1)}, u32[]{:S(2)}, u32[]{:S(2)}) async-start(f32[16,3,128]{2,1,0:T(4,128)} %group_sums.1), calls=%async_computation | async-start | bytes 65536 | tf_op jit(solution)/shard_map/all_to_all | solution.py:34
  15.8 15.4 %collective-permute-start = (f32[8,448]{1,0:T(8,128)S(1)}, f32[8,448]{1,0:T(8,128)S(1)}, u32[]{:S(2)}, u32[]{:S(2)}) collective-permute-start(f32[8,448]{1,0:T(8,128)S(1)} %stack.41.tok_a), channel_id=1, source_target_pairs={{0,16},{16,0},{1,17},{17,1},{2,18},{18,2},{3,19},{19,3},{4,20},{20... | collective-permute-start | bytes 43016 | tf_op jit(solution)/shard_map/ppermute | solution.py:21
  17.4 16.3 %all-to-all-start.1 = ((f32[16,3,128]{2,1,0:T(4,128)}), f32[16,3,128]{2,1,0:T(4,128)S(1)}, u32[]{:S(2)}, u32[]{:S(2)}) async-start(f32[16,3,128]{2,1,0:T(4,128)} %stats_spread.1), calls=%async_computation.1 | async-start | bytes 65536 | tf_op jit(solution)/shard_map/all_to_all | solution.py:34
  27.5 43.0 %copy-start.11 = (s32[4]{0:T(128)}, s32[4]{0:T(128)S(1)}, u32[]{:S(2)}) copy-start(s32[4]{0:T(128)S(1)} %pad_add_fusion.pos.refs_0_) | copy-start | bytes 52
  42.5 73.5 %copy-start = (f32[3,224,1024]{2,1,0:T(8,128)S(1)}, f32[3,224,1024]{2,1,0:T(8,128)}, u32[]{:S(2)}) copy-start(f32[3,224,1024]{2,1,0:T(8,128)} %refs_7_.1) | copy-start | bytes 8257540
  42.5 13.3 %collective-permute-start.10 = (bf16[4,64,896]{2,1,0:T(8,128)(2,1)S(1)}, bf16[4,64,896]{2,1,0:T(8,128)(2,1)S(1)}, u32[]{:S(2)}, u32[]{:S(2)}) collective-permute-start(bf16[4,64,896]{2,1,0:T(8,128)(2,1)S(1)} %get-tuple-element.38), channel_id=1, source_target_pairs={{0,64},{32,96},{64,0},{96,32},{1,65},{33,97},{65,1},{97,33},{2,66}... | collective-permute-start | bytes 1376264 | tf_op jit(solution)/shard_map/ppermute | solution.py:26
  43.8 20.4 %collective-permute-start.11 = (bf16[4,64,896]{2,1,0:T(8,128)(2,1)S(1)}, bf16[4,64,896]{2,1,0:T(8,128)(2,1)S(1)}, u32[]{:S(2)}, u32[]{:S(2)}) collective-permute-start(bf16[4,64,896]{2,1,0:T(8,128)(2,1)S(1)} %get-tuple-element.39), channel_id=1, source_target_pairs={{0,96},{32,0},{64,32},{96,64},{1,97},{33,1},{65,33},{97,65},{2,98}... | collective-permute-start | bytes 1376264 | tf_op jit(solution)/shard_map/ppermute | solution.py:26
  45.3 21.1 %collective-permute-start.9 = (bf16[4,64,896]{2,1,0:T(8,128)(2,1)S(1)}, bf16[4,64,896]{2,1,0:T(8,128)(2,1)S(1)}, u32[]{:S(2)}, u32[]{:S(2)}) collective-permute-start(bf16[4,64,896]{2,1,0:T(8,128)(2,1)S(1)} %get-tuple-element.37), channel_id=1, source_target_pairs={{0,32},{32,64},{64,96},{96,0},{1,33},{33,65},{65,97},{97,1},{2,34}... | collective-permute-start | bytes 1376264 | tf_op jit(solution)/shard_map/ppermute | solution.py:26
  45.3 24.1 %collective-permute-start.3 = (bf16[4,64,896]{2,1,0:T(8,128)(2,1)S(1)}, bf16[4,64,896]{2,1,0:T(8,128)(2,1)S(1)}, u32[]{:S(2)}, u32[]{:S(2)}) collective-permute-start(bf16[4,64,896]{2,1,0:T(8,128)(2,1)S(1)} %get-tuple-element.29), channel_id=1, source_target_pairs={{0,4},{4,8},{8,12},{12,0},{1,5},{5,9},{9,13},{13,1},{2,6},{6,10},{... | collective-permute-start | bytes 1376264 | tf_op jit(solution)/shard_map/ppermute | solution.py:26
  46.4 24.1 %collective-permute-start.4 = (bf16[4,64,896]{2,1,0:T(8,128)(2,1)S(1)}, bf16[4,64,896]{2,1,0:T(8,128)(2,1)S(1)}, u32[]{:S(2)}, u32[]{:S(2)}) collective-permute-start(bf16[4,64,896]{2,1,0:T(8,128)(2,1)S(1)} %get-tuple-element.30), channel_id=1, source_target_pairs={{0,8},{4,12},{8,0},{12,4},{1,9},{5,13},{9,1},{13,5},{2,10},{6,14},... | collective-permute-start | bytes 1376264 | tf_op jit(solution)/shard_map/ppermute | solution.py:26
  55.8 14.7 %collective-permute-start.5 = (bf16[4,64,896]{2,1,0:T(8,128)(2,1)S(1)}, bf16[4,64,896]{2,1,0:T(8,128)(2,1)S(1)}, u32[]{:S(2)}, u32[]{:S(2)}) collective-permute-start(bf16[4,64,896]{2,1,0:T(8,128)(2,1)S(1)} %get-tuple-element.31), channel_id=1, source_target_pairs={{0,12},{4,0},{8,4},{12,8},{1,13},{5,1},{9,5},{13,9},{2,14},{6,2},{... | collective-permute-start | bytes 1376264 | tf_op jit(solution)/shard_map/ppermute | solution.py:26
  67.1 7.8 %collective-permute-start.12 = (bf16[64,896]{1,0:T(8,128)(2,1)S(1)}, bf16[64,896]{1,0:T(8,128)(2,1)S(1)}, u32[]{:S(2)}, u32[]{:S(2)}) collective-permute-start(bf16[64,896]{1,0:T(8,128)(2,1)S(1)} %get-tuple-element.41), channel_id=1, source_target_pairs={{0,4},{4,8},{8,12},{12,0},{1,5},{5,9},{9,13},{13,1},{2,6},{6,10},{... | collective-permute-start | bytes 344072 | tf_op jit(solution)/shard_map/ppermute | solution.py:26
  67.5 8.7 %collective-permute-start.13 = (bf16[64,896]{1,0:T(8,128)(2,1)S(1)}, bf16[64,896]{1,0:T(8,128)(2,1)S(1)}, u32[]{:S(2)}, u32[]{:S(2)}) collective-permute-start(bf16[64,896]{1,0:T(8,128)(2,1)S(1)} %get-tuple-element.42), channel_id=1, source_target_pairs={{0,8},{4,12},{8,0},{12,4},{1,9},{5,13},{9,1},{13,5},{2,10},{6,14},... | collective-permute-start | bytes 344072 | tf_op jit(solution)/shard_map/ppermute | solution.py:26
  69.3 6.8 %collective-permute-start.14 = (bf16[64,896]{1,0:T(8,128)(2,1)S(1)}, bf16[64,896]{1,0:T(8,128)(2,1)S(1)}, u32[]{:S(2)}, u32[]{:S(2)}) collective-permute-start(bf16[64,896]{1,0:T(8,128)(2,1)S(1)} %get-tuple-element.43), channel_id=1, source_target_pairs={{0,12},{4,0},{8,4},{12,8},{1,13},{5,1},{9,5},{13,9},{2,14},{6,2},{... | collective-permute-start | bytes 344072 | tf_op jit(solution)/shard_map/ppermute | solution.py:26
  71.3 44.7 %copy-start.12 = (s32[4]{0:T(128)S(1)}, s32[4]{0:T(128)}, u32[]{:S(2)}) copy-start(s32[4]{0:T(128)} %copy-done.11) | copy-start | bytes 52
  71.3 4.9 %collective-permute-start.6 = (bf16[64,896]{1,0:T(8,128)(2,1)S(1)}, bf16[64,896]{1,0:T(8,128)(2,1)S(1)}, u32[]{:S(2)}, u32[]{:S(2)}) collective-permute-start(bf16[64,896]{1,0:T(8,128)(2,1)S(1)} %get-tuple-element.33), channel_id=1, source_target_pairs={{0,32},{32,64},{64,96},{96,0},{1,33},{33,65},{65,97},{97,1},{2,34}... | collective-permute-start | bytes 344072 | tf_op jit(solution)/shard_map/ppermute | solution.py:26
  72.6 6.5 %collective-permute-start.7 = (bf16[64,896]{1,0:T(8,128)(2,1)S(1)}, bf16[64,896]{1,0:T(8,128)(2,1)S(1)}, u32[]{:S(2)}, u32[]{:S(2)}) collective-permute-start(bf16[64,896]{1,0:T(8,128)(2,1)S(1)} %get-tuple-element.34), channel_id=1, source_target_pairs={{0,64},{32,96},{64,0},{96,32},{1,65},{33,97},{65,1},{97,33},{2,66}... | collective-permute-start | bytes 344072 | tf_op jit(solution)/shard_map/ppermute | solution.py:26
  75.0 4.6 %collective-permute-start.8 = (bf16[64,896]{1,0:T(8,128)(2,1)S(1)}, bf16[64,896]{1,0:T(8,128)(2,1)S(1)}, u32[]{:S(2)}, u32[]{:S(2)}) collective-permute-start(bf16[64,896]{1,0:T(8,128)(2,1)S(1)} %get-tuple-element.35), channel_id=1, source_target_pairs={{0,96},{32,0},{64,32},{96,64},{1,97},{33,1},{65,33},{97,65},{2,98}... | collective-permute-start | bytes 344072 | tf_op jit(solution)/shard_map/ppermute | solution.py:26
  111.7 68.2 %all-to-all-start.4 = ((bf16[16,120,256]{2,1,0:T(8,128)(2,1)}), bf16[16,120,256]{2,1,0:T(8,128)(2,1)}, u32[]{:S(2)}, u32[]{:S(2)}) async-start(bf16[16,120,256]{2,1,0:T(8,128)(2,1)} %bitcast.38), calls=%async_computation.4 | async-start | bytes 1966080 | tf_op jit(solution)/shard_map/all_to_all | solution.py:34
  117.7 53.2 %collective-permute-start.16 = (bf16[2,3,112,256]{3,2,1,0:T(8,128)(2,1)S(1)}, bf16[2,3,112,256]{3,2,1,0:T(8,128)(2,1)S(1)}, u32[]{:S(2)}, u32[]{:S(2)}) collective-permute-start(bf16[2,3,112,256]{3,2,1,0:T(8,128)(2,1)S(1)} %get-tuple-element.45), channel_id=1, source_target_pairs={{0,1},{1,2},{2,3},{3,0},{4,5},{5,6},{6,7},{7,4},{8,9},{9,10},{10,1... | collective-permute-start | bytes 1032200 | tf_op jit(solution)/shard_map/ppermute | solution.py:26
  119.9 51.0 %collective-permute-start.17 = (bf16[2,3,112,256]{3,2,1,0:T(8,128)(2,1)S(1)}, bf16[2,3,112,256]{3,2,1,0:T(8,128)(2,1)S(1)}, u32[]{:S(2)}, u32[]{:S(2)}) collective-permute-start(bf16[2,3,112,256]{3,2,1,0:T(8,128)(2,1)S(1)} %get-tuple-element.46), channel_id=1, source_target_pairs={{0,2},{1,3},{2,0},{3,1},{4,6},{5,7},{6,4},{7,5},{8,10},{9,11},{10,... | collective-permute-start | bytes 1032200 | tf_op jit(solution)/shard_map/ppermute | solution.py:26
  123.2 47.7 %collective-permute-start.18 = (bf16[2,3,112,256]{3,2,1,0:T(8,128)(2,1)S(1)}, bf16[2,3,112,256]{3,2,1,0:T(8,128)(2,1)S(1)}, u32[]{:S(2)}, u32[]{:S(2)}) collective-permute-start(bf16[2,3,112,256]{3,2,1,0:T(8,128)(2,1)S(1)} %get-tuple-element.47), channel_id=1, source_target_pairs={{0,3},{1,0},{2,1},{3,2},{4,7},{5,4},{6,5},{7,6},{8,11},{9,8},{10,9... | collective-permute-start | bytes 1032200 | tf_op jit(solution)/shard_map/ppermute | solution.py:26
  174.1 18.2 %collective-permute-start.20 = (bf16[4,3,112,256]{3,2,1,0:T(8,128)(2,1)S(1)}, bf16[4,3,112,256]{3,2,1,0:T(8,128)(2,1)}, u32[]{:S(2)}, u32[]{:S(2)}) collective-permute-start(bf16[4,3,112,256]{3,2,1,0:T(8,128)(2,1)S(1)} %get-tuple-element.48.own.refs_4_), channel_id=1, source_target_pairs={{0,8},{4,12},{8,0},{12,4},{1,9},{5,13},{9,1},{13,5},{2,10},{6,14},... | collective-permute-start | bytes 2064392 | tf_op jit(solution)/shard_map/ppermute | solution.py:26
  177.2 30.7 %collective-permute-start.19 = (bf16[4,3,112,256]{3,2,1,0:T(8,128)(2,1)}, bf16[4,3,112,256]{3,2,1,0:T(8,128)(2,1)}, u32[]{:S(2)}, u32[]{:S(2)}) collective-permute-start(bf16[4,3,112,256]{3,2,1,0:T(8,128)(2,1)} %get-tuple-element.49), channel_id=1, source_target_pairs={{0,4},{4,8},{8,12},{12,0},{1,5},{5,9},{9,13},{13,1},{2,6},{6,10},{... | collective-permute-start | bytes 2064392 | tf_op jit(solution)/shard_map/ppermute | solution.py:26
  177.6 30.8 %collective-permute-start.21 = (bf16[4,3,112,256]{3,2,1,0:T(8,128)(2,1)}, bf16[4,3,112,256]{3,2,1,0:T(8,128)(2,1)}, u32[]{:S(2)}, u32[]{:S(2)}) collective-permute-start(bf16[4,3,112,256]{3,2,1,0:T(8,128)(2,1)} %get-tuple-element.49), channel_id=1, source_target_pairs={{0,12},{4,0},{8,4},{12,8},{1,13},{5,1},{9,5},{13,9},{2,14},{6,2},{... | collective-permute-start | bytes 2064392 | tf_op jit(solution)/shard_map/ppermute | solution.py:26
  179.9 44.9 %collective-permute-start.15 = (bf16[16,120,256]{2,1,0:T(8,128)(2,1)}, bf16[16,120,256]{2,1,0:T(8,128)(2,1)}, u32[]{:S(2)}, u32[]{:S(2)}) collective-permute-start(bf16[16,120,256]{2,1,0:T(8,128)(2,1)} %all-to-all-done.4.refs_0_.refs_1_.refs_2_), channel_id=1, source_target_pairs={{0,16},{16,0},{1,17},{17,1},{2,18},{18,2},{3,19},{19,3},{4,20},{20... | collective-permute-start | bytes 2949128 | tf_op jit(solution)/shard_map/ppermute | solution.py:21
  181.2 27.7 %collective-permute-start.22 = (bf16[4,3,112,256]{3,2,1,0:T(8,128)(2,1)S(1)}, bf16[4,3,112,256]{3,2,1,0:T(8,128)(2,1)S(1)}, u32[]{:S(2)}, u32[]{:S(2)}) collective-permute-start(bf16[4,3,112,256]{3,2,1,0:T(8,128)(2,1)S(1)} %get-tuple-element.48.own.refs_4_), channel_id=1, source_target_pairs={{0,16},{16,0},{1,17},{17,1},{2,18},{18,2},{3,19},{19,3},{4,20},{20... | collective-permute-start | bytes 2064392 | tf_op jit(solution)/shard_map/ppermute | solution.py:21
  192.4 20.2 %collective-permute-start.24 = (bf16[4,3,112,256]{3,2,1,0:T(8,128)(2,1)}, bf16[4,3,112,256]{3,2,1,0:T(8,128)(2,1)S(1)}, u32[]{:S(2)}, u32[]{:S(2)}) collective-permute-start(bf16[4,3,112,256]{3,2,1,0:T(8,128)(2,1)} %collective-permute-done.20.own.refs_6_), channel_id=1, source_target_pairs={{0,16},{16,0},{1,17},{17,1},{2,18},{18,2},{3,19},{19,3},{4,20},{20... | collective-permute-start | bytes 2064392 | tf_op jit(solution)/shard_map/ppermute | solution.py:21
  208.0 8.3 %collective-permute-start.23 = (bf16[4,3,112,256]{3,2,1,0:T(8,128)(2,1)}, bf16[4,3,112,256]{3,2,1,0:T(8,128)(2,1)S(1)}, u32[]{:S(2)}, u32[]{:S(2)}) collective-permute-start(bf16[4,3,112,256]{3,2,1,0:T(8,128)(2,1)} %collective-permute-done.19.own.refs_5_), channel_id=1, source_target_pairs={{0,16},{16,0},{1,17},{17,1},{2,18},{18,2},{3,19},{19,3},{4,20},{20... | collective-permute-start | bytes 2064392 | tf_op jit(solution)/shard_map/ppermute | solution.py:21
  208.4 11.4 %collective-permute-start.25 = (bf16[4,3,112,256]{3,2,1,0:T(8,128)(2,1)}, bf16[4,3,112,256]{3,2,1,0:T(8,128)(2,1)}, u32[]{:S(2)}, u32[]{:S(2)}) collective-permute-start(bf16[4,3,112,256]{3,2,1,0:T(8,128)(2,1)} %collective-permute-done.21.own.refs_7_), channel_id=1, source_target_pairs={{0,16},{16,0},{1,17},{17,1},{2,18},{18,2},{3,19},{19,3},{4,20},{20... | collective-permute-start | bytes 2064392 | tf_op jit(solution)/shard_map/ppermute | solution.py:21
  (15 other events, 57.6 us)

commit v9 on v7

--- a/solution.py
+++ b/solution.py
@@ -347,36 +347,58 @@
     )(pos, *([master] * 8))
 
 
-def regroup_kernel(pos, *refs):
-    parts, (same, cross), sems = refs[:4], refs[4:6], refs[6]
+def mark_kernel(src, out):
+    out[...] = src[...]
+
+
+def mark(value):
+    return pl.pallas_call(
+        mark_kernel,
+        out_shape=jax.ShapeDtypeStruct(value.shape, value.dtype),
+        compiler_params=params(),
+        name="mark",
+    )(value)
+
+
+def regroup_kernel(pos, after, *refs):
+    parts, outs, (held, sems, out_sems) = refs[:4], refs[4:6], refs[6:]
     xl = pos[1] % 2
     copies = []
     for d in range(4):
-        copies.append(pltpu.make_async_copy(parts[d].at[xl], same.at[d], sems.at[2 * d]))
-        copies.append(pltpu.make_async_copy(parts[d].at[1 - xl], cross.at[d], sems.at[2 * d + 1]))
-    for copy in copies:
-        copy.start()
-    for copy in copies:
-        copy.wait()
-
-
-def regroup(pos, parts):
+        for k, at in enumerate((xl, 1 - xl)):
+            into = pltpu.make_async_copy(parts[d].at[at], held.at[d, k], sems.at[d, k])
+            away = pltpu.make_async_copy(held.at[d, k], outs[k].at[d], out_sems.at[d, k])
+            copies.append((into, away))
+    for into, _ in copies:
+        into.start()
+    for into, away in copies:
+        into.wait()
+        away.start()
+    for _, away in copies:
+        away.wait()
+
+
+def regroup(pos, parts, after):
     shape = (4, *parts[0].shape[1:])
-    whole = lambda s: pl.BlockSpec(s, lambda i, p: (0,) * len(s))
+    far = pl.BlockSpec(memory_space=pltpu.HBM)
     return pl.pallas_call(
         regroup_kernel,
         out_shape=[jax.ShapeDtypeStruct(shape, bf16)] * 2,
         grid_spec=pltpu.PrefetchScalarGridSpec(
             num_scalar_prefetch=1,
             grid=(1,),
-            in_specs=[pl.BlockSpec(memory_space=pltpu.HBM)] * 4,
-            out_specs=[whole(shape)] * 2,
-            scratch_shapes=[pltpu.SemaphoreType.DMA((8,))],
+            in_specs=[pl.BlockSpec(memory_space=pl.ANY)] + [far] * 4,
+            out_specs=[far] * 2,
+            scratch_shapes=[
+                pltpu.VMEM((4, 2, *shape[1:]), bf16),
+                pltpu.SemaphoreType.DMA((4, 2)),
+                pltpu.SemaphoreType.DMA((4, 2)),
+            ],
         ),
         compiler_params=params(),
         cost_estimate=cost(parts[0].size, 16 * parts[0].size),
         name="regroup",
-    )(pos, *parts)
+    )(pos, after, *parts)
 
 
 def place_rest_kernel(pos, *refs):
@@ -494,7 +516,7 @@
 
     parts = rest_blocks(pos, master)
     parts = spread_out(parts, "zh")
-    same, cross = regroup(pos, parts)
+    same, cross = regroup(pos, parts, mark(rewards))
     rest = spread_out([same, cross, same, cross], "x")
     part = part.reshape(n_z, part.shape[0] // n_z, part.shape[1])
     zl = lax.axis_size("zl")

time: 229 us -> 229 us (level)
  no operation moved by 1% of the time
where the time goes in v9:
time: 229 us; the launch traced here: 226 us
  waiting for transfers between devices  94.4 us (41%)
  starting transfers between devices  57.3 us (25%)
  Pallas kernels  35 us (15%)
  blocking collectives  29.2 us (13%)
  local copies, waits for them, and re-layouts  4.16 us (2%)
  matrix products  3.9 us (2%)
    ppermute x18, waiting for transfers between devices, shifted(): return lax.ppermute(value, axis, [(i, (i + by) % n) for i in range(n)])  89 us
    ppermute x18, starting transfers between devices, shifted(): return lax.ppermute(value, axis, [(i, (i + by) % n) for i in range(n)])  29.9 us
    all_to_all x2, blocking collectives, exchanged(): return lax.all_to_all(blocks, axis, split_axis=0, concat_axis=0, tiled=True)  29.2 us
    all_to_all x3, starting transfers between devices, exchanged(): return lax.all_to_all(blocks, axis, split_axis=0, concat_axis=0, tiled=True)  21.1 us
    pallas_call x1, Pallas kernels, partial_product(): pl.pallas_call(partial_kernel, out_shape=[jax.ShapeDtypeStruct(shape, bf1...  8.78 us
    pallas_call x1, Pallas kernels, place_rest(): pl.pallas_call(place_rest_kernel, out_shape=jax.ShapeDtypeStruct((layers,...  6.95 us
    ppermute x8, starting transfers between devices, swapped(): return lax.ppermute(value, 'c', [(0, 1), (1, 0)])  6.29 us
    pallas_call x1, Pallas kernels, finish(): pl.pallas_call(lambda *refs: finish_kernel(entries, *refs), out_shape=jax...  5.21 us
  transfers between devices with their start and end apart: 29, of which 13 were waited for; matrix products, arithmetic and copies ran while one was open for 2% of the time, Pallas kernels for 8%

profile of v9, /device:TPU:33, one launch (start us, length us, event | category | flops | bytes accessed | tf_op | source)
XLA Modules:
  0.0 226.4 jit_solution(17921403777176788649)
XLA Ops:
  3.5 6.8 %all-to-all-start = ((f32[16,3,128]{2,1,0:T(4,128)}), f32[16,3,128]{2,1,0:T(4,128)S(1)}, u32[]{:S(2)}, u32[]{:S(2)}) async-start(f32[16,3,128]{2,1,0:T(4,128)} %group_sums.1), calls=%async_computation | async-start | bytes 65536 | tf_op jit(solution)/shard_map/all_to_all | solution.py:34
  17.4 10.0 %all-to-all-start.1 = ((f32[16,3,128]{2,1,0:T(4,128)}), f32[16,3,128]{2,1,0:T(4,128)S(1)}, u32[]{:S(2)}, u32[]{:S(2)}) async-start(f32[16,3,128]{2,1,0:T(4,128)} %stats_spread.1), calls=%async_computation.1 | async-start | bytes 65536 | tf_op jit(solution)/shard_map/all_to_all | solution.py:34
  31.2 2.5 %all-to-all-done.1.stats = f32[16,3,128]{2,1,0:T(4,128)S(1)} async-done(((f32[16,3,128]{2,1,0:T(4,128)}), f32[16,3,128]{2,1,0:T(4,128)S(1)}, u32[]{:S(2)}, u32[]{:S(2)}) %all-to-all-start.1) | async-done | bytes 24608 | tf_op jit(solution)/shard_map/all_to_all | solution.py:34
  33.7 8.8 %partial_product.1 = (bf16[4,64,896]{2,1,0:T(8,128)(2,1)S(1)}, bf16[4,64,896]{2,1,0:T(8,128)(2,1)S(1)}, bf16[4,64,896]{2,1,0:T(8,128)(2,1)S(1)}, bf16[4,64,896]{...) custom-call(s32[4]{0:T(128)S(1)} %pad_add_fusion.pos.refs_0_, ...), custom_call_target="tpu_custom_call" | custom-call | flops 3288334336 | bytes 10092544 | tf_op jit(solution)/shard_map/partial_product/pallas_call | solution.py:173
  43.8 1.5 collective-permute-start.11
  46.4 2.4 %collective-permute-start.4 = (bf16[4,64,896]{2,1,0:T(8,128)(2,1)S(1)}, bf16[4,64,896]{2,1,0:T(8,128)(2,1)S(1)}, u32[]{:S(2)}, u32[]{:S(2)}) collective-permute-start(bf16[4,64,896]{2,1,0:T(8,128)(2,1)S(1)} %get-tuple-element.30), channel_id=1, source_target_pairs={{0,8},{4,12},{8,0},{12,4},{1,9},{5,13},{9,1},{13,5},{2,10},{6,14},... | collective-permute-start | bytes 1376264 | tf_op jit(solution)/shard_map/ppermute | solution.py:26
  48.8 7.0 %collective-permute-done.10.refs_3_ = bf16[4,64,896]{2,1,0:T(8,128)(2,1)S(1)} collective-permute-done((bf16[4,64,896]{2,1,0:T(8,128)(2,1)S(1)}, bf16[4,64,896]{2,1,0:T(8,128)(2,1)S(1)}, u32[]{:S(2)}, u32[]{:S(2)}) %collective-permute-start.10) | collective-permute-done | bytes 458784 | tf_op jit(solution)/shard_map/ppermute | solution.py:26
  56.7 7.5 %collective-permute-done.11.refs_4_ = bf16[4,64,896]{2,1,0:T(8,128)(2,1)S(1)} collective-permute-done((bf16[4,64,896]{2,1,0:T(8,128)(2,1)S(1)}, bf16[4,64,896]{2,1,0:T(8,128)(2,1)S(1)}, u32[]{:S(2)}, u32[]{:S(2)}) %collective-permute-start.11) | collective-permute-done | bytes 458784 | tf_op jit(solution)/shard_map/ppermute | solution.py:26
  64.2 2.2 collective-permute-done.9.refs_2_
  67.5 1.8 collective-permute-start.13
  72.5 2.4 %collective-permute-start.7 = (bf16[64,896]{1,0:T(8,128)(2,1)S(1)}, bf16[64,896]{1,0:T(8,128)(2,1)S(1)}, u32[]{:S(2)}, u32[]{:S(2)}) collective-permute-start(bf16[64,896]{1,0:T(8,128)(2,1)S(1)} %get-tuple-element.34), channel_id=1, source_target_pairs={{0,64},{32,96},{64,0},{96,32},{1,65},{33,97},{65,1},{97,33},{2,66}... | collective-permute-start | bytes 344072 | tf_op jit(solution)/shard_map/ppermute | solution.py:26
  76.2 2.8 %collective-permute-done.7.refs_2_ = bf16[64,896]{1,0:T(8,128)(2,1)S(1)} collective-permute-done((bf16[64,896]{1,0:T(8,128)(2,1)S(1)}, bf16[64,896]{1,0:T(8,128)(2,1)S(1)}, u32[]{:S(2)}, u32[]{:S(2)}) %collective-permute-start.7) | collective-permute-done | bytes 114720 | tf_op jit(solution)/shard_map/ppermute | solution.py:26
  79.8 11.7 %all_to_all.25.src = bf16[8,112,128]{2,1,0:T(8,128)(2,1)S(1)} all-to-all(bf16[8,112,128]{2,1,0:T(8,128)(2,1)S(1)} %bitcast.36), channel_id=1, replica_groups=mesh['zl'=2,'y'=4,'c'=2,'x'=4,'zh'=4] {'zh','zl'}, dimensions={0} | all-to-all | bytes 458752 | tf_op jit(solution)/shard_map/all_to_all | solution.py:34
  91.5 17.5 %all_to_all.26 = bf16[16,112,128]{2,1,0:T(8,128)(2,1)} all-to-all(bf16[16,112,128]{2,1,0:T(8,128)(2,1)S(1)} %sum_spread.1), channel_id=1, replica_groups=mesh['zl'=2,'y'=4,'c'=2,'x'=4,'zh'=4] {'zl','y','c'}, dimensions={0} | all-to-all | bytes 917504 | tf_op jit(solution)/shard_map/all_to_all | solution.py:34
  109.0 2.8 %send_blocks.1 = bf16[2,4,2,120,256]{4,3,2,1,0:T(8,128)(2,1)} custom-call(s32[4]{0:T(128)} %copy-done.9, bf16[2,4,2,112,128]{4,3,2,1,0:T(8,128)(2,1)} %bitcast.34), custom_call_target="tpu_custom_call" | custom-call | flops 917504 | bytes 1835008 | tf_op jit(solution)/shard_map/send_blocks/pallas_call | solution.py:270
  111.8 4.3 %all-to-all-start.4 = ((bf16[16,120,256]{2,1,0:T(8,128)(2,1)}), bf16[16,120,256]{2,1,0:T(8,128)(2,1)}, u32[]{:S(2)}, u32[]{:S(2)}) async-start(bf16[16,120,256]{2,1,0:T(8,128)(2,1)} %bitcast.38), calls=%async_computation.4 | async-start | bytes 1966080 | tf_op jit(solution)/shard_map/all_to_all | solution.py:34
  116.2 1.6 rest_blocks.1
  117.8 2.2 collective-permute-start.16
  120.0 3.3 %collective-permute-start.17 = (bf16[2,3,112,256]{3,2,1,0:T(8,128)(2,1)S(1)}, bf16[2,3,112,256]{3,2,1,0:T(8,128)(2,1)S(1)}, u32[]{:S(2)}, u32[]{:S(2)}) collective-permute-start(bf16[2,3,112,256]{3,2,1,0:T(8,128)(2,1)S(1)} %get-tuple-element.46), channel_id=1, source_target_pairs={{0,2},{1,3},{2,0},{3,1},{4,6},{5,7},{6,4},{7,5},{8,10},{9,11},{10,... | collective-permute-start | bytes 1032200 | tf_op jit(solution)/shard_map/ppermute | solution.py:26
  123.3 3.3 %collective-permute-start.18 = (bf16[2,3,112,256]{3,2,1,0:T(8,128)(2,1)S(1)}, bf16[2,3,112,256]{3,2,1,0:T(8,128)(2,1)S(1)}, u32[]{:S(2)}, u32[]{:S(2)}) collective-permute-start(bf16[2,3,112,256]{3,2,1,0:T(8,128)(2,1)S(1)} %get-tuple-element.47), channel_id=1, source_target_pairs={{0,3},{1,0},{2,1},{3,2},{4,7},{5,4},{6,5},{7,6},{8,11},{9,8},{10,9... | collective-permute-start | bytes 1032200 | tf_op jit(solution)/shard_map/ppermute | solution.py:26
  126.6 44.4 %collective-permute-done.16.refs_1_ = bf16[2,3,112,256]{3,2,1,0:T(8,128)(2,1)S(1)} collective-permute-done((bf16[2,3,112,256]{3,2,1,0:T(8,128)(2,1)S(1)}, bf16[2,3,112,256]{3,2,1,0:T(8,128)(2,1)S(1)}, u32[]{:S(2)}, u32[]{:S(2)}) %collective-permute-start.16) | collective-permute-done | bytes 344096 | tf_op jit(solution)/shard_map/ppermute | solution.py:26
  171.0 3.5 %regroup.1 = (bf16[4,3,112,256]{3,2,1,0:T(8,128)(2,1)}, bf16[4,3,112,256]{3,2,1,0:T(8,128)(2,1)}) custom-call(s32[4]{0:T(128)S(1)} %copy-done.10, f32[1,4]{1,0:T(1,128)S(1)} %mark.1.after, bf16[2,3,112,256]{3,2,1,0:T(8,128)(2,1)S(1)} %get-tuple-element.44.refs_0_, bf16[2,3,112,256]{3,2,1,0:T(8,128)(2,1)S(1)} %collective-permute-done.16.refs_1_, ...), custom_call_target="tpu_custom_call" | custom-call | flops 172032 | bytes 2752512 | tf_op jit(solution)/shard_map/regroup/pallas_call | solution.py:384
  174.5 3.1 %collective-permute-start.20 = (bf16[4,3,112,256]{3,2,1,0:T(8,128)(2,1)}, bf16[4,3,112,256]{3,2,1,0:T(8,128)(2,1)}, u32[]{:S(2)}, u32[]{:S(2)}) collective-permute-start(bf16[4,3,112,256]{3,2,1,0:T(8,128)(2,1)} %get-tuple-element.48.refs_0_.refs_4_), channel_id=1, source_target_pairs={{0,8},{4,12},{8,0},{12,4},{1,9},{5,13},{9,1},{13,5},{2,10},{6,14},... | collective-permute-start | bytes 2064392 | tf_op jit(solution)/shard_map/ppermute | solution.py:26
  178.0 2.3 collective-permute-start.21
  180.2 1.4 collective-permute-start.15
  181.6 11.3 %collective-permute-done.20.refs_2_.refs_6_ = bf16[4,3,112,256]{3,2,1,0:T(8,128)(2,1)} collective-permute-done((bf16[4,3,112,256]{3,2,1,0:T(8,128)(2,1)}, bf16[4,3,112,256]{3,2,1,0:T(8,128)(2,1)}, u32[]{:S(2)}, u32[]{:S(2)}) %collective-permute-start.20) | collective-permute-done | bytes 688160 | tf_op jit(solution)/shard_map/ppermute | solution.py:26
  192.9 2.3 %collective-permute-start.24 = (bf16[4,3,112,256]{3,2,1,0:T(8,128)(2,1)}, bf16[4,3,112,256]{3,2,1,0:T(8,128)(2,1)S(1)}, u32[]{:S(2)}, u32[]{:S(2)}) collective-permute-start(bf16[4,3,112,256]{3,2,1,0:T(8,128)(2,1)} %collective-permute-done.20.refs_2_.refs_6_), channel_id=1, source_target_pairs={{0,16},{16,0},{1,17},{17,1},{2,18},{18,2},{3,19},{19,3},{4,20},{20... | collective-permute-start | bytes 2064392 | tf_op jit(solution)/shard_map/ppermute | solution.py:21
  195.3 13.2 %collective-permute-done.19.refs_1_.refs_5_ = bf16[4,3,112,256]{3,2,1,0:T(8,128)(2,1)} collective-permute-done((bf16[4,3,112,256]{3,2,1,0:T(8,128)(2,1)}, bf16[4,3,112,256]{3,2,1,0:T(8,128)(2,1)}, u32[]{:S(2)}, u32[]{:S(2)}) %collective-permute-start.19) | collective-permute-done | bytes 688160 | tf_op jit(solution)/shard_map/ppermute | solution.py:26
  209.5 1.5 collective-permute-done.23.refs_5_.refs_9_
  212.1 6.9 %place_rest.1.refs_12_ = bf16[3,4,4,2,112,256]{5,4,3,2,1,0:T(8,128)(2,1)} custom-call(s32[4]{0:T(128)} %copy-done.9, bf16[4,3,112,256]{3,2,1,0:T(8,128)(2,1)} %get-tuple-element.48.refs_0_.refs_4_, bf16[4,3,112,256]{3,2,1,0:T(8,128)(2,1)} %collective-permute-done.19.refs_1_.refs_5_, bf16[4,3,112,256]{3,2,1,0:T(8,128)(2,1)} %collective-permute-done.20.refs_2_.refs_6_, ...), custom_call_target="tpu_custom_call" | custom-call | flops 344064 | bytes 11010048 | tf_op jit(solution)/shard_map/place_rest/pallas_call | solution.py:419
  219.1 2.0 update.1
  221.2 5.2 %finish.1 = bf16[3,4,4,2,112,256]{5,4,3,2,1,0:T(8,128)(2,1)} custom-call(s32[4]{0:T(128)S(1)} %copy-done.11, bf16[16,120,256]{2,1,0:T(8,128)(2,1)} %all-to-all-done.4.refs_0_.refs_1_.refs_2_, bf16[16,120,256]{2,1,0:T(8,128)(2,1)} %all-to-all-done.4.refs_0_.refs_1_.refs_2_, ...), custom_call_target="tpu_custom_call", output_to_operand_aliasing={{}: (12, {})} | custom-call | flops 3932160 | bytes 11796480 | tf_op jit(solution)/shard_map/finish/pallas_call | solution.py:458
  (88 shorter events, 26.1 us)
Async XLA Ops:
  0.6 33.1 %collective-permute-start.2 = (bf16[448,3584]{1,0:T(8,128)(2,1)}, bf16[448,3584]{1,0:T(8,128)(2,1)}, u32[]{:S(2)}, u32[]{:S(2)}) collective-permute-start(bf16[448,3584]{1,0:T(8,128)(2,1)} %hid_a.1), channel_id=1, source_target_pairs={{0,16},{16,0},{1,17},{17,1},{2,18},{18,2},{3,19},{19,3},{4,20},{20... | collective-permute-start | bytes 9633800 | tf_op jit(solution)/shard_map/ppermute | solution.py:21
  1.4 26.1 %collective-permute-start.1 = (bf16[448,1024]{1,0:T(8,128)(2,1)}, bf16[448,1024]{1,0:T(8,128)(2,1)S(1)}, u32[]{:S(2)}, u32[]{:S(2)}) collective-permute-start(bf16[448,1024]{1,0:T(8,128)(2,1)} %cot_a.1), channel_id=1, source_target_pairs={{0,16},{16,0},{1,17},{17,1},{2,18},{18,2},{3,19},{19,3},{4,20},{20... | collective-permute-start | bytes 2752520 | tf_op jit(solution)/shard_map/ppermute | solution.py:21
  3.5 13.2 %all-to-all-start = ((f32[16,3,128]{2,1,0:T(4,128)}), f32[16,3,128]{2,1,0:T(4,128)S(1)}, u32[]{:S(2)}, u32[]{:S(2)}) async-start(f32[16,3,128]{2,1,0:T(4,128)} %group_sums.1), calls=%async_computation | async-start | bytes 65536 | tf_op jit(solution)/shard_map/all_to_all | solution.py:34
  15.8 15.4 %collective-permute-start = (f32[8,448]{1,0:T(8,128)S(1)}, f32[8,448]{1,0:T(8,128)S(1)}, u32[]{:S(2)}, u32[]{:S(2)}) collective-permute-start(f32[8,448]{1,0:T(8,128)S(1)} %stack.41.tok_a), channel_id=1, source_target_pairs={{0,16},{16,0},{1,17},{17,1},{2,18},{18,2},{3,19},{19,3},{4,20},{20... | collective-permute-start | bytes 43016 | tf_op jit(solution)/shard_map/ppermute | solution.py:21
  17.4 16.3 %all-to-all-start.1 = ((f32[16,3,128]{2,1,0:T(4,128)}), f32[16,3,128]{2,1,0:T(4,128)S(1)}, u32[]{:S(2)}, u32[]{:S(2)}) async-start(f32[16,3,128]{2,1,0:T(4,128)} %stats_spread.1), calls=%async_computation.1 | async-start | bytes 65536 | tf_op jit(solution)/shard_map/all_to_all | solution.py:34
  27.5 43.0 %copy-start.9 = (s32[4]{0:T(128)}, s32[4]{0:T(128)S(1)}, u32[]{:S(2)}) copy-start(s32[4]{0:T(128)S(1)} %pad_add_fusion.pos.refs_0_) | copy-start | bytes 52
  42.5 13.3 %collective-permute-start.10 = (bf16[4,64,896]{2,1,0:T(8,128)(2,1)S(1)}, bf16[4,64,896]{2,1,0:T(8,128)(2,1)S(1)}, u32[]{:S(2)}, u32[]{:S(2)}) collective-permute-start(bf16[4,64,896]{2,1,0:T(8,128)(2,1)S(1)} %get-tuple-element.38), channel_id=1, source_target_pairs={{0,64},{32,96},{64,0},{96,32},{1,65},{33,97},{65,1},{97,33},{2,66}... | collective-permute-start | bytes 1376264 | tf_op jit(solution)/shard_map/ppermute | solution.py:26
  43.8 20.4 %collective-permute-start.11 = (bf16[4,64,896]{2,1,0:T(8,128)(2,1)S(1)}, bf16[4,64,896]{2,1,0:T(8,128)(2,1)S(1)}, u32[]{:S(2)}, u32[]{:S(2)}) collective-permute-start(bf16[4,64,896]{2,1,0:T(8,128)(2,1)S(1)} %get-tuple-element.39), channel_id=1, source_target_pairs={{0,96},{32,0},{64,32},{96,64},{1,97},{33,1},{65,33},{97,65},{2,98}... | collective-permute-start | bytes 1376264 | tf_op jit(solution)/shard_map/ppermute | solution.py:26
  45.2 21.1 %collective-permute-start.9 = (bf16[4,64,896]{2,1,0:T(8,128)(2,1)S(1)}, bf16[4,64,896]{2,1,0:T(8,128)(2,1)S(1)}, u32[]{:S(2)}, u32[]{:S(2)}) collective-permute-start(bf16[4,64,896]{2,1,0:T(8,128)(2,1)S(1)} %get-tuple-element.37), channel_id=1, source_target_pairs={{0,32},{32,64},{64,96},{96,0},{1,33},{33,65},{65,97},{97,1},{2,34}... | collective-permute-start | bytes 1376264 | tf_op jit(solution)/shard_map/ppermute | solution.py:26
  45.2 24.1 %collective-permute-start.3 = (bf16[4,64,896]{2,1,0:T(8,128)(2,1)S(1)}, bf16[4,64,896]{2,1,0:T(8,128)(2,1)S(1)}, u32[]{:S(2)}, u32[]{:S(2)}) collective-permute-start(bf16[4,64,896]{2,1,0:T(8,128)(2,1)S(1)} %get-tuple-element.29), channel_id=1, source_target_pairs={{0,4},{4,8},{8,12},{12,0},{1,5},{5,9},{9,13},{13,1},{2,6},{6,10},{... | collective-permute-start | bytes 1376264 | tf_op jit(solution)/shard_map/ppermute | solution.py:26
  46.4 24.1 %collective-permute-start.4 = (bf16[4,64,896]{2,1,0:T(8,128)(2,1)S(1)}, bf16[4,64,896]{2,1,0:T(8,128)(2,1)S(1)}, u32[]{:S(2)}, u32[]{:S(2)}) collective-permute-start(bf16[4,64,896]{2,1,0:T(8,128)(2,1)S(1)} %get-tuple-element.30), channel_id=1, source_target_pairs={{0,8},{4,12},{8,0},{12,4},{1,9},{5,13},{9,1},{13,5},{2,10},{6,14},... | collective-permute-start | bytes 1376264 | tf_op jit(solution)/shard_map/ppermute | solution.py:26
  55.8 14.7 %collective-permute-start.5 = (bf16[4,64,896]{2,1,0:T(8,128)(2,1)S(1)}, bf16[4,64,896]{2,1,0:T(8,128)(2,1)S(1)}, u32[]{:S(2)}, u32[]{:S(2)}) collective-permute-start(bf16[4,64,896]{2,1,0:T(8,128)(2,1)S(1)} %get-tuple-element.31), channel_id=1, source_target_pairs={{0,12},{4,0},{8,4},{12,8},{1,13},{5,1},{9,5},{13,9},{2,14},{6,2},{... | collective-permute-start | bytes 1376264 | tf_op jit(solution)/shard_map/ppermute | solution.py:26
  67.1 7.8 %collective-permute-start.12 = (bf16[64,896]{1,0:T(8,128)(2,1)S(1)}, bf16[64,896]{1,0:T(8,128)(2,1)S(1)}, u32[]{:S(2)}, u32[]{:S(2)}) collective-permute-start(bf16[64,896]{1,0:T(8,128)(2,1)S(1)} %get-tuple-element.41), channel_id=1, source_target_pairs={{0,4},{4,8},{8,12},{12,0},{1,5},{5,9},{9,13},{13,1},{2,6},{6,10},{... | collective-permute-start | bytes 344072 | tf_op jit(solution)/shard_map/ppermute | solution.py:26
  67.5 8.7 %collective-permute-start.13 = (bf16[64,896]{1,0:T(8,128)(2,1)S(1)}, bf16[64,896]{1,0:T(8,128)(2,1)S(1)}, u32[]{:S(2)}, u32[]{:S(2)}) collective-permute-start(bf16[64,896]{1,0:T(8,128)(2,1)S(1)} %get-tuple-element.42), channel_id=1, source_target_pairs={{0,8},{4,12},{8,0},{12,4},{1,9},{5,13},{9,1},{13,5},{2,10},{6,14},... | collective-permute-start | bytes 344072 | tf_op jit(solution)/shard_map/ppermute | solution.py:26
  69.3 6.8 %collective-permute-start.14 = (bf16[64,896]{1,0:T(8,128)(2,1)S(1)}, bf16[64,896]{1,0:T(8,128)(2,1)S(1)}, u32[]{:S(2)}, u32[]{:S(2)}) collective-permute-start(bf16[64,896]{1,0:T(8,128)(2,1)S(1)} %get-tuple-element.43), channel_id=1, source_target_pairs={{0,12},{4,0},{8,4},{12,8},{1,13},{5,1},{9,5},{13,9},{2,14},{6,2},{... | collective-permute-start | bytes 344072 | tf_op jit(solution)/shard_map/ppermute | solution.py:26
  71.3 4.9 %collective-permute-start.6 = (bf16[64,896]{1,0:T(8,128)(2,1)S(1)}, bf16[64,896]{1,0:T(8,128)(2,1)S(1)}, u32[]{:S(2)}, u32[]{:S(2)}) collective-permute-start(bf16[64,896]{1,0:T(8,128)(2,1)S(1)} %get-tuple-element.33), channel_id=1, source_target_pairs={{0,32},{32,64},{64,96},{96,0},{1,33},{33,65},{65,97},{97,1},{2,34}... | collective-permute-start | bytes 344072 | tf_op jit(solution)/shard_map/ppermute | solution.py:26
  72.5 6.5 %collective-permute-start.7 = (bf16[64,896]{1,0:T(8,128)(2,1)S(1)}, bf16[64,896]{1,0:T(8,128)(2,1)S(1)}, u32[]{:S(2)}, u32[]{:S(2)}) collective-permute-start(bf16[64,896]{1,0:T(8,128)(2,1)S(1)} %get-tuple-element.34), channel_id=1, source_target_pairs={{0,64},{32,96},{64,0},{96,32},{1,65},{33,97},{65,1},{97,33},{2,66}... | collective-permute-start | bytes 344072 | tf_op jit(solution)/shard_map/ppermute | solution.py:26
  74.9 4.6 %collective-permute-start.8 = (bf16[64,896]{1,0:T(8,128)(2,1)S(1)}, bf16[64,896]{1,0:T(8,128)(2,1)S(1)}, u32[]{:S(2)}, u32[]{:S(2)}) collective-permute-start(bf16[64,896]{1,0:T(8,128)(2,1)S(1)} %get-tuple-element.35), channel_id=1, source_target_pairs={{0,96},{32,0},{64,32},{96,64},{1,97},{33,1},{65,33},{97,65},{2,98}... | collective-permute-start | bytes 344072 | tf_op jit(solution)/shard_map/ppermute | solution.py:26
  79.6 36.6 %copy-start.10 = (s32[4]{0:T(128)S(1)}, s32[4]{0:T(128)}, u32[]{:S(2)}) copy-start(s32[4]{0:T(128)} %copy-done.9) | copy-start | bytes 52
  111.8 68.5 %all-to-all-start.4 = ((bf16[16,120,256]{2,1,0:T(8,128)(2,1)}), bf16[16,120,256]{2,1,0:T(8,128)(2,1)}, u32[]{:S(2)}, u32[]{:S(2)}) async-start(bf16[16,120,256]{2,1,0:T(8,128)(2,1)} %bitcast.38), calls=%async_computation.4 | async-start | bytes 1966080 | tf_op jit(solution)/shard_map/all_to_all | solution.py:34
  117.8 53.1 %collective-permute-start.16 = (bf16[2,3,112,256]{3,2,1,0:T(8,128)(2,1)S(1)}, bf16[2,3,112,256]{3,2,1,0:T(8,128)(2,1)S(1)}, u32[]{:S(2)}, u32[]{:S(2)}) collective-permute-start(bf16[2,3,112,256]{3,2,1,0:T(8,128)(2,1)S(1)} %get-tuple-element.45), channel_id=1, source_target_pairs={{0,1},{1,2},{2,3},{3,0},{4,5},{5,6},{6,7},{7,4},{8,9},{9,10},{10,1... | collective-permute-start | bytes 1032200 | tf_op jit(solution)/shard_map/ppermute | solution.py:26
  120.0 51.0 %collective-permute-start.17 = (bf16[2,3,112,256]{3,2,1,0:T(8,128)(2,1)S(1)}, bf16[2,3,112,256]{3,2,1,0:T(8,128)(2,1)S(1)}, u32[]{:S(2)}, u32[]{:S(2)}) collective-permute-start(bf16[2,3,112,256]{3,2,1,0:T(8,128)(2,1)S(1)} %get-tuple-element.46), channel_id=1, source_target_pairs={{0,2},{1,3},{2,0},{3,1},{4,6},{5,7},{6,4},{7,5},{8,10},{9,11},{10,... | collective-permute-start | bytes 1032200 | tf_op jit(solution)/shard_map/ppermute | solution.py:26
  123.3 47.7 %collective-permute-start.18 = (bf16[2,3,112,256]{3,2,1,0:T(8,128)(2,1)S(1)}, bf16[2,3,112,256]{3,2,1,0:T(8,128)(2,1)S(1)}, u32[]{:S(2)}, u32[]{:S(2)}) collective-permute-start(bf16[2,3,112,256]{3,2,1,0:T(8,128)(2,1)S(1)} %get-tuple-element.47), channel_id=1, source_target_pairs={{0,3},{1,0},{2,1},{3,2},{4,7},{5,4},{6,5},{7,6},{8,11},{9,8},{10,9... | collective-permute-start | bytes 1032200 | tf_op jit(solution)/shard_map/ppermute | solution.py:26
  174.5 18.5 %collective-permute-start.20 = (bf16[4,3,112,256]{3,2,1,0:T(8,128)(2,1)}, bf16[4,3,112,256]{3,2,1,0:T(8,128)(2,1)}, u32[]{:S(2)}, u32[]{:S(2)}) collective-permute-start(bf16[4,3,112,256]{3,2,1,0:T(8,128)(2,1)} %get-tuple-element.48.refs_0_.refs_4_), channel_id=1, source_target_pairs={{0,8},{4,12},{8,0},{12,4},{1,9},{5,13},{9,1},{13,5},{2,10},{6,14},... | collective-permute-start | bytes 2064392 | tf_op jit(solution)/shard_map/ppermute | solution.py:26
  177.6 41.5 %copy-start.1 = (bf16[16,112,128]{2,1,0:T(8,128)(2,1)S(1)}, bf16[16,112,128]{2,1,0:T(8,128)(2,1)}, u32[]{:S(2)}) copy-start(bf16[16,112,128]{2,1,0:T(8,128)(2,1)} %all_to_all.26) | copy-start | bytes 1376260
  177.6 31.0 %collective-permute-start.19 = (bf16[4,3,112,256]{3,2,1,0:T(8,128)(2,1)}, bf16[4,3,112,256]{3,2,1,0:T(8,128)(2,1)}, u32[]{:S(2)}, u32[]{:S(2)}) collective-permute-start(bf16[4,3,112,256]{3,2,1,0:T(8,128)(2,1)} %get-tuple-element.49), channel_id=1, source_target_pairs={{0,4},{4,8},{8,12},{12,0},{1,5},{5,9},{9,13},{13,1},{2,6},{6,10},{... | collective-permute-start | bytes 2064392 | tf_op jit(solution)/shard_map/ppermute | solution.py:26
  178.0 31.0 %collective-permute-start.21 = (bf16[4,3,112,256]{3,2,1,0:T(8,128)(2,1)}, bf16[4,3,112,256]{3,2,1,0:T(8,128)(2,1)}, u32[]{:S(2)}, u32[]{:S(2)}) collective-permute-start(bf16[4,3,112,256]{3,2,1,0:T(8,128)(2,1)} %get-tuple-element.49), channel_id=1, source_target_pairs={{0,12},{4,0},{8,4},{12,8},{1,13},{5,1},{9,5},{13,9},{2,14},{6,2},{... | collective-permute-start | bytes 2064392 | tf_op jit(solution)/shard_map/ppermute | solution.py:26
  180.2 40.9 %collective-permute-start.15 = (bf16[16,120,256]{2,1,0:T(8,128)(2,1)}, bf16[16,120,256]{2,1,0:T(8,128)(2,1)}, u32[]{:S(2)}, u32[]{:S(2)}) collective-permute-start(bf16[16,120,256]{2,1,0:T(8,128)(2,1)} %all-to-all-done.4.refs_0_.refs_1_.refs_2_), channel_id=1, source_target_pairs={{0,16},{16,0},{1,17},{17,1},{2,18},{18,2},{3,19},{19,3},{4,20},{20... | collective-permute-start | bytes 2949128 | tf_op jit(solution)/shard_map/ppermute | solution.py:21
  181.6 27.9 %collective-permute-start.22 = (bf16[4,3,112,256]{3,2,1,0:T(8,128)(2,1)}, bf16[4,3,112,256]{3,2,1,0:T(8,128)(2,1)S(1)}, u32[]{:S(2)}, u32[]{:S(2)}) collective-permute-start(bf16[4,3,112,256]{3,2,1,0:T(8,128)(2,1)} %get-tuple-element.48.refs_0_.refs_4_), channel_id=1, source_target_pairs={{0,16},{16,0},{1,17},{17,1},{2,18},{18,2},{3,19},{19,3},{4,20},{20... | collective-permute-start | bytes 2064392 | tf_op jit(solution)/shard_map/ppermute | solution.py:21
  192.9 16.5 %collective-permute-start.24 = (bf16[4,3,112,256]{3,2,1,0:T(8,128)(2,1)}, bf16[4,3,112,256]{3,2,1,0:T(8,128)(2,1)S(1)}, u32[]{:S(2)}, u32[]{:S(2)}) collective-permute-start(bf16[4,3,112,256]{3,2,1,0:T(8,128)(2,1)} %collective-permute-done.20.refs_2_.refs_6_), channel_id=1, source_target_pairs={{0,16},{16,0},{1,17},{17,1},{2,18},{18,2},{3,19},{19,3},{4,20},{20... | collective-permute-start | bytes 2064392 | tf_op jit(solution)/shard_map/ppermute | solution.py:21
  208.5 2.5 %collective-permute-start.23 = (bf16[4,3,112,256]{3,2,1,0:T(8,128)(2,1)}, bf16[4,3,112,256]{3,2,1,0:T(8,128)(2,1)S(1)}, u32[]{:S(2)}, u32[]{:S(2)}) collective-permute-start(bf16[4,3,112,256]{3,2,1,0:T(8,128)(2,1)} %collective-permute-done.19.refs_1_.refs_5_), channel_id=1, source_target_pairs={{0,16},{16,0},{1,17},{17,1},{2,18},{18,2},{3,19},{19,3},{4,20},{20... | collective-permute-start | bytes 2064392 | tf_op jit(solution)/shard_map/ppermute | solution.py:21
  209.0 3.1 %collective-permute-start.25 = (bf16[4,3,112,256]{3,2,1,0:T(8,128)(2,1)}, bf16[4,3,112,256]{3,2,1,0:T(8,128)(2,1)}, u32[]{:S(2)}, u32[]{:S(2)}) collective-permute-start(bf16[4,3,112,256]{3,2,1,0:T(8,128)(2,1)} %collective-permute-done.21.refs_3_.refs_7_), channel_id=1, source_target_pairs={{0,16},{16,0},{1,17},{17,1},{2,18},{18,2},{3,19},{19,3},{4,20},{20... | collective-permute-start | bytes 2064392 | tf_op jit(solution)/shard_map/ppermute | solution.py:21
  (14 other events, 65.7 us)
